TPU v7x, 32 devices: a whole 2x2x4 slice. The times are simulated.
32 devices in a mesh: dp: 8 (over y, x, core), tensor: 4 (over z).
Axes of the slice: x: 2, y: 2, z: 4, core: 2. Of those that a mesh axis runs over, the one named last changes fastest.
Arguments:
- hidden_in: bfloat16 [24576, 1536], P(('dp', 'tensor')), may hold values from -6 to 6
- out_grad: bfloat16 [24576, 1536], P(('dp', 'tensor')), may hold values from -6 to 6
- segment_ids: int32 [8, 1024], P('dp'), may hold values from 0 to 3, never falling along the last dimension, each value on 1 to 512 neighbouring positions
- expert_ids: int32 [24576, 8], P('dp'), may hold values from 0 to 39, all different within a row
- fill_order: int32 [8, 24576], P('dp'), may hold values from 0 to 24575, each once within a row
- attention_gain: bfloat16 [1536], P('dp'), may hold values from 0.5 to 1.5
- query_weight: bfloat16 [1536, 1536], P('dp', 'tensor'), may hold values from -0.625 to 0.625
- key_weight: bfloat16 [1536, 512], P('dp', 'tensor'), may hold values from -0.625 to 0.625
- value_weight: bfloat16 [1536, 512], P('dp', 'tensor'), may hold values from -0.15625 to 0.15625
- output_weight: bfloat16 [1536, 1536], P('tensor', 'dp'), may hold values from -3 to 3
- mixture_gain: bfloat16 [1536], P('dp'), may hold values from 0.5 to 1.5
- router_weight: bfloat16 [1536, 40], P('dp'), may hold values from -0.079589844 to 0.079589844
- gate_weight: bfloat16 [40, 1536, 512], P('tensor', 'dp'), may hold values from -0.15625 to 0.15625
- up_weight: bfloat16 [40, 1536, 512], P('tensor', 'dp'), may hold values from -0.15625 to 0.15625
- down_weight: bfloat16 [40, 512, 1536], P('tensor', None, 'dp'), may hold values from -4 to 4
Outputs:
- block_output: bfloat16 [24576, 1536], P(('dp', 'tensor'))
- input_grad: float32 [24576, 1536], P(('dp', 'tensor'))
- attention_gain_grad: float32 [1536], P(('dp', 'tensor'))
- query_weight_grad: float32 [1536, 1536], P('dp', 'tensor')
- key_weight_grad: float32 [1536, 512], P('dp', 'tensor')
- value_weight_grad: float32 [1536, 512], P('dp', 'tensor')
- output_weight_grad: float32 [1536, 1536], P('tensor', 'dp')
- mixture_gain_grad: float32 [1536], P(('dp', 'tensor'))
- router_weight_grad: float32 [1536, 40], P(('dp', 'tensor'))
- gate_weight_grad: float32 [40, 1536, 512], P('tensor', 'dp')
- up_weight_grad: float32 [40, 1536, 512], P('tensor', 'dp')
- down_weight_grad: float32 [40, 512, 1536], P('tensor', None, 'dp')
Inputs may be any that keep to these rules, and one draw needn't show every extreme that they name: `segment_ids`: within a group the continuation numbers never fall; each of the 4 numbers labels 1 to 512 positions. `expert_ids`: A token's 8 experts are distinct. `fill_order`: each row lists every pair number t * 8 + k of the group's tokens once.
All inputs are finite; a program needn't handle non-finite values.
Results may differ from a plain program's by a relative error of at most 0.022.
Values may be sent and summed in bfloat16 or wider, within the bound.
A program may use at most 640 MiB of HBM per device.

v0:
```python
import jax
import jax.numpy as jnp
from jax import lax
from jax.sharding import PartitionSpec as P

D = 1536
HD = 64
EXPERTS = 40
TOPK = 8
PROMPT = 2048
NCONT = 4
QBLK = 512
EBLK = 1
TOK_GRP = 3072
CAP = 768


ATTN_SCALE = 0.015625
RESIDUAL_SCALE = 0.22
NORM_EPS = 1e-06
ROPE_BASE = 10000.0
MASKED = -1e30
HIGHEST = lax.Precision.HIGHEST


def rms_forward(values, gain_row):
    inverse_rms = lax.rsqrt(jnp.mean(values * values, axis=-1, keepdims=True) + NORM_EPS)
    unit_rows = values * inverse_rms
    return (unit_rows * gain_row, unit_rows, inverse_rms)


def rms_backward(gradient, unit_rows, inverse_rms, gain_row):
    gain_grad = jnp.sum(gradient * unit_rows, axis=0)
    scaled = gradient * gain_row
    mean_term = jnp.mean(scaled * unit_rows, axis=-1, keepdims=True)
    return (inverse_rms * (scaled - unit_rows * mean_term), gain_grad)


def group_layout(segment_row, prompt_length):
    cont_length = segment_row.shape[0]
    segment_marks = (segment_row[:, None] == jnp.arange(NCONT, dtype=jnp.int32)[None, :]).astype(
        jnp.int32
    )
    segment_sizes = jnp.sum(segment_marks, axis=0)
    segment_starts = jnp.cumsum(segment_sizes) - segment_sizes
    token_starts = jnp.sum(segment_marks * segment_starts[None, :], axis=1)
    inside = jnp.arange(cont_length, dtype=jnp.int32) - token_starts
    positions = jnp.concatenate(
        [jnp.arange(prompt_length, dtype=jnp.int32), prompt_length + inside]
    )
    segments = jnp.concatenate([jnp.zeros((prompt_length,), jnp.int32), segment_row + 1])
    return (positions, segments)


def allowed(query_index, query_segment, key_index, key_segment):
    causal = key_index[None, :] <= query_index[:, None]
    shared = (key_segment[None, :] == 0) | (key_segment[None, :] == query_segment[:, None])
    return causal & shared


def rope_tables(positions, head_size):
    halfway = head_size // 2
    frequency = ROPE_BASE ** (-(2.0 * jnp.arange(halfway, dtype=jnp.float32)) / head_size)
    angles = positions.astype(jnp.float32)[:, None] * frequency[None, :]
    return (jnp.cos(angles), jnp.sin(angles))


def rotate(values, cosine_table, sine_table):
    halfway = values.shape[-1] // 2
    first_half = values[..., :halfway]
    second_half = values[..., halfway:]
    cosine_part = cosine_table[:, None, :]
    sine_part = sine_table[:, None, :]
    return jnp.concatenate(
        [
            first_half * cosine_part - second_half * sine_part,
            second_half * cosine_part + first_half * sine_part,
        ],
        axis=-1,
    )


def rotate_back(gradient, cosine_table, sine_table):
    halfway = gradient.shape[-1] // 2
    first_half = gradient[..., :halfway]
    second_half = gradient[..., halfway:]
    cosine_part = cosine_table[:, None, :]
    sine_part = sine_table[:, None, :]
    return jnp.concatenate(
        [
            first_half * cosine_part + second_half * sine_part,
            second_half * cosine_part - first_half * sine_part,
        ],
        axis=-1,
    )


def silu_slope(values):
    sigmoid_part = jax.nn.sigmoid(values)
    return sigmoid_part * (1.0 + values * (1.0 - sigmoid_part))


def route_slots(expert_row, order_row):
    pair_count = expert_row.shape[0] * expert_row.shape[1]
    ordered = jnp.take(expert_row.reshape(pair_count), order_row)
    onehot = ordered[:, None] == jnp.arange(EXPERTS, dtype=jnp.int32)[None, :]
    rank_block = 256
    blocks = pair_count // rank_block
    pair_marks = onehot.astype(jnp.bfloat16).reshape(blocks, rank_block, EXPERTS)
    lower_ones = (jnp.arange(rank_block)[:, None] >= jnp.arange(rank_block)[None, :]).astype(
        jnp.bfloat16
    )
    within = jnp.einsum(
        "ij,bje->bie", lower_ones, pair_marks, preferred_element_type=jnp.float32
    ).astype(jnp.int32)
    totals = within[:, -1, :]
    before = jnp.cumsum(totals, axis=0) - totals
    counts = (within + before[:, None, :]).reshape(pair_count, EXPERTS)
    pair_rank = jnp.sum(jnp.where(onehot, counts, 0), axis=1) - 1
    slot_index = jnp.where(pair_rank < CAP, ordered * CAP + pair_rank, EXPERTS * CAP)
    return jnp.full((EXPERTS * CAP,), -1, jnp.int32).at[slot_index].set(order_row, mode="drop")


def block_scores(query_rot, key_rot, segments, row_start, key_end, local_groups, group_ratio):
    queries = query_rot[row_start:key_end].reshape(
        key_end - row_start, local_groups, group_ratio, HD
    )
    raw_scores = (
        jnp.einsum("qgrd,kgd->grqk", queries, key_rot[:key_end], preferred_element_type=jnp.float32)
        * ATTN_SCALE
    )
    visible = allowed(
        jnp.arange(row_start, key_end, dtype=jnp.int32),
        segments[row_start:key_end],
        jnp.arange(key_end, dtype=jnp.int32),
        segments[:key_end],
    )
    return (jnp.where(visible[None, None], raw_scores, MASKED), queries)


def fetch_experts(gate_weight, up_weight, down_weight):
    return (
        lax.all_gather(gate_weight, "dp", axis=1, tiled=True),
        lax.all_gather(up_weight, "dp", axis=1, tiled=True),
        lax.all_gather(down_weight, "dp", axis=2, tiled=True),
    )


def reduce_experts(grads):
    return (
        lax.psum_scatter(
            grads[0].astype(jnp.bfloat16), "dp", scatter_dimension=1, tiled=True
        ).astype(jnp.float32),
        lax.psum_scatter(
            grads[1].astype(jnp.bfloat16), "dp", scatter_dimension=1, tiled=True
        ).astype(jnp.float32),
        lax.psum_scatter(
            grads[2].astype(jnp.bfloat16), "dp", scatter_dimension=2, tiled=True
        ).astype(jnp.float32),
    )


def local(
    hidden_in,
    out_grad,
    segment_ids,
    expert_ids,
    fill_order,
    attention_gain,
    query_weight,
    key_weight,
    value_weight,
    output_weight,
    mixture_gain,
    router_weight,
    gate_weight,
    up_weight,
    down_weight,
):
    local_heads = query_weight.shape[1] // HD
    local_groups = key_weight.shape[1] // HD
    group_ratio = local_heads // local_groups
    block_count = TOK_GRP // QBLK
    local_experts = gate_weight.shape[0]
    block_total = local_experts // EBLK
    slot_rows = EBLK * CAP
    gain_one, query_full, key_full, value_full, output_full, gain_two, router_full = (
        lax.all_gather(attention_gain, "dp", axis=0, tiled=True),
        lax.all_gather(query_weight, "dp", axis=0, tiled=True),
        lax.all_gather(key_weight, "dp", axis=0, tiled=True),
        lax.all_gather(value_weight, "dp", axis=0, tiled=True),
        lax.all_gather(output_weight, "dp", axis=1, tiled=True),
        lax.all_gather(mixture_gain, "dp", axis=0, tiled=True),
        lax.all_gather(router_weight, "dp", axis=0, tiled=True),
    )
    gain_one = gain_one.astype(jnp.float32)
    gain_two = gain_two.astype(jnp.float32)
    residual = hidden_in.astype(jnp.float32)
    normed_shard, unit_one, inverse_one = rms_forward(residual, gain_one)
    normed_full = lax.all_gather(normed_shard.astype(jnp.bfloat16), "tensor", axis=0, tiled=True)
    positions, segments = group_layout(segment_ids[0], PROMPT)
    cosine_table, sine_table = rope_tables(positions, HD)
    query_pre = jnp.dot(normed_full, query_full, preferred_element_type=jnp.float32).reshape(
        TOK_GRP, local_heads, HD
    )
    key_pre = jnp.dot(normed_full, key_full, preferred_element_type=jnp.float32).reshape(
        TOK_GRP, local_groups, HD
    )
    value_low = (
        jnp.dot(normed_full, value_full, preferred_element_type=jnp.float32)
        .astype(jnp.bfloat16)
        .reshape(TOK_GRP, local_groups, HD)
    )
    query_rot = rotate(query_pre, cosine_table, sine_table).astype(jnp.bfloat16)
    key_rot = rotate(key_pre, cosine_table, sine_table).astype(jnp.bfloat16)
    mixed_blocks = []
    logsum_blocks = []
    for block_index in range(block_count):
        row_start = block_index * QBLK
        key_end = row_start + QBLK
        scores, queries = block_scores(
            query_rot, key_rot, segments, row_start, key_end, local_groups, group_ratio
        )
        top_score = jnp.max(scores, axis=-1, keepdims=True)
        shifted_exp = jnp.exp(scores - top_score)
        total_exp = jnp.sum(shifted_exp, axis=-1, keepdims=True)
        soft_weights = (shifted_exp / total_exp).astype(jnp.bfloat16)
        logsum_blocks.append(top_score + jnp.log(total_exp))
        mixed = jnp.einsum(
            "grqk,kgd->qgrd", soft_weights, value_low[:key_end], preferred_element_type=jnp.float32
        )
        mixed_blocks.append(mixed.astype(jnp.bfloat16).reshape(QBLK, local_heads * HD))
    mixed_full = jnp.concatenate(mixed_blocks, axis=0)
    attended = lax.psum_scatter(
        jnp.dot(mixed_full, output_full, preferred_element_type=jnp.float32).astype(jnp.bfloat16),
        "tensor",
        scatter_dimension=0,
        tiled=True,
    ).astype(jnp.float32)
    middle = residual + RESIDUAL_SCALE * attended
    normed_two, unit_two, inverse_two = rms_forward(middle, gain_two)
    mixture_in = lax.all_gather(normed_two.astype(jnp.bfloat16), "tensor", axis=0, tiled=True)
    gate_full, up_full, down_full = fetch_experts(gate_weight, up_weight, down_weight)
    logits = jnp.dot(mixture_in, router_full, preferred_element_type=jnp.float32)
    routed_marks = (
        expert_ids[:, :, None] == jnp.arange(EXPERTS, dtype=jnp.int32)[None, None, :]
    ).astype(jnp.float32)
    routed = jnp.sum(routed_marks * logits[:, None, :], axis=-1)
    gates = jax.nn.softmax(routed, axis=-1)
    slot_pair_all = route_slots(expert_ids, fill_order[0])
    first_slot = lax.axis_index("tensor") * (local_experts * CAP)
    slot_pair = lax.dynamic_slice_in_dim(slot_pair_all, first_slot, local_experts * CAP, 0)
    slot_valid = slot_pair >= 0
    safe_pair = jnp.maximum(slot_pair, 0)
    slot_token = safe_pair // TOPK
    slot_gate = jnp.where(slot_valid, jnp.take(gates.reshape(-1), safe_pair), 0.0)

    def expert_forward(running, block_data):
        gate_block, up_block, down_block, tokens_here, gate_here = block_data
        inputs = jnp.take(mixture_in, tokens_here, axis=0).reshape(EBLK, CAP, D)
        gate_pre = jnp.einsum(
            "ecd,edf->ecf", inputs, gate_block, preferred_element_type=jnp.float32
        )
        up_pre = jnp.einsum("ecd,edf->ecf", inputs, up_block, preferred_element_type=jnp.float32)
        hidden_units = (gate_here[:, :, None] * jax.nn.silu(gate_pre) * up_pre).astype(jnp.bfloat16)
        outputs = jnp.einsum(
            "ecf,efd->ecd", hidden_units, down_block, preferred_element_type=jnp.float32
        )
        running = running.at[tokens_here].add(outputs.reshape(slot_rows, D))
        return (running, (gate_pre, up_pre, hidden_units))

    forward_blocks = (
        gate_full.reshape(block_total, EBLK, D, -1),
        up_full.reshape(block_total, EBLK, D, -1),
        down_full.reshape(block_total, EBLK, -1, D),
        slot_token.reshape(block_total, slot_rows),
        slot_gate.reshape(block_total, EBLK, CAP),
    )
    mixture_sum, kept_pre = lax.scan(
        expert_forward, jnp.zeros((TOK_GRP, D), jnp.float32), forward_blocks
    )
    mixture_part = lax.psum_scatter(
        mixture_sum.astype(jnp.bfloat16), "tensor", scatter_dimension=0, tiled=True
    ).astype(jnp.float32)
    block_output = (middle + RESIDUAL_SCALE * mixture_part).astype(jnp.bfloat16)
    cotangent_full = lax.all_gather(out_grad, "tensor", axis=0, tiled=True)
    gate_full, up_full, down_full = fetch_experts(gate_weight, up_weight, down_weight)

    def expert_backward(carried, block_data):
        grad_rows, pair_grad = carried
        (
            gate_block,
            up_block,
            down_block,
            tokens_here,
            gate_here,
            valid_here,
            pairs_here,
            gate_pre,
            up_pre,
            hidden_units,
        ) = block_data
        inputs = jnp.take(mixture_in, tokens_here, axis=0).reshape(EBLK, CAP, D)
        out_rows = (
            (RESIDUAL_SCALE * jnp.take(cotangent_full, tokens_here, axis=0).astype(jnp.float32))
            .astype(jnp.bfloat16)
            .reshape(EBLK, CAP, D)
        )
        hidden_grad = jnp.einsum(
            "ecd,efd->ecf", out_rows, down_block, preferred_element_type=jnp.float32
        )
        activated = jax.nn.silu(gate_pre)
        gate_grad_slot = jnp.sum(activated * up_pre * hidden_grad, axis=-1).reshape(slot_rows)
        pair_grad = pair_grad.at[pairs_here].add(jnp.where(valid_here, gate_grad_slot, 0.0))
        product_grad = gate_here[:, :, None] * hidden_grad
        gate_pre_grad = (product_grad * up_pre * silu_slope(gate_pre)).astype(jnp.bfloat16)
        up_pre_grad = (product_grad * activated).astype(jnp.bfloat16)
        block_grads = (
            jnp.einsum("ecd,ecf->edf", inputs, gate_pre_grad, preferred_element_type=jnp.float32),
            jnp.einsum("ecd,ecf->edf", inputs, up_pre_grad, preferred_element_type=jnp.float32),
            jnp.einsum("ecf,ecd->efd", hidden_units, out_rows, preferred_element_type=jnp.float32),
        )
        input_rows = jnp.einsum(
            "ecf,edf->ecd", gate_pre_grad, gate_block, preferred_element_type=jnp.float32
        ) + jnp.einsum("ecf,edf->ecd", up_pre_grad, up_block, preferred_element_type=jnp.float32)
        input_rows = input_rows.astype(jnp.bfloat16).reshape(slot_rows, D).astype(jnp.float32)
        grad_rows = grad_rows.at[tokens_here].add(input_rows)
        return ((grad_rows, pair_grad), block_grads)

    backward_blocks = (
        gate_full.reshape(block_total, EBLK, D, -1),
        up_full.reshape(block_total, EBLK, D, -1),
        down_full.reshape(block_total, EBLK, -1, D),
        slot_token.reshape(block_total, slot_rows),
        slot_gate.reshape(block_total, EBLK, CAP),
        slot_valid.reshape(block_total, slot_rows),
        safe_pair.reshape(block_total, slot_rows),
        kept_pre[0],
        kept_pre[1],
        kept_pre[2],
    )
    start_carry = (jnp.zeros((TOK_GRP, D), jnp.float32), jnp.zeros((TOK_GRP * TOPK,), jnp.float32))
    (grad_in_mixture, gate_grad_pair), stacked_grads = lax.scan(
        expert_backward, start_carry, backward_blocks
    )
    expert_parts = (
        stacked_grads[0].reshape((local_experts,) + stacked_grads[0].shape[2:]),
        stacked_grads[1].reshape((local_experts,) + stacked_grads[1].shape[2:]),
        stacked_grads[2].reshape((local_experts,) + stacked_grads[2].shape[2:]),
    )
    expert_parts = reduce_experts(expert_parts)
    gate_weight_grad, up_weight_grad, down_weight_grad = expert_parts
    gates_grad = gate_grad_pair.reshape(TOK_GRP, TOPK)
    routed_grad = gates * (gates_grad - jnp.sum(gates * gates_grad, axis=-1, keepdims=True))
    logits_grad = jnp.sum(routed_marks * routed_grad[:, :, None], axis=1)
    router_part = jnp.einsum(
        "td,te->de", mixture_in, logits_grad, precision=HIGHEST, preferred_element_type=jnp.float32
    )
    grad_in_mixture = grad_in_mixture + jnp.einsum(
        "te,de->td", logits_grad, router_full.astype(jnp.float32), precision=HIGHEST
    )
    mixture_grad_shard = lax.psum_scatter(
        grad_in_mixture.astype(jnp.bfloat16), "tensor", scatter_dimension=0, tiled=True
    ).astype(jnp.float32)
    middle_norm_grad, gain_two_grad = rms_backward(
        mixture_grad_shard, unit_two, inverse_two, gain_two
    )
    middle_grad = out_grad.astype(jnp.float32) + middle_norm_grad
    attended_grad = lax.all_gather(
        (RESIDUAL_SCALE * middle_grad).astype(jnp.bfloat16), "tensor", axis=0, tiled=True
    )
    output_part = jnp.einsum(
        "tf,td->fd", mixed_full, attended_grad, preferred_element_type=jnp.float32
    )
    mixed_grad = jnp.einsum(
        "td,fd->tf", attended_grad, output_full, preferred_element_type=jnp.float32
    ).astype(jnp.bfloat16)
    mixed_grad = mixed_grad.reshape(TOK_GRP, local_groups, group_ratio, HD)
    key_grad = jnp.zeros((TOK_GRP, local_groups, HD), jnp.float32)
    value_grad = jnp.zeros((TOK_GRP, local_groups, HD), jnp.float32)
    query_blocks = []
    for block_index in range(block_count):
        row_start = block_index * QBLK
        key_end = row_start + QBLK
        scores, queries = block_scores(
            query_rot, key_rot, segments, row_start, key_end, local_groups, group_ratio
        )
        soft_full = jnp.exp(scores - logsum_blocks[block_index])
        soft_low = soft_full.astype(jnp.bfloat16)
        out_block = mixed_grad[row_start:key_end]
        weight_grad = jnp.einsum(
            "qgrd,kgd->grqk", out_block, value_low[:key_end], preferred_element_type=jnp.float32
        )
        delta = jnp.sum(soft_full * weight_grad, axis=-1, keepdims=True)
        score_grad = (soft_full * (weight_grad - delta)).astype(jnp.bfloat16)
        query_blocks.append(
            jnp.einsum(
                "grqk,kgd->qgrd", score_grad, key_rot[:key_end], preferred_element_type=jnp.float32
            )
            * ATTN_SCALE
        )
        key_grad = key_grad.at[:key_end].add(
            jnp.einsum("grqk,qgrd->kgd", score_grad, queries, preferred_element_type=jnp.float32)
            * ATTN_SCALE
        )
        value_grad = value_grad.at[:key_end].add(
            jnp.einsum("grqk,qgrd->kgd", soft_low, out_block, preferred_element_type=jnp.float32)
        )
    query_rot_grad = jnp.concatenate(query_blocks, axis=0).reshape(TOK_GRP, local_heads, HD)
    query_grad = (
        rotate_back(query_rot_grad, cosine_table, sine_table)
        .astype(jnp.bfloat16)
        .reshape(TOK_GRP, local_heads * HD)
    )
    key_grad_low = (
        rotate_back(key_grad, cosine_table, sine_table)
        .astype(jnp.bfloat16)
        .reshape(TOK_GRP, local_groups * HD)
    )
    value_grad_low = value_grad.astype(jnp.bfloat16).reshape(TOK_GRP, local_groups * HD)
    query_part = jnp.einsum(
        "td,tf->df", normed_full, query_grad, preferred_element_type=jnp.float32
    )
    key_part = jnp.einsum(
        "td,tf->df", normed_full, key_grad_low, preferred_element_type=jnp.float32
    )
    value_part = jnp.einsum(
        "td,tf->df", normed_full, value_grad_low, preferred_element_type=jnp.float32
    )
    total_rows = jnp.einsum("tf,df->td", query_grad, query_full, preferred_element_type=jnp.float32)
    total_rows = total_rows + jnp.einsum(
        "tf,df->td", key_grad_low, key_full, preferred_element_type=jnp.float32
    )
    normed_grad = lax.psum_scatter(
        (
            total_rows
            + jnp.einsum(
                "tf,df->td", value_grad_low, value_full, preferred_element_type=jnp.float32
            )
        ).astype(jnp.bfloat16),
        "tensor",
        scatter_dimension=0,
        tiled=True,
    ).astype(jnp.float32)
    input_norm_grad, gain_one_grad = rms_backward(normed_grad, unit_one, inverse_one, gain_one)
    input_grad = middle_grad + input_norm_grad
    query_weight_grad, key_weight_grad, value_weight_grad, output_weight_grad = (
        lax.psum_scatter(
            query_part.astype(jnp.bfloat16), "dp", scatter_dimension=0, tiled=True
        ).astype(jnp.float32),
        lax.psum_scatter(
            key_part.astype(jnp.bfloat16), "dp", scatter_dimension=0, tiled=True
        ).astype(jnp.float32),
        lax.psum_scatter(
            value_part.astype(jnp.bfloat16), "dp", scatter_dimension=0, tiled=True
        ).astype(jnp.float32),
        lax.psum_scatter(
            output_part.astype(jnp.bfloat16), "dp", scatter_dimension=1, tiled=True
        ).astype(jnp.float32),
    )
    attention_gain_grad, mixture_gain_grad, router_weight_grad = (
        lax.psum_scatter(gain_one_grad, ("dp", "tensor"), scatter_dimension=0, tiled=True),
        lax.psum_scatter(gain_two_grad, ("dp", "tensor"), scatter_dimension=0, tiled=True),
        lax.psum_scatter(router_part, ("dp", "tensor"), scatter_dimension=0, tiled=True),
    )
    return (
        block_output,
        input_grad,
        attention_gain_grad,
        query_weight_grad,
        key_weight_grad,
        value_weight_grad,
        output_weight_grad,
        mixture_gain_grad,
        router_weight_grad,
        gate_weight_grad,
        up_weight_grad,
        down_weight_grad,
    )


def solution(mesh):
    in_specs = (
        P(("dp", "tensor"), None),
        P(("dp", "tensor"), None),
        P("dp", None),
        P("dp", None),
        P("dp", None),
        P("dp"),
        P("dp", "tensor"),
        P("dp", "tensor"),
        P("dp", "tensor"),
        P("tensor", "dp"),
        P("dp"),
        P("dp", None),
        P("tensor", "dp", None),
        P("tensor", "dp", None),
        P("tensor", None, "dp"),
    )
    out_specs = (
        P(("dp", "tensor"), None),
        P(("dp", "tensor"), None),
        P(("dp", "tensor")),
        P("dp", "tensor"),
        P("dp", "tensor"),
        P("dp", "tensor"),
        P("tensor", "dp"),
        P(("dp", "tensor")),
        P(("dp", "tensor"), None),
        P("tensor", "dp", None),
        P("tensor", "dp", None),
        P("tensor", None, "dp"),
    )
    return jax.shard_map(local, mesh=mesh, in_specs=in_specs, out_specs=out_specs, check_vma=False)
```

profile of v0, /device:TPU:0, one launch (start us, length us, event | category | flops | bytes accessed | tf_op | source)
XLA Modules:
  0.0 3573.6 jit_solution(11710512213824030261)
XLA Ops:
  13.1 16.0 all-reduce.8
  66.7 133.0 %all-gather.11.cloned.1.call-done = bf16[3072,1536]{1,0:T(8,128)(2,1)} async-done(((bf16[768,1536]{1,0:T(8,128)(2,1)}), bf16[3072,1536]{1,0:T(8,128)(2,1)}) %all-gather.11.cloned.1.call-update) | async-done | bytes 9437200 | tf_op jit(solution)/shard_map/all_gather | solution.py:200
  286.0 14.1 fusion.271
  300.2 12.9 fusion.63
  313.2 13.0 fusion.197
  326.2 14.3 fusion.272
  340.6 14.8 fusion.58
  355.4 14.4 fusion.198
  390.9 160.7 %reduce-scatter.15.cloned.1.call-done = bf16[768,1536]{1,0:T(8,128)(2,1)} async-done(((bf16[3072,1536]{1,0:T(8,128)(2,1)}), bf16[768,1536]{1,0:T(8,128)(2,1)}) %reduce-scatter.15.cloned.1.call-update) | async-done | bytes 2359312 | tf_op jit(solution)/shard_map/reduce_scatter | solution.py:234
  562.6 135.7 %gather_fusion.3 = s32[24576]{0:T(1024)S(1)} fusion(s32[24576]{0:T(1024)S(1)} %reshape.1305, s32[24576]{0:T(1024)S(1)} %broadcast_clamp_fusion), kind=kCustom, calls=%fused_computation.3 | custom fusion | bytes 294912 | tf_op jit(solution)/shard_map/jit(_take)/gather | solution.py:105
  722.4 90.3 %scatter_custom_fusion.3 = s32[30720]{0:T(1024)S(1)} fusion(s32[24576]{0:T(1024)S(1)} %bitcast.676, s32[24576]{0:T(1024)S(1)} %bitcast.663, s32[]{:T(128)} %constant.475.clone.1), kind=kCustom, calls=%fused_computation.372 | custom fusion | bytes 122884 | tf_op jit(solution)/shard_map/scatter | solution.py:121
  823.4 20.5 copy.277
  853.1 39.8 %gather_fusion.4 = f32[7680]{0:T(1024)S(1)} fusion(f32[24576]{0:T(1024)S(1)} %div.120, s32[8192]{0:T(1024)S(1)} %pad_clamp_fusion.2), kind=kCustom, calls=%fused_computation.4 | custom fusion | bytes 92160 | tf_op jit(solution)/shard_map/jit(_take)/gather | solution.py:256
  894.3 86.9 %all-gather.21.cloned.1.call-done = bf16[10,1536,512]{2,1,0:T(8,128)(2,1)} async-done(((bf16[10,192,512]{2,1,0:T(8,128)(2,1)}), bf16[10,1536,512]{2,1,0:T(8,128)(2,1)}) %all-gather.21.cloned.1.call-update) | async-done | bytes 15728656 | tf_op jit(solution)/shard_map/all_gather | solution.py:144
  990.6 502.1 %while.48 = (s32[]{:T(128)}, f32[3072,1536]{1,0:T(8,128)}, f32[10,1,768,512]{3,2,1,0:T(8,128)}, f32[10,1,768,512]{3,2,1,0:T(8,128)}, bf16[10,1,768,512]{3,2,1,0:...) while((s32[]{:T(128)}, f32[3072,1536]{1,0:T(8,128)}, ...), condition=%wide.region_26.28_spmd, body=%wide.region_24.27_spmd.sunk | while | flops 3630180352 | bytes 51166636 | solution.py:279
  1016.2 24.6 scatter_fusion
  1066.4 24.6 scatter_fusion
  1116.5 24.5 scatter_fusion
  1166.6 24.5 scatter_fusion
  1216.6 24.5 scatter_fusion
  1266.6 24.5 scatter_fusion
  1316.6 24.5 scatter_fusion
  1366.6 24.5 scatter_fusion
  1416.7 24.5 scatter_fusion
  1466.8 24.5 scatter_fusion
  1501.5 787.7 %while.49 = (s32[]{:T(128)}, f32[3072,1536]{1,0:T(8,128)}, f32[24576]{0:T(1024)S(1)}, bf16[10,1,1536,512]{3,2,1,0:T(8,128)(2,1)}, bf16[10,1,1536,512]{3,2,1,0:T(...) while((s32[]{:T(128)}, f32[3072,1536]{1,0:T(8,128)}, ...), condition=%wide.region_32.34_spmd, body=%wide.region_28.33_spmd.sunk | while | flops 7270970368 | bytes 115688072 | solution.py:343
  1557.1 23.5 scatter_custom_fusion.12
  1635.3 23.5 scatter_custom_fusion.12
  1714.2 23.5 scatter_custom_fusion.12
  1792.8 23.5 scatter_custom_fusion.12
  1871.5 23.5 scatter_custom_fusion.12
  1950.2 23.5 scatter_custom_fusion.12
  2029.0 23.5 scatter_custom_fusion.12
  2107.8 23.5 scatter_custom_fusion.12
  2186.5 23.5 scatter_custom_fusion.12
  2265.4 23.5 scatter_custom_fusion.12
  2292.1 14.3 add_convert_fusion.2
  2306.5 160.3 %reduce-scatter.19.cloned.1.call-done = bf16[768,1536]{1,0:T(8,128)(2,1)} async-done(((bf16[3072,1536]{1,0:T(8,128)(2,1)}), bf16[768,1536]{1,0:T(8,128)(2,1)}) %reduce-scatter.19.cloned.1.call-update) | async-done | bytes 2359312 | tf_op jit(solution)/shard_map/reduce_scatter | solution.py:362
  2476.0 13.3 fusion.279
  2490.1 13.6 fusion.80
  2507.1 13.4 fusion.81
  2520.8 123.0 %all-gather.27.cloned.1.call-done = bf16[3072,1536]{1,0:T(8,128)(2,1)} async-done(((bf16[768,1536]{1,0:T(8,128)(2,1)}), bf16[3072,1536]{1,0:T(8,128)(2,1)}) %all-gather.27.cloned.1.call-update) | async-done | bytes 9437200 | tf_op jit(solution)/shard_map/all_gather | solution.py:369
  2681.9 12.5 fusion.72
  2714.6 13.5 fusion.74
  2744.3 15.0 fusion.142
  2759.4 19.5 fusion.148
  2786.2 17.9 fusion.64
  2804.1 17.5 fusion.66
  2830.1 23.7 fusion.59
  2853.8 32.7 fusion.61
  2886.5 11.6 fusion.131
  2898.2 28.5 fusion.55
  2926.7 33.1 fusion.57
  2959.8 13.5 fusion.132
  2975.3 11.9 fusion.184
  3053.7 17.2 add_convert_fusion.1
  3071.0 11.3 convert_element_type.285
  3096.1 15.5 reduce-scatter.27.cloned.1.call-done
  3113.0 35.4 reduce-scatter.25.cloned.1.call-done
  3149.9 38.3 %reduce-scatter.29.cloned.1.call-done = bf16[384,192]{0,1:T(8,128)(2,1)} async-done(((bf16[384,1536]{0,1:T(8,128)(2,1)}), bf16[384,192]{0,1:T(8,128)(2,1)}) %reduce-scatter.29.cloned.1.call-update) | async-done | bytes 147472 | tf_op jit(solution)/shard_map/reduce_scatter | solution.py:457
  3189.8 38.8 %reduce-scatter.23.cloned.1.call-done = bf16[192,384]{1,0:T(8,128)(2,1)} async-done(((bf16[1536,384]{1,0:T(8,128)(2,1)}), bf16[192,384]{1,0:T(8,128)(2,1)}) %reduce-scatter.23.cloned.1.call-update) | async-done | bytes 147472 | tf_op jit(solution)/shard_map/reduce_scatter | solution.py:448
  3230.3 161.8 %reduce-scatter.21.cloned.1.call-done = bf16[768,1536]{1,0:T(8,128)(2,1)} async-done(((bf16[3072,1536]{1,0:T(8,128)(2,1)}), bf16[768,1536]{1,0:T(8,128)(2,1)}) %reduce-scatter.21.cloned.1.call-update) | async-done | bytes 2359312 | tf_op jit(solution)/shard_map/reduce_scatter | solution.py:434
  3395.3 45.0 %all-reduce.7 = (f32[1536]{0:T(1024)S(1)}, f32[1536]{0:T(1024)S(1)}) all-reduce(f32[1536]{0:T(1024)S(1)} %get-tuple-element.521, f32[1536]{0:T(1024)S(1)} %copy-done.129), channel_id=6, replica_groups=mesh['dp'=8,'tensor'=4] {'dp','tensor'}, use_global_device_ids=true, to_apply=%region_46.48.clone | all-reduce | flops 3072 | bytes 24576
  3441.4 116.3 %reduce-scatter.17.cloned.1.call-done = bf16[768,1536]{1,0:T(8,128)(2,1)} async-done(((bf16[3072,1536]{1,0:T(8,128)(2,1)}), bf16[768,1536]{1,0:T(8,128)(2,1)}) %reduce-scatter.17.cloned.1.call-update) | async-done | bytes 2359312 | tf_op jit(solution)/shard_map/reduce_scatter | solution.py:282
  (960 shorter events, 1238.3 us)
Async XLA Ops:
  7.2 192.5 %all-gather.11.cloned.1.call-start = ((), (), s32[]{:S(2)}) async-start(), calls=%async_computation.12 | async-start | bytes 11796480 | tf_op jit(solution)/shard_map/all_gather | solution.py:200
  7.2 27.8 copy-start.126
  7.2 29.1 copy-start.124
  7.3 37.6 %copy-start.125 = (bf16[192,128]{1,0:T(8,128)(2,1)S(1)}, bf16[192,128]{1,0:T(8,128)(2,1)}, u32[]{:S(2)}) copy-start(bf16[192,128]{1,0:T(8,128)(2,1)} %param.57) | copy-start | bytes 147460
  9.5 25.5 copy-start.122
  33.4 190.3 %all-gather.13.cloned.1.call-start = ((), (), s32[]{:S(2)}) async-start(), calls=%async_computation.13 | async-start | bytes 1327104 | tf_op jit(solution)/shard_map/all_gather | solution.py:189
  34.2 346.4 %all-gather.15.cloned.1.call-start = ((), (), s32[]{:S(2)}) async-start(), calls=%async_computation.14 | async-start | bytes 1327104 | tf_op jit(solution)/shard_map/all_gather | solution.py:192
  34.9 516.7 %reduce-scatter.15.cloned.1.call-start = ((), (), s32[]{:S(2)}) async-start(), calls=%async_computation.15 | async-start | bytes 11796480 | tf_op jit(solution)/shard_map/reduce_scatter | solution.py:234
  44.9 165.2 %copy-start.51 = (bf16[1536,128]{1,0:T(8,128)(2,1)}, bf16[1536,128]{1,0:T(8,128)(2,1)S(1)}, u32[]{:S(2)}) copy-start(bf16[1536,128]{1,0:T(8,128)(2,1)S(1)} %all_gather.48) | copy-start | bytes 1179652
  55.0 151.8 %copy-start.41 = (bf16[1536,128]{1,0:T(8,128)(2,1)}, bf16[1536,128]{1,0:T(8,128)(2,1)S(1)}, u32[]{:S(2)}) copy-start(bf16[1536,128]{1,0:T(8,128)(2,1)S(1)} %all_gather.47) | copy-start | bytes 1179652
  60.1 170.6 %copy-start.28 = (f32[3072,32]{0,1:T(8,128)}, f32[3072,32]{0,1:T(8,128)S(1)}, u32[]{:S(2)}) copy-start(f32[3072,32]{0,1:T(8,128)S(1)} %get-tuple-element.623) | copy-start | bytes 1179652
  60.1 170.6 %copy-start.30 = (f32[3072,32]{0,1:T(8,128)}, f32[3072,32]{0,1:T(8,128)S(1)}, u32[]{:S(2)}) copy-start(f32[3072,32]{0,1:T(8,128)S(1)} %get-tuple-element.624) | copy-start | bytes 1179652
  206.8 28.0 copy-start.75
  213.5 32.3 copy-start.16
  213.5 112.6 %copy-start.13 = (bf16[3072,2,32]{0,2,1:T(8,128)(2,1)}, bf16[3072,2,32]{0,2,1:T(8,128)(2,1)S(1)}, u32[]{:S(2)}) copy-start(bf16[3072,2,32]{0,2,1:T(8,128)(2,1)S(1)} %get-tuple-element.621) | copy-start | bytes 1179652
  277.7 92.0 %copy-start.106 = (f32[2,3,512]{2,1,0:T(4,128)}, f32[2,3,512]{2,1,0:T(4,128)S(1)}, u32[]{:S(2)}) copy-start(f32[2,3,512]{2,1,0:T(4,128)S(1)} %get-tuple-element.633) | copy-start | bytes 36868
  286.0 83.7 %copy-start.108 = (f32[2,3,512]{2,1,0:T(4,128)}, f32[2,3,512]{2,1,0:T(4,128)S(1)}, u32[]{:S(2)}) copy-start(f32[2,3,512]{2,1,0:T(4,128)S(1)} %fusion.68) | copy-start | bytes 36868
  390.2 161.4 %copy-start.3 = (bf16[768,1536]{1,0:T(8,128)(2,1)S(1)}, bf16[768,1536]{1,0:T(8,128)(2,1)}, u32[]{:S(2)}) copy-start(bf16[768,1536]{1,0:T(8,128)(2,1)} %param.49) | copy-start | bytes 7077892
  390.2 433.1 %all-gather.23.cloned.1.call-start = ((), (), s32[]{:S(2)}) async-start(), calls=%async_computation.19 | async-start | bytes 17694720 | tf_op jit(solution)/shard_map/all_gather | solution.py:145
  390.8 453.1 %all-gather.17.cloned.1.call-start = ((), (), s32[]{:S(2)}) async-start(), calls=%async_computation.16 | async-start | bytes 11796480 | tf_op jit(solution)/shard_map/all_gather | solution.py:242
  390.9 166.5 %copy-start.83 = (f32[1536]{0:T(1024)}, f32[1536]{0:T(1024)S(1)}, u32[]{:S(2)}) copy-start(f32[1536]{0:T(1024)S(1)} %convert_element_type.283) | copy-start | bytes 18436
  557.5 336.8 %all-gather.19.cloned.1.call-start = ((), (), s32[]{:S(2)}) async-start(), calls=%async_computation.17 | async-start | bytes 17694720 | tf_op jit(solution)/shard_map/all_gather | solution.py:143
  558.2 423.0 %all-gather.21.cloned.1.call-start = ((), (), s32[]{:S(2)}) async-start(), calls=%async_computation.18 | async-start | bytes 17694720 | tf_op jit(solution)/shard_map/all_gather | solution.py:144
  559.0 933.7 %all-gather.25.cloned.1.call-start = ((), (), s32[]{:S(2)}) async-start(), calls=%async_computation.21 | async-start | bytes 11796480 | tf_op jit(solution)/shard_map/all_gather | solution.py:286
  559.7 1907.1 %reduce-scatter.19.cloned.1.call-start = ((), (), s32[]{:S(2)}) async-start(), calls=%async_computation.22 | async-start | bytes 11796480 | tf_op jit(solution)/shard_map/reduce_scatter | solution.py:362
  716.6 96.9 %copy-start.131 = (bf16[192,40]{0,1:T(8,128)(2,1)S(1)}, bf16[192,40]{0,1:T(8,128)(2,1)}, u32[]{:S(2)}) copy-start(bf16[192,40]{0,1:T(8,128)(2,1)} %param.60) | copy-start | bytes 46084
  851.9 41.1 %copy-start.86 = (f32[3072]{0:T(1024)}, f32[3072]{0:T(1024)S(1)}, u32[]{:S(2)}) copy-start(f32[3072]{0:T(1024)S(1)} %fusion.241) | copy-start | bytes 36868
  1016.2 24.6 copy-start.12
  1066.4 24.6 copy-start.12
  1116.5 24.6 copy-start.12
  1166.6 24.6 copy-start.12
  1216.6 24.6 copy-start.12
  1266.6 24.6 copy-start.12
  1316.6 24.6 copy-start.12
  1366.6 24.6 copy-start.12
  1416.7 24.6 copy-start.12
  1501.5 789.0 %copy-start.48 = (f32[3072,8]{0,1:T(8,128)S(1)}, f32[3072,8]{0,1:T(8,128)}, u32[]{:S(2)}) copy-start(f32[3072,8]{0,1:T(8,128)} %copy-done.47) | copy-start | bytes 294916
  1501.5 789.0 %copy-start.78 = (f32[3072]{0:T(1024)S(1)}, f32[3072]{0:T(1024)}, u32[]{:S(2)}) copy-start(f32[3072]{0:T(1024)} %copy-done.77) | copy-start | bytes 36868
  1501.5 789.0 %copy-start.87 = (f32[3072]{0:T(1024)S(1)}, f32[3072]{0:T(1024)}, u32[]{:S(2)}) copy-start(f32[3072]{0:T(1024)} %copy-done.86) | copy-start | bytes 36868
  1501.5 790.6 %copy-start.68 = (bf16[1536,40]{0,1:T(8,128)(2,1)S(1)}, bf16[1536,40]{0,1:T(8,128)(2,1)}, u32[]{:S(2)}) copy-start(bf16[1536,40]{0,1:T(8,128)(2,1)} %copy-done.67) | copy-start | bytes 368644
  2306.4 160.4 %copy-start.4 = (bf16[768,1536]{1,0:T(8,128)(2,1)S(1)}, bf16[768,1536]{1,0:T(8,128)(2,1)}, u32[]{:S(2)}) copy-start(bf16[768,1536]{1,0:T(8,128)(2,1)} %param.49) | copy-start | bytes 7077892
  2306.4 160.4 %copy-start.84 = (f32[1536]{0:T(1024)S(1)}, f32[1536]{0:T(1024)}, u32[]{:S(2)}) copy-start(f32[1536]{0:T(1024)} %copy-done.83) | copy-start | bytes 18436
  2306.4 160.4 %copy-start.95 = (f32[768]{0:T(1024)S(1)}, f32[768]{0:T(1024)}, u32[]{:S(2)}) copy-start(f32[768]{0:T(1024)} %copy-done.94) | copy-start | bytes 9220
  2306.4 337.4 %all-gather.27.cloned.1.call-start = ((), (), s32[]{:S(2)}) async-start(), calls=%async_computation.23 | async-start | bytes 11796480 | tf_op jit(solution)/shard_map/all_gather | solution.py:369
  2475.9 606.4 %reduce-scatter.37.cloned.1.call-start = ((), (), s32[]{:S(2)}) async-start(), calls=%async_computation.32 | async-start | bytes 811008
  2489.3 594.5 %reduce-scatter.35.cloned.1.call-start = ((), (), s32[]{:S(2)}) async-start(), calls=%async_computation.31 | async-start | bytes 17694720 | tf_op jit(solution)/shard_map/reduce_scatter | solution.py:157
  2490.1 597.8 %reduce-scatter.31.cloned.1.call-start = ((), (), s32[]{:S(2)}) async-start(), calls=%async_computation.29 | async-start | bytes 17694720 | tf_op jit(solution)/shard_map/reduce_scatter | solution.py:151
  2503.9 588.0 %reduce-scatter.33.cloned.1.call-start = ((), (), s32[]{:S(2)}) async-start(), calls=%async_computation.30 | async-start | bytes 17694720 | tf_op jit(solution)/shard_map/reduce_scatter | solution.py:154
  2520.5 123.3 %copy-start.133 = (bf16[384,1536]{0,1:T(8,128)(2,1)S(1)}, bf16[384,1536]{0,1:T(8,128)(2,1)}, u32[]{:S(2)}) copy-start(bf16[384,1536]{0,1:T(8,128)(2,1)} %all-gather.15.cloned.1.call-done) | copy-start | bytes 3538948
  2520.5 591.1 %reduce-scatter.27.cloned.1.call-start = ((), (), s32[]{:S(2)}) async-start(), calls=%async_computation.27 | async-start | bytes 442368 | tf_op jit(solution)/shard_map/reduce_scatter | solution.py:454
  2853.8 32.7 copy-start.49
  2926.7 33.1 copy-start.37
  3001.5 146.9 %reduce-scatter.25.cloned.1.call-start = ((), (), s32[]{:S(2)}) async-start(), calls=%async_computation.26 | async-start | bytes 442368 | tf_op jit(solution)/shard_map/reduce_scatter | solution.py:451
  3009.9 178.3 %reduce-scatter.29.cloned.1.call-start = ((), (), s32[]{:S(2)}) async-start(), calls=%async_computation.28 | async-start | bytes 1327104 | tf_op jit(solution)/shard_map/reduce_scatter | solution.py:457
  3023.2 205.4 %reduce-scatter.23.cloned.1.call-start = ((), (), s32[]{:S(2)}) async-start(), calls=%async_computation.25 | async-start | bytes 1327104 | tf_op jit(solution)/shard_map/reduce_scatter | solution.py:448
  3034.1 358.0 %reduce-scatter.21.cloned.1.call-start = ((), (), s32[]{:S(2)}) async-start(), calls=%async_computation.24 | async-start | bytes 11796480 | tf_op jit(solution)/shard_map/reduce_scatter | solution.py:434
  3070.9 486.7 %reduce-scatter.17.cloned.1.call-start = ((), (), s32[]{:S(2)}) async-start(), calls=%async_computation.20 | async-start | bytes 11796480 | tf_op jit(solution)/shard_map/reduce_scatter | solution.py:282
  3091.9 300.2 %copy-start.5 = (bf16[768,1536]{1,0:T(8,128)(2,1)S(1)}, bf16[768,1536]{1,0:T(8,128)(2,1)}, u32[]{:S(2)}) copy-start(bf16[768,1536]{1,0:T(8,128)(2,1)} %param.49) | copy-start | bytes 7077892
  3091.9 300.2 %copy-start.93 = (f32[1536]{0:T(1024)S(1)}, f32[1536]{0:T(1024)}, u32[]{:S(2)}) copy-start(f32[1536]{0:T(1024)} %copy-done.92) | copy-start | bytes 18436
  3091.9 300.2 %copy-start.123 = (f32[768]{0:T(1024)S(1)}, f32[768]{0:T(1024)}, u32[]{:S(2)}) copy-start(f32[768]{0:T(1024)} %copy-done.122) | copy-start | bytes 9220
  3091.9 303.4 %copy-start.129 = (f32[1536]{0:T(1024)S(1)}, f32[1536]{0:T(1024)}, u32[]{:S(2)}) copy-start(f32[1536]{0:T(1024)} %get-tuple-element.519) | copy-start | bytes 18436
  3091.9 465.8 %copy-start.85 = (f32[1536]{0:T(1024)S(1)}, f32[1536]{0:T(1024)}, u32[]{:S(2)}) copy-start(f32[1536]{0:T(1024)} %copy-done.83) | copy-start | bytes 18436
  3091.9 465.8 %copy-start.96 = (f32[768]{0:T(1024)S(1)}, f32[768]{0:T(1024)}, u32[]{:S(2)}) copy-start(f32[768]{0:T(1024)} %copy-done.94) | copy-start | bytes 9220
  3091.9 465.8 %copy-start.128 = (f32[768]{0:T(1024)S(1)}, f32[768]{0:T(1024)}, u32[]{:S(2)}) copy-start(f32[768]{0:T(1024)} %copy-done.127) | copy-start | bytes 9220
  (165 other events, 980.7 us)
Sparse Core Ops, SparseCore 0:
  33.6 166.1 all-gather.10
  201.6 22.0 all-gather.12
  225.6 23.9 all-gather.14
  390.4 161.1 reduce-scatter.14
  553.3 86.2 all-gather.22
  641.6 166.7 all-gather.16
  810.3 83.6 all-gather.18
  895.9 85.2 all-gather.20
  982.8 166.7 all-gather.24
  2306.5 160.1 reduce-scatter.18
  2476.1 167.6 all-gather.26
  2648.8 94.4 reduce-scatter.36
  2746.7 106.4 reduce-scatter.34
  2856.6 107.3 reduce-scatter.30
  2967.3 107.3 reduce-scatter.32
  3077.6 33.8 reduce-scatter.26
  3114.5 33.8 reduce-scatter.24
  3151.5 36.6 reduce-scatter.28
  3192.0 36.6 reduce-scatter.22
  3230.9 161.1 reduce-scatter.20
  3394.4 163.2 reduce-scatter.16
where the time goes:
time: 3580 us; the launch traced here: 3570 us
  waiting for transfers between devices  1090 us (30%)
  matrix products  807 us (23%)
  other arithmetic  797 us (22%)
  local copies, waits for them, and re-layouts  773 us (22%)
  blocking collectives  89.3 us (2%)
    scatter-add x10, other arithmetic, expert_forward(): running = running.at[tokens_here].add(outputs.reshape(slot_rows, D))  246 us
    scatter-add x10, other arithmetic, expert_backward(): grad_rows = grad_rows.at[tokens_here].add(input_rows)  235 us
    reduce_scatter x1, waiting for transfers between devices, local(): lax.psum_scatter((total_rows + jnp.einsum('tf,df->td', value_grad_low, va...  162 us
    reduce_scatter x1, waiting for transfers between devices, local(): lax.psum_scatter(jnp.dot(mixed_full, output_full, preferred_element_type=...  161 us
    reduce_scatter x1, waiting for transfers between devices, local(): lax.psum_scatter(grad_in_mixture.astype(jnp.bfloat16), 'tensor', scatter_...  160 us
    gather x2, local copies, waits for them, and re-layouts, route_slots(): ordered = jnp.take(expert_row.reshape(pair_count), order_row)  136 us
    all_gather x1, waiting for transfers between devices, local(): lax.all_gather(normed_shard.astype(jnp.bfloat16), 'tensor', axis=0, tiled...  133 us
    all_gather x1, waiting for transfers between devices, local(): lax.all_gather((RESIDUAL_SCALE * middle_grad).astype(jnp.bfloat16), 'tens...  123 us
  transfers between devices with their start and end apart: 21, of which 12 were waited for; matrix products, arithmetic and copies ran while one was open for 42% of the time, Pallas kernels for 0%

commit v1 on v0

--- a/solution.py
+++ b/solution.py
@@ -1,6 +1,8 @@
 import jax
 import jax.numpy as jnp
 from jax import lax
+from jax.experimental import pallas as pl
+from jax.experimental.pallas import tpu as pltpu
 from jax.sharding import PartitionSpec as P
 
 D = 1536
@@ -10,7 +12,6 @@
 PROMPT = 2048
 NCONT = 4
 QBLK = 512
-EBLK = 1
 TOK_GRP = 3072
 CAP = 768
 
@@ -100,9 +101,9 @@
     return sigmoid_part * (1.0 + values * (1.0 - sigmoid_part))
 
 
-def route_slots(expert_row, order_row):
+def route_slots(expert_row, order_row, first_slot, slot_count):
     pair_count = expert_row.shape[0] * expert_row.shape[1]
-    ordered = jnp.take(expert_row.reshape(pair_count), order_row)
+    ordered = table_lookup(expert_row.reshape(pair_count), order_row)
     onehot = ordered[:, None] == jnp.arange(EXPERTS, dtype=jnp.int32)[None, :]
     rank_block = 256
     blocks = pair_count // rank_block
@@ -117,8 +118,112 @@
     before = jnp.cumsum(totals, axis=0) - totals
     counts = (within + before[:, None, :]).reshape(pair_count, EXPERTS)
     pair_rank = jnp.sum(jnp.where(onehot, counts, 0), axis=1) - 1
-    slot_index = jnp.where(pair_rank < CAP, ordered * CAP + pair_rank, EXPERTS * CAP)
-    return jnp.full((EXPERTS * CAP,), -1, jnp.int32).at[slot_index].set(order_row, mode="drop")
+    local_slot = ordered * CAP + pair_rank - first_slot
+    kept = (pair_rank < CAP) & (local_slot >= 0) & (local_slot < slot_count)
+    local_slot = jnp.where(kept, local_slot, -1)
+    return invert_slots(local_slot, order_row, slot_count)
+
+
+def _gather_rows_kernel(tok_ref, src_ref, out_ref, buf, sem):
+    rows = buf.shape[0]
+    base = pl.program_id(0) * rows
+
+    def start(s, carry):
+        t = tok_ref[base + s]
+        pltpu.make_async_copy(src_ref.at[pl.ds(t, 1)], buf.at[pl.ds(s, 1)], sem).start()
+        return carry
+
+    lax.fori_loop(0, rows, start, 0, unroll=8)
+    pltpu.make_async_copy(src_ref.at[pl.ds(0, rows)], buf, sem).wait()
+    out_ref[...] = buf[...].astype(out_ref.dtype)
+
+
+def gather_rows(tok, src, rows, out_dtype):
+    blocks, width = tok.shape[0] // rows, src.shape[1]
+    return pl.pallas_call(
+        _gather_rows_kernel,
+        grid_spec=pltpu.PrefetchScalarGridSpec(
+            num_scalar_prefetch=1,
+            grid=(blocks,),
+            in_specs=[pl.BlockSpec(memory_space=pl.ANY)],
+            out_specs=pl.BlockSpec((rows, width), lambda b, tok: (b, 0)),
+            scratch_shapes=[pltpu.VMEM((rows, width), jnp.float32), pltpu.SemaphoreType.DMA(())],
+        ),
+        out_shape=jax.ShapeDtypeStruct((tok.shape[0], width), out_dtype),
+    )(tok, src)
+
+
+def _combine_rows_kernel(tok_ref, add_ref, out_ref, acc_ref, sem):
+    rows = add_ref.shape[0]
+    step = pl.program_id(0)
+
+    @pl.when(step == 0)
+    def _():
+        acc_ref[...] = jnp.zeros_like(acc_ref)
+
+    base = step * rows
+
+    def body(s, carry):
+        t = tok_ref[base + s]
+        acc_ref[pl.ds(t, 1), :] += add_ref[pl.ds(s, 1), :]
+        return carry
+
+    lax.fori_loop(0, rows, body, 0, unroll=8)
+
+    @pl.when(step == pl.num_programs(0) - 1)
+    def _():
+        copy = pltpu.make_async_copy(acc_ref, out_ref, sem)
+        copy.start()
+        copy.wait()
+
+
+def combine_rows(tok, addend, rows, total_rows):
+    blocks, width = tok.shape[0] // rows, addend.shape[1]
+    return pl.pallas_call(
+        _combine_rows_kernel,
+        grid_spec=pltpu.PrefetchScalarGridSpec(
+            num_scalar_prefetch=1,
+            grid=(blocks,),
+            in_specs=[pl.BlockSpec((rows, width), lambda b, tok: (b, 0))],
+            out_specs=pl.BlockSpec(memory_space=pl.ANY),
+            scratch_shapes=[
+                pltpu.VMEM((total_rows, width), jnp.float32),
+                pltpu.SemaphoreType.DMA(()),
+            ],
+        ),
+        out_shape=jax.ShapeDtypeStruct((total_rows, width), jnp.float32),
+        compiler_params=pltpu.CompilerParams(vmem_limit_bytes=48 * 1024 * 1024),
+    )(tok, addend)
+
+
+def table_lookup(table, index):
+    lanes = 128
+    high_count = table.shape[0] // lanes
+    low_marks = (index[:, None] % lanes == jnp.arange(lanes)[None, :]).astype(jnp.bfloat16)
+    picked = jnp.dot(
+        low_marks,
+        table.reshape(high_count, lanes).astype(jnp.bfloat16).T,
+        preferred_element_type=jnp.float32,
+    )
+    high_marks = index[:, None] // lanes == jnp.arange(high_count)[None, :]
+    return jnp.sum(jnp.where(high_marks, picked, 0.0), axis=1).astype(jnp.int32)
+
+
+def invert_slots(local_slot, values, slot_count):
+    lanes = 128
+    high_count = slot_count // lanes
+    column_marks = (local_slot[:, None] // lanes == jnp.arange(high_count)[None, :]).astype(
+        jnp.bfloat16
+    )
+    lane_marks = local_slot[:, None] % lanes == jnp.arange(lanes)[None, :]
+    shifted = values + 1
+    parts = []
+    for digit in (shifted // 256, shifted % 256):
+        spread = jnp.where(lane_marks, digit[:, None], 0).astype(jnp.bfloat16)
+        parts.append(
+            jnp.einsum("ic,il->cl", column_marks, spread, preferred_element_type=jnp.float32)
+        )
+    return (256.0 * parts[0] + parts[1]).astype(jnp.int32).reshape(slot_count) - 1
 
 
 def block_scores(query_rot, key_rot, segments, row_start, key_end, local_groups, group_ratio):
@@ -182,8 +287,6 @@
     group_ratio = local_heads // local_groups
     block_count = TOK_GRP // QBLK
     local_experts = gate_weight.shape[0]
-    block_total = local_experts // EBLK
-    slot_rows = EBLK * CAP
     gain_one, query_full, key_full, value_full, output_full, gain_two, router_full = (
         lax.all_gather(attention_gain, "dp", axis=0, tiled=True),
         lax.all_gather(query_weight, "dp", axis=0, tiled=True),
@@ -247,106 +350,54 @@
     ).astype(jnp.float32)
     routed = jnp.sum(routed_marks * logits[:, None, :], axis=-1)
     gates = jax.nn.softmax(routed, axis=-1)
-    slot_pair_all = route_slots(expert_ids, fill_order[0])
-    first_slot = lax.axis_index("tensor") * (local_experts * CAP)
-    slot_pair = lax.dynamic_slice_in_dim(slot_pair_all, first_slot, local_experts * CAP, 0)
+    slot_count = local_experts * CAP
+    first_slot = lax.axis_index("tensor") * slot_count
+    slot_pair = route_slots(expert_ids, fill_order[0], first_slot, slot_count)
     slot_valid = slot_pair >= 0
     safe_pair = jnp.maximum(slot_pair, 0)
     slot_token = safe_pair // TOPK
     slot_gate = jnp.where(slot_valid, jnp.take(gates.reshape(-1), safe_pair), 0.0)
-
-    def expert_forward(running, block_data):
-        gate_block, up_block, down_block, tokens_here, gate_here = block_data
-        inputs = jnp.take(mixture_in, tokens_here, axis=0).reshape(EBLK, CAP, D)
-        gate_pre = jnp.einsum(
-            "ecd,edf->ecf", inputs, gate_block, preferred_element_type=jnp.float32
-        )
-        up_pre = jnp.einsum("ecd,edf->ecf", inputs, up_block, preferred_element_type=jnp.float32)
-        hidden_units = (gate_here[:, :, None] * jax.nn.silu(gate_pre) * up_pre).astype(jnp.bfloat16)
-        outputs = jnp.einsum(
-            "ecf,efd->ecd", hidden_units, down_block, preferred_element_type=jnp.float32
-        )
-        running = running.at[tokens_here].add(outputs.reshape(slot_rows, D))
-        return (running, (gate_pre, up_pre, hidden_units))
-
-    forward_blocks = (
-        gate_full.reshape(block_total, EBLK, D, -1),
-        up_full.reshape(block_total, EBLK, D, -1),
-        down_full.reshape(block_total, EBLK, -1, D),
-        slot_token.reshape(block_total, slot_rows),
-        slot_gate.reshape(block_total, EBLK, CAP),
-    )
-    mixture_sum, kept_pre = lax.scan(
-        expert_forward, jnp.zeros((TOK_GRP, D), jnp.float32), forward_blocks
-    )
+    slot_gate = slot_gate.reshape(local_experts, CAP, 1)
+
+    inputs = gather_rows(slot_token, mixture_in.astype(jnp.float32), CAP, jnp.bfloat16).reshape(
+        local_experts, CAP, D
+    )
+    gate_pre = jnp.einsum("ecd,edf->ecf", inputs, gate_full, preferred_element_type=jnp.float32)
+    up_pre = jnp.einsum("ecd,edf->ecf", inputs, up_full, preferred_element_type=jnp.float32)
+    activated = jax.nn.silu(gate_pre)
+    hidden_units = (slot_gate * activated * up_pre).astype(jnp.bfloat16)
+    expert_out = jnp.einsum(
+        "ecf,efd->ecd", hidden_units, down_full, preferred_element_type=jnp.float32
+    )
+    mixture_sum = combine_rows(slot_token, expert_out.reshape(slot_count, D), CAP, TOK_GRP)
     mixture_part = lax.psum_scatter(
         mixture_sum.astype(jnp.bfloat16), "tensor", scatter_dimension=0, tiled=True
     ).astype(jnp.float32)
     block_output = (middle + RESIDUAL_SCALE * mixture_part).astype(jnp.bfloat16)
     cotangent_full = lax.all_gather(out_grad, "tensor", axis=0, tiled=True)
-    gate_full, up_full, down_full = fetch_experts(gate_weight, up_weight, down_weight)
-
-    def expert_backward(carried, block_data):
-        grad_rows, pair_grad = carried
-        (
-            gate_block,
-            up_block,
-            down_block,
-            tokens_here,
-            gate_here,
-            valid_here,
-            pairs_here,
-            gate_pre,
-            up_pre,
-            hidden_units,
-        ) = block_data
-        inputs = jnp.take(mixture_in, tokens_here, axis=0).reshape(EBLK, CAP, D)
-        out_rows = (
-            (RESIDUAL_SCALE * jnp.take(cotangent_full, tokens_here, axis=0).astype(jnp.float32))
-            .astype(jnp.bfloat16)
-            .reshape(EBLK, CAP, D)
-        )
-        hidden_grad = jnp.einsum(
-            "ecd,efd->ecf", out_rows, down_block, preferred_element_type=jnp.float32
-        )
-        activated = jax.nn.silu(gate_pre)
-        gate_grad_slot = jnp.sum(activated * up_pre * hidden_grad, axis=-1).reshape(slot_rows)
-        pair_grad = pair_grad.at[pairs_here].add(jnp.where(valid_here, gate_grad_slot, 0.0))
-        product_grad = gate_here[:, :, None] * hidden_grad
-        gate_pre_grad = (product_grad * up_pre * silu_slope(gate_pre)).astype(jnp.bfloat16)
-        up_pre_grad = (product_grad * activated).astype(jnp.bfloat16)
-        block_grads = (
-            jnp.einsum("ecd,ecf->edf", inputs, gate_pre_grad, preferred_element_type=jnp.float32),
-            jnp.einsum("ecd,ecf->edf", inputs, up_pre_grad, preferred_element_type=jnp.float32),
-            jnp.einsum("ecf,ecd->efd", hidden_units, out_rows, preferred_element_type=jnp.float32),
-        )
-        input_rows = jnp.einsum(
-            "ecf,edf->ecd", gate_pre_grad, gate_block, preferred_element_type=jnp.float32
-        ) + jnp.einsum("ecf,edf->ecd", up_pre_grad, up_block, preferred_element_type=jnp.float32)
-        input_rows = input_rows.astype(jnp.bfloat16).reshape(slot_rows, D).astype(jnp.float32)
-        grad_rows = grad_rows.at[tokens_here].add(input_rows)
-        return ((grad_rows, pair_grad), block_grads)
-
-    backward_blocks = (
-        gate_full.reshape(block_total, EBLK, D, -1),
-        up_full.reshape(block_total, EBLK, D, -1),
-        down_full.reshape(block_total, EBLK, -1, D),
-        slot_token.reshape(block_total, slot_rows),
-        slot_gate.reshape(block_total, EBLK, CAP),
-        slot_valid.reshape(block_total, slot_rows),
-        safe_pair.reshape(block_total, slot_rows),
-        kept_pre[0],
-        kept_pre[1],
-        kept_pre[2],
-    )
-    start_carry = (jnp.zeros((TOK_GRP, D), jnp.float32), jnp.zeros((TOK_GRP * TOPK,), jnp.float32))
-    (grad_in_mixture, gate_grad_pair), stacked_grads = lax.scan(
-        expert_backward, start_carry, backward_blocks
-    )
+    scaled_cotangent = (
+        (RESIDUAL_SCALE * cotangent_full.astype(jnp.float32)).astype(jnp.bfloat16).astype(jnp.float32)
+    )
+    out_rows = gather_rows(slot_token, scaled_cotangent, CAP, jnp.bfloat16).reshape(
+        local_experts, CAP, D
+    )
+    hidden_grad = jnp.einsum("ecd,efd->ecf", out_rows, down_full, preferred_element_type=jnp.float32)
+    gate_grad_slot = jnp.sum(activated * up_pre * hidden_grad, axis=-1).reshape(slot_count)
+    gate_grad_pair = jnp.zeros((TOK_GRP * TOPK,), jnp.float32).at[safe_pair].add(
+        jnp.where(slot_valid, gate_grad_slot, 0.0)
+    )
+    product_grad = slot_gate * hidden_grad
+    gate_pre_grad = (product_grad * up_pre * silu_slope(gate_pre)).astype(jnp.bfloat16)
+    up_pre_grad = (product_grad * activated).astype(jnp.bfloat16)
+    input_rows = jnp.einsum(
+        "ecf,edf->ecd", gate_pre_grad, gate_full, preferred_element_type=jnp.float32
+    ) + jnp.einsum("ecf,edf->ecd", up_pre_grad, up_full, preferred_element_type=jnp.float32)
+    input_rows = input_rows.astype(jnp.bfloat16).astype(jnp.float32).reshape(slot_count, D)
+    grad_in_mixture = combine_rows(slot_token, input_rows, CAP, TOK_GRP)
     expert_parts = (
-        stacked_grads[0].reshape((local_experts,) + stacked_grads[0].shape[2:]),
-        stacked_grads[1].reshape((local_experts,) + stacked_grads[1].shape[2:]),
-        stacked_grads[2].reshape((local_experts,) + stacked_grads[2].shape[2:]),
+        jnp.einsum("ecd,ecf->edf", inputs, gate_pre_grad, preferred_element_type=jnp.float32),
+        jnp.einsum("ecd,ecf->edf", inputs, up_pre_grad, preferred_element_type=jnp.float32),
+        jnp.einsum("ecf,ecd->efd", hidden_units, out_rows, preferred_element_type=jnp.float32),
     )
     expert_parts = reduce_experts(expert_parts)
     gate_weight_grad, up_weight_grad, down_weight_grad = expert_parts

time: 3580 us -> 2730 us (0.76)
  local copies, waits for them, and re-layouts: 773 us -> 86.2 us
  other arithmetic: 797 us -> 375 us
  Pallas kernels: 0 us -> 387 us
  matrix products: 807 us -> 732 us
  waiting for transfers between devices: 1090 us -> 1040 us
    scatter-add x30 -> x1, other arithmetic: 531 us -> 44.7 us  [local(): jnp.zeros((TOK_GRP * TOPK,), jnp.float32).at[safe_pair]]
    gather x32 -> x0, local copies, waits for them, and re-layouts: 452 us -> none  [the longest x2 136 us: route_slots(): ordered = jnp.take(expert_row.reshape(pair_count), order_row)]
    pallas_call x0 -> x4, Pallas kernels: none -> 387 us  [the longest x2 255 us: gather_rows(): pl.pallas_call(_gather_rows_kernel, grid_spec=pltpu.PrefetchScalarGridSpe...]
    all_gather x1, waiting for transfers between devices: 0.01 us -> 95.4 us  [local(): cotangent_full = lax.all_gather(out_grad, 'tensor', axis=0, tiled=True)]
    scatter x1 -> x0, local copies, waits for them, and re-layouts: 90.3 us -> none  [route_slots(): jnp.full((EXPERTS * CAP,), -1, jnp.int32).at[slot_index]]
    all_gather x1, waiting for transfers between devices: 86.9 us -> 0.02 us  [fetch_experts(): lax.all_gather(up_weight, 'dp', axis=1, tiled=True)]
    dot_general x90 -> x12, matrix products: 347 us -> 272 us  [the longest x1 34 us: local(): jnp.einsum('ecf,edf->ecd', up_pre_grad, up_full, preferred_element_type=j...]
    dynamic_slice x80 -> x0, local copies, waits for them, and re-layouts: 64.1 us -> none  [the longest x40 49.8 us: local(): lax.scan(expert_backward, start_carry, backward_blocks)]
  transfers between devices with their start and end apart: 21 -> 21, of which waited for: 12 -> 11; matrix products, arithmetic and copies ran while one was open for 42% -> 33% of each run, Pallas kernels for 0% -> 12%
where the time goes in v1:
time: 2730 us
  waiting for transfers between devices  1040 us (38%)
  matrix products  732 us (27%)
  Pallas kernels  387 us (14%)
  other arithmetic  375 us (14%)
  blocking collectives  88.5 us (3%)
  local copies, waits for them, and re-layouts  86.2 us (3%)
    pallas_call x2, Pallas kernels, gather_rows(): pl.pallas_call(_gather_rows_kernel, grid_spec=pltpu.PrefetchScalarGridSpe...  255 us
    reduce_scatter x1, waiting for transfers between devices, local(): lax.psum_scatter((total_rows + jnp.einsum('tf,df->td', value_grad_low, va...  162 us
    reduce_scatter x1, waiting for transfers between devices, local(): lax.psum_scatter(grad_in_mixture.astype(jnp.bfloat16), 'tensor', scatter_...  161 us
    reduce_scatter x1, waiting for transfers between devices, local(): lax.psum_scatter(jnp.dot(mixed_full, output_full, preferred_element_type=...  161 us
    all_gather x1, waiting for transfers between devices, local(): lax.all_gather(normed_shard.astype(jnp.bfloat16), 'tensor', axis=0, tiled...  133 us
    pallas_call x2, Pallas kernels, combine_rows(): pl.pallas_call(_combine_rows_kernel, grid_spec=pltpu.PrefetchScalarGridSp...  132 us
    reduce_scatter x1, waiting for transfers between devices, local(): lax.psum_scatter(mixture_sum.astype(jnp.bfloat16), 'tensor', scatter_dime...  116 us
    convert_element_type x6, other arithmetic, local(): score_grad = (soft_full * (weight_grad - delta)).astype(jnp.bfloat16)  109 us
  transfers between devices with their start and end apart: 21, of which 11 were waited for; matrix products, arithmetic and copies ran while one was open for 33% of the time, Pallas kernels for 12%

profile of v1, /device:TPU:0, one launch (start us, length us, event | category | flops | bytes accessed | tf_op | source)
XLA Modules:
  0.0 2727.9 jit_solution(8277209054610568303)
XLA Ops:
  13.1 16.0 all-reduce.8
  44.8 9.8 all_gather.44
  66.4 133.3 %all-gather.11.cloned.1.call-done = bf16[3072,1536]{1,0:T(8,128)(2,1)} async-done(((bf16[768,1536]{1,0:T(8,128)(2,1)}), bf16[3072,1536]{1,0:T(8,128)(2,1)}) %all-gather.11.cloned.1.call-update) | async-done | bytes 9437200 | tf_op jit(solution)/shard_map/all_gather | solution.py:303
  213.5 10.2 all-gather.13.cloned.1.call-done
  254.4 8.9 fusion.22
  286.3 14.1 fusion.242
  300.4 12.7 fusion.8
  313.2 13.0 fusion.154
  326.2 14.3 fusion.243
  340.5 14.8 fusion.3
  355.3 14.4 fusion.155
  369.7 10.6 fusion.153
  381.9 9.0 convolution_convert_fusion.3
  391.6 160.7 %reduce-scatter.15.cloned.1.call-done = bf16[768,1536]{1,0:T(8,128)(2,1)} async-done(((bf16[3072,1536]{1,0:T(8,128)(2,1)}), bf16[768,1536]{1,0:T(8,128)(2,1)}) %reduce-scatter.15.cloned.1.call-update) | async-done | bytes 2359312 | tf_op jit(solution)/shard_map/reduce_scatter | solution.py:337
  559.9 9.2 all-gather
  570.7 14.6 fusion.99
  626.0 95.4 %all-gather.25.cloned.1.call-done = bf16[3072,1536]{1,0:T(8,128)(2,1)} async-done(((bf16[768,1536]{1,0:T(8,128)(2,1)}), bf16[3072,1536]{1,0:T(8,128)(2,1)}) %all-gather.25.cloned.1.call-update) | async-done | bytes 9437200 | tf_op jit(solution)/shard_map/all_gather | solution.py:377
  721.4 14.8 fusion.40.src_ref
  736.2 127.4 %shard_map.250 = bf16[7680,1536]{1,0:T(8,128)(2,1)} custom-call(s32[7680]{0:T(1024)} %get-tuple-element.219.tok_ref, f32[3072,1536]{1,0:T(8,128)} %fusion.40.src_ref), custom_call_target="tpu_custom_call" | custom-call | tf_op jit(solution)/shard_map/pallas_call | solution.py:143
  863.7 24.7 all-gather.17.cloned.1.call-done
  888.4 14.3 convert_element_type.316.src_ref
  902.7 127.6 %shard_map.248 = bf16[7680,1536]{1,0:T(8,128)(2,1)} custom-call(s32[7680]{0:T(1024)} %get-tuple-element.219.tok_ref, f32[3072,1536]{1,0:T(8,128)} %convert_element_type.316.src_ref), custom_call_target="tpu_custom_call" | custom-call | tf_op jit(solution)/shard_map/pallas_call | solution.py:143
  1037.7 28.4 %fusion.249 = f32[10,768,512]{1,2,0:T(8,128)} fusion(bf16[10,768,1536]{2,1,0:T(8,128)(2,1)} %bitcast.493, bf16[10,1536,512]{2,1,0:T(8,128)(2,1)} %all-gather.21.cloned.1.call-done), kind=kOutput, calls=%fused_computation.400 | convolution fusion | flops 12079595520 | bytes 55050240 | tf_op jit(solution)/shard_map/ecd,edf->ecf/dot_general | solution.py:366
  1066.1 28.6 %fusion.248 = f32[10,768,512]{1,2,0:T(8,128)} fusion(bf16[10,768,1536]{2,1,0:T(8,128)(2,1)} %bitcast.494, bf16[10,1536,512]{2,1,0:T(8,128)(2,1)} %all-gather.19.cloned.1.call-done), kind=kOutput, calls=%fused_computation.399 | convolution fusion | flops 12079595520 | bytes 55050240 | tf_op jit(solution)/shard_map/ecd,edf->ecf/dot_general | solution.py:365
  1094.7 53.6 %all-gather.23.cloned.1.call-done = bf16[10,512,1536]{1,2,0:T(8,128)(2,1)} async-done(((bf16[10,512,192]{1,2,0:T(8,128)(2,1)}), bf16[10,512,1536]{1,2,0:T(8,128)(2,1)}) %all-gather.23.cloned.1.call-update) | async-done | bytes 15728656 | tf_op jit(solution)/shard_map/all_gather | solution.py:250
  1148.3 31.5 %multiply_reduce_fusion = (f32[10,768]{1,0:T(8,128)S(1)}, f32[10,768,512]{1,2,0:T(8,128)}) fusion(f32[10,768,512]{1,2,0:T(8,128)} %fusion.249, f32[10,768,512]{1,2,0:T(8,128)} %fusion.248, bf16[10,768,1536]{2,1,0:T(8,128)(2,1)} %bitcast.497, bf16[10,512,1536]{1,2,0:T(8,128)(2,1)} %all-gather.23.cloned.1.call-done), kind=kOutput, calls=%fused_computation.57 | convolution fusion | flops 12107112448 | bytes 86538240 | tf_op jit(solution)/shard_map/ecd,efd->ecf/dot_general | solution.py:384
  1179.9 44.7 %scatter_custom_fusion = f32[24576]{0:T(1024)S(1)} fusion(s32[7680]{0:T(1024)S(1)} %maximum_bitcast_fusion, f32[7680]{0:T(1024)S(1)} %get-tuple-element.182, f32[]{:T(128)} %constant.434.clone.1), kind=kCustom, calls=%fused_computation.327 | custom fusion | flops 7680 | bytes 98308 | tf_op jit(solution)/shard_map/scatter-add | solution.py:386
  1227.6 39.8 %gather_fusion = f32[7680]{0:T(1024)S(1)} fusion(f32[24576]{0:T(1024)S(1)} %div.161, s32[8192]{0:T(1024)S(1)} %pad_clamp_fusion), kind=kCustom, calls=%fused_computation | custom fusion | bytes 92160 | tf_op jit(solution)/shard_map/jit(_take)/gather | solution.py:359
  1267.5 24.9 multiply_convert_fusion.1
  1292.3 27.3 %fusion.251 = f32[10,768,1536]{2,1,0:T(8,128)} fusion(bf16[10,768,512]{1,2,0:T(8,128)(2,1)} %get-tuple-element.185, bf16[10,1536,512]{2,1,0:T(8,128)(2,1)} %all-gather.19.cloned.1.call-done), kind=kOutput, calls=%fused_computation.402 | convolution fusion | flops 12079595520 | bytes 70778880 | tf_op jit(solution)/shard_map/ecf,edf->ecd/dot_general | solution.py:392
  1319.6 34.0 %add_convert_fusion = bf16[10,768,1536]{2,1,0:T(8,128)(2,1)} fusion(f32[10,768,1536]{2,1,0:T(8,128)} %fusion.251, bf16[10,768,512]{1,2,0:T(8,128)(2,1)} %get-tuple-element.184, bf16[10,1536,512]{2,1,0:T(8,128)(2,1)} %all-gather.21.cloned.1.call-done), kind=kOutput, calls=%fused_computation.2 | convolution fusion | flops 12103188480 | bytes 94371840 | tf_op jit(solution)/shard_map/ecf,edf->ecd/dot_general | solution.py:394
  1353.6 25.7 bitcast_convert_fusion.add_ref
  1379.4 66.0 %shard_map.251 = f32[3072,1536]{1,0:T(8,128)} custom-call(s32[7680]{0:T(1024)S(1)} %copy-done, f32[7680,1536]{1,0:T(8,128)} %bitcast_convert_fusion.add_ref), custom_call_target="tpu_custom_call" | custom-call | tf_op jit(solution)/shard_map/pallas_call | solution.py:182
  1445.4 14.7 add_convert_fusion.2
  1460.2 160.9 %reduce-scatter.19.cloned.1.call-done = bf16[768,1536]{1,0:T(8,128)(2,1)} async-done(((bf16[3072,1536]{1,0:T(8,128)(2,1)}), bf16[768,1536]{1,0:T(8,128)(2,1)}) %reduce-scatter.19.cloned.1.call-update) | async-done | bytes 2359312 | tf_op jit(solution)/shard_map/reduce_scatter | solution.py:413
  1630.3 13.1 fusion.254
  1643.5 22.9 convolution_convert_fusion
  1666.4 21.4 convolution_convert_fusion.1
  1691.1 21.4 convolution_convert_fusion.2
  1712.8 85.3 %all-gather.27.cloned.1.call-done = bf16[3072,1536]{1,0:T(8,128)(2,1)} async-done(((bf16[768,1536]{1,0:T(8,128)(2,1)}), bf16[3072,1536]{1,0:T(8,128)(2,1)}) %all-gather.27.cloned.1.call-update) | async-done | bytes 9437200 | tf_op jit(solution)/shard_map/all_gather | solution.py:420
  1836.2 12.5 fusion.17
  1868.9 13.5 fusion.19
  1888.0 10.7 fusion.135
  1898.7 15.1 fusion.96
  1913.7 19.4 fusion.103
  1940.5 17.9 fusion.9
  1958.4 17.5 fusion.11
  1984.4 23.7 fusion.4
  2008.0 32.8 %fusion.6 = bf16[2,3,512,2560]{2,3,1,0:T(8,128)(2,1)} fusion(f32[2,2560,512,3]{2,1,3,0:T(8,128)} %get-tuple-element.244, f32[2,3,512,2560]{2,3,1,0:T(8,128)} %get-tuple-element.230, f32[2,3,512]{2,1,0:T(4,128)S(1)} %get-tuple-element.243, f32[2,3,512]{2,1,0:T(4,128)S(1)} %log_add_fusion.1), kind=kLoop, calls=%fused_computation.17 | loop fusion | flops 31457280 | bytes 78667776 | tf_op jit(solution)/shard_map/convert_element_type | solution.py:446
  2040.9 11.6 fusion.85
  2052.5 28.6 %fusion = (f32[2,3,512]{2,1,0:T(4,128)S(1)}, f32[2,3072,512,3]{2,1,3,0:T(8,128)}) fusion(f32[2,3,512,3072]{2,3,1,0:T(8,128)} %get-tuple-element.232, f32[2,3,512]{2,1,0:T(4,128)S(1)} %copy-done.67, bf16[3072,2,64,1]{0,2,3,1:T(8,128)(2,1)S(1)} %bitcast.500, bf16[512,2,3,64]{0,3,2,1:T(8,128)(2,1)S(1)} %bitcast.505), kind=kOutput, calls=%fused_computation.5 | convolution fusion | flops 1236268032 | bytes 76701696 | tf_op jit(solution)/shard_map/qgrd,kgd->grqk/dot_general | solution.py:442
  2081.0 33.0 %fusion.2 = bf16[2,3,512,3072]{2,3,1,0:T(8,128)(2,1)} fusion(f32[2,3072,512,3]{2,1,3,0:T(8,128)} %get-tuple-element.246, f32[2,3,512,3072]{2,3,1,0:T(8,128)} %get-tuple-element.232, f32[2,3,512]{2,1,0:T(4,128)S(1)} %get-tuple-element.245, f32[2,3,512]{2,1,0:T(4,128)S(1)} %copy-done.67), kind=kLoop, calls=%fused_computation.7 | loop fusion | flops 37748736 | bytes 94396416 | tf_op jit(solution)/shard_map/convert_element_type | solution.py:446
  2114.1 13.5 fusion.86
  2129.6 11.9 fusion.141
  2141.5 10.0 fusion.149
  2188.4 10.6 fusion.252
  2207.8 17.5 add_convert_fusion.1
  2225.6 27.5 %fusion.250 = f32[10,768,1536]{2,1,0:T(8,128)} fusion(bf16[10,768,512]{1,2,0:T(8,128)(2,1)} %get-tuple-element.186, bf16[10,512,1536]{1,2,0:T(8,128)(2,1)} %all-gather.23.cloned.1.call-done), kind=kOutput, calls=%fused_computation.401 | convolution fusion | flops 12079595520 | bytes 70778880 | tf_op jit(solution)/shard_map/ecf,efd->ecd/dot_general | solution.py:369
  2253.0 66.3 %shard_map.249 = f32[3072,1536]{1,0:T(8,128)} custom-call(s32[7680]{0:T(1024)S(1)} %copy-done.1, f32[7680,1536]{1,0:T(8,128)} %bitcast.488), custom_call_target="tpu_custom_call" | custom-call | tf_op jit(solution)/shard_map/pallas_call | solution.py:182
  2319.4 11.3 convert_element_type.318
  2349.0 34.0 %reduce-scatter.23.cloned.1.call-done = bf16[192,384]{1,0:T(8,128)(2,1)} async-done(((bf16[1536,384]{1,0:T(8,128)(2,1)}), bf16[192,384]{1,0:T(8,128)(2,1)}) %reduce-scatter.23.cloned.1.call-update) | async-done | bytes 147472 | tf_op jit(solution)/shard_map/reduce_scatter | solution.py:499
  2384.6 161.8 %reduce-scatter.21.cloned.1.call-done = bf16[768,1536]{1,0:T(8,128)(2,1)} async-done(((bf16[3072,1536]{1,0:T(8,128)(2,1)}), bf16[768,1536]{1,0:T(8,128)(2,1)}) %reduce-scatter.21.cloned.1.call-update) | async-done | bytes 2359312 | tf_op jit(solution)/shard_map/reduce_scatter | solution.py:485
  2549.6 44.9 %all-reduce.7 = (f32[1536]{0:T(1024)S(1)}, f32[1536]{0:T(1024)S(1)}) all-reduce(f32[1536]{0:T(1024)S(1)} %get-tuple-element.174, f32[1536]{0:T(1024)S(1)} %copy-done.121), channel_id=6, replica_groups=mesh['dp'=8,'tensor'=4] {'dp','tensor'}, use_global_device_ids=true, to_apply=%region_40.41.clone | all-reduce | flops 3072 | bytes 24576
  2595.7 116.2 %reduce-scatter.17.cloned.1.call-done = bf16[768,1536]{1,0:T(8,128)(2,1)} async-done(((bf16[3072,1536]{1,0:T(8,128)(2,1)}), bf16[768,1536]{1,0:T(8,128)(2,1)}) %reduce-scatter.17.cloned.1.call-update) | async-done | bytes 2359312 | tf_op jit(solution)/shard_map/reduce_scatter | solution.py:373
  (489 shorter events, 334.9 us)
Async XLA Ops:
  7.2 27.8 %copy-start.118 = (s32[1,1024]{1,0:T(1,128)S(1)}, s32[1,1024]{1,0:T(1,128)}, u32[]{:S(2)}) copy-start(s32[1,1024]{1,0:T(1,128)} %param.45) | copy-start | bytes 12292
  7.2 29.1 %copy-start.115 = (bf16[192,128]{1,0:T(8,128)(2,1)S(1)}, bf16[192,128]{1,0:T(8,128)(2,1)}, u32[]{:S(2)}) copy-start(bf16[192,128]{1,0:T(8,128)(2,1)} %param.50) | copy-start | bytes 147460
  7.2 37.6 %copy-start.116 = (bf16[192,128]{1,0:T(8,128)(2,1)S(1)}, bf16[192,128]{1,0:T(8,128)(2,1)}, u32[]{:S(2)}) copy-start(bf16[192,128]{1,0:T(8,128)(2,1)} %param.51) | copy-start | bytes 147460
  7.2 192.5 %all-gather.11.cloned.1.call-start = ((), (), s32[]{:S(2)}) async-start(), calls=%async_computation.12 | async-start | bytes 11796480 | tf_op jit(solution)/shard_map/all_gather | solution.py:303
  9.5 26.8 copy-start.113
  33.4 190.3 %all-gather.13.cloned.1.call-start = ((), (), s32[]{:S(2)}) async-start(), calls=%async_computation.13 | async-start | bytes 1327104 | tf_op jit(solution)/shard_map/all_gather | solution.py:292
  34.2 346.4 %all-gather.15.cloned.1.call-start = ((), (), s32[]{:S(2)}) async-start(), calls=%async_computation.14 | async-start | bytes 1327104 | tf_op jit(solution)/shard_map/all_gather | solution.py:295
  34.9 517.3 %reduce-scatter.15.cloned.1.call-start = ((), (), s32[]{:S(2)}) async-start(), calls=%async_computation.15 | async-start | bytes 11796480 | tf_op jit(solution)/shard_map/reduce_scatter | solution.py:337
  44.8 165.3 %copy-start.46 = (bf16[1536,128]{1,0:T(8,128)(2,1)}, bf16[1536,128]{1,0:T(8,128)(2,1)S(1)}, u32[]{:S(2)}) copy-start(bf16[1536,128]{1,0:T(8,128)(2,1)S(1)} %all_gather.45) | copy-start | bytes 1179652
  54.6 152.1 %copy-start.38 = (bf16[1536,128]{1,0:T(8,128)(2,1)}, bf16[1536,128]{1,0:T(8,128)(2,1)S(1)}, u32[]{:S(2)}) copy-start(bf16[1536,128]{1,0:T(8,128)(2,1)S(1)} %all_gather.44) | copy-start | bytes 1179652
  59.7 171.1 %copy-start.25 = (f32[3072,32]{0,1:T(8,128)}, f32[3072,32]{0,1:T(8,128)S(1)}, u32[]{:S(2)}) copy-start(f32[3072,32]{0,1:T(8,128)S(1)} %get-tuple-element.215) | copy-start | bytes 1179652
  59.7 171.1 %copy-start.27 = (f32[3072,32]{0,1:T(8,128)}, f32[3072,32]{0,1:T(8,128)S(1)}, u32[]{:S(2)}) copy-start(f32[3072,32]{0,1:T(8,128)S(1)} %get-tuple-element.216) | copy-start | bytes 1179652
  206.8 28.0 %copy-start.69 = (bf16[512,128]{0,1:T(8,128)(2,1)}, bf16[512,128]{0,1:T(8,128)(2,1)S(1)}, u32[]{:S(2)}) copy-start(bf16[512,128]{0,1:T(8,128)(2,1)S(1)} %slice.486) | copy-start | bytes 393220
  213.5 32.3 %copy-start.15 = (bf16[3072,2,32]{0,2,1:T(8,128)(2,1)}, bf16[3072,2,32]{0,2,1:T(8,128)(2,1)S(1)}, u32[]{:S(2)}) copy-start(bf16[3072,2,32]{0,2,1:T(8,128)(2,1)S(1)} %get-tuple-element.208) | copy-start | bytes 1179652
  213.5 112.7 %copy-start.12 = (bf16[3072,2,32]{0,2,1:T(8,128)(2,1)}, bf16[3072,2,32]{0,2,1:T(8,128)(2,1)S(1)}, u32[]{:S(2)}) copy-start(bf16[3072,2,32]{0,2,1:T(8,128)(2,1)S(1)} %get-tuple-element.207) | copy-start | bytes 1179652
  278.0 91.7 %copy-start.97 = (f32[2,3,512]{2,1,0:T(4,128)}, f32[2,3,512]{2,1,0:T(4,128)S(1)}, u32[]{:S(2)}) copy-start(f32[2,3,512]{2,1,0:T(4,128)S(1)} %get-tuple-element.227) | copy-start | bytes 36868
  286.3 83.4 %copy-start.99 = (f32[2,3,512]{2,1,0:T(4,128)}, f32[2,3,512]{2,1,0:T(4,128)S(1)}, u32[]{:S(2)}) copy-start(f32[2,3,512]{2,1,0:T(4,128)S(1)} %fusion.13) | copy-start | bytes 36868
  340.5 14.8 copy-start.105
  340.5 14.8 copy-start.23
  355.3 14.4 copy-start.107
  390.9 161.4 %copy-start.5 = (bf16[768,1536]{1,0:T(8,128)(2,1)S(1)}, bf16[768,1536]{1,0:T(8,128)(2,1)}, u32[]{:S(2)}) copy-start(bf16[768,1536]{1,0:T(8,128)(2,1)} %param.43) | copy-start | bytes 7077892
  390.9 330.5 %all-gather.25.cloned.1.call-start = ((), (), s32[]{:S(2)}) async-start(), calls=%async_computation.21 | async-start | bytes 11796480 | tf_op jit(solution)/shard_map/all_gather | solution.py:377
  391.5 496.9 %all-gather.17.cloned.1.call-start = ((), (), s32[]{:S(2)}) async-start(), calls=%async_computation.16 | async-start | bytes 11796480 | tf_op jit(solution)/shard_map/all_gather | solution.py:345
  391.6 166.0 %copy-start.75 = (f32[1536]{0:T(1024)}, f32[1536]{0:T(1024)S(1)}, u32[]{:S(2)}) copy-start(f32[1536]{0:T(1024)S(1)} %convert_element_type.314) | copy-start | bytes 18436
  557.6 480.1 %all-gather.21.cloned.1.call-start = ((), (), s32[]{:S(2)}) async-start(), calls=%async_computation.18 | async-start | bytes 17694720 | tf_op jit(solution)/shard_map/all_gather | solution.py:249
  558.3 507.8 %all-gather.19.cloned.1.call-start = ((), (), s32[]{:S(2)}) async-start(), calls=%async_computation.17 | async-start | bytes 17694720 | tf_op jit(solution)/shard_map/all_gather | solution.py:248
  559.1 589.2 %all-gather.23.cloned.1.call-start = ((), (), s32[]{:S(2)}) async-start(), calls=%async_computation.19 | async-start | bytes 17694720 | tf_op jit(solution)/shard_map/all_gather | solution.py:250
  559.8 1061.3 %reduce-scatter.19.cloned.1.call-start = ((), (), s32[]{:S(2)}) async-start(), calls=%async_computation.22 | async-start | bytes 11796480 | tf_op jit(solution)/shard_map/reduce_scatter | solution.py:413
  569.3 461.0 %copy-start.62 = (bf16[1536,40]{0,1:T(8,128)(2,1)}, bf16[1536,40]{0,1:T(8,128)(2,1)S(1)}, u32[]{:S(2)}) copy-start(bf16[1536,40]{0,1:T(8,128)(2,1)S(1)} %reshape.1276) | copy-start | bytes 368644
  1227.6 39.8 %copy-start.117 = (pred[10,768]{1,0:T(8,128)(4,1)S(1)}, pred[10,768]{1,0:T(8,128)(4,1)}, u32[]{:S(2)}) copy-start(pred[10,768]{1,0:T(8,128)(4,1)} %le.182) | copy-start | bytes 23044
  1353.6 25.8 copy-start
  1379.4 66.0 %copy-start.63 = (bf16[1536,40]{0,1:T(8,128)(2,1)S(1)}, bf16[1536,40]{0,1:T(8,128)(2,1)}, u32[]{:S(2)}) copy-start(bf16[1536,40]{0,1:T(8,128)(2,1)} %copy-done.62) | copy-start | bytes 368644
  1460.1 161.0 %copy-start.6 = (bf16[768,1536]{1,0:T(8,128)(2,1)S(1)}, bf16[768,1536]{1,0:T(8,128)(2,1)}, u32[]{:S(2)}) copy-start(bf16[768,1536]{1,0:T(8,128)(2,1)} %param.43) | copy-start | bytes 7077892
  1460.1 161.0 %copy-start.76 = (f32[1536]{0:T(1024)S(1)}, f32[1536]{0:T(1024)}, u32[]{:S(2)}) copy-start(f32[1536]{0:T(1024)} %copy-done.75) | copy-start | bytes 18436
  1460.1 161.0 %copy-start.85 = (f32[768]{0:T(1024)S(1)}, f32[768]{0:T(1024)}, u32[]{:S(2)}) copy-start(f32[768]{0:T(1024)} %copy-done.84) | copy-start | bytes 9220
  1460.1 338.0 %all-gather.27.cloned.1.call-start = ((), (), s32[]{:S(2)}) async-start(), calls=%async_computation.23 | async-start | bytes 11796480 | tf_op jit(solution)/shard_map/all_gather | solution.py:420
  1630.2 700.5 %reduce-scatter.37.cloned.1.call-start = ((), (), s32[]{:S(2)}) async-start(), calls=%async_computation.32 | async-start | bytes 811008
  1643.4 688.7 %reduce-scatter.35.cloned.1.call-start = ((), (), s32[]{:S(2)}) async-start(), calls=%async_computation.31 | async-start | bytes 17694720 | tf_op jit(solution)/shard_map/reduce_scatter | solution.py:262
  1666.4 669.8 %reduce-scatter.33.cloned.1.call-start = ((), (), s32[]{:S(2)}) async-start(), calls=%async_computation.30 | async-start | bytes 17694720 | tf_op jit(solution)/shard_map/reduce_scatter | solution.py:259
  1688.0 652.4 %reduce-scatter.31.cloned.1.call-start = ((), (), s32[]{:S(2)}) async-start(), calls=%async_computation.29 | async-start | bytes 17694720 | tf_op jit(solution)/shard_map/reduce_scatter | solution.py:256
  1712.6 85.6 %copy-start.124 = (bf16[384,1536]{0,1:T(8,128)(2,1)S(1)}, bf16[384,1536]{0,1:T(8,128)(2,1)}, u32[]{:S(2)}) copy-start(bf16[384,1536]{0,1:T(8,128)(2,1)} %all-gather.15.cloned.1.call-done) | copy-start | bytes 3538948
  1712.6 631.9 %reduce-scatter.27.cloned.1.call-start = ((), (), s32[]{:S(2)}) async-start(), calls=%async_computation.27 | async-start | bytes 442368 | tf_op jit(solution)/shard_map/reduce_scatter | solution.py:505
  1898.6 15.1 copy-start.29
  1958.4 22.0 copy-start.35
  2008.0 32.8 %copy-start.44 = (bf16[512,6,64]{0,2,1:T(8,128)(2,1)S(1)}, bf16[512,6,64]{0,2,1:T(8,128)(2,1)}, u32[]{:S(2)}) copy-start(bf16[512,6,64]{0,2,1:T(8,128)(2,1)} %get-tuple-element.206) | copy-start | bytes 1179652
  2081.0 33.0 %copy-start.34 = (bf16[512,6,64]{0,2,1:T(8,128)(2,1)S(1)}, bf16[512,6,64]{0,2,1:T(8,128)(2,1)}, u32[]{:S(2)}) copy-start(bf16[512,6,64]{0,2,1:T(8,128)(2,1)} %get-tuple-element.201) | copy-start | bytes 1179652
  2114.1 15.5 copy-start.14
  2114.1 15.5 copy-start.19
  2127.7 23.9 slice-start.3
  2129.6 21.9 slice-start.4
  2129.6 21.9 slice-start.5
  2155.8 190.1 %reduce-scatter.25.cloned.1.call-start = ((), (), s32[]{:S(2)}) async-start(), calls=%async_computation.26 | async-start | bytes 442368 | tf_op jit(solution)/shard_map/reduce_scatter | solution.py:502
  2164.2 183.1 %reduce-scatter.29.cloned.1.call-start = ((), (), s32[]{:S(2)}) async-start(), calls=%async_computation.28 | async-start | bytes 1327104 | tf_op jit(solution)/shard_map/reduce_scatter | solution.py:508
  2177.5 205.4 %reduce-scatter.23.cloned.1.call-start = ((), (), s32[]{:S(2)}) async-start(), calls=%async_computation.25 | async-start | bytes 1327104 | tf_op jit(solution)/shard_map/reduce_scatter | solution.py:499
  2188.4 358.0 %reduce-scatter.21.cloned.1.call-start = ((), (), s32[]{:S(2)}) async-start(), calls=%async_computation.24 | async-start | bytes 11796480 | tf_op jit(solution)/shard_map/reduce_scatter | solution.py:485
  2225.3 27.8 %copy-start.1 = (s32[7680]{0:T(1024)S(1)}, s32[7680]{0:T(1024)}, u32[]{:S(2)}) copy-start(s32[7680]{0:T(1024)} %get-tuple-element.219.tok_ref) | copy-start | bytes 92164
  2225.3 486.7 %reduce-scatter.17.cloned.1.call-start = ((), (), s32[]{:S(2)}) async-start(), calls=%async_computation.20 | async-start | bytes 11796480 | tf_op jit(solution)/shard_map/reduce_scatter | solution.py:373
  2336.1 210.3 %copy-start.7 = (bf16[768,1536]{1,0:T(8,128)(2,1)S(1)}, bf16[768,1536]{1,0:T(8,128)(2,1)}, u32[]{:S(2)}) copy-start(bf16[768,1536]{1,0:T(8,128)(2,1)} %param.43) | copy-start | bytes 7077892
  2336.2 210.3 %copy-start.83 = (f32[1536]{0:T(1024)S(1)}, f32[1536]{0:T(1024)}, u32[]{:S(2)}) copy-start(f32[1536]{0:T(1024)} %copy-done.82) | copy-start | bytes 18436
  2336.2 210.3 %copy-start.114 = (f32[768]{0:T(1024)S(1)}, f32[768]{0:T(1024)}, u32[]{:S(2)}) copy-start(f32[768]{0:T(1024)} %copy-done.113) | copy-start | bytes 9220
  2340.4 209.2 %copy-start.121 = (f32[1536]{0:T(1024)S(1)}, f32[1536]{0:T(1024)}, u32[]{:S(2)}) copy-start(f32[1536]{0:T(1024)} %get-tuple-element.172) | copy-start | bytes 18436
  2340.4 371.6 %copy-start.77 = (f32[1536]{0:T(1024)S(1)}, f32[1536]{0:T(1024)}, u32[]{:S(2)}) copy-start(f32[1536]{0:T(1024)} %copy-done.75) | copy-start | bytes 18436
  2340.4 371.6 %copy-start.86 = (f32[768]{0:T(1024)S(1)}, f32[768]{0:T(1024)}, u32[]{:S(2)}) copy-start(f32[768]{0:T(1024)} %copy-done.84) | copy-start | bytes 9220
  2340.4 371.6 %copy-start.120 = (f32[768]{0:T(1024)S(1)}, f32[768]{0:T(1024)}, u32[]{:S(2)}) copy-start(f32[768]{0:T(1024)} %copy-done.119) | copy-start | bytes 9220
  (92 other events, 558.6 us)
Sparse Core Ops, SparseCore 0:
  33.5 166.1 all-gather.10
  201.6 22.0 all-gather.12
  225.6 23.9 all-gather.14
  391.0 161.1 reduce-scatter.14
  553.7 167.6 all-gather.24
  723.4 164.9 all-gather.16
  890.3 83.4 all-gather.20
  975.7 85.2 all-gather.18
  1062.9 85.2 all-gather.22
  1460.2 160.7 reduce-scatter.18
  1630.3 167.7 all-gather.26
  1803.1 94.4 reduce-scatter.36
  1901.0 106.4 reduce-scatter.34
  2010.9 107.3 reduce-scatter.32
  2121.6 107.3 reduce-scatter.30
  2231.9 33.8 reduce-scatter.26
  2268.7 33.8 reduce-scatter.24
  2305.8 36.6 reduce-scatter.28
  2346.3 36.6 reduce-scatter.22
  2385.2 161.1 reduce-scatter.20
  2548.8 163.1 reduce-scatter.16

commit v2 on v1

--- a/solution.py
+++ b/solution.py
@@ -253,15 +253,9 @@
 
 def reduce_experts(grads):
     return (
-        lax.psum_scatter(
-            grads[0].astype(jnp.bfloat16), "dp", scatter_dimension=1, tiled=True
-        ).astype(jnp.float32),
-        lax.psum_scatter(
-            grads[1].astype(jnp.bfloat16), "dp", scatter_dimension=1, tiled=True
-        ).astype(jnp.float32),
-        lax.psum_scatter(
-            grads[2].astype(jnp.bfloat16), "dp", scatter_dimension=2, tiled=True
-        ).astype(jnp.float32),
+        lax.psum_scatter(grads[0], "dp", scatter_dimension=1, tiled=True).astype(jnp.float32),
+        lax.psum_scatter(grads[1], "dp", scatter_dimension=1, tiled=True).astype(jnp.float32),
+        lax.psum_scatter(grads[2], "dp", scatter_dimension=2, tiled=True).astype(jnp.float32),
     )
 
 
@@ -301,6 +295,11 @@
     residual = hidden_in.astype(jnp.float32)
     normed_shard, unit_one, inverse_one = rms_forward(residual, gain_one)
     normed_full = lax.all_gather(normed_shard.astype(jnp.bfloat16), "tensor", axis=0, tiled=True)
+    gate_weight, up_weight, normed_full = lax.optimization_barrier(
+        (gate_weight, up_weight, normed_full)
+    )
+    gate_full = lax.all_gather(gate_weight, "dp", axis=1, tiled=True)
+    up_full = lax.all_gather(up_weight, "dp", axis=1, tiled=True)
     positions, segments = group_layout(segment_ids[0], PROMPT)
     cosine_table, sine_table = rope_tables(positions, HD)
     query_pre = jnp.dot(normed_full, query_full, preferred_element_type=jnp.float32).reshape(
@@ -334,8 +333,14 @@
         )
         mixed_blocks.append(mixed.astype(jnp.bfloat16).reshape(QBLK, local_heads * HD))
     mixed_full = jnp.concatenate(mixed_blocks, axis=0)
+    attended_partial = jnp.dot(
+        mixed_full, output_full, preferred_element_type=jnp.float32
+    ).astype(jnp.bfloat16)
+    attended_partial, gate_full, up_full = lax.optimization_barrier(
+        (attended_partial, gate_full, up_full)
+    )
     attended = lax.psum_scatter(
-        jnp.dot(mixed_full, output_full, preferred_element_type=jnp.float32).astype(jnp.bfloat16),
+        attended_partial,
         "tensor",
         scatter_dimension=0,
         tiled=True,
@@ -343,7 +348,8 @@
     middle = residual + RESIDUAL_SCALE * attended
     normed_two, unit_two, inverse_two = rms_forward(middle, gain_two)
     mixture_in = lax.all_gather(normed_two.astype(jnp.bfloat16), "tensor", axis=0, tiled=True)
-    gate_full, up_full, down_full = fetch_experts(gate_weight, up_weight, down_weight)
+    down_weight, mixture_in = lax.optimization_barrier((down_weight, mixture_in))
+    down_full = lax.all_gather(down_weight, "dp", axis=2, tiled=True)
     logits = jnp.dot(mixture_in, router_full, preferred_element_type=jnp.float32)
     routed_marks = (
         expert_ids[:, :, None] == jnp.arange(EXPERTS, dtype=jnp.int32)[None, None, :]
@@ -370,14 +376,15 @@
         "ecf,efd->ecd", hidden_units, down_full, preferred_element_type=jnp.float32
     )
     mixture_sum = combine_rows(slot_token, expert_out.reshape(slot_count, D), CAP, TOK_GRP)
+    out_grad_held, down_full = lax.optimization_barrier((out_grad, down_full))
+    cotangent_full = lax.all_gather(out_grad_held, "tensor", axis=0, tiled=True)
+    scaled_cotangent = (
+        (RESIDUAL_SCALE * cotangent_full.astype(jnp.float32)).astype(jnp.bfloat16).astype(jnp.float32)
+    )
+    scaled_cotangent, mixture_sum = lax.optimization_barrier((scaled_cotangent, mixture_sum))
     mixture_part = lax.psum_scatter(
         mixture_sum.astype(jnp.bfloat16), "tensor", scatter_dimension=0, tiled=True
     ).astype(jnp.float32)
-    block_output = (middle + RESIDUAL_SCALE * mixture_part).astype(jnp.bfloat16)
-    cotangent_full = lax.all_gather(out_grad, "tensor", axis=0, tiled=True)
-    scaled_cotangent = (
-        (RESIDUAL_SCALE * cotangent_full.astype(jnp.float32)).astype(jnp.bfloat16).astype(jnp.float32)
-    )
     out_rows = gather_rows(slot_token, scaled_cotangent, CAP, jnp.bfloat16).reshape(
         local_experts, CAP, D
     )
@@ -394,13 +401,17 @@
     ) + jnp.einsum("ecf,edf->ecd", up_pre_grad, up_full, preferred_element_type=jnp.float32)
     input_rows = input_rows.astype(jnp.bfloat16).astype(jnp.float32).reshape(slot_count, D)
     grad_in_mixture = combine_rows(slot_token, input_rows, CAP, TOK_GRP)
+    (inputs, gate_pre_grad, up_pre_grad, hidden_units, out_rows), grad_in_mixture = (
+        lax.optimization_barrier(
+            ((inputs, gate_pre_grad, up_pre_grad, hidden_units, out_rows), grad_in_mixture)
+        )
+    )
     expert_parts = (
         jnp.einsum("ecd,ecf->edf", inputs, gate_pre_grad, preferred_element_type=jnp.float32),
         jnp.einsum("ecd,ecf->edf", inputs, up_pre_grad, preferred_element_type=jnp.float32),
         jnp.einsum("ecf,ecd->efd", hidden_units, out_rows, preferred_element_type=jnp.float32),
     )
-    expert_parts = reduce_experts(expert_parts)
-    gate_weight_grad, up_weight_grad, down_weight_grad = expert_parts
+    expert_parts = tuple(part.astype(jnp.bfloat16) for part in expert_parts)
     gates_grad = gate_grad_pair.reshape(TOK_GRP, TOPK)
     routed_grad = gates * (gates_grad - jnp.sum(gates * gates_grad, axis=-1, keepdims=True))
     logits_grad = jnp.sum(routed_marks * routed_grad[:, :, None], axis=1)
@@ -410,8 +421,12 @@
     grad_in_mixture = grad_in_mixture + jnp.einsum(
         "te,de->td", logits_grad, router_full.astype(jnp.float32), precision=HIGHEST
     )
+    mixture_grad_low, mixture_part = lax.optimization_barrier(
+        (grad_in_mixture.astype(jnp.bfloat16), mixture_part)
+    )
+    block_output = (middle + RESIDUAL_SCALE * mixture_part).astype(jnp.bfloat16)
     mixture_grad_shard = lax.psum_scatter(
-        grad_in_mixture.astype(jnp.bfloat16), "tensor", scatter_dimension=0, tiled=True
+        mixture_grad_low, "tensor", scatter_dimension=0, tiled=True
     ).astype(jnp.float32)
     middle_norm_grad, gain_two_grad = rms_backward(
         mixture_grad_shard, unit_two, inverse_two, gain_two
@@ -419,6 +434,13 @@
     middle_grad = out_grad.astype(jnp.float32) + middle_norm_grad
     attended_grad = lax.all_gather(
         (RESIDUAL_SCALE * middle_grad).astype(jnp.bfloat16), "tensor", axis=0, tiled=True
+    )
+    expert_parts, router_part, attended_grad = lax.optimization_barrier(
+        (expert_parts, router_part, attended_grad)
+    )
+    expert_grads = reduce_experts(expert_parts)
+    router_weight_grad = lax.psum_scatter(
+        router_part, ("dp", "tensor"), scatter_dimension=0, tiled=True
     )
     output_part = jnp.einsum(
         "tf,td->fd", mixed_full, attended_grad, preferred_element_type=jnp.float32
@@ -457,6 +479,11 @@
         value_grad = value_grad.at[:key_end].add(
             jnp.einsum("grqk,qgrd->kgd", soft_low, out_block, preferred_element_type=jnp.float32)
         )
+        if block_index == block_count - 2:
+            key_grad, value_grad, expert_grads, router_weight_grad = lax.optimization_barrier(
+                (key_grad, value_grad, expert_grads, router_weight_grad)
+            )
+    gate_weight_grad, up_weight_grad, down_weight_grad = expert_grads
     query_rot_grad = jnp.concatenate(query_blocks, axis=0).reshape(TOK_GRP, local_heads, HD)
     query_grad = (
         rotate_back(query_rot_grad, cosine_table, sine_table)
@@ -469,50 +496,48 @@
         .reshape(TOK_GRP, local_groups * HD)
     )
     value_grad_low = value_grad.astype(jnp.bfloat16).reshape(TOK_GRP, local_groups * HD)
-    query_part = jnp.einsum(
-        "td,tf->df", normed_full, query_grad, preferred_element_type=jnp.float32
-    )
-    key_part = jnp.einsum(
-        "td,tf->df", normed_full, key_grad_low, preferred_element_type=jnp.float32
-    )
-    value_part = jnp.einsum(
-        "td,tf->df", normed_full, value_grad_low, preferred_element_type=jnp.float32
-    )
     total_rows = jnp.einsum("tf,df->td", query_grad, query_full, preferred_element_type=jnp.float32)
     total_rows = total_rows + jnp.einsum(
         "tf,df->td", key_grad_low, key_full, preferred_element_type=jnp.float32
     )
+    normed_grad_low = (
+        total_rows
+        + jnp.einsum("tf,df->td", value_grad_low, value_full, preferred_element_type=jnp.float32)
+    ).astype(jnp.bfloat16)
+    normed_grad_low, query_grad, key_grad_low, value_grad_low = lax.optimization_barrier(
+        (normed_grad_low, query_grad, key_grad_low, value_grad_low)
+    )
     normed_grad = lax.psum_scatter(
-        (
-            total_rows
-            + jnp.einsum(
-                "tf,df->td", value_grad_low, value_full, preferred_element_type=jnp.float32
-            )
-        ).astype(jnp.bfloat16),
-        "tensor",
-        scatter_dimension=0,
-        tiled=True,
-    ).astype(jnp.float32)
+        normed_grad_low, "tensor", scatter_dimension=0, tiled=True
+    ).astype(jnp.float32)
+    query_part = jnp.einsum(
+        "td,tf->df", normed_full, query_grad, preferred_element_type=jnp.float32
+    )
+    key_part = jnp.einsum(
+        "td,tf->df", normed_full, key_grad_low, preferred_element_type=jnp.float32
+    )
+    value_part = jnp.einsum(
+        "td,tf->df", normed_full, value_grad_low, preferred_element_type=jnp.float32
+    )
+    projection_parts = jnp.concatenate(
+        [query_part, key_part, value_part], axis=1
+    ).astype(jnp.bfloat16)
+    projection_parts, normed_grad = lax.optimization_barrier((projection_parts, normed_grad))
     input_norm_grad, gain_one_grad = rms_backward(normed_grad, unit_one, inverse_one, gain_one)
     input_grad = middle_grad + input_norm_grad
-    query_weight_grad, key_weight_grad, value_weight_grad, output_weight_grad = (
-        lax.psum_scatter(
-            query_part.astype(jnp.bfloat16), "dp", scatter_dimension=0, tiled=True
-        ).astype(jnp.float32),
-        lax.psum_scatter(
-            key_part.astype(jnp.bfloat16), "dp", scatter_dimension=0, tiled=True
-        ).astype(jnp.float32),
-        lax.psum_scatter(
-            value_part.astype(jnp.bfloat16), "dp", scatter_dimension=0, tiled=True
-        ).astype(jnp.float32),
-        lax.psum_scatter(
-            output_part.astype(jnp.bfloat16), "dp", scatter_dimension=1, tiled=True
-        ).astype(jnp.float32),
-    )
-    attention_gain_grad, mixture_gain_grad, router_weight_grad = (
+    projection_grads = lax.psum_scatter(
+        projection_parts, "dp", scatter_dimension=0, tiled=True
+    ).astype(jnp.float32)
+    query_width, key_width = query_part.shape[1], key_part.shape[1]
+    query_weight_grad = projection_grads[:, :query_width]
+    key_weight_grad = projection_grads[:, query_width : query_width + key_width]
+    value_weight_grad = projection_grads[:, query_width + key_width :]
+    output_weight_grad = lax.psum_scatter(
+        output_part.astype(jnp.bfloat16), "dp", scatter_dimension=1, tiled=True
+    ).astype(jnp.float32)
+    attention_gain_grad, mixture_gain_grad = (
         lax.psum_scatter(gain_one_grad, ("dp", "tensor"), scatter_dimension=0, tiled=True),
         lax.psum_scatter(gain_two_grad, ("dp", "tensor"), scatter_dimension=0, tiled=True),
-        lax.psum_scatter(router_part, ("dp", "tensor"), scatter_dimension=0, tiled=True),
     )
     return (
         block_output,

time: 2730 us -> 2750 us (level)
  local copies, waits for them, and re-layouts: 86.2 us -> 164 us
  waiting for transfers between devices: 1040 us -> 994 us
    all_gather x1, waiting for transfers between devices: 24.7 us -> 168 us  [local(): lax.all_gather(normed_two.astype(jnp.bfloat16), 'tensor', axis=0, tiled=T...]
    reduce_scatter x1, waiting for transfers between devices: 116 us -> 0.01 us  [local(): lax.psum_scatter(mixture_sum.astype(jnp.bfloat16), 'tensor', scatter_dime...]
    all_gather x4, waiting for transfers between devices: 149 us -> 43.4 us  [the longest x1 43.3 us: local(): down_full = lax.all_gather(down_weight, 'dp', axis=2, tiled=True)]
    unnamed x285 -> x353, local copies, waits for them, and re-layouts: 25.8 us -> 104 us
    reduce_scatter x1, waiting for transfers between devices: 0.01 us -> 34.5 us  [local(): lax.psum_scatter(output_part.astype(jnp.bfloat16), 'dp', scatter_dimensio...]
    all_gather x1, waiting for transfers between devices: 133 us -> 165 us  [local(): lax.all_gather(normed_shard.astype(jnp.bfloat16), 'tensor', axis=0, tiled...]
    reduce_scatter x9 -> x5, waiting for transfers between devices: 517 us -> 488 us  [the longest x1 193 us: local(): lax.psum_scatter(mixture_grad_low, 'tensor', scatter_dimension=0, tiled=T...]
  transfers between devices with their start and end apart: 21 -> 19, of which waited for: 11 -> 8; matrix products, arithmetic and copies ran while one was open for 33% -> 42% of each run, Pallas kernels for 12% -> 9%
where the time goes in v2:
time: 2750 us
  waiting for transfers between devices  994 us (36%)
  matrix products  748 us (27%)
  Pallas kernels  374 us (14%)
  other arithmetic  368 us (13%)
  local copies, waits for them, and re-layouts  164 us (6%)
  blocking collectives  84.8 us (3%)
    pallas_call x2, Pallas kernels, gather_rows(): pl.pallas_call(_gather_rows_kernel, grid_spec=pltpu.PrefetchScalarGridSpe...  242 us
    reduce_scatter x1, waiting for transfers between devices, local(): lax.psum_scatter(mixture_grad_low, 'tensor', scatter_dimension=0, tiled=T...  193 us
    all_gather x1, waiting for transfers between devices, local(): lax.all_gather(normed_two.astype(jnp.bfloat16), 'tensor', axis=0, tiled=T...  168 us
    all_gather x1, waiting for transfers between devices, local(): lax.all_gather(normed_shard.astype(jnp.bfloat16), 'tensor', axis=0, tiled...  165 us
    reduce_scatter x1, waiting for transfers between devices, local(): lax.psum_scatter(attended_partial, 'tensor', scatter_dimension=0, tiled=T...  161 us
    reduce_scatter x1, waiting for transfers between devices, local(): lax.psum_scatter(normed_grad_low, 'tensor', scatter_dimension=0, tiled=True)  134 us
    pallas_call x2, Pallas kernels, combine_rows(): pl.pallas_call(_combine_rows_kernel, grid_spec=pltpu.PrefetchScalarGridSp...  131 us
    convert_element_type x6, other arithmetic, local(): score_grad = (soft_full * (weight_grad - delta)).astype(jnp.bfloat16)  118 us
  transfers between devices with their start and end apart: 19, of which 8 were waited for; matrix products, arithmetic and copies ran while one was open for 42% of the time, Pallas kernels for 9%

profile of v2, /device:TPU:0, one launch (start us, length us, event | category | flops | bytes accessed | tf_op | source)
XLA Modules:
  0.0 2751.7 jit_solution(7223788942006787156)
XLA Ops:
  10.9 16.0 all-reduce.8
  35.0 164.7 %all-gather.11.cloned.1.call-done = bf16[3072,1536]{1,0:T(8,128)(2,1)} async-done(((bf16[768,1536]{1,0:T(8,128)(2,1)}), bf16[3072,1536]{1,0:T(8,128)(2,1)}) %all-gather.11.cloned.1.call-update) | async-done | bytes 9437200 | tf_op jit(solution)/shard_map/all_gather | solution.py:297
  200.1 9.5 all_gather.45
  209.6 9.9 all_gather.44
  292.5 9.9 fusion.22
  326.2 11.0 fusion.153
  337.3 14.6 fusion.242
  351.9 12.6 fusion.8
  364.5 13.0 fusion.154
  377.6 14.8 fusion.243
  392.4 14.9 fusion.3
  407.3 15.0 fusion.155
  433.3 160.9 %reduce-scatter.17.cloned.1.call-done = bf16[768,1536]{1,0:T(8,128)(2,1)} async-done(((bf16[3072,1536]{1,0:T(8,128)(2,1)}), bf16[768,1536]{1,0:T(8,128)(2,1)}) %reduce-scatter.17.cloned.1.call-update) | async-done | bytes 2359312 | tf_op jit(solution)/shard_map/reduce_scatter | solution.py:342
  599.6 167.8 %all-gather.21.cloned.1.call-done = bf16[3072,1536]{1,0:T(8,128)(2,1)} async-done(((bf16[768,1536]{1,0:T(8,128)(2,1)}), bf16[3072,1536]{1,0:T(8,128)(2,1)}) %all-gather.21.cloned.1.call-update) | async-done | bytes 9437200 | tf_op jit(solution)/shard_map/all_gather | solution.py:350
  769.6 14.7 fusion.99
  809.6 43.3 %all-gather.23.cloned.1.call-done = bf16[10,512,1536]{1,2,0:T(8,128)(2,1)} async-done(((bf16[10,512,192]{1,2,0:T(8,128)(2,1)}), bf16[10,512,1536]{1,2,0:T(8,128)(2,1)}) %all-gather.23.cloned.1.call-update) | async-done | bytes 15728656 | tf_op jit(solution)/shard_map/all_gather | solution.py:352
  853.8 9.6 all-gather
  879.7 12.7 convert_element_type.302.src_ref
  902.2 39.8 %gather_fusion = f32[7680]{0:T(1024)S(1)} fusion(f32[24576]{0:T(1024)S(1)} %div.161, s32[8192]{0:T(1024)S(1)} %pad_clamp_fusion), kind=kCustom, calls=%fused_computation | custom fusion | bytes 92160 | tf_op jit(solution)/shard_map/jit(_take)/gather | solution.py:365
  942.0 121.2 %shard_map.248 = bf16[7680,1536]{1,0:T(8,128)(2,1)} custom-call(s32[7680]{0:T(1024)} %get-tuple-element.401.tok_ref, f32[3072,1536]{1,0:T(8,128)} %convert_element_type.302.src_ref), custom_call_target="tpu_custom_call" | custom-call | tf_op jit(solution)/shard_map/pallas_call | solution.py:143
  1063.3 27.8 %fusion.248 = f32[10,768,512]{1,2,0:T(8,128)} fusion(bf16[10,768,1536]{2,1,0:T(8,128)(2,1)} %bitcast.508, bf16[10,1536,512]{2,1,0:T(8,128)(2,1)} %all-gather.17.cloned.1.call-done), kind=kOutput, calls=%fused_computation.400 | convolution fusion | flops 12079595520 | bytes 55050240 | tf_op jit(solution)/shard_map/ecd,edf->ecf/dot_general | solution.py:371
  1091.1 32.8 %multiply_convert_fusion.3 = (bf16[10,768,512]{1,2,0:T(8,128)(2,1)}, f32[10,768,512]{1,2,0:T(8,128)}) fusion(f32[10,768]{1,0:T(8,128)S(1)} %select_select_fusion, f32[10,768,512]{1,2,0:T(8,128)} %fusion.248, bf16[10,768,1536]{2,1,0:T(8,128)(2,1)} %bitcast.509, bf16[10,1536,512]{2,1,0:T(8,128)(2,1)} %all-gather.19.cloned.1.call-done), kind=kOutput, calls=%fused_computation.60 | convolution fusion | flops 12107120640 | bytes 78673920 | tf_op jit(solution)/shard_map/ecd,edf->ecf/dot_general | solution.py:372
  1123.9 27.3 fusion.249
  1151.2 65.9 %shard_map.249 = f32[3072,1536]{1,0:T(8,128)} custom-call(s32[7680]{0:T(1024)S(1)} %copy-done, f32[7680,1536]{1,0:T(8,128)} %bitcast.499), custom_call_target="tpu_custom_call" | custom-call | tf_op jit(solution)/shard_map/pallas_call | solution.py:182
  1217.2 12.8 fusion.40.src_ref
  1230.0 121.2 %shard_map.250 = bf16[7680,1536]{1,0:T(8,128)(2,1)} custom-call(s32[7680]{0:T(1024)} %get-tuple-element.401.tok_ref, f32[3072,1536]{1,0:T(8,128)} %fusion.40.src_ref), custom_call_target="tpu_custom_call" | custom-call | tf_op jit(solution)/shard_map/pallas_call | solution.py:143
  1351.2 11.3 convert_element_type.311
  1362.6 34.0 %multiply_reduce_fusion = (f32[10,768]{1,0:T(8,128)S(1)}, bf16[10,768,512]{1,2,0:T(8,128)(2,1)}, bf16[10,768,512]{1,2,0:T(8,128)(2,1)}) fusion(f32[10,768,512]{1,2,0:T(8,128)} %get-tuple-element.416, f32[10,768,512]{1,2,0:T(8,128)} %fusion.248, f32[10,768]{1,0:T(8,128)S(1)} %select_select_fusion, bf16[10,768,1536]{2,1,0:T(8,128)(2,1)} %bitcast.512, ...), kind=kOutput, calls=%fused_computation.57 | convolution fusion | flops 12146434048 | bytes 86568960 | tf_op jit(solution)/shard_map/ecd,efd->ecf/dot_general | solution.py:391
  1396.7 44.3 %scatter_custom_fusion = f32[24576]{0:T(1024)S(1)} fusion(s32[7680]{0:T(1024)} %copy-done.99, f32[7680]{0:T(1024)S(1)} %bitcast_select_fusion.6, f32[]{:T(128)} %constant.434.clone.1), kind=kCustom, calls=%fused_computation.327 | custom fusion | flops 7680 | bytes 98816 | tf_op jit(solution)/shard_map/scatter-add | solution.py:393
  1442.3 27.9 %fusion.250 = f32[10,768,1536]{2,1,0:T(8,128)} fusion(bf16[10,768,512]{1,2,0:T(8,128)(2,1)} %get-tuple-element.225, bf16[10,1536,512]{2,1,0:T(8,128)(2,1)} %all-gather.17.cloned.1.call-done), kind=kOutput, calls=%fused_computation.402 | convolution fusion | flops 12079595520 | bytes 70778880 | tf_op jit(solution)/shard_map/ecf,edf->ecd/dot_general | solution.py:399
  1470.1 34.6 %add_convert_fusion = bf16[10,768,1536]{2,1,0:T(8,128)(2,1)} fusion(f32[10,768,1536]{2,1,0:T(8,128)} %fusion.250, bf16[10,768,512]{1,2,0:T(8,128)(2,1)} %get-tuple-element.226, bf16[10,1536,512]{2,1,0:T(8,128)(2,1)} %all-gather.19.cloned.1.call-done), kind=kOutput, calls=%fused_computation.2 | convolution fusion | flops 12103188480 | bytes 94371840 | tf_op jit(solution)/shard_map/ecf,edf->ecd/dot_general | solution.py:401
  1504.7 25.8 bitcast_convert_fusion.add_ref
  1530.5 65.5 %shard_map.251 = f32[3072,1536]{1,0:T(8,128)} custom-call(s32[7680]{0:T(1024)S(1)} %copy-done.1, f32[7680,1536]{1,0:T(8,128)} %bitcast_convert_fusion.add_ref), custom_call_target="tpu_custom_call" | custom-call | tf_op jit(solution)/shard_map/pallas_call | solution.py:182
  1596.7 14.4 add_convert_fusion.2
  1615.6 192.8 %reduce-scatter.21.cloned.1.call-done = bf16[768,1536]{1,0:T(8,128)(2,1)} async-done(((bf16[3072,1536]{1,0:T(8,128)(2,1)}), bf16[768,1536]{1,0:T(8,128)(2,1)}) %reduce-scatter.21.cloned.1.call-update) | async-done | bytes 2359312 | tf_op jit(solution)/shard_map/reduce_scatter | solution.py:428
  1825.3 23.0 convolution_convert_fusion.1
  1848.2 21.4 convolution_convert_fusion.2
  1869.6 21.6 convolution_convert_fusion
  1891.2 94.2 %all-gather.27.cloned.1.call-done = bf16[3072,1536]{1,0:T(8,128)(2,1)} async-done(((bf16[768,1536]{1,0:T(8,128)(2,1)}), bf16[3072,1536]{1,0:T(8,128)(2,1)}) %all-gather.27.cloned.1.call-update) | async-done | bytes 9437200 | tf_op jit(solution)/shard_map/all_gather | solution.py:435
  1986.8 30.5 %copy.505 = bf16[10,512,1536]{1,0,2:T(8,128)(2,1)} copy(bf16[10,512,1536]{2,1,0:T(8,128)(2,1)} %convolution_convert_fusion) | data formatting | bytes 31457280
  2017.3 24.8 copy.512
  2074.0 9.7 fusion.33
  2083.8 13.0 fusion.17
  2096.8 24.3 fusion.9
  2121.2 20.5 fusion.19
  2145.4 16.5 fusion.11
  2161.9 24.6 fusion.4
  2203.3 33.8 %fusion.6 = bf16[2,3,512,2560]{2,3,1,0:T(8,128)(2,1)} fusion(f32[2,2560,512,3]{2,1,3,0:T(8,128)} %get-tuple-element.426, f32[2,3,512,2560]{2,3,1,0:T(8,128)} %get-tuple-element.412, f32[2,3,512]{2,1,0:T(4,128)S(1)} %copy-done.108, f32[2,3,512]{2,1,0:T(4,128)S(1)} %log_add_fusion.1), kind=kLoop, calls=%fused_computation.17 | loop fusion | flops 31457280 | bytes 78667776 | tf_op jit(solution)/shard_map/convert_element_type | solution.py:468
  2237.1 9.7 fusion.149
  2246.8 29.6 %fusion = (f32[2,3,512]{2,1,0:T(4,128)}, f32[2,3072,512,3]{2,1,3,0:T(8,128)}) fusion(f32[2,3,512,3072]{2,3,1,0:T(8,128)} %get-tuple-element.414, f32[2,3,512]{2,1,0:T(4,128)S(1)} %copy-done.75, bf16[3072,2,64,1]{0,2,3,1:T(8,128)(2,1)S(1)} %bitcast.515, bf16[512,2,3,64]{0,3,2,1:T(8,128)(2,1)S(1)} %bitcast.524), kind=kOutput, calls=%fused_computation.5 | convolution fusion | flops 1236268032 | bytes 76701696 | tf_op jit(solution)/shard_map/qgrd,kgd->grqk/dot_general | solution.py:464
  2276.4 32.6 %fusion.2 = bf16[2,3,512,3072]{2,3,1,0:T(8,128)(2,1)} fusion(f32[2,3072,512,3]{2,1,3,0:T(8,128)} %get-tuple-element.428, f32[2,3,512,3072]{2,3,1,0:T(8,128)} %get-tuple-element.414, f32[2,3,512]{2,1,0:T(4,128)} %get-tuple-element.427, f32[2,3,512]{2,1,0:T(4,128)} %log_add_fusion), kind=kLoop, calls=%fused_computation.7 | loop fusion | flops 37748736 | bytes 94396416 | tf_op jit(solution)/shard_map/convert_element_type | solution.py:468
  2309.1 10.8 fusion.139
  2355.9 10.9 fusion.85
  2366.7 10.9 fusion.135
  2377.7 11.4 fusion.252
  2389.1 14.3 fusion.96
  2427.4 15.8 fusion.103
  2443.2 9.8 fusion.86
  2463.1 17.1 add_convert_fusion.1
  2480.3 9.7 convolution_convert_fusion.7
  2504.6 134.0 %reduce-scatter.27.cloned.1.call-done = bf16[768,1536]{1,0:T(8,128)(2,1)} async-done(((bf16[3072,1536]{1,0:T(8,128)(2,1)}), bf16[768,1536]{1,0:T(8,128)(2,1)}) %reduce-scatter.27.cloned.1.call-update) | async-done | bytes 2359312 | tf_op jit(solution)/shard_map/reduce_scatter | solution.py:510
  2645.4 34.5 %reduce-scatter.29.cloned.1.call-done = bf16[384,192]{0,1:T(8,128)(2,1)} async-done(((bf16[384,1536]{0,1:T(8,128)(2,1)}), bf16[384,192]{0,1:T(8,128)(2,1)}) %reduce-scatter.29.cloned.1.call-update) | async-done | bytes 147472 | tf_op jit(solution)/shard_map/reduce_scatter | solution.py:535
  2690.9 39.7 %all-reduce.7 = (f32[1536]{0:T(1024)S(1)}, f32[1536]{0:T(1024)S(1)}) all-reduce(f32[1536]{0:T(1024)S(1)} %get-tuple-element.356, f32[1536]{0:T(1024)S(1)} %copy-done.138), channel_id=10, replica_groups=mesh['dp'=8,'tensor'=4] {'dp','tensor'}, use_global_device_ids=true, to_apply=%region_44.45.clone | all-reduce | flops 3072 | bytes 24576
  2731.7 9.7 fusion.77
  (558 shorter events, 361.6 us)
Async XLA Ops:
  7.2 192.6 %copy-start.137 = (s32[1,1024]{1,0:T(1,128)S(1)}, s32[1,1024]{1,0:T(1,128)}, u32[]{:S(2)}) copy-start(s32[1,1024]{1,0:T(1,128)} %param.45) | copy-start | bytes 12292
  7.2 192.9 %copy-start.133 = (bf16[192,128]{1,0:T(8,128)(2,1)S(1)}, bf16[192,128]{1,0:T(8,128)(2,1)}, u32[]{:S(2)}) copy-start(bf16[192,128]{1,0:T(8,128)(2,1)} %param.50) | copy-start | bytes 147460
  7.2 202.4 %copy-start.134 = (bf16[192,128]{1,0:T(8,128)(2,1)S(1)}, bf16[192,128]{1,0:T(8,128)(2,1)}, u32[]{:S(2)}) copy-start(bf16[192,128]{1,0:T(8,128)(2,1)} %param.51) | copy-start | bytes 147460
  7.2 192.5 %all-gather.11.cloned.1.call-start = ((), (), s32[]{:S(2)}) async-start(), calls=%async_computation.10 | async-start | bytes 11796480 | tf_op jit(solution)/shard_map/all_gather | solution.py:297
  33.4 210.0 %all-gather.13.cloned.1.call-start = ((), (), s32[]{:S(2)}) async-start(), calls=%async_computation.11 | async-start | bytes 1327104 | tf_op jit(solution)/shard_map/all_gather | solution.py:286
  34.2 388.2 %all-gather.15.cloned.1.call-start = ((), (), s32[]{:S(2)}) async-start(), calls=%async_computation.12 | async-start | bytes 1327104 | tf_op jit(solution)/shard_map/all_gather | solution.py:289
  34.9 397.7 %all-gather.17.cloned.1.call-start = ((), (), s32[]{:S(2)}) async-start(), calls=%async_computation.13 | async-start | bytes 17694720 | tf_op jit(solution)/shard_map/all_gather | solution.py:301
  199.7 232.9 %all-gather.19.cloned.1.call-start = ((), (), s32[]{:S(2)}) async-start(), calls=%async_computation.14 | async-start | bytes 17694720 | tf_op jit(solution)/shard_map/all_gather | solution.py:302
  209.6 43.2 %copy-start.54 = (bf16[1536,128]{1,0:T(8,128)(2,1)}, bf16[1536,128]{1,0:T(8,128)(2,1)S(1)}, u32[]{:S(2)}) copy-start(bf16[1536,128]{1,0:T(8,128)(2,1)S(1)} %all_gather.45) | copy-start | bytes 1179652
  219.6 20.5 copy-start.41
  226.5 33.5 %copy-start.25 = (f32[3072,32]{0,1:T(8,128)}, f32[3072,32]{0,1:T(8,128)S(1)}, u32[]{:S(2)}) copy-start(f32[3072,32]{0,1:T(8,128)S(1)} %get-tuple-element.397) | copy-start | bytes 1179652
  226.5 33.5 %copy-start.28 = (f32[3072,32]{0,1:T(8,128)}, f32[3072,32]{0,1:T(8,128)S(1)}, u32[]{:S(2)}) copy-start(f32[3072,32]{0,1:T(8,128)S(1)} %get-tuple-element.398) | copy-start | bytes 1179652
  260.2 23.0 copy-start.12
  260.2 117.3 %copy-start.10 = (bf16[3072,2,32]{0,2,1:T(8,128)(2,1)}, bf16[3072,2,32]{0,2,1:T(8,128)(2,1)S(1)}, u32[]{:S(2)}) copy-start(bf16[3072,2,32]{0,2,1:T(8,128)(2,1)S(1)} %get-tuple-element.385) | copy-start | bytes 1179652
  271.7 322.6 %reduce-scatter.17.cloned.1.call-start = ((), (), s32[]{:S(2)}) async-start(), calls=%async_computation.15 | async-start | bytes 11796480 | tf_op jit(solution)/shard_map/reduce_scatter | solution.py:342
  432.6 161.6 %copy-start.5 = (bf16[768,1536]{1,0:T(8,128)(2,1)S(1)}, bf16[768,1536]{1,0:T(8,128)(2,1)}, u32[]{:S(2)}) copy-start(bf16[768,1536]{1,0:T(8,128)(2,1)} %param.43) | copy-start | bytes 7077892
  432.7 334.8 %all-gather.21.cloned.1.call-start = ((), (), s32[]{:S(2)}) async-start(), calls=%async_computation.16 | async-start | bytes 11796480 | tf_op jit(solution)/shard_map/all_gather | solution.py:350
  433.3 166.3 %copy-start.88 = (f32[1536]{0:T(1024)}, f32[1536]{0:T(1024)S(1)}, u32[]{:S(2)}) copy-start(f32[1536]{0:T(1024)S(1)} %convert_element_type.300) | copy-start | bytes 18436
  597.1 170.4 %copy-start.73 = (s32[3072,8]{0,1:T(8,128)S(1)}, s32[3072,8]{0,1:T(8,128)}, u32[]{:S(2)}) copy-start(s32[3072,8]{0,1:T(8,128)} %param.46) | copy-start | bytes 294916
  597.1 171.6 %copy-start.100 = (f32[768]{0:T(1024)}, f32[768]{0:T(1024)S(1)}, u32[]{:S(2)}) copy-start(f32[768]{0:T(1024)S(1)} %add_rsqrt_fusion) | copy-start | bytes 9220
  597.1 171.6 %copy-start.104 = (s32[1,24576]{1,0:T(1,128)S(1)}, s32[1,24576]{1,0:T(1,128)}, u32[]{:S(2)}) copy-start(s32[1,24576]{1,0:T(1,128)} %param.47) | copy-start | bytes 294916
  599.6 253.3 %all-gather.23.cloned.1.call-start = ((), (), s32[]{:S(2)}) async-start(), calls=%async_computation.17 | async-start | bytes 17694720 | tf_op jit(solution)/shard_map/all_gather | solution.py:352
  767.5 449.7 %all-gather.25.cloned.1.call-start = ((), (), s32[]{:S(2)}) async-start(), calls=%async_computation.18 | async-start | bytes 11796480 | tf_op jit(solution)/shard_map/all_gather | solution.py:380
  802.6 51.1 %copy-start.139 = (bf16[192,40]{0,1:T(8,128)(2,1)S(1)}, bf16[192,40]{0,1:T(8,128)(2,1)}, u32[]{:S(2)}) copy-start(bf16[192,40]{0,1:T(8,128)(2,1)} %param.54) | copy-start | bytes 46084
  852.9 758.2 %reduce-scatter.19.cloned.1.call-start = ((), (), s32[]{:S(2)}) async-start(), calls=%async_computation.19 | async-start | bytes 11796480 | tf_op jit(solution)/shard_map/reduce_scatter | solution.py:385
  863.6 28.9 %copy-start.69 = (bf16[1536,40]{0,1:T(8,128)(2,1)}, bf16[1536,40]{0,1:T(8,128)(2,1)S(1)}, u32[]{:S(2)}) copy-start(bf16[1536,40]{0,1:T(8,128)(2,1)S(1)} %reshape.1276) | copy-start | bytes 368644
  1123.9 27.3 copy-start
  1362.5 445.9 %reduce-scatter.21.cloned.1.call-start = ((), (), s32[]{:S(2)}) async-start(), calls=%async_computation.20 | async-start | bytes 11796480 | tf_op jit(solution)/shard_map/reduce_scatter | solution.py:428
  1362.6 34.1 %copy-start.107 = (pred[60,128]{1,0:T(8,128)(4,1)S(1)}, pred[60,128]{1,0:T(8,128)(4,1)}, u32[]{:S(2)}) copy-start(pred[60,128]{1,0:T(8,128)(4,1)} %copy-done.106) | copy-start | bytes 23044
  1504.7 25.8 copy-start.1
  1530.5 65.6 %copy-start.49 = (f32[3072,8]{0,1:T(8,128)S(1)}, f32[3072,8]{0,1:T(8,128)}, u32[]{:S(2)}) copy-start(f32[3072,8]{0,1:T(8,128)} %copy-done.48) | copy-start | bytes 294916
  1530.5 65.6 %copy-start.81 = (f32[3072]{0:T(1024)S(1)}, f32[3072]{0:T(1024)}, u32[]{:S(2)}) copy-start(f32[3072]{0:T(1024)} %copy-done.80) | copy-start | bytes 36868
  1530.5 65.6 %copy-start.92 = (f32[3072]{0:T(1024)S(1)}, f32[3072]{0:T(1024)}, u32[]{:S(2)}) copy-start(f32[3072]{0:T(1024)} %copy-done.91) | copy-start | bytes 36868
  1530.5 65.7 %copy-start.74 = (s32[3072,8]{0,1:T(8,128)S(1)}, s32[3072,8]{0,1:T(8,128)}, u32[]{:S(2)}) copy-start(s32[3072,8]{0,1:T(8,128)} %param.46) | copy-start | bytes 294916
  1530.5 66.2 %copy-start.70 = (bf16[1536,40]{0,1:T(8,128)(2,1)S(1)}, bf16[1536,40]{0,1:T(8,128)(2,1)}, u32[]{:S(2)}) copy-start(bf16[1536,40]{0,1:T(8,128)(2,1)} %copy-done.69) | copy-start | bytes 368644
  1615.5 192.9 %copy-start.6 = (bf16[768,1536]{1,0:T(8,128)(2,1)S(1)}, bf16[768,1536]{1,0:T(8,128)(2,1)}, u32[]{:S(2)}) copy-start(bf16[768,1536]{1,0:T(8,128)(2,1)} %param.43) | copy-start | bytes 7077892
  1615.5 192.9 %copy-start.89 = (f32[1536]{0:T(1024)S(1)}, f32[1536]{0:T(1024)}, u32[]{:S(2)}) copy-start(f32[1536]{0:T(1024)} %copy-done.88) | copy-start | bytes 18436
  1615.5 192.9 %copy-start.101 = (f32[768]{0:T(1024)S(1)}, f32[768]{0:T(1024)}, u32[]{:S(2)}) copy-start(f32[768]{0:T(1024)} %copy-done.100) | copy-start | bytes 9220
  1615.6 369.8 %all-gather.27.cloned.1.call-start = ((), (), s32[]{:S(2)}) async-start(), calls=%async_computation.21 | async-start | bytes 11796480 | tf_op jit(solution)/shard_map/all_gather | solution.py:435
  1817.6 585.9 %reduce-scatter.33.cloned.1.call-start = ((), (), s32[]{:S(2)}) async-start(), calls=%async_computation.27 | async-start | bytes 811008
  1986.6 418.2 %reduce-scatter.31.cloned.1.call-start = ((), (), s32[]{:S(2)}) async-start(), calls=%async_computation.26 | async-start | bytes 17694720
  2042.2 377.1 %reduce-scatter.23.cloned.1.call-start = ((), (), s32[]{:S(2)}) async-start(), calls=%async_computation.22 | async-start | bytes 17694720 | tf_op jit(solution)/shard_map/reduce_scatter | solution.py:256
  2042.8 380.6 %reduce-scatter.25.cloned.1.call-start = ((), (), s32[]{:S(2)}) async-start(), calls=%async_computation.23 | async-start | bytes 17694720 | tf_op jit(solution)/shard_map/reduce_scatter | solution.py:257
  2043.0 31.0 %copy-start.86 = (f32[2,3,512]{2,1,0:T(4,128)}, f32[2,3,512]{2,1,0:T(4,128)S(1)}, u32[]{:S(2)}) copy-start(f32[2,3,512]{2,1,0:T(4,128)S(1)} %log_add_fusion.4) | copy-start | bytes 36868
  2043.0 40.7 %copy-start.82 = (f32[2,3,512]{2,1,0:T(4,128)}, f32[2,3,512]{2,1,0:T(4,128)S(1)}, u32[]{:S(2)}) copy-start(f32[2,3,512]{2,1,0:T(4,128)S(1)} %log_add_fusion.3) | copy-start | bytes 36868
  2053.6 108.3 %copy-start.32 = (bf16[512,384]{0,1:T(8,128)(2,1)}, bf16[512,384]{0,1:T(8,128)(2,1)S(1)}, u32[]{:S(2)}) copy-start(bf16[512,384]{0,1:T(8,128)(2,1)S(1)} %get-tuple-element.374) | copy-start | bytes 1179652
  2096.8 24.3 copy-start.83
  2121.1 20.6 slice-start
  2121.1 20.6 slice-start.1
  2121.1 20.6 slice-start.2
  2121.2 21.9 slice-start.3
  2121.2 23.1 slice-start.4
  2121.2 24.2 slice-start.5
  2186.5 452.0 %reduce-scatter.27.cloned.1.call-start = ((), (), s32[]{:S(2)}) async-start(), calls=%async_computation.24 | async-start | bytes 11796480 | tf_op jit(solution)/shard_map/reduce_scatter | solution.py:510
  2309.0 24.5 slice-start.12
  2309.1 24.5 slice-start.13
  2480.2 199.6 %reduce-scatter.29.cloned.1.call-start = ((), (), s32[]{:S(2)}) async-start(), calls=%async_computation.25 | async-start | bytes 1327104 | tf_op jit(solution)/shard_map/reduce_scatter | solution.py:535
  2490.0 251.5 %reduce-scatter.35.cloned.1.call-start = ((), (), s32[]{:S(2)}) async-start(), calls=%async_computation.28 | async-start | bytes 2211840
  2645.4 41.7 %copy-start.7 = (bf16[768,1536]{1,0:T(8,128)(2,1)S(1)}, bf16[768,1536]{1,0:T(8,128)(2,1)}, u32[]{:S(2)}) copy-start(bf16[768,1536]{1,0:T(8,128)(2,1)} %param.43) | copy-start | bytes 7077892
  2645.4 41.7 %copy-start.98 = (f32[1536]{0:T(1024)S(1)}, f32[1536]{0:T(1024)}, u32[]{:S(2)}) copy-start(f32[1536]{0:T(1024)} %copy-done.97) | copy-start | bytes 18436
  2645.4 41.7 %copy-start.132 = (f32[768]{0:T(1024)S(1)}, f32[768]{0:T(1024)}, u32[]{:S(2)}) copy-start(f32[768]{0:T(1024)} %copy-done.131) | copy-start | bytes 9220
  2681.5 50.2 %copy-start.90 = (f32[1536]{0:T(1024)S(1)}, f32[1536]{0:T(1024)}, u32[]{:S(2)}) copy-start(f32[1536]{0:T(1024)} %copy-done.88) | copy-start | bytes 18436
  2681.5 50.2 %copy-start.102 = (f32[768]{0:T(1024)S(1)}, f32[768]{0:T(1024)}, u32[]{:S(2)}) copy-start(f32[768]{0:T(1024)} %copy-done.100) | copy-start | bytes 9220
  2681.5 50.2 %copy-start.136 = (f32[768]{0:T(1024)S(1)}, f32[768]{0:T(1024)}, u32[]{:S(2)}) copy-start(f32[768]{0:T(1024)} %copy-done.135) | copy-start | bytes 9220
  (119 other events, 856.7 us)
Sparse Core Ops, SparseCore 0:
  33.6 166.1 all-gather.10
  201.6 22.1 all-gather.12
  225.7 23.9 all-gather.14
  251.4 85.2 all-gather.16
  338.5 85.2 all-gather.18
  432.8 161.4 reduce-scatter.16
  599.7 167.6 all-gather.20
  769.3 83.4 all-gather.22
  854.4 166.7 all-gather.24
  1362.7 191.7 reduce-scatter.18
  1615.7 192.6 reduce-scatter.20
  1817.7 167.7 all-gather.26
  1991.1 94.4 reduce-scatter.32
  2089.0 109.0 reduce-scatter.30
  2201.4 107.3 reduce-scatter.22
  2312.2 107.3 reduce-scatter.24
  2480.4 158.1 reduce-scatter.26
  2642.2 37.6 reduce-scatter.28
  2683.3 40.1 reduce-scatter.34

commit v3 on v2

--- a/solution.py
+++ b/solution.py
@@ -124,76 +124,110 @@
     return invert_slots(local_slot, order_row, slot_count)
 
 
-def _gather_rows_kernel(tok_ref, src_ref, out_ref, buf, sem):
-    rows = buf.shape[0]
-    base = pl.program_id(0) * rows
-
-    def start(s, carry):
+def _gather_rows_kernel(tok_ref, *refs):
+    count = (len(refs) - 1) // 4
+    sources, outs = refs[:count], refs[count : 2 * count]
+    copies, rows_bufs, sem = refs[2 * count : 3 * count], refs[3 * count : 4 * count], refs[-1]
+    rows = rows_bufs[0].shape[0]
+    step = pl.program_id(0)
+
+    @pl.when(step == 0)
+    def _():
+        for source, copy in zip(sources, copies):
+            transfer = pltpu.make_async_copy(source, copy, sem)
+            transfer.start()
+            transfer.wait()
+
+    base = step * rows
+
+    def body(s, carry):
         t = tok_ref[base + s]
-        pltpu.make_async_copy(src_ref.at[pl.ds(t, 1)], buf.at[pl.ds(s, 1)], sem).start()
+        for copy, rows_buf in zip(copies, rows_bufs):
+            rows_buf[pl.ds(s, 1), :] = copy[pl.ds(t, 1), :]
         return carry
 
-    lax.fori_loop(0, rows, start, 0, unroll=8)
-    pltpu.make_async_copy(src_ref.at[pl.ds(0, rows)], buf, sem).wait()
-    out_ref[...] = buf[...].astype(out_ref.dtype)
-
-
-def gather_rows(tok, src, rows, out_dtype):
-    blocks, width = tok.shape[0] // rows, src.shape[1]
+    lax.fori_loop(0, rows, body, 0, unroll=8)
+    for out, rows_buf in zip(outs, rows_bufs):
+        out[...] = rows_buf[...].astype(out.dtype)
+
+
+def gather_rows(tok, sources, rows, out_dtypes):
+    blocks = tok.shape[0] // rows
     return pl.pallas_call(
         _gather_rows_kernel,
         grid_spec=pltpu.PrefetchScalarGridSpec(
             num_scalar_prefetch=1,
             grid=(blocks,),
-            in_specs=[pl.BlockSpec(memory_space=pl.ANY)],
-            out_specs=pl.BlockSpec((rows, width), lambda b, tok: (b, 0)),
-            scratch_shapes=[pltpu.VMEM((rows, width), jnp.float32), pltpu.SemaphoreType.DMA(())],
+            in_specs=[pl.BlockSpec(memory_space=pl.ANY) for _ in sources],
+            out_specs=[
+                pl.BlockSpec((rows, source.shape[1]), lambda b, tok: (b, 0)) for source in sources
+            ],
+            scratch_shapes=[pltpu.VMEM(source.shape, jnp.float32) for source in sources]
+            + [pltpu.VMEM((rows, source.shape[1]), jnp.float32) for source in sources]
+            + [pltpu.SemaphoreType.DMA(())],
         ),
-        out_shape=jax.ShapeDtypeStruct((tok.shape[0], width), out_dtype),
-    )(tok, src)
-
-
-def _combine_rows_kernel(tok_ref, add_ref, out_ref, acc_ref, sem):
-    rows = add_ref.shape[0]
+        out_shape=[
+            jax.ShapeDtypeStruct((tok.shape[0], source.shape[1]), dtype)
+            for source, dtype in zip(sources, out_dtypes)
+        ],
+        compiler_params=pltpu.CompilerParams(vmem_limit_bytes=56 * 1024 * 1024),
+    )(tok, *sources)
+
+
+def _combine_rows_kernel(tok_ref, *refs):
+    count = (len(refs) - 1) // 4
+    addends, outs = refs[:count], refs[count : 2 * count]
+    totals, rows_bufs, sem = refs[2 * count : 3 * count], refs[3 * count : 4 * count], refs[-1]
+    rows = rows_bufs[0].shape[0]
     step = pl.program_id(0)
 
     @pl.when(step == 0)
     def _():
-        acc_ref[...] = jnp.zeros_like(acc_ref)
-
+        for total in totals:
+            total[...] = jnp.zeros_like(total)
+
+    for addend, rows_buf in zip(addends, rows_bufs):
+        rows_buf[...] = addend[...].astype(jnp.float32)
     base = step * rows
 
     def body(s, carry):
         t = tok_ref[base + s]
-        acc_ref[pl.ds(t, 1), :] += add_ref[pl.ds(s, 1), :]
+        for total, rows_buf in zip(totals, rows_bufs):
+            total[pl.ds(t, 1), :] += rows_buf[pl.ds(s, 1), :]
         return carry
 
     lax.fori_loop(0, rows, body, 0, unroll=8)
 
     @pl.when(step == pl.num_programs(0) - 1)
     def _():
-        copy = pltpu.make_async_copy(acc_ref, out_ref, sem)
-        copy.start()
-        copy.wait()
-
-
-def combine_rows(tok, addend, rows, total_rows):
-    blocks, width = tok.shape[0] // rows, addend.shape[1]
+        for total, out in zip(totals, outs):
+            transfer = pltpu.make_async_copy(total, out, sem)
+            transfer.start()
+            transfer.wait()
+
+
+def combine_rows(tok, addends, rows, total_rows):
+    blocks = tok.shape[0] // rows
     return pl.pallas_call(
         _combine_rows_kernel,
         grid_spec=pltpu.PrefetchScalarGridSpec(
             num_scalar_prefetch=1,
             grid=(blocks,),
-            in_specs=[pl.BlockSpec((rows, width), lambda b, tok: (b, 0))],
-            out_specs=pl.BlockSpec(memory_space=pl.ANY),
+            in_specs=[
+                pl.BlockSpec((rows, addend.shape[1]), lambda b, tok: (b, 0)) for addend in addends
+            ],
+            out_specs=[pl.BlockSpec(memory_space=pl.ANY) for _ in addends],
             scratch_shapes=[
-                pltpu.VMEM((total_rows, width), jnp.float32),
-                pltpu.SemaphoreType.DMA(()),
-            ],
+                pltpu.VMEM((total_rows, addend.shape[1]), jnp.float32) for addend in addends
+            ]
+            + [pltpu.VMEM((rows, addend.shape[1]), jnp.float32) for addend in addends]
+            + [pltpu.SemaphoreType.DMA(())],
         ),
-        out_shape=jax.ShapeDtypeStruct((total_rows, width), jnp.float32),
-        compiler_params=pltpu.CompilerParams(vmem_limit_bytes=48 * 1024 * 1024),
-    )(tok, addend)
+        out_shape=[
+            jax.ShapeDtypeStruct((total_rows, addend.shape[1]), jnp.float32) for addend in addends
+        ],
+        compiler_params=pltpu.CompilerParams(vmem_limit_bytes=56 * 1024 * 1024),
+    )(tok, *addends)
 
 
 def table_lookup(table, index):
@@ -362,12 +396,19 @@
     slot_valid = slot_pair >= 0
     safe_pair = jnp.maximum(slot_pair, 0)
     slot_token = safe_pair // TOPK
-    slot_gate = jnp.where(slot_valid, jnp.take(gates.reshape(-1), safe_pair), 0.0)
-    slot_gate = slot_gate.reshape(local_experts, CAP, 1)
-
-    inputs = gather_rows(slot_token, mixture_in.astype(jnp.float32), CAP, jnp.bfloat16).reshape(
-        local_experts, CAP, D
-    )
+    slot_choice = safe_pair % TOPK
+    side_lanes = 128
+    gate_table = jnp.pad(gates, ((0, 0), (0, side_lanes - TOPK)))
+    inputs, gate_rows = gather_rows(
+        slot_token,
+        (mixture_in.astype(jnp.float32), gate_table),
+        CAP,
+        (jnp.bfloat16, jnp.float32),
+    )
+    inputs = inputs.reshape(local_experts, CAP, D)
+    choice_marks = slot_choice[:, None] == jnp.arange(side_lanes)[None, :]
+    slot_gate = jnp.sum(jnp.where(choice_marks, gate_rows, 0.0), axis=1)
+    slot_gate = jnp.where(slot_valid, slot_gate, 0.0).reshape(local_experts, CAP, 1)
     gate_pre = jnp.einsum("ecd,edf->ecf", inputs, gate_full, preferred_element_type=jnp.float32)
     up_pre = jnp.einsum("ecd,edf->ecf", inputs, up_full, preferred_element_type=jnp.float32)
     activated = jax.nn.silu(gate_pre)
@@ -375,7 +416,7 @@
     expert_out = jnp.einsum(
         "ecf,efd->ecd", hidden_units, down_full, preferred_element_type=jnp.float32
     )
-    mixture_sum = combine_rows(slot_token, expert_out.reshape(slot_count, D), CAP, TOK_GRP)
+    (mixture_sum,) = combine_rows(slot_token, (expert_out.reshape(slot_count, D),), CAP, TOK_GRP)
     out_grad_held, down_full = lax.optimization_barrier((out_grad, down_full))
     cotangent_full = lax.all_gather(out_grad_held, "tensor", axis=0, tiled=True)
     scaled_cotangent = (
@@ -385,13 +426,12 @@
     mixture_part = lax.psum_scatter(
         mixture_sum.astype(jnp.bfloat16), "tensor", scatter_dimension=0, tiled=True
     ).astype(jnp.float32)
-    out_rows = gather_rows(slot_token, scaled_cotangent, CAP, jnp.bfloat16).reshape(
-        local_experts, CAP, D
-    )
+    (out_rows,) = gather_rows(slot_token, (scaled_cotangent,), CAP, (jnp.bfloat16,))
+    out_rows = out_rows.reshape(local_experts, CAP, D)
     hidden_grad = jnp.einsum("ecd,efd->ecf", out_rows, down_full, preferred_element_type=jnp.float32)
     gate_grad_slot = jnp.sum(activated * up_pre * hidden_grad, axis=-1).reshape(slot_count)
-    gate_grad_pair = jnp.zeros((TOK_GRP * TOPK,), jnp.float32).at[safe_pair].add(
-        jnp.where(slot_valid, gate_grad_slot, 0.0)
+    gate_grad_rows = jnp.where(
+        choice_marks & slot_valid[:, None], gate_grad_slot[:, None], 0.0
     )
     product_grad = slot_gate * hidden_grad
     gate_pre_grad = (product_grad * up_pre * silu_slope(gate_pre)).astype(jnp.bfloat16)
@@ -399,8 +439,10 @@
     input_rows = jnp.einsum(
         "ecf,edf->ecd", gate_pre_grad, gate_full, preferred_element_type=jnp.float32
     ) + jnp.einsum("ecf,edf->ecd", up_pre_grad, up_full, preferred_element_type=jnp.float32)
-    input_rows = input_rows.astype(jnp.bfloat16).astype(jnp.float32).reshape(slot_count, D)
-    grad_in_mixture = combine_rows(slot_token, input_rows, CAP, TOK_GRP)
+    input_rows = input_rows.astype(jnp.bfloat16).reshape(slot_count, D)
+    grad_in_mixture, gate_grad_table = combine_rows(
+        slot_token, (input_rows, gate_grad_rows), CAP, TOK_GRP
+    )
     (inputs, gate_pre_grad, up_pre_grad, hidden_units, out_rows), grad_in_mixture = (
         lax.optimization_barrier(
             ((inputs, gate_pre_grad, up_pre_grad, hidden_units, out_rows), grad_in_mixture)
@@ -412,7 +454,7 @@
         jnp.einsum("ecf,ecd->efd", hidden_units, out_rows, preferred_element_type=jnp.float32),
     )
     expert_parts = tuple(part.astype(jnp.bfloat16) for part in expert_parts)
-    gates_grad = gate_grad_pair.reshape(TOK_GRP, TOPK)
+    gates_grad = gate_grad_table[:, :TOPK]
     routed_grad = gates * (gates_grad - jnp.sum(gates * gates_grad, axis=-1, keepdims=True))
     logits_grad = jnp.sum(routed_marks * routed_grad[:, :, None], axis=1)
     router_part = jnp.einsum(

time: 2750 us -> 2490 us (0.905)
  Pallas kernels: 374 us -> 235 us
  other arithmetic: 368 us -> 319 us
  local copies, waits for them, and re-layouts: 164 us -> 122 us
  waiting for transfers between devices: 994 us -> 962 us
    pallas_call x2, Pallas kernels: 242 us -> 95.4 us  [gather_rows(): pl.pallas_call(_gather_rows_kernel, grid_spec=pltpu.PrefetchScalarGridSpe...]
    scatter-add x1 -> x0, other arithmetic: 44.3 us -> none  [local(): jnp.zeros((TOK_GRP * TOPK,), jnp.float32).at[safe_pair]]
    gather x2 -> x0, local copies, waits for them, and re-layouts: 39.8 us -> none  [local(): jnp.take(gates.reshape(-1), safe_pair)]
    reduce_scatter x1, waiting for transfers between devices: 193 us -> 161 us  [local(): lax.psum_scatter(mixture_grad_low, 'tensor', scatter_dimension=0, tiled=T...]
    unnamed x353 -> x343, local copies, waits for them, and re-layouts: 104 us -> 102 us
where the time goes in v3:
time: 2490 us
  waiting for transfers between devices  962 us (39%)
  matrix products  747 us (30%)
  other arithmetic  319 us (13%)
  Pallas kernels  235 us (9%)
  local copies, waits for them, and re-layouts  122 us (5%)
  blocking collectives  84.7 us (3%)
    all_gather x1, waiting for transfers between devices, local(): lax.all_gather(normed_two.astype(jnp.bfloat16), 'tensor', axis=0, tiled=T...  168 us
    all_gather x1, waiting for transfers between devices, local(): lax.all_gather(normed_shard.astype(jnp.bfloat16), 'tensor', axis=0, tiled...  165 us
    reduce_scatter x1, waiting for transfers between devices, local(): lax.psum_scatter(attended_partial, 'tensor', scatter_dimension=0, tiled=T...  161 us
    reduce_scatter x1, waiting for transfers between devices, local(): lax.psum_scatter(mixture_grad_low, 'tensor', scatter_dimension=0, tiled=T...  161 us
    pallas_call x2, Pallas kernels, combine_rows(): pl.pallas_call(_combine_rows_kernel, grid_spec=pltpu.PrefetchScalarGridSp...  140 us
    reduce_scatter x1, waiting for transfers between devices, local(): lax.psum_scatter(normed_grad_low, 'tensor', scatter_dimension=0, tiled=True)  133 us
    convert_element_type x6, other arithmetic, local(): score_grad = (soft_full * (weight_grad - delta)).astype(jnp.bfloat16)  119 us
    unnamed x343, local copies, waits for them, and re-layouts  102 us
  transfers between devices with their start and end apart: 19, of which 8 were waited for; matrix products, arithmetic and copies ran while one was open for 42% of the time, Pallas kernels for 9%

profile of v3, /device:TPU:0, one launch (start us, length us, event | category | flops | bytes accessed | tf_op | source)
XLA Modules:
  0.0 2487.4 jit_solution(9585528058067852599)
XLA Ops:
  10.9 16.0 all-reduce.9
  35.0 164.7 %all-gather.11.cloned.1.call-done = bf16[3072,1536]{1,0:T(8,128)(2,1)} async-done(((bf16[768,1536]{1,0:T(8,128)(2,1)}), bf16[3072,1536]{1,0:T(8,128)(2,1)}) %all-gather.11.cloned.1.call-update) | async-done | bytes 9437200 | tf_op jit(solution)/shard_map/all_gather | solution.py:331
  200.1 9.5 all_gather.45
  209.7 9.9 all_gather.44
  283.3 9.3 fusion.240
  292.6 9.9 fusion.22
  326.3 11.0 fusion.155
  337.3 14.6 fusion.242
  351.9 12.6 fusion.8
  364.6 13.0 fusion.156
  377.6 14.5 fusion.243
  392.1 15.0 fusion.3
  407.1 15.0 fusion.157
  423.7 8.8 convolution_convert_fusion.3
  433.1 161.1 %reduce-scatter.17.cloned.1.call-done = bf16[768,1536]{1,0:T(8,128)(2,1)} async-done(((bf16[3072,1536]{1,0:T(8,128)(2,1)}), bf16[768,1536]{1,0:T(8,128)(2,1)}) %reduce-scatter.17.cloned.1.call-update) | async-done | bytes 2359312 | tf_op jit(solution)/shard_map/reduce_scatter | solution.py:376
  599.6 167.8 %all-gather.21.cloned.1.call-done = bf16[3072,1536]{1,0:T(8,128)(2,1)} async-done(((bf16[768,1536]{1,0:T(8,128)(2,1)}), bf16[3072,1536]{1,0:T(8,128)(2,1)}) %all-gather.21.cloned.1.call-update) | async-done | bytes 9437200 | tf_op jit(solution)/shard_map/all_gather | solution.py:384
  769.5 14.7 fusion.101
  809.5 43.4 %all-gather.23.cloned.1.call-done = bf16[10,512,1536]{1,2,0:T(8,128)(2,1)} async-done(((bf16[10,512,192]{1,2,0:T(8,128)(2,1)}), bf16[10,512,1536]{1,2,0:T(8,128)(2,1)}) %all-gather.23.cloned.1.call-update) | async-done | bytes 15728656 | tf_op jit(solution)/shard_map/all_gather | solution.py:386
  853.7 9.6 all-gather
  879.0 12.7 convert_element_type.303.refs_0_
  901.2 50.7 %shard_map.248 = (bf16[7680,1536]{1,0:T(8,128)(2,1)}, f32[7680,128]{1,0:T(8,128)}) custom-call(s32[7680]{0:T(1024)} %get-tuple-element.406.tok_ref, f32[3072,1536]{1,0:T(8,128)} %convert_element_type.303.refs_0_, f32[3072,128]{1,0:T(8,128)} %pad.33.refs_1_), custom_call_target="tpu_custom_call" | custom-call | tf_op jit(solution)/shard_map/pallas_call | solution.py:156
  958.1 27.8 %fusion.248 = f32[10,768,512]{1,2,0:T(8,128)} fusion(bf16[10,768,1536]{2,1,0:T(8,128)(2,1)} %bitcast.579, bf16[10,1536,512]{2,1,0:T(8,128)(2,1)} %all-gather.17.cloned.1.call-done), kind=kOutput, calls=%fused_computation.398 | convolution fusion | flops 12079595520 | bytes 55050240 | tf_op jit(solution)/shard_map/ecd,edf->ecf/dot_general | solution.py:412
  985.9 32.7 %multiply_convert_fusion.3 = (bf16[10,768,512]{1,2,0:T(8,128)(2,1)}, f32[10,768,512]{1,2,0:T(8,128)}) fusion(f32[10,768]{1,0:T(8,128)S(1)} %broadcast_select_fusion, f32[10,768,512]{1,2,0:T(8,128)} %fusion.248, bf16[10,768,1536]{2,1,0:T(8,128)(2,1)} %bitcast.580, bf16[10,1536,512]{2,1,0:T(8,128)(2,1)} %all-gather.19.cloned.1.call-done), kind=kOutput, calls=%fused_computation.57 | convolution fusion | flops 12107120640 | bytes 78673920 | tf_op jit(solution)/shard_map/ecd,edf->ecf/dot_general | solution.py:413
  1018.6 27.2 %fusion.249 = f32[10,768,1536]{2,1,0:T(8,128)} fusion(bf16[10,768,512]{1,2,0:T(8,128)(2,1)} %get-tuple-element.235, bf16[10,512,1536]{1,2,0:T(8,128)(2,1)} %all-gather.23.cloned.1.call-done), kind=kOutput, calls=%fused_computation.399 | convolution fusion | flops 12079595520 | bytes 70778880 | tf_op jit(solution)/shard_map/ecf,efd->ecd/dot_general | solution.py:416
  1045.8 68.6 %shard_map.249 = f32[3072,1536]{1,0:T(8,128)} custom-call(s32[7680]{0:T(1024)} %get-tuple-element.406.tok_ref, f32[7680,1536]{1,0:T(8,128)} %bitcast.507), custom_call_target="tpu_custom_call" | custom-call | tf_op jit(solution)/shard_map/pallas_call | solution.py:211
  1114.5 12.9 fusion.40.refs_0_
  1127.3 11.3 convert_element_type.312
  1138.7 44.7 %shard_map.250 = bf16[7680,1536]{1,0:T(8,128)(2,1)} custom-call(s32[7680]{0:T(1024)} %get-tuple-element.406.tok_ref, f32[3072,1536]{1,0:T(8,128)} %fusion.40.refs_0_), custom_call_target="tpu_custom_call" | custom-call | tf_op jit(solution)/shard_map/pallas_call | solution.py:156
  1183.4 34.5 %multiply_reduce_fusion = (f32[10,768]{1,0:T(8,128)S(1)}, bf16[10,768,512]{1,2,0:T(8,128)(2,1)}, bf16[10,768,512]{1,2,0:T(8,128)(2,1)}) fusion(f32[10,768,512]{1,2,0:T(8,128)} %get-tuple-element.425, f32[10,768,512]{1,2,0:T(8,128)} %fusion.248, f32[10,768]{1,0:T(8,128)S(1)} %broadcast_select_fusion, bf16[10,768,1536]{2,1,0:T(8,128)(2,1)} %bitcast.517, ...), kind=kOutput, calls=%fused_computation.54 | convolution fusion | flops 12146434048 | bytes 86568960 | tf_op jit(solution)/shard_map/ecd,efd->ecf/dot_general | solution.py:431
  1225.7 27.2 %fusion.250 = f32[10,768,1536]{2,1,0:T(8,128)} fusion(bf16[10,768,512]{1,2,0:T(8,128)(2,1)} %get-tuple-element.233, bf16[10,1536,512]{2,1,0:T(8,128)(2,1)} %all-gather.17.cloned.1.call-done), kind=kOutput, calls=%fused_computation.400 | convolution fusion | flops 12079595520 | bytes 70778880 | tf_op jit(solution)/shard_map/ecf,edf->ecd/dot_general | solution.py:439
  1253.0 34.0 %add_convert_fusion = bf16[10,768,1536]{2,1,0:T(8,128)(2,1)} fusion(f32[10,768,1536]{2,1,0:T(8,128)} %fusion.250, bf16[10,768,512]{1,2,0:T(8,128)(2,1)} %get-tuple-element.234, bf16[10,1536,512]{2,1,0:T(8,128)(2,1)} %all-gather.19.cloned.1.call-done), kind=kOutput, calls=%fused_computation | convolution fusion | flops 12103188480 | bytes 94371840 | tf_op jit(solution)/shard_map/ecf,edf->ecd/dot_general | solution.py:441
  1287.0 71.5 %shard_map.251 = (f32[3072,1536]{1,0:T(8,128)}, f32[3072,128]{1,0:T(8,128)}) custom-call(s32[7680]{0:T(1024)} %get-tuple-element.406.tok_ref, bf16[7680,1536]{1,0:T(8,128)(2,1)} %bitcast.515, f32[7680,128]{1,0:T(8,128)} %fusion.81.refs_1_), custom_call_target="tpu_custom_call" | custom-call | tf_op jit(solution)/shard_map/pallas_call | solution.py:211
  1364.6 14.3 add_convert_fusion.2
  1383.4 160.6 %reduce-scatter.21.cloned.1.call-done = bf16[768,1536]{1,0:T(8,128)(2,1)} async-done(((bf16[3072,1536]{1,0:T(8,128)(2,1)}), bf16[768,1536]{1,0:T(8,128)(2,1)}) %reduce-scatter.21.cloned.1.call-update) | async-done | bytes 2359312 | tf_op jit(solution)/shard_map/reduce_scatter | solution.py:470
  1560.7 23.0 convolution_convert_fusion.1
  1583.7 21.4 convolution_convert_fusion.2
  1605.1 21.5 convolution_convert_fusion
  1626.6 94.4 %all-gather.27.cloned.1.call-done = bf16[3072,1536]{1,0:T(8,128)(2,1)} async-done(((bf16[768,1536]{1,0:T(8,128)(2,1)}), bf16[3072,1536]{1,0:T(8,128)(2,1)}) %all-gather.27.cloned.1.call-update) | async-done | bytes 9437200 | tf_op jit(solution)/shard_map/all_gather | solution.py:477
  1722.3 30.9 %copy.501 = bf16[10,512,1536]{1,0,2:T(8,128)(2,1)} copy(bf16[10,512,1536]{2,1,0:T(8,128)(2,1)} %convolution_convert_fusion) | data formatting | bytes 31457280
  1753.1 24.8 copy.508
  1809.6 9.7 fusion.33
  1819.4 13.1 fusion.17
  1832.4 24.2 fusion.9
  1856.7 20.7 fusion.19
  1881.0 16.5 fusion.11
  1897.5 24.5 fusion.4
  1938.8 34.2 %fusion.6 = bf16[2,3,512,2560]{2,3,1,0:T(8,128)(2,1)} fusion(f32[2,2560,512,3]{2,1,3,0:T(8,128)} %get-tuple-element.435, f32[2,3,512,2560]{2,3,1,0:T(8,128)} %get-tuple-element.421, f32[2,3,512]{2,1,0:T(4,128)S(1)} %copy-done.103, f32[2,3,512]{2,1,0:T(4,128)S(1)} %log_add_fusion.1), kind=kLoop, calls=%fused_computation.15 | loop fusion | flops 31457280 | bytes 78667776 | tf_op jit(solution)/shard_map/convert_element_type | solution.py:510
  1973.1 9.7 fusion.151
  1982.8 29.4 %fusion = (f32[2,3,512]{2,1,0:T(4,128)}, f32[2,3072,512,3]{2,1,3,0:T(8,128)}) fusion(f32[2,3,512,3072]{2,3,1,0:T(8,128)} %get-tuple-element.423, f32[2,3,512]{2,1,0:T(4,128)S(1)} %copy-done.73, bf16[3072,2,64,1]{0,2,3,1:T(8,128)(2,1)S(1)} %bitcast.520, bf16[512,2,3,64]{0,3,2,1:T(8,128)(2,1)S(1)} %bitcast.529), kind=kOutput, calls=%fused_computation.3 | convolution fusion | flops 1236268032 | bytes 76701696 | tf_op jit(solution)/shard_map/qgrd,kgd->grqk/dot_general | solution.py:506
  2012.2 32.9 %fusion.2 = bf16[2,3,512,3072]{2,3,1,0:T(8,128)(2,1)} fusion(f32[2,3072,512,3]{2,1,3,0:T(8,128)} %get-tuple-element.437, f32[2,3,512,3072]{2,3,1,0:T(8,128)} %get-tuple-element.423, f32[2,3,512]{2,1,0:T(4,128)} %get-tuple-element.436, f32[2,3,512]{2,1,0:T(4,128)} %log_add_fusion), kind=kLoop, calls=%fused_computation.5 | loop fusion | flops 37748736 | bytes 94396416 | tf_op jit(solution)/shard_map/convert_element_type | solution.py:510
  2045.1 10.8 fusion.141
  2092.2 10.9 fusion.87
  2103.1 10.8 fusion.137
  2113.9 11.3 fusion.252
  2125.2 14.1 fusion.98
  2163.3 15.8 fusion.105
  2179.1 9.8 fusion.88
  2190.2 8.9 fusion.253
  2199.0 17.0 add_convert_fusion.1
  2216.1 10.2 convolution_convert_fusion.7
  2241.0 133.3 %reduce-scatter.27.cloned.1.call-done = bf16[768,1536]{1,0:T(8,128)(2,1)} async-done(((bf16[3072,1536]{1,0:T(8,128)(2,1)}), bf16[768,1536]{1,0:T(8,128)(2,1)}) %reduce-scatter.27.cloned.1.call-update) | async-done | bytes 2359312 | tf_op jit(solution)/shard_map/reduce_scatter | solution.py:552
  2381.1 34.5 %reduce-scatter.29.cloned.1.call-done = bf16[384,192]{0,1:T(8,128)(2,1)} async-done(((bf16[384,1536]{0,1:T(8,128)(2,1)}), bf16[384,192]{0,1:T(8,128)(2,1)}) %reduce-scatter.29.cloned.1.call-update) | async-done | bytes 147472 | tf_op jit(solution)/shard_map/reduce_scatter | solution.py:577
  2426.6 39.6 %all-reduce.8 = (f32[1536]{0:T(1024)S(1)}, f32[1536]{0:T(1024)S(1)}) all-reduce(f32[1536]{0:T(1024)S(1)} %get-tuple-element.364, f32[1536]{0:T(1024)S(1)} %copy-done.133), channel_id=10, replica_groups=mesh['dp'=8,'tensor'=4] {'dp','tensor'}, use_global_device_ids=true, to_apply=%region_44.45.clone | all-reduce | flops 3072 | bytes 24576
  2467.4 9.7 fusion.77
  (543 shorter events, 351.5 us)
Async XLA Ops:
  7.2 192.6 %copy-start.132 = (s32[1,1024]{1,0:T(1,128)S(1)}, s32[1,1024]{1,0:T(1,128)}, u32[]{:S(2)}) copy-start(s32[1,1024]{1,0:T(1,128)} %param.45) | copy-start | bytes 12292
  7.2 192.9 %copy-start.128 = (bf16[192,128]{1,0:T(8,128)(2,1)S(1)}, bf16[192,128]{1,0:T(8,128)(2,1)}, u32[]{:S(2)}) copy-start(bf16[192,128]{1,0:T(8,128)(2,1)} %param.50) | copy-start | bytes 147460
  7.2 202.5 %copy-start.129 = (bf16[192,128]{1,0:T(8,128)(2,1)S(1)}, bf16[192,128]{1,0:T(8,128)(2,1)}, u32[]{:S(2)}) copy-start(bf16[192,128]{1,0:T(8,128)(2,1)} %param.51) | copy-start | bytes 147460
  7.2 192.5 %all-gather.11.cloned.1.call-start = ((), (), s32[]{:S(2)}) async-start(), calls=%async_computation.10 | async-start | bytes 11796480 | tf_op jit(solution)/shard_map/all_gather | solution.py:331
  33.4 210.0 %all-gather.13.cloned.1.call-start = ((), (), s32[]{:S(2)}) async-start(), calls=%async_computation.11 | async-start | bytes 1327104 | tf_op jit(solution)/shard_map/all_gather | solution.py:320
  34.2 388.1 %all-gather.15.cloned.1.call-start = ((), (), s32[]{:S(2)}) async-start(), calls=%async_computation.12 | async-start | bytes 1327104 | tf_op jit(solution)/shard_map/all_gather | solution.py:323
  34.9 397.5 %all-gather.17.cloned.1.call-start = ((), (), s32[]{:S(2)}) async-start(), calls=%async_computation.13 | async-start | bytes 17694720 | tf_op jit(solution)/shard_map/all_gather | solution.py:335
  199.7 232.7 %all-gather.19.cloned.1.call-start = ((), (), s32[]{:S(2)}) async-start(), calls=%async_computation.14 | async-start | bytes 17694720 | tf_op jit(solution)/shard_map/all_gather | solution.py:336
  209.7 43.1 %copy-start.52 = (bf16[1536,128]{1,0:T(8,128)(2,1)}, bf16[1536,128]{1,0:T(8,128)(2,1)S(1)}, u32[]{:S(2)}) copy-start(bf16[1536,128]{1,0:T(8,128)(2,1)S(1)} %all_gather.45) | copy-start | bytes 1179652
  219.6 20.5 copy-start.41
  226.5 33.5 %copy-start.25 = (f32[3072,32]{0,1:T(8,128)}, f32[3072,32]{0,1:T(8,128)S(1)}, u32[]{:S(2)}) copy-start(f32[3072,32]{0,1:T(8,128)S(1)} %get-tuple-element.407) | copy-start | bytes 1179652
  226.5 33.5 %copy-start.28 = (f32[3072,32]{0,1:T(8,128)}, f32[3072,32]{0,1:T(8,128)S(1)}, u32[]{:S(2)}) copy-start(f32[3072,32]{0,1:T(8,128)S(1)} %get-tuple-element.408) | copy-start | bytes 1179652
  243.4 18.9 copy-start.76
  260.2 23.1 copy-start.10
  260.2 117.4 %copy-start.8 = (bf16[3072,2,32]{0,2,1:T(8,128)(2,1)}, bf16[3072,2,32]{0,2,1:T(8,128)(2,1)S(1)}, u32[]{:S(2)}) copy-start(bf16[3072,2,32]{0,2,1:T(8,128)(2,1)S(1)} %get-tuple-element.395) | copy-start | bytes 1179652
  271.7 322.5 %reduce-scatter.17.cloned.1.call-start = ((), (), s32[]{:S(2)}) async-start(), calls=%async_computation.15 | async-start | bytes 11796480 | tf_op jit(solution)/shard_map/reduce_scatter | solution.py:376
  432.4 161.8 %copy-start.3 = (bf16[768,1536]{1,0:T(8,128)(2,1)S(1)}, bf16[768,1536]{1,0:T(8,128)(2,1)}, u32[]{:S(2)}) copy-start(bf16[768,1536]{1,0:T(8,128)(2,1)} %param.43) | copy-start | bytes 7077892
  432.5 334.9 %all-gather.21.cloned.1.call-start = ((), (), s32[]{:S(2)}) async-start(), calls=%async_computation.16 | async-start | bytes 11796480 | tf_op jit(solution)/shard_map/all_gather | solution.py:384
  433.1 166.4 %copy-start.84 = (f32[1536]{0:T(1024)}, f32[1536]{0:T(1024)S(1)}, u32[]{:S(2)}) copy-start(f32[1536]{0:T(1024)S(1)} %convert_element_type.301) | copy-start | bytes 18436
  597.0 170.5 %copy-start.71 = (s32[3072,8]{0,1:T(8,128)S(1)}, s32[3072,8]{0,1:T(8,128)}, u32[]{:S(2)}) copy-start(s32[3072,8]{0,1:T(8,128)} %param.46) | copy-start | bytes 294916
  597.1 171.6 %copy-start.97 = (f32[768]{0:T(1024)}, f32[768]{0:T(1024)S(1)}, u32[]{:S(2)}) copy-start(f32[768]{0:T(1024)S(1)} %add_rsqrt_fusion) | copy-start | bytes 9220
  597.1 171.6 %copy-start.101 = (s32[1,24576]{1,0:T(1,128)S(1)}, s32[1,24576]{1,0:T(1,128)}, u32[]{:S(2)}) copy-start(s32[1,24576]{1,0:T(1,128)} %param.47) | copy-start | bytes 294916
  599.5 253.3 %all-gather.23.cloned.1.call-start = ((), (), s32[]{:S(2)}) async-start(), calls=%async_computation.17 | async-start | bytes 17694720 | tf_op jit(solution)/shard_map/all_gather | solution.py:386
  767.4 347.0 %all-gather.25.cloned.1.call-start = ((), (), s32[]{:S(2)}) async-start(), calls=%async_computation.18 | async-start | bytes 11796480 | tf_op jit(solution)/shard_map/all_gather | solution.py:421
  802.5 51.2 %copy-start.134 = (bf16[192,40]{0,1:T(8,128)(2,1)S(1)}, bf16[192,40]{0,1:T(8,128)(2,1)}, u32[]{:S(2)}) copy-start(bf16[192,40]{0,1:T(8,128)(2,1)} %param.54) | copy-start | bytes 46084
  852.9 526.0 %reduce-scatter.19.cloned.1.call-start = ((), (), s32[]{:S(2)}) async-start(), calls=%async_computation.19 | async-start | bytes 11796480 | tf_op jit(solution)/shard_map/reduce_scatter | solution.py:426
  863.5 28.1 %copy-start.67 = (bf16[1536,40]{0,1:T(8,128)(2,1)}, bf16[1536,40]{0,1:T(8,128)(2,1)S(1)}, u32[]{:S(2)}) copy-start(bf16[1536,40]{0,1:T(8,128)(2,1)S(1)} %reshape.1171) | copy-start | bytes 368644
  878.9 73.0 %copy-start.95 = (s32[7680]{0:T(1024)}, s32[7680]{0:T(1024)S(1)}, u32[]{:S(2)}) copy-start(s32[7680]{0:T(1024)S(1)} %get-tuple-element.405) | copy-start | bytes 92164
  899.0 52.9 %copy-start.87 = (f32[3072]{0:T(1024)}, f32[3072]{0:T(1024)S(1)}, u32[]{:S(2)}) copy-start(f32[3072]{0:T(1024)S(1)} %get-tuple-element.370) | copy-start | bytes 36868
  899.5 52.4 %copy-start.16 = (f32[3072,8]{1,0:T(8,128)}, f32[3072,8]{1,0:T(8,128)S(1)}, u32[]{:S(2)}) copy-start(f32[3072,8]{1,0:T(8,128)S(1)} %copy.409) | copy-start | bytes 294916
  1138.6 405.4 %reduce-scatter.21.cloned.1.call-start = ((), (), s32[]{:S(2)}) async-start(), calls=%async_computation.20 | async-start | bytes 11796480 | tf_op jit(solution)/shard_map/reduce_scatter | solution.py:470
  1183.4 34.5 %copy-start.96 = (s32[7680]{0:T(1024)S(1)}, s32[7680]{0:T(1024)}, u32[]{:S(2)}) copy-start(s32[7680]{0:T(1024)} %copy-done.95) | copy-start | bytes 92164
  1287.0 71.5 %copy-start.17 = (f32[3072,8]{1,0:T(8,128)S(1)}, f32[3072,8]{1,0:T(8,128)}, u32[]{:S(2)}) copy-start(f32[3072,8]{1,0:T(8,128)} %copy-done.16) | copy-start | bytes 294916
  1287.0 71.5 %copy-start.88 = (f32[3072]{0:T(1024)S(1)}, f32[3072]{0:T(1024)}, u32[]{:S(2)}) copy-start(f32[3072]{0:T(1024)} %copy-done.87) | copy-start | bytes 36868
  1383.3 160.7 %copy-start.4 = (bf16[768,1536]{1,0:T(8,128)(2,1)S(1)}, bf16[768,1536]{1,0:T(8,128)(2,1)}, u32[]{:S(2)}) copy-start(bf16[768,1536]{1,0:T(8,128)(2,1)} %param.43) | copy-start | bytes 7077892
  1383.3 160.7 %copy-start.85 = (f32[1536]{0:T(1024)S(1)}, f32[1536]{0:T(1024)}, u32[]{:S(2)}) copy-start(f32[1536]{0:T(1024)} %copy-done.84) | copy-start | bytes 18436
  1383.3 160.7 %copy-start.98 = (f32[768]{0:T(1024)S(1)}, f32[768]{0:T(1024)}, u32[]{:S(2)}) copy-start(f32[768]{0:T(1024)} %copy-done.97) | copy-start | bytes 9220
  1383.4 337.7 %all-gather.27.cloned.1.call-start = ((), (), s32[]{:S(2)}) async-start(), calls=%async_computation.21 | async-start | bytes 11796480 | tf_op jit(solution)/shard_map/all_gather | solution.py:477
  1553.2 586.2 %reduce-scatter.33.cloned.1.call-start = ((), (), s32[]{:S(2)}) async-start(), calls=%async_computation.27 | async-start | bytes 811008
  1722.2 418.6 %reduce-scatter.31.cloned.1.call-start = ((), (), s32[]{:S(2)}) async-start(), calls=%async_computation.26 | async-start | bytes 17694720
  1778.1 377.1 %reduce-scatter.23.cloned.1.call-start = ((), (), s32[]{:S(2)}) async-start(), calls=%async_computation.22 | async-start | bytes 17694720 | tf_op jit(solution)/shard_map/reduce_scatter | solution.py:290
  1778.7 380.6 %reduce-scatter.25.cloned.1.call-start = ((), (), s32[]{:S(2)}) async-start(), calls=%async_computation.23 | async-start | bytes 17694720 | tf_op jit(solution)/shard_map/reduce_scatter | solution.py:291
  1778.8 30.8 %copy-start.82 = (f32[2,3,512]{2,1,0:T(4,128)}, f32[2,3,512]{2,1,0:T(4,128)S(1)}, u32[]{:S(2)}) copy-start(f32[2,3,512]{2,1,0:T(4,128)S(1)} %log_add_fusion.4) | copy-start | bytes 36868
  1778.9 40.4 %copy-start.78 = (f32[2,3,512]{2,1,0:T(4,128)}, f32[2,3,512]{2,1,0:T(4,128)S(1)}, u32[]{:S(2)}) copy-start(f32[2,3,512]{2,1,0:T(4,128)S(1)} %log_add_fusion.3) | copy-start | bytes 36868
  1789.4 108.1 %copy-start.32 = (bf16[512,384]{0,1:T(8,128)(2,1)}, bf16[512,384]{0,1:T(8,128)(2,1)S(1)}, u32[]{:S(2)}) copy-start(bf16[512,384]{0,1:T(8,128)(2,1)S(1)} %get-tuple-element.384) | copy-start | bytes 1179652
  1832.4 24.3 copy-start.79
  1856.7 20.8 slice-start
  1856.7 20.8 slice-start.1
  1856.7 20.8 slice-start.2
  1856.7 21.9 slice-start.3
  1856.7 23.1 slice-start.4
  1856.7 24.3 slice-start.5
  1881.0 16.5 copy-start.54
  1922.1 452.3 %reduce-scatter.27.cloned.1.call-start = ((), (), s32[]{:S(2)}) async-start(), calls=%async_computation.24 | async-start | bytes 11796480 | tf_op jit(solution)/shard_map/reduce_scatter | solution.py:552
  2045.1 25.0 %slice-start.12 = ((s8[12582912]{0:T(1024)(128)(4,1)}), s8[4194304]{0:T(1024)(128)(4,1)S(1)}, s32[]{:S(2)}) async-start(s8[12582912]{0:T(1024)(128)(4,1)} %bitcast.505), calls=%async_computation.41 | async-start | bytes 8388608
  2045.1 25.0 %slice-start.13 = ((s8[12582912]{0:T(1024)(128)(4,1)}), s8[4194304]{0:T(1024)(128)(4,1)S(1)}, s32[]{:S(2)}) async-start(s8[12582912]{0:T(1024)(128)(4,1)} %bitcast.505), calls=%async_computation.42 | async-start | bytes 8388608
  2216.1 199.5 %reduce-scatter.29.cloned.1.call-start = ((), (), s32[]{:S(2)}) async-start(), calls=%async_computation.25 | async-start | bytes 1327104 | tf_op jit(solution)/shard_map/reduce_scatter | solution.py:577
  2226.4 250.8 %reduce-scatter.35.cloned.1.call-start = ((), (), s32[]{:S(2)}) async-start(), calls=%async_computation.28 | async-start | bytes 2211840
  2381.1 41.7 %copy-start.5 = (bf16[768,1536]{1,0:T(8,128)(2,1)S(1)}, bf16[768,1536]{1,0:T(8,128)(2,1)}, u32[]{:S(2)}) copy-start(bf16[768,1536]{1,0:T(8,128)(2,1)} %param.43) | copy-start | bytes 7077892
  2381.1 41.7 %copy-start.94 = (f32[1536]{0:T(1024)S(1)}, f32[1536]{0:T(1024)}, u32[]{:S(2)}) copy-start(f32[1536]{0:T(1024)} %copy-done.93) | copy-start | bytes 18436
  2381.1 41.7 %copy-start.127 = (f32[768]{0:T(1024)S(1)}, f32[768]{0:T(1024)}, u32[]{:S(2)}) copy-start(f32[768]{0:T(1024)} %copy-done.126) | copy-start | bytes 9220
  2417.3 50.1 %copy-start.86 = (f32[1536]{0:T(1024)S(1)}, f32[1536]{0:T(1024)}, u32[]{:S(2)}) copy-start(f32[1536]{0:T(1024)} %copy-done.84) | copy-start | bytes 18436
  2417.3 50.1 %copy-start.99 = (f32[768]{0:T(1024)S(1)}, f32[768]{0:T(1024)}, u32[]{:S(2)}) copy-start(f32[768]{0:T(1024)} %copy-done.97) | copy-start | bytes 9220
  2417.3 50.1 %copy-start.131 = (f32[768]{0:T(1024)S(1)}, f32[768]{0:T(1024)}, u32[]{:S(2)}) copy-start(f32[768]{0:T(1024)} %copy-done.130) | copy-start | bytes 9220
  (114 other events, 817.3 us)
Sparse Core Ops, SparseCore 0:
  33.6 166.1 all-gather.10
  201.6 22.2 all-gather.12
  225.7 23.9 all-gather.14
  251.5 85.2 all-gather.16
  338.5 85.2 all-gather.18
  432.6 161.5 reduce-scatter.16
  599.6 167.7 all-gather.20
  769.3 83.4 all-gather.22
  854.4 166.7 all-gather.24
  1138.7 160.9 reduce-scatter.18
  1383.5 160.4 reduce-scatter.20
  1553.3 167.7 all-gather.26
  1726.7 94.4 reduce-scatter.32
  1824.5 109.0 reduce-scatter.30
  1936.9 107.3 reduce-scatter.22
  2047.7 107.3 reduce-scatter.24
  2216.2 158.0 reduce-scatter.26
  2378.0 37.6 reduce-scatter.28
  2419.0 40.1 reduce-scatter.34

commit v4 on v3

--- a/solution.py
+++ b/solution.py
@@ -289,7 +289,11 @@
     return (
         lax.psum_scatter(grads[0], "dp", scatter_dimension=1, tiled=True).astype(jnp.float32),
         lax.psum_scatter(grads[1], "dp", scatter_dimension=1, tiled=True).astype(jnp.float32),
-        lax.psum_scatter(grads[2], "dp", scatter_dimension=2, tiled=True).astype(jnp.float32),
+        jnp.swapaxes(
+            lax.psum_scatter(grads[2], "dp", scatter_dimension=1, tiled=True).astype(jnp.float32),
+            1,
+            2,
+        ),
     )
 
 
@@ -324,6 +328,7 @@
         lax.all_gather(mixture_gain, "dp", axis=0, tiled=True),
         lax.all_gather(router_weight, "dp", axis=0, tiled=True),
     )
+    output_all = lax.all_gather(output_full, "tensor", axis=0, tiled=True)
     gain_one = gain_one.astype(jnp.float32)
     gain_two = gain_two.astype(jnp.float32)
     residual = hidden_in.astype(jnp.float32)
@@ -367,18 +372,9 @@
         )
         mixed_blocks.append(mixed.astype(jnp.bfloat16).reshape(QBLK, local_heads * HD))
     mixed_full = jnp.concatenate(mixed_blocks, axis=0)
-    attended_partial = jnp.dot(
-        mixed_full, output_full, preferred_element_type=jnp.float32
-    ).astype(jnp.bfloat16)
-    attended_partial, gate_full, up_full = lax.optimization_barrier(
-        (attended_partial, gate_full, up_full)
-    )
-    attended = lax.psum_scatter(
-        attended_partial,
-        "tensor",
-        scatter_dimension=0,
-        tiled=True,
-    ).astype(jnp.float32)
+    mixed_full, gate_full, up_full = lax.optimization_barrier((mixed_full, gate_full, up_full))
+    mixed_own = lax.all_to_all(mixed_full, "tensor", 0, 1, tiled=True)
+    attended = jnp.dot(mixed_own, output_all, preferred_element_type=jnp.float32)
     middle = residual + RESIDUAL_SCALE * attended
     normed_two, unit_two, inverse_two = rms_forward(middle, gain_two)
     mixture_in = lax.all_gather(normed_two.astype(jnp.bfloat16), "tensor", axis=0, tiled=True)
@@ -451,7 +447,7 @@
     expert_parts = (
         jnp.einsum("ecd,ecf->edf", inputs, gate_pre_grad, preferred_element_type=jnp.float32),
         jnp.einsum("ecd,ecf->edf", inputs, up_pre_grad, preferred_element_type=jnp.float32),
-        jnp.einsum("ecf,ecd->efd", hidden_units, out_rows, preferred_element_type=jnp.float32),
+        jnp.einsum("ecd,ecf->edf", out_rows, hidden_units, preferred_element_type=jnp.float32),
     )
     expert_parts = tuple(part.astype(jnp.bfloat16) for part in expert_parts)
     gates_grad = gate_grad_table[:, :TOPK]
@@ -474,23 +470,29 @@
         mixture_grad_shard, unit_two, inverse_two, gain_two
     )
     middle_grad = out_grad.astype(jnp.float32) + middle_norm_grad
-    attended_grad = lax.all_gather(
-        (RESIDUAL_SCALE * middle_grad).astype(jnp.bfloat16), "tensor", axis=0, tiled=True
-    )
-    expert_parts, router_part, attended_grad = lax.optimization_barrier(
-        (expert_parts, router_part, attended_grad)
+    attended_grad = (RESIDUAL_SCALE * middle_grad).astype(jnp.bfloat16)
+    mixed_grad_own = jnp.einsum(
+        "td,fd->tf", attended_grad, output_all, preferred_element_type=jnp.float32
+    ).astype(jnp.bfloat16)
+    mixed_grad = lax.all_to_all(mixed_grad_own, "tensor", 1, 0, tiled=True)
+    expert_parts, router_part, mixed_grad = lax.optimization_barrier(
+        (expert_parts, router_part, mixed_grad)
     )
     expert_grads = reduce_experts(expert_parts)
     router_weight_grad = lax.psum_scatter(
         router_part, ("dp", "tensor"), scatter_dimension=0, tiled=True
     )
     output_part = jnp.einsum(
-        "tf,td->fd", mixed_full, attended_grad, preferred_element_type=jnp.float32
-    )
-    mixed_grad = jnp.einsum(
-        "td,fd->tf", attended_grad, output_full, preferred_element_type=jnp.float32
+        "tf,td->fd", mixed_own, attended_grad, preferred_element_type=jnp.float32
     ).astype(jnp.bfloat16)
+    output_part = lax.psum_scatter(output_part, "dp", scatter_dimension=1, tiled=True)
     mixed_grad = mixed_grad.reshape(TOK_GRP, local_groups, group_ratio, HD)
+    output_weight_grad = lax.psum_scatter(
+        output_part, "tensor", scatter_dimension=0, tiled=True
+    ).astype(jnp.float32)
+    mixture_gain_grad = lax.psum_scatter(
+        gain_two_grad, ("dp", "tensor"), scatter_dimension=0, tiled=True
+    )
     key_grad = jnp.zeros((TOK_GRP, local_groups, HD), jnp.float32)
     value_grad = jnp.zeros((TOK_GRP, local_groups, HD), jnp.float32)
     query_blocks = []
@@ -522,8 +524,22 @@
             jnp.einsum("grqk,qgrd->kgd", soft_low, out_block, preferred_element_type=jnp.float32)
         )
         if block_index == block_count - 2:
-            key_grad, value_grad, expert_grads, router_weight_grad = lax.optimization_barrier(
-                (key_grad, value_grad, expert_grads, router_weight_grad)
+            (
+                key_grad,
+                value_grad,
+                expert_grads,
+                router_weight_grad,
+                output_weight_grad,
+                mixture_gain_grad,
+            ) = lax.optimization_barrier(
+                (
+                    key_grad,
+                    value_grad,
+                    expert_grads,
+                    router_weight_grad,
+                    output_weight_grad,
+                    mixture_gain_grad,
+                )
             )
     gate_weight_grad, up_weight_grad, down_weight_grad = expert_grads
     query_rot_grad = jnp.concatenate(query_blocks, axis=0).reshape(TOK_GRP, local_heads, HD)
@@ -574,12 +590,9 @@
     query_weight_grad = projection_grads[:, :query_width]
     key_weight_grad = projection_grads[:, query_width : query_width + key_width]
     value_weight_grad = projection_grads[:, query_width + key_width :]
-    output_weight_grad = lax.psum_scatter(
-        output_part.astype(jnp.bfloat16), "dp", scatter_dimension=1, tiled=True
-    ).astype(jnp.float32)
-    attention_gain_grad, mixture_gain_grad = (
-        lax.psum_scatter(gain_one_grad, ("dp", "tensor"), scatter_dimension=0, tiled=True),
-        lax.psum_scatter(gain_two_grad, ("dp", "tensor"), scatter_dimension=0, tiled=True),
+
+    attention_gain_grad = lax.psum_scatter(
+        gain_one_grad, ("dp", "tensor"), scatter_dimension=0, tiled=True
     )
     return (
         block_output,

time: 2490 us -> 2370 us (0.952)
  waiting for transfers between devices: 962 us -> 856 us
  blocking collectives: 84.7 us -> 126 us
  local copies, waits for them, and re-layouts: 122 us -> 90.8 us
  other arithmetic: 319 us -> 294 us
    reduce_scatter x2, waiting for transfers between devices: 196 us -> 0.02 us  [the longest x1 0.02 us: local(): lax.psum_scatter(output_part, 'dp', scatter_dimension=1, tiled=True)]
    all_to_all x0 -> x2, waiting for transfers between devices: none -> 117 us  [the longest x1 113 us: local(): mixed_own = lax.all_to_all(mixed_full, 'tensor', 0, 1, tiled=True)]
    all_gather x1, waiting for transfers between devices: 94.4 us -> 12.6 us  [local(): output_all = lax.all_gather(output_full, 'tensor', axis=0, tiled=True)]
    unnamed x343 -> x319, local copies, waits for them, and re-layouts: 102 us -> 50.4 us
    reduce_scatter x1, waiting for transfers between devices: 0.01 us -> 41.2 us  [reduce_experts(): lax.psum_scatter(grads[1], 'dp', scatter_dimension=1, tiled=True)]
    unnamed x2 -> x3, blocking collectives: 55.7 us -> 95.6 us
  transfers between devices with their start and end apart: 19 -> 21, of which waited for: 8 -> 10; matrix products, arithmetic and copies ran while one was open for 42% -> 41% of each run, Pallas kernels for 9% -> 10%
where the time goes in v4:
time: 2370 us
  waiting for transfers between devices  856 us (36%)
  matrix products  738 us (31%)
  other arithmetic  294 us (12%)
  Pallas kernels  234 us (10%)
  blocking collectives  126 us (5%)
  local copies, waits for them, and re-layouts  90.8 us (4%)
    all_gather x1, waiting for transfers between devices, local(): lax.all_gather(normed_two.astype(jnp.bfloat16), 'tensor', axis=0, tiled=T...  165 us
    all_gather x1, waiting for transfers between devices, local(): lax.all_gather(normed_shard.astype(jnp.bfloat16), 'tensor', axis=0, tiled...  165 us
    reduce_scatter x1, waiting for transfers between devices, local(): lax.psum_scatter(mixture_grad_low, 'tensor', scatter_dimension=0, tiled=T...  163 us
    reduce_scatter x1, waiting for transfers between devices, local(): lax.psum_scatter(normed_grad_low, 'tensor', scatter_dimension=0, tiled=True)  145 us
    pallas_call x2, Pallas kernels, combine_rows(): pl.pallas_call(_combine_rows_kernel, grid_spec=pltpu.PrefetchScalarGridSp...  139 us
    all_to_all x1, waiting for transfers between devices, local(): mixed_own = lax.all_to_all(mixed_full, 'tensor', 0, 1, tiled=True)  113 us
    convert_element_type x6, other arithmetic, local(): score_grad = (soft_full * (weight_grad - delta)).astype(jnp.bfloat16)  105 us
    unnamed x3, blocking collectives  95.6 us
  transfers between devices with their start and end apart: 21, of which 10 were waited for; matrix products, arithmetic and copies ran while one was open for 41% of the time, Pallas kernels for 10%

profile of v4, /device:TPU:0, one launch (start us, length us, event | category | flops | bytes accessed | tf_op | source)
XLA Modules:
  0.0 2365.6 jit_solution(8977680991608928042)
XLA Ops:
  10.8 16.0 all-reduce.8
  35.0 164.7 %all-gather.11.cloned.1.call-done = bf16[3072,1536]{1,0:T(8,128)(2,1)} async-done(((bf16[768,1536]{1,0:T(8,128)(2,1)}), bf16[3072,1536]{1,0:T(8,128)(2,1)}) %all-gather.11.cloned.1.call-update) | async-done | bytes 9437200 | tf_op jit(solution)/shard_map/all_gather | solution.py:336
  200.7 9.5 all_gather.45
  210.3 11.4 all_gather.44
  261.0 14.2 fusion.245
  275.3 14.7 fusion.3
  290.0 16.2 fusion.157
  307.1 14.3 fusion.244
  321.4 12.7 fusion.8
  334.2 13.3 fusion.156
  362.7 10.6 fusion.155
  374.3 10.3 fusion.242
  384.5 9.0 fusion.22
  393.6 8.5 fusion.154
  428.4 113.4 %all-to-all-done = bf16[4,768,384]{2,1,0:T(8,128)(2,1)} async-done(((bf16[4,768,384]{2,1,0:T(8,128)(2,1)}), bf16[4,768,384]{2,1,0:T(8,128)(2,1)}, u32[]{:S(2)}, u32[]{:S(2)}) %all-to-all-start) | async-done | bytes 2359328 | tf_op jit(solution)/shard_map/all_to_all | solution.py:376
  546.5 12.6 all-gather.21.cloned.1.call-done
  570.1 165.3 %all-gather.23.cloned.1.call-done = bf16[3072,1536]{1,0:T(8,128)(2,1)} async-done(((bf16[768,1536]{1,0:T(8,128)(2,1)}), bf16[3072,1536]{1,0:T(8,128)(2,1)}) %all-gather.23.cloned.1.call-update) | async-done | bytes 9437200 | tf_op jit(solution)/shard_map/all_gather | solution.py:380
  737.5 14.5 fusion.101
  777.3 43.5 %all-gather.25.cloned.1.call-done = bf16[10,512,1536]{1,2,0:T(8,128)(2,1)} async-done(((bf16[10,512,192]{1,2,0:T(8,128)(2,1)}), bf16[10,512,1536]{1,2,0:T(8,128)(2,1)}) %all-gather.25.cloned.1.call-update) | async-done | bytes 15728656 | tf_op jit(solution)/shard_map/all_gather | solution.py:382
  821.7 9.4 all-gather
  831.3 7.8 fusion.179
  847.0 12.7 convert_element_type.293.refs_0_
  869.3 50.7 %shard_map.248 = (bf16[7680,1536]{1,0:T(8,128)(2,1)}, f32[7680,128]{1,0:T(8,128)}) custom-call(s32[7680]{0:T(1024)} %get-tuple-element.420.tok_ref, f32[3072,1536]{1,0:T(8,128)} %convert_element_type.293.refs_0_, f32[3072,128]{1,0:T(8,128)} %pad.33.refs_1_), custom_call_target="tpu_custom_call" | custom-call | tf_op jit(solution)/shard_map/pallas_call | solution.py:156
  926.2 27.7 %fusion.250 = f32[10,768,512]{1,2,0:T(8,128)} fusion(bf16[10,768,1536]{2,1,0:T(8,128)(2,1)} %bitcast.588, bf16[10,1536,512]{2,1,0:T(8,128)(2,1)} %all-gather.15.cloned.1.call-done), kind=kOutput, calls=%fused_computation.401 | convolution fusion | flops 12079595520 | bytes 55050240 | tf_op jit(solution)/shard_map/ecd,edf->ecf/dot_general | solution.py:408
  953.9 32.7 %multiply_convert_fusion.3 = (bf16[10,768,512]{1,2,0:T(8,128)(2,1)}, f32[10,768,512]{1,2,0:T(8,128)}) fusion(f32[10,768]{1,0:T(8,128)S(1)} %broadcast_select_fusion, f32[10,768,512]{1,2,0:T(8,128)} %fusion.250, bf16[10,768,1536]{2,1,0:T(8,128)(2,1)} %bitcast.589, bf16[10,1536,512]{2,1,0:T(8,128)(2,1)} %all-gather.17.cloned.1.call-done), kind=kOutput, calls=%fused_computation.57 | convolution fusion | flops 12107120640 | bytes 78673920 | tf_op jit(solution)/shard_map/ecd,edf->ecf/dot_general | solution.py:409
  986.6 27.3 %fusion.251 = f32[10,768,1536]{2,1,0:T(8,128)} fusion(bf16[10,768,512]{1,2,0:T(8,128)(2,1)} %get-tuple-element.238, bf16[10,512,1536]{1,2,0:T(8,128)(2,1)} %all-gather.25.cloned.1.call-done), kind=kOutput, calls=%fused_computation.402 | convolution fusion | flops 12079595520 | bytes 70778880 | tf_op jit(solution)/shard_map/ecf,efd->ecd/dot_general | solution.py:412
  1013.9 68.1 %shard_map.249 = f32[3072,1536]{1,0:T(8,128)} custom-call(s32[7680]{0:T(1024)} %get-tuple-element.420.tok_ref, f32[7680,1536]{1,0:T(8,128)} %bitcast.516), custom_call_target="tpu_custom_call" | custom-call | tf_op jit(solution)/shard_map/pallas_call | solution.py:211
  1082.1 12.9 fusion.40.refs_0_
  1095.0 11.3 convert_element_type.302
  1106.3 44.4 %shard_map.250 = bf16[7680,1536]{1,0:T(8,128)(2,1)} custom-call(s32[7680]{0:T(1024)} %get-tuple-element.420.tok_ref, f32[3072,1536]{1,0:T(8,128)} %fusion.40.refs_0_), custom_call_target="tpu_custom_call" | custom-call | tf_op jit(solution)/shard_map/pallas_call | solution.py:156
  1150.7 34.5 %multiply_reduce_fusion = (f32[10,768]{1,0:T(8,128)S(1)}, bf16[10,768,512]{1,2,0:T(8,128)(2,1)}, bf16[10,768,512]{1,2,0:T(8,128)(2,1)}) fusion(f32[10,768,512]{1,2,0:T(8,128)} %get-tuple-element.441, f32[10,768,512]{1,2,0:T(8,128)} %fusion.250, f32[10,768]{1,0:T(8,128)S(1)} %broadcast_select_fusion, bf16[10,768,1536]{2,1,0:T(8,128)(2,1)} %bitcast.522, ...), kind=kOutput, calls=%fused_computation.54 | convolution fusion | flops 12146434048 | bytes 86568960 | tf_op jit(solution)/shard_map/ecd,efd->ecf/dot_general | solution.py:427
  1185.3 7.8 fusion.81.refs_1_
  1193.1 27.3 %fusion.252 = f32[10,768,1536]{2,1,0:T(8,128)} fusion(bf16[10,768,512]{1,2,0:T(8,128)(2,1)} %get-tuple-element.235, bf16[10,1536,512]{2,1,0:T(8,128)(2,1)} %all-gather.15.cloned.1.call-done), kind=kOutput, calls=%fused_computation.403 | convolution fusion | flops 12079595520 | bytes 70778880 | tf_op jit(solution)/shard_map/ecf,edf->ecd/dot_general | solution.py:435
  1220.4 34.2 %add_convert_fusion = bf16[10,768,1536]{2,1,0:T(8,128)(2,1)} fusion(f32[10,768,1536]{2,1,0:T(8,128)} %fusion.252, bf16[10,768,512]{1,2,0:T(8,128)(2,1)} %get-tuple-element.236, bf16[10,1536,512]{2,1,0:T(8,128)(2,1)} %all-gather.17.cloned.1.call-done), kind=kOutput, calls=%fused_computation | convolution fusion | flops 12103188480 | bytes 94371840 | tf_op jit(solution)/shard_map/ecf,edf->ecd/dot_general | solution.py:437
  1254.6 71.2 %shard_map.251 = (f32[3072,1536]{1,0:T(8,128)}, f32[3072,128]{1,0:T(8,128)}) custom-call(s32[7680]{0:T(1024)} %get-tuple-element.420.tok_ref, bf16[7680,1536]{1,0:T(8,128)(2,1)} %bitcast.521, f32[7680,128]{1,0:T(8,128)} %fusion.81.refs_1_), custom_call_target="tpu_custom_call" | custom-call | tf_op jit(solution)/shard_map/pallas_call | solution.py:211
  1332.0 14.3 add_convert_fusion.2
  1350.9 162.8 %reduce-scatter.19.cloned.1.call-done = bf16[768,1536]{1,0:T(8,128)(2,1)} async-done(((bf16[3072,1536]{1,0:T(8,128)(2,1)}), bf16[768,1536]{1,0:T(8,128)(2,1)}) %reduce-scatter.19.cloned.1.call-update) | async-done | bytes 2359312 | tf_op jit(solution)/shard_map/reduce_scatter | solution.py:466
  1532.0 22.7 convolution_convert_fusion.1
  1554.6 8.3 convolution_convert_fusion.5
  1569.0 21.7 convolution_convert_fusion.2
  1597.9 21.4 convolution_convert_fusion
  1628.6 38.0 %all-reduce.6 = f32[1536]{0:T(1024)S(1)} all-reduce(f32[1536]{0:T(1024)S(1)} %get-tuple-element.380), channel_id=10, replica_groups=mesh['dp'=8,'tensor'=4] {'dp','tensor'}, use_global_device_ids=true, to_apply=%region_43.44.clone | all-reduce | flops 1536 | bytes 12288
  1708.5 11.9 fusion.17
  1720.4 16.9 fusion.9
  1737.3 20.2 fusion.19
  1765.7 17.5 fusion.11
  1783.2 24.7 %fusion.4 = (f32[2,3,512]{2,1,0:T(4,128)S(1)}, f32[2,2560,512,3]{2,1,3,0:T(8,128)}) fusion(f32[2,3,512,2560]{2,3,1,0:T(8,128)} %get-tuple-element.435, f32[2,3,512]{2,1,0:T(4,128)S(1)} %log_add_fusion.1, bf16[2560,2,64,1]{0,2,3,1:T(8,128)(2,1)S(1)} %bitcast.560, bf16[512,2,3,64]{0,3,2,1:T(8,128)(2,1)S(1)} %bitcast.537), kind=kOutput, calls=%fused_computation.13 | convolution fusion | flops 1030222848 | bytes 63987712 | tf_op jit(solution)/shard_map/qgrd,kgd->grqk/dot_general | solution.py:508
  1827.0 28.2 %fusion.6 = bf16[2,3,512,2560]{2,3,1,0:T(8,128)(2,1)} fusion(f32[2,2560,512,3]{2,1,3,0:T(8,128)} %get-tuple-element.451, f32[2,3,512,2560]{2,3,1,0:T(8,128)} %get-tuple-element.435, f32[2,3,512]{2,1,0:T(4,128)S(1)} %get-tuple-element.450, f32[2,3,512]{2,1,0:T(4,128)S(1)} %log_add_fusion.1), kind=kLoop, calls=%fused_computation.15 | loop fusion | flops 31457280 | bytes 78667776 | tf_op jit(solution)/shard_map/convert_element_type | solution.py:512
  1855.3 9.2 fusion.151
  1864.5 29.7 %fusion = (f32[2,3,512]{2,1,0:T(4,128)S(1)}, f32[2,3072,512,3]{2,1,3,0:T(8,128)}) fusion(f32[2,3,512,3072]{2,3,1,0:T(8,128)} %get-tuple-element.437, f32[2,3,512]{2,1,0:T(4,128)S(1)} %copy-done.72, bf16[3072,2,64,1]{0,2,3,1:T(8,128)(2,1)S(1)} %bitcast.525, bf16[512,2,3,64]{0,3,2,1:T(8,128)(2,1)S(1)} %bitcast.535), kind=kOutput, calls=%fused_computation.3 | convolution fusion | flops 1236268032 | bytes 76701696 | tf_op jit(solution)/shard_map/qgrd,kgd->grqk/dot_general | solution.py:508
  1894.2 32.4 %fusion.2 = bf16[2,3,512,3072]{2,3,1,0:T(8,128)(2,1)} fusion(f32[2,3072,512,3]{2,1,3,0:T(8,128)} %get-tuple-element.453, f32[2,3,512,3072]{2,3,1,0:T(8,128)} %get-tuple-element.437, f32[2,3,512]{2,1,0:T(4,128)S(1)} %get-tuple-element.452, f32[2,3,512]{2,1,0:T(4,128)S(1)} %copy-done.72), kind=kLoop, calls=%fused_computation.5 | loop fusion | flops 37748736 | bytes 94396416 | tf_op jit(solution)/shard_map/convert_element_type | solution.py:512
  1926.7 10.9 fusion.141
  1963.0 8.4 fusion.120
  1971.4 12.5 fusion.87
  1983.9 13.0 fusion.137
  1996.9 11.1 fusion.254
  2008.0 13.6 fusion.98
  2034.5 41.2 %reduce-scatter.23.cloned.1.call-done = bf16[10,192,512]{2,1,0:T(8,128)(2,1)} async-done(((bf16[10,1536,512]{2,1,0:T(8,128)(2,1)}), bf16[10,192,512]{2,1,0:T(8,128)(2,1)}) %reduce-scatter.23.cloned.1.call-update) | async-done | bytes 1966096 | tf_op jit(solution)/shard_map/reduce_scatter | solution.py:291
  2079.7 15.8 fusion.105
  2095.5 9.7 fusion.88
  2106.5 8.9 fusion.255
  2115.5 17.2 add_convert_fusion.1
  2149.4 144.7 %reduce-scatter.29.cloned.1.call-done = bf16[768,1536]{1,0:T(8,128)(2,1)} async-done(((bf16[3072,1536]{1,0:T(8,128)(2,1)}), bf16[768,1536]{1,0:T(8,128)(2,1)}) %reduce-scatter.29.cloned.1.call-update) | async-done | bytes 2359312 | tf_op jit(solution)/shard_map/reduce_scatter | solution.py:568
  2306.2 41.5 %all-reduce.7 = f32[1536]{0:T(1024)S(1)} all-reduce(f32[1536]{0:T(1024)S(1)} %get-tuple-element.378), channel_id=12, replica_groups=mesh['dp'=8,'tensor'=4] {'dp','tensor'}, use_global_device_ids=true, to_apply=%region_47.48.clone | all-reduce | flops 1536 | bytes 12288
  (538 shorter events, 365.0 us)
Async XLA Ops:
  7.2 192.6 %all-gather.11.cloned.1.call-start = ((), (), s32[]{:S(2)}) async-start(), calls=%async_computation.12 | async-start | bytes 11796480 | tf_op jit(solution)/shard_map/all_gather | solution.py:336
  26.9 173.5 %copy-start.123 = (s32[1,1024]{1,0:T(1,128)S(1)}, s32[1,1024]{1,0:T(1,128)}, u32[]{:S(2)}) copy-start(s32[1,1024]{1,0:T(1,128)} %param.45) | copy-start | bytes 12292
  26.9 173.8 %copy-start.121 = (bf16[192,128]{1,0:T(8,128)(2,1)S(1)}, bf16[192,128]{1,0:T(8,128)(2,1)}, u32[]{:S(2)}) copy-start(bf16[192,128]{1,0:T(8,128)(2,1)} %param.50) | copy-start | bytes 147460
  29.1 181.1 %copy-start.122 = (bf16[192,128]{1,0:T(8,128)(2,1)S(1)}, bf16[192,128]{1,0:T(8,128)(2,1)}, u32[]{:S(2)}) copy-start(bf16[192,128]{1,0:T(8,128)(2,1)} %param.51) | copy-start | bytes 147460
  33.5 202.0 %all-gather.19.cloned.1.call-start = ((), (), s32[]{:S(2)}) async-start(), calls=%async_computation.16 | async-start | bytes 1327104 | tf_op jit(solution)/shard_map/all_gather | solution.py:327
  34.2 216.7 %all-gather.13.cloned.1.call-start = ((), (), s32[]{:S(2)}) async-start(), calls=%async_computation.13 | async-start | bytes 1327104 | tf_op jit(solution)/shard_map/all_gather | solution.py:324
  34.9 387.6 %all-gather.15.cloned.1.call-start = ((), (), s32[]{:S(2)}) async-start(), calls=%async_computation.14 | async-start | bytes 17694720 | tf_op jit(solution)/shard_map/all_gather | solution.py:340
  199.8 224.0 %all-gather.17.cloned.1.call-start = ((), (), s32[]{:S(2)}) async-start(), calls=%async_computation.15 | async-start | bytes 17694720 | tf_op jit(solution)/shard_map/all_gather | solution.py:341
  200.3 358.7 %all-gather.21.cloned.1.call-start = ((), (), s32[]{:S(2)}) async-start(), calls=%async_computation.17 | async-start | bytes 5898240 | tf_op jit(solution)/shard_map/all_gather | solution.py:331
  210.3 36.3 %copy-start.46 = (bf16[1536,128]{1,0:T(8,128)(2,1)}, bf16[1536,128]{1,0:T(8,128)(2,1)S(1)}, u32[]{:S(2)}) copy-start(bf16[1536,128]{1,0:T(8,128)(2,1)S(1)} %all_gather.45) | copy-start | bytes 1179652
  221.6 20.9 copy-start.35
  228.5 29.9 %copy-start.23 = (f32[3072,32]{0,1:T(8,128)}, f32[3072,32]{0,1:T(8,128)S(1)}, u32[]{:S(2)}) copy-start(f32[3072,32]{0,1:T(8,128)S(1)} %get-tuple-element.421) | copy-start | bytes 1179652
  228.5 29.9 %copy-start.25 = (f32[3072,32]{0,1:T(8,128)}, f32[3072,32]{0,1:T(8,128)S(1)}, u32[]{:S(2)}) copy-start(f32[3072,32]{0,1:T(8,128)S(1)} %get-tuple-element.422) | copy-start | bytes 1179652
  242.6 47.4 %copy-start.16 = (bf16[3072,128]{0,1:T(8,128)(2,1)}, bf16[3072,128]{0,1:T(8,128)(2,1)S(1)}, u32[]{:S(2)}) copy-start(bf16[3072,128]{0,1:T(8,128)(2,1)S(1)} %convolution_convert_fusion.4) | copy-start | bytes 2359300
  259.6 47.5 %copy-start.10 = (bf16[3072,2,32]{0,2,1:T(8,128)(2,1)}, bf16[3072,2,32]{0,2,1:T(8,128)(2,1)S(1)}, u32[]{:S(2)}) copy-start(bf16[3072,2,32]{0,2,1:T(8,128)(2,1)S(1)} %get-tuple-element.410) | copy-start | bytes 1179652
  259.6 152.9 %copy-start.8 = (bf16[3072,2,32]{0,2,1:T(8,128)(2,1)}, bf16[3072,2,32]{0,2,1:T(8,128)(2,1)S(1)}, u32[]{:S(2)}) copy-start(bf16[3072,2,32]{0,2,1:T(8,128)(2,1)S(1)} %get-tuple-element.409) | copy-start | bytes 1179652
  261.0 46.1 %copy-start.44 = (bf16[512,6,64]{0,2,1:T(8,128)(2,1)}, bf16[512,6,64]{0,2,1:T(8,128)(2,1)S(1)}, u32[]{:S(2)}) copy-start(bf16[512,6,64]{0,2,1:T(8,128)(2,1)S(1)} %get-tuple-element.408) | copy-start | bytes 1179652
  418.2 140.8 %copy-start.6 = (bf16[768,1536]{1,0:T(8,128)(2,1)S(1)}, bf16[768,1536]{1,0:T(8,128)(2,1)}, u32[]{:S(2)}) copy-start(bf16[768,1536]{1,0:T(8,128)(2,1)} %param.43) | copy-start | bytes 7077892
  423.8 118.0 %all-to-all-start = ((bf16[4,768,384]{2,1,0:T(8,128)(2,1)}), bf16[4,768,384]{2,1,0:T(8,128)(2,1)}, u32[]{:S(2)}, u32[]{:S(2)}) async-start(bf16[4,768,384]{2,1,0:T(8,128)(2,1)} %bitcast.60), calls=%async_computation | async-start | bytes 4718592 | tf_op jit(solution)/shard_map/all_to_all | solution.py:376
  428.4 307.0 %all-gather.23.cloned.1.call-start = ((), (), s32[]{:S(2)}) async-start(), calls=%async_computation.18 | async-start | bytes 11796480 | tf_op jit(solution)/shard_map/all_gather | solution.py:380
  428.4 137.6 %copy-start.92 = (f32[1536]{0:T(1024)}, f32[1536]{0:T(1024)S(1)}, u32[]{:S(2)}) copy-start(f32[1536]{0:T(1024)S(1)} %convert_element_type.291) | copy-start | bytes 18436
  566.0 169.5 %copy-start.70 = (s32[3072,8]{0,1:T(8,128)S(1)}, s32[3072,8]{0,1:T(8,128)}, u32[]{:S(2)}) copy-start(s32[3072,8]{0,1:T(8,128)} %param.46) | copy-start | bytes 294916
  566.0 170.7 %copy-start.97 = (f32[768]{0:T(1024)}, f32[768]{0:T(1024)S(1)}, u32[]{:S(2)}) copy-start(f32[768]{0:T(1024)S(1)} %add_rsqrt_fusion) | copy-start | bytes 9220
  568.1 168.5 %copy-start.95 = (s32[1,24576]{1,0:T(1,128)S(1)}, s32[1,24576]{1,0:T(1,128)}, u32[]{:S(2)}) copy-start(s32[1,24576]{1,0:T(1,128)} %param.47) | copy-start | bytes 294916
  570.0 250.8 %all-gather.25.cloned.1.call-start = ((), (), s32[]{:S(2)}) async-start(), calls=%async_computation.19 | async-start | bytes 17694720 | tf_op jit(solution)/shard_map/all_gather | solution.py:382
  735.4 346.6 %all-gather.27.cloned.1.call-start = ((), (), s32[]{:S(2)}) async-start(), calls=%async_computation.20 | async-start | bytes 11796480 | tf_op jit(solution)/shard_map/all_gather | solution.py:417
  770.4 51.3 %copy-start.124 = (bf16[192,40]{0,1:T(8,128)(2,1)S(1)}, bf16[192,40]{0,1:T(8,128)(2,1)}, u32[]{:S(2)}) copy-start(bf16[192,40]{0,1:T(8,128)(2,1)} %param.54) | copy-start | bytes 46084
  820.8 525.5 %reduce-scatter.17.cloned.1.call-start = ((), (), s32[]{:S(2)}) async-start(), calls=%async_computation.21 | async-start | bytes 11796480 | tf_op jit(solution)/shard_map/reduce_scatter | solution.py:422
  831.3 28.4 %copy-start.66 = (bf16[1536,40]{0,1:T(8,128)(2,1)}, bf16[1536,40]{0,1:T(8,128)(2,1)S(1)}, u32[]{:S(2)}) copy-start(bf16[1536,40]{0,1:T(8,128)(2,1)S(1)} %reshape.1177) | copy-start | bytes 368644
  847.0 73.0 %copy-start.88 = (s32[7680]{0:T(1024)}, s32[7680]{0:T(1024)S(1)}, u32[]{:S(2)}) copy-start(s32[7680]{0:T(1024)S(1)} %get-tuple-element.419) | copy-start | bytes 92164
  867.0 52.9 %copy-start.82 = (f32[3072]{0:T(1024)}, f32[3072]{0:T(1024)S(1)}, u32[]{:S(2)}) copy-start(f32[3072]{0:T(1024)S(1)} %get-tuple-element.384) | copy-start | bytes 36868
  867.5 52.4 %copy-start.14 = (f32[3072,8]{1,0:T(8,128)}, f32[3072,8]{1,0:T(8,128)S(1)}, u32[]{:S(2)}) copy-start(f32[3072,8]{1,0:T(8,128)S(1)} %copy.576) | copy-start | bytes 294916
  1106.3 407.4 %reduce-scatter.19.cloned.1.call-start = ((), (), s32[]{:S(2)}) async-start(), calls=%async_computation.22 | async-start | bytes 11796480 | tf_op jit(solution)/shard_map/reduce_scatter | solution.py:466
  1150.7 34.6 %copy-start.89 = (s32[7680]{0:T(1024)S(1)}, s32[7680]{0:T(1024)}, u32[]{:S(2)}) copy-start(s32[7680]{0:T(1024)} %copy-done.88) | copy-start | bytes 92164
  1254.6 71.3 %copy-start.15 = (f32[3072,8]{1,0:T(8,128)S(1)}, f32[3072,8]{1,0:T(8,128)}, u32[]{:S(2)}) copy-start(f32[3072,8]{1,0:T(8,128)} %copy-done.14) | copy-start | bytes 294916
  1254.6 71.3 %copy-start.83 = (f32[3072]{0:T(1024)S(1)}, f32[3072]{0:T(1024)}, u32[]{:S(2)}) copy-start(f32[3072]{0:T(1024)} %copy-done.82) | copy-start | bytes 36868
  1350.8 162.9 %copy-start.93 = (f32[1536]{0:T(1024)S(1)}, f32[1536]{0:T(1024)}, u32[]{:S(2)}) copy-start(f32[1536]{0:T(1024)} %copy-done.92) | copy-start | bytes 18436
  1350.8 162.9 %copy-start.98 = (f32[768]{0:T(1024)S(1)}, f32[768]{0:T(1024)}, u32[]{:S(2)}) copy-start(f32[768]{0:T(1024)} %copy-done.97) | copy-start | bytes 9220
  1350.8 167.4 %copy-start.27 = (bf16[768,1536]{1,0:T(8,128)(2,1)S(1)}, bf16[768,1536]{1,0:T(8,128)(2,1)}, u32[]{:S(2)}) copy-start(bf16[768,1536]{1,0:T(8,128)(2,1)} %param.44) | copy-start | bytes 7077892
  1350.8 273.3 %reduce-scatter.27.cloned.1.call-start = ((), (), s32[]{:S(2)}) async-start(), calls=%async_computation.26 | async-start | bytes 5308416 | tf_op jit(solution)/shard_map/reduce_scatter | solution.py:488
  1564.6 58.2 %all-to-all-start.1 = ((bf16[768,4,384]{2,0,1:T(8,128)(2,1)}), bf16[768,4,384]{2,0,1:T(8,128)(2,1)S(1)}, u32[]{:S(2)}, u32[]{:S(2)}) async-start(bf16[768,4,384]{2,0,1:T(8,128)(2,1)} %bitcast.534), calls=%async_computation.3 | async-start | bytes 4718592 | tf_op jit(solution)/shard_map/all_to_all | solution.py:477
  1569.0 452.7 %reduce-scatter.31.cloned.1.call-start = ((), (), s32[]{:S(2)}) async-start(), calls=%async_computation.28 | async-start | bytes 811008
  1624.0 399.0 %reduce-scatter.33.cloned.1.call-start = ((), (), s32[]{:S(2)}) async-start(), calls=%async_computation.29 | async-start | bytes 983040
  1626.4 400.1 %reduce-scatter.21.cloned.1.call-start = ((), (), s32[]{:S(2)}) async-start(), calls=%async_computation.23 | async-start | bytes 17694720 | tf_op jit(solution)/shard_map/reduce_scatter | solution.py:290
  1627.1 403.4 %reduce-scatter.25.cloned.1.call-start = ((), (), s32[]{:S(2)}) async-start(), calls=%async_computation.25 | async-start | bytes 17694720 | tf_op jit(solution)/shard_map/reduce_scatter | solution.py:293
  1627.7 448.0 %reduce-scatter.23.cloned.1.call-start = ((), (), s32[]{:S(2)}) async-start(), calls=%async_computation.24 | async-start | bytes 17694720 | tf_op jit(solution)/shard_map/reduce_scatter | solution.py:291
  1627.8 74.2 %copy-start.80 = (f32[2,3,512]{2,1,0:T(4,128)}, f32[2,3,512]{2,1,0:T(4,128)S(1)}, u32[]{:S(2)}) copy-start(f32[2,3,512]{2,1,0:T(4,128)S(1)} %log_add_fusion.4) | copy-start | bytes 36868
  1627.9 109.4 %copy-start.77 = (f32[2,3,512]{2,1,0:T(4,128)}, f32[2,3,512]{2,1,0:T(4,128)S(1)}, u32[]{:S(2)}) copy-start(f32[2,3,512]{2,1,0:T(4,128)S(1)} %log_add_fusion.3) | copy-start | bytes 36868
  1627.9 129.6 %copy-start.79 = (f32[2,3,512]{2,1,0:T(4,128)}, f32[2,3,512]{2,1,0:T(4,128)S(1)}, u32[]{:S(2)}) copy-start(f32[2,3,512]{2,1,0:T(4,128)S(1)} %log_add_fusion.2) | copy-start | bytes 36868
  1677.0 31.5 %copy-start.38 = (bf16[512,384]{0,1:T(8,128)(2,1)}, bf16[512,384]{0,1:T(8,128)(2,1)S(1)}, u32[]{:S(2)}) copy-start(bf16[512,384]{0,1:T(8,128)(2,1)S(1)} %copy.595) | copy-start | bytes 1179652
  1678.3 42.1 %copy-start.37 = (bf16[512,384]{0,1:T(8,128)(2,1)}, bf16[512,384]{0,1:T(8,128)(2,1)S(1)}, u32[]{:S(2)}) copy-start(bf16[512,384]{0,1:T(8,128)(2,1)S(1)} %copy.597) | copy-start | bytes 1179652
  1679.7 103.5 %copy-start.30 = (bf16[512,384]{0,1:T(8,128)(2,1)}, bf16[512,384]{0,1:T(8,128)(2,1)S(1)}, u32[]{:S(2)}) copy-start(bf16[512,384]{0,1:T(8,128)(2,1)S(1)} %copy.599) | copy-start | bytes 1179652
  1691.2 173.3 %copy-start.29 = (bf16[512,384]{0,1:T(8,128)(2,1)}, bf16[512,384]{0,1:T(8,128)(2,1)S(1)}, u32[]{:S(2)}) copy-start(bf16[512,384]{0,1:T(8,128)(2,1)S(1)} %copy.601) | copy-start | bytes 1179652
  1737.3 23.4 slice-start.3
  1737.3 26.0 %slice-start.4 = ((s8[25165824]{0:T(1024)(128)(4,1)}), s8[4194304]{0:T(1024)(128)(4,1)S(1)}, s32[]{:S(2)}) async-start(s8[25165824]{0:T(1024)(128)(4,1)} %bitcast.506), calls=%async_computation.35 | async-start | bytes 8388608
  1737.3 28.4 %slice-start.5 = ((s8[25165824]{0:T(1024)(128)(4,1)}), s8[4194304]{0:T(1024)(128)(4,1)S(1)}, s32[]{:S(2)}) async-start(s8[25165824]{0:T(1024)(128)(4,1)} %bitcast.506), calls=%async_computation.36 | async-start | bytes 8388608
  1807.9 486.2 %reduce-scatter.29.cloned.1.call-start = ((), (), s32[]{:S(2)}) async-start(), calls=%async_computation.27 | async-start | bytes 11796480 | tf_op jit(solution)/shard_map/reduce_scatter | solution.py:568
  1926.7 21.8 slice-start.15
  1926.7 21.8 slice-start.16
  2030.5 49.2 %copy-start.73 = (f32[2,3,512]{2,1,0:T(4,128)S(1)}, f32[2,3,512]{2,1,0:T(4,128)}, u32[]{:S(2)}) copy-start(f32[2,3,512]{2,1,0:T(4,128)} %log_add_fusion) | copy-start | bytes 36868
  2132.7 222.7 %reduce-scatter.35.cloned.1.call-start = ((), (), s32[]{:S(2)}) async-start(), calls=%async_computation.30 | async-start | bytes 2211840
  2149.3 153.2 %copy-start.7 = (bf16[768,1536]{1,0:T(8,128)(2,1)S(1)}, bf16[768,1536]{1,0:T(8,128)(2,1)}, u32[]{:S(2)}) copy-start(bf16[768,1536]{1,0:T(8,128)(2,1)} %param.43) | copy-start | bytes 7077892
  2149.3 153.3 %copy-start.91 = (f32[1536]{0:T(1024)S(1)}, f32[1536]{0:T(1024)}, u32[]{:S(2)}) copy-start(f32[1536]{0:T(1024)} %copy-done.90) | copy-start | bytes 18436
  2149.4 153.3 %copy-start.120 = (f32[768]{0:T(1024)S(1)}, f32[768]{0:T(1024)}, u32[]{:S(2)}) copy-start(f32[768]{0:T(1024)} %copy-done.119) | copy-start | bytes 9220
  (106 other events, 746.4 us)
Sparse Core Ops, SparseCore 0:
  33.6 166.1 all-gather.10
  201.6 22.6 all-gather.18
  226.2 23.3 all-gather.12
  251.4 85.2 all-gather.14
  338.4 85.2 all-gather.16
  425.2 133.8 all-gather.20
  570.2 165.1 all-gather.22
  737.3 83.4 all-gather.24
  822.4 166.7 all-gather.26
  1106.4 162.0 reduce-scatter.16
  1350.9 162.6 reduce-scatter.18
  1532.1 54.7 reduce-scatter.26
  1624.2 95.3 reduce-scatter.30
  1721.7 22.1 reduce-scatter.32
  1747.3 106.8 reduce-scatter.20
  1857.5 107.3 reduce-scatter.24
  1968.3 107.3 reduce-scatter.22
  2132.8 161.1 reduce-scatter.28
  2302.7 41.1 reduce-scatter.34

commit v5 on v4

--- a/solution.py
+++ b/solution.py
@@ -319,16 +319,17 @@
     group_ratio = local_heads // local_groups
     block_count = TOK_GRP // QBLK
     local_experts = gate_weight.shape[0]
-    gain_one, query_full, key_full, value_full, output_full, gain_two, router_full = (
+    gain_one, query_full, key_full, value_full, gain_two, router_full = (
         lax.all_gather(attention_gain, "dp", axis=0, tiled=True),
         lax.all_gather(query_weight, "dp", axis=0, tiled=True),
         lax.all_gather(key_weight, "dp", axis=0, tiled=True),
         lax.all_gather(value_weight, "dp", axis=0, tiled=True),
-        lax.all_gather(output_weight, "dp", axis=1, tiled=True),
         lax.all_gather(mixture_gain, "dp", axis=0, tiled=True),
         lax.all_gather(router_weight, "dp", axis=0, tiled=True),
     )
-    output_all = lax.all_gather(output_full, "tensor", axis=0, tiled=True)
+    output_all = lax.all_gather(
+        lax.all_gather(output_weight, "tensor", axis=0, tiled=True), "dp", axis=1, tiled=True
+    )
     gain_one = gain_one.astype(jnp.float32)
     gain_two = gain_two.astype(jnp.float32)
     residual = hidden_in.astype(jnp.float32)
@@ -415,6 +416,12 @@
     (mixture_sum,) = combine_rows(slot_token, (expert_out.reshape(slot_count, D),), CAP, TOK_GRP)
     out_grad_held, down_full = lax.optimization_barrier((out_grad, down_full))
     cotangent_full = lax.all_gather(out_grad_held, "tensor", axis=0, tiled=True)
+    projection_local, cotangent_full = lax.optimization_barrier(
+        (jnp.concatenate([query_weight, key_weight, value_weight], axis=1), cotangent_full)
+    )
+    projection_all = lax.all_gather(
+        lax.all_gather(projection_local, "tensor", axis=1, tiled=True), "dp", axis=0, tiled=True
+    )
     scaled_cotangent = (
         (RESIDUAL_SCALE * cotangent_full.astype(jnp.float32)).astype(jnp.bfloat16).astype(jnp.float32)
     )
@@ -439,9 +446,13 @@
     grad_in_mixture, gate_grad_table = combine_rows(
         slot_token, (input_rows, gate_grad_rows), CAP, TOK_GRP
     )
-    (inputs, gate_pre_grad, up_pre_grad, hidden_units, out_rows), grad_in_mixture = (
+    (inputs, gate_pre_grad, up_pre_grad, hidden_units, out_rows), grad_in_mixture, projection_all = (
         lax.optimization_barrier(
-            ((inputs, gate_pre_grad, up_pre_grad, hidden_units, out_rows), grad_in_mixture)
+            (
+                (inputs, gate_pre_grad, up_pre_grad, hidden_units, out_rows),
+                grad_in_mixture,
+                projection_all,
+            )
         )
     )
     expert_parts = (
@@ -479,9 +490,14 @@
         (expert_parts, router_part, mixed_grad)
     )
     expert_grads = reduce_experts(expert_parts)
-    router_weight_grad = lax.psum_scatter(
-        router_part, ("dp", "tensor"), scatter_dimension=0, tiled=True
-    )
+    router_and_gain = lax.psum_scatter(
+        jnp.concatenate([router_part, gain_two_grad[:, None]], axis=1),
+        ("dp", "tensor"),
+        scatter_dimension=0,
+        tiled=True,
+    )
+    router_weight_grad = router_and_gain[:, : router_part.shape[1]]
+    mixture_gain_grad = router_and_gain[:, router_part.shape[1]]
     output_part = jnp.einsum(
         "tf,td->fd", mixed_own, attended_grad, preferred_element_type=jnp.float32
     ).astype(jnp.bfloat16)
@@ -490,9 +506,6 @@
     output_weight_grad = lax.psum_scatter(
         output_part, "tensor", scatter_dimension=0, tiled=True
     ).astype(jnp.float32)
-    mixture_gain_grad = lax.psum_scatter(
-        gain_two_grad, ("dp", "tensor"), scatter_dimension=0, tiled=True
-    )
     key_grad = jnp.zeros((TOK_GRP, local_groups, HD), jnp.float32)
     value_grad = jnp.zeros((TOK_GRP, local_groups, HD), jnp.float32)
     query_blocks = []
@@ -554,20 +567,11 @@
         .reshape(TOK_GRP, local_groups * HD)
     )
     value_grad_low = value_grad.astype(jnp.bfloat16).reshape(TOK_GRP, local_groups * HD)
-    total_rows = jnp.einsum("tf,df->td", query_grad, query_full, preferred_element_type=jnp.float32)
-    total_rows = total_rows + jnp.einsum(
-        "tf,df->td", key_grad_low, key_full, preferred_element_type=jnp.float32
-    )
-    normed_grad_low = (
-        total_rows
-        + jnp.einsum("tf,df->td", value_grad_low, value_full, preferred_element_type=jnp.float32)
-    ).astype(jnp.bfloat16)
-    normed_grad_low, query_grad, key_grad_low, value_grad_low = lax.optimization_barrier(
-        (normed_grad_low, query_grad, key_grad_low, value_grad_low)
-    )
-    normed_grad = lax.psum_scatter(
-        normed_grad_low, "tensor", scatter_dimension=0, tiled=True
-    ).astype(jnp.float32)
+    projection_grad = jnp.concatenate([query_grad, key_grad_low, value_grad_low], axis=1)
+    projection_grad_own = lax.all_to_all(projection_grad, "tensor", 0, 1, tiled=True)
+    normed_grad = jnp.einsum(
+        "tf,df->td", projection_grad_own, projection_all, preferred_element_type=jnp.float32
+    )
     query_part = jnp.einsum(
         "td,tf->df", normed_full, query_grad, preferred_element_type=jnp.float32
     )

time: 2370 us -> 2390 us (level)
  matrix products: 738 us -> 700 us
  waiting for transfers between devices: 856 us -> 889 us
    reduce_scatter x1 -> x0, waiting for transfers between devices: 145 us -> none  [local(): lax.psum_scatter(normed_grad_low, 'tensor', scatter_dimension=0, tiled=True)]
    all_gather x1, waiting for transfers between devices: 0.02 us -> 127 us  [local(): cotangent_full = lax.all_gather(out_grad_held, 'tensor', axis=0, tiled=True)]
    all_to_all x0 -> x1, waiting for transfers between devices: none -> 76.4 us  [local(): lax.all_to_all(projection_grad, 'tensor', 0, 1, tiled=True)]
    all_to_all x1, waiting for transfers between devices: 113 us -> 54.7 us  [local(): mixed_own = lax.all_to_all(mixed_full, 'tensor', 0, 1, tiled=True)]
    reduce_scatter x1, waiting for transfers between devices: 41.2 us -> 95.3 us  [reduce_experts(): lax.psum_scatter(grads[1], 'dp', scatter_dimension=1, tiled=True)]
    unnamed x3 -> x2, blocking collectives: 95.6 us -> 53 us
    all_gather x0 -> x2, blocking collectives: none -> 38.1 us  [the longest x1 20.7 us: local(): lax.all_gather(projection_local, 'tensor', axis=1, tiled=True)]
    dot_general x3 -> x1, matrix products: 37.2 us -> 11.4 us  [local(): jnp.einsum('tf,df->td', projection_grad_own, projection_all, preferred_el...]
  transfers between devices with their start and end apart: 21 -> 21, of which waited for: 10 -> 9; matrix products, arithmetic and copies ran while one was open for 41% -> 41% of each run, Pallas kernels for 10% -> 10%
where the time goes in v5:
time: 2390 us; the launch traced here: 2380 us
  waiting for transfers between devices  889 us (37%)
  matrix products  700 us (29%)
  other arithmetic  300 us (13%)
  Pallas kernels  237 us (10%)
  blocking collectives  119 us (5%)
  local copies, waits for them, and re-layouts  97.8 us (4%)
    all_gather x1, waiting for transfers between devices, local(): lax.all_gather(normed_shard.astype(jnp.bfloat16), 'tensor', axis=0, tiled...  165 us
    all_gather x1, waiting for transfers between devices, local(): lax.all_gather(normed_two.astype(jnp.bfloat16), 'tensor', axis=0, tiled=T...  165 us
    reduce_scatter x1, waiting for transfers between devices, local(): lax.psum_scatter(mixture_grad_low, 'tensor', scatter_dimension=0, tiled=T...  152 us
    pallas_call x2, Pallas kernels, combine_rows(): pl.pallas_call(_combine_rows_kernel, grid_spec=pltpu.PrefetchScalarGridSp...  140 us
    all_gather x1, waiting for transfers between devices, local(): cotangent_full = lax.all_gather(out_grad_held, 'tensor', axis=0, tiled=True)  127 us
    convert_element_type x6, other arithmetic, local(): score_grad = (soft_full * (weight_grad - delta)).astype(jnp.bfloat16)  105 us
    pallas_call x2, Pallas kernels, gather_rows(): pl.pallas_call(_gather_rows_kernel, grid_spec=pltpu.PrefetchScalarGridSpe...  96.5 us
    reduce_scatter x1, waiting for transfers between devices, reduce_experts(): lax.psum_scatter(grads[1], 'dp', scatter_dimension=1, tiled=True)  95.3 us
  transfers between devices with their start and end apart: 21, of which 9 were waited for; matrix products, arithmetic and copies ran while one was open for 41% of the time, Pallas kernels for 10%

profile of v5, /device:TPU:0, one launch (start us, length us, event | category | flops | bytes accessed | tf_op | source)
XLA Modules:
  0.0 2376.3 jit_solution(10497486215047069058)
XLA Ops:
  10.8 16.0 all-reduce.7
  34.3 165.5 %all-gather.11.cloned.1.call-done = bf16[3072,1536]{1,0:T(8,128)(2,1)} async-done(((bf16[768,1536]{1,0:T(8,128)(2,1)}), bf16[3072,1536]{1,0:T(8,128)(2,1)}) %all-gather.11.cloned.1.call-update) | async-done | bytes 9437200 | tf_op jit(solution)/shard_map/all_gather | solution.py:337
  200.4 17.5 all_gather.55
  219.2 9.5 all_gather.51
  228.7 9.5 all_gather.50
  265.2 8.6 fusion.248
  277.2 14.6 fusion.245
  291.8 14.8 fusion.3
  306.6 14.7 fusion.157
  322.3 14.2 fusion.244
  336.5 12.6 fusion.8
  349.1 15.9 fusion.156
  380.2 11.0 fusion.155
  392.1 8.4 fusion.242
  400.5 8.9 fusion.22
  409.4 8.4 fusion.154
  443.2 54.7 %all-to-all-done = bf16[4,768,384]{2,1,0:T(8,128)(2,1)} async-done(((bf16[4,768,384]{2,1,0:T(8,128)(2,1)}), bf16[4,768,384]{2,1,0:T(8,128)(2,1)}, u32[]{:S(2)}, u32[]{:S(2)}) %all-to-all-start) | async-done | bytes 2359328 | tf_op jit(solution)/shard_map/all_to_all | solution.py:377
  513.4 165.4 %all-gather.21.cloned.1.call-done = bf16[3072,1536]{1,0:T(8,128)(2,1)} async-done(((bf16[768,1536]{1,0:T(8,128)(2,1)}), bf16[3072,1536]{1,0:T(8,128)(2,1)}) %all-gather.21.cloned.1.call-update) | async-done | bytes 9437200 | tf_op jit(solution)/shard_map/all_gather | solution.py:381
  678.9 9.2 all-gather
  689.7 14.6 fusion.101
  725.2 39.0 %all-gather.23.cloned.1.call-done = bf16[10,512,1536]{1,2,0:T(8,128)(2,1)} async-done(((bf16[10,512,192]{1,2,0:T(8,128)(2,1)}), bf16[10,512,1536]{1,2,0:T(8,128)(2,1)}) %all-gather.23.cloned.1.call-update) | async-done | bytes 15728656 | tf_op jit(solution)/shard_map/all_gather | solution.py:383
  785.3 12.8 convert_element_type.299.refs_0_
  805.4 127.2 %all-gather.25.cloned.1.call-done = bf16[3072,1536]{1,0:T(8,128)(2,1)} async-done(((bf16[768,1536]{1,0:T(8,128)(2,1)}), bf16[3072,1536]{1,0:T(8,128)(2,1)}) %all-gather.25.cloned.1.call-update) | async-done | bytes 9437200 | tf_op jit(solution)/shard_map/all_gather | solution.py:418
  932.6 20.7 all_gather.62
  955.6 51.9 %shard_map.248 = (bf16[7680,1536]{1,0:T(8,128)(2,1)}, f32[7680,128]{1,0:T(8,128)}) custom-call(s32[7680]{0:T(1024)} %get-tuple-element.418.tok_ref, f32[3072,1536]{1,0:T(8,128)} %convert_element_type.299.refs_0_, f32[3072,128]{1,0:T(8,128)} %pad.33.refs_1_), custom_call_target="tpu_custom_call" | custom-call | tf_op jit(solution)/shard_map/pallas_call | solution.py:156
  1013.7 27.6 %fusion.250 = f32[10,768,512]{1,2,0:T(8,128)} fusion(bf16[10,768,1536]{2,1,0:T(8,128)(2,1)} %bitcast.587, bf16[10,1536,512]{2,1,0:T(8,128)(2,1)} %all-gather.15.cloned.1.call-done), kind=kOutput, calls=%fused_computation.403 | convolution fusion | flops 12079595520 | bytes 55050240 | tf_op jit(solution)/shard_map/ecd,edf->ecf/dot_general | solution.py:409
  1041.3 32.7 %multiply_convert_fusion.3 = (bf16[10,768,512]{1,2,0:T(8,128)(2,1)}, f32[10,768,512]{1,2,0:T(8,128)}) fusion(f32[10,768]{1,0:T(8,128)S(1)} %broadcast_select_fusion, f32[10,768,512]{1,2,0:T(8,128)} %fusion.250, bf16[10,768,1536]{2,1,0:T(8,128)(2,1)} %bitcast.588, bf16[10,1536,512]{2,1,0:T(8,128)(2,1)} %all-gather.17.cloned.1.call-done), kind=kOutput, calls=%fused_computation.56 | convolution fusion | flops 12107120640 | bytes 78673920 | tf_op jit(solution)/shard_map/ecd,edf->ecf/dot_general | solution.py:410
  1074.0 27.2 %fusion.251 = f32[10,768,1536]{2,1,0:T(8,128)} fusion(bf16[10,768,512]{1,2,0:T(8,128)(2,1)} %get-tuple-element.239, bf16[10,512,1536]{1,2,0:T(8,128)(2,1)} %all-gather.23.cloned.1.call-done), kind=kOutput, calls=%fused_computation.404 | convolution fusion | flops 12079595520 | bytes 70778880 | tf_op jit(solution)/shard_map/ecf,efd->ecd/dot_general | solution.py:413
  1101.2 68.7 %shard_map.249 = f32[3072,1536]{1,0:T(8,128)} custom-call(s32[7680]{0:T(1024)} %get-tuple-element.418.tok_ref, f32[7680,1536]{1,0:T(8,128)} %bitcast.519), custom_call_target="tpu_custom_call" | custom-call | tf_op jit(solution)/shard_map/pallas_call | solution.py:211
  1169.9 13.0 fusion.40.refs_0_
  1182.9 11.3 convert_element_type.308
  1194.2 44.7 %shard_map.250 = bf16[7680,1536]{1,0:T(8,128)(2,1)} custom-call(s32[7680]{0:T(1024)} %get-tuple-element.418.tok_ref, f32[3072,1536]{1,0:T(8,128)} %fusion.40.refs_0_), custom_call_target="tpu_custom_call" | custom-call | tf_op jit(solution)/shard_map/pallas_call | solution.py:156
  1238.9 34.4 %multiply_reduce_fusion = (f32[10,768]{1,0:T(8,128)S(1)}, bf16[10,768,512]{1,2,0:T(8,128)(2,1)}, bf16[10,768,512]{1,2,0:T(8,128)(2,1)}) fusion(f32[10,768,512]{1,2,0:T(8,128)} %get-tuple-element.439, f32[10,768,512]{1,2,0:T(8,128)} %fusion.250, f32[10,768]{1,0:T(8,128)S(1)} %broadcast_select_fusion, bf16[10,768,1536]{2,1,0:T(8,128)(2,1)} %bitcast.523, ...), kind=kOutput, calls=%fused_computation.53 | convolution fusion | flops 12146434048 | bytes 86568960 | tf_op jit(solution)/shard_map/ecd,efd->ecf/dot_general | solution.py:434
  1281.1 27.3 %fusion.252 = f32[10,768,1536]{2,1,0:T(8,128)} fusion(bf16[10,768,512]{1,2,0:T(8,128)(2,1)} %get-tuple-element.236, bf16[10,1536,512]{2,1,0:T(8,128)(2,1)} %all-gather.15.cloned.1.call-done), kind=kOutput, calls=%fused_computation.405 | convolution fusion | flops 12079595520 | bytes 70778880 | tf_op jit(solution)/shard_map/ecf,edf->ecd/dot_general | solution.py:442
  1308.4 33.9 %add_convert_fusion = bf16[10,768,1536]{2,1,0:T(8,128)(2,1)} fusion(f32[10,768,1536]{2,1,0:T(8,128)} %fusion.252, bf16[10,768,512]{1,2,0:T(8,128)(2,1)} %get-tuple-element.237, bf16[10,1536,512]{2,1,0:T(8,128)(2,1)} %all-gather.17.cloned.1.call-done), kind=kOutput, calls=%fused_computation | convolution fusion | flops 12103188480 | bytes 94371840 | tf_op jit(solution)/shard_map/ecf,edf->ecd/dot_general | solution.py:444
  1342.3 71.7 %shard_map.251 = (f32[3072,1536]{1,0:T(8,128)}, f32[3072,128]{1,0:T(8,128)}) custom-call(s32[7680]{0:T(1024)} %get-tuple-element.418.tok_ref, bf16[7680,1536]{1,0:T(8,128)(2,1)} %bitcast.522, f32[7680,128]{1,0:T(8,128)} %fusion.81.refs_1_), custom_call_target="tpu_custom_call" | custom-call | tf_op jit(solution)/shard_map/pallas_call | solution.py:211
  1420.3 14.3 add_convert_fusion.1
  1446.7 151.9 %reduce-scatter.18.cloned.1.call-done = bf16[768,1536]{1,0:T(8,128)(2,1)} async-done(((bf16[3072,1536]{1,0:T(8,128)(2,1)}), bf16[768,1536]{1,0:T(8,128)(2,1)}) %reduce-scatter.18.cloned.1.call-update) | async-done | bytes 2359312 | tf_op jit(solution)/shard_map/reduce_scatter | solution.py:477
  1616.2 23.0 convolution_convert_fusion.1
  1639.2 8.2 convolution_convert_fusion.5
  1653.7 21.5 convolution_convert_fusion.2
  1675.2 21.5 convolution_convert_fusion
  1696.7 10.7 all-to-all-done.1
  1755.7 11.8 fusion.17
  1767.5 13.4 fusion.19
  1787.1 15.9 fusion.9
  1803.0 17.2 fusion.11
  1828.9 25.7 %fusion.4 = (f32[2,3,512]{2,1,0:T(4,128)S(1)}, f32[2,2560,512,3]{2,1,3,0:T(8,128)}) fusion(f32[2,3,512,2560]{2,3,1,0:T(8,128)} %get-tuple-element.433, f32[2,3,512]{2,1,0:T(4,128)S(1)} %log_add_fusion.1, bf16[2560,2,64,1]{0,2,3,1:T(8,128)(2,1)S(1)} %bitcast.557, bf16[512,2,3,64]{0,3,2,1:T(8,128)(2,1)S(1)} %bitcast.535), kind=kOutput, calls=%fused_computation.13 | convolution fusion | flops 1030222848 | bytes 63987712 | tf_op jit(solution)/shard_map/qgrd,kgd->grqk/dot_general | solution.py:521
  1854.6 28.1 %fusion.6 = bf16[2,3,512,2560]{2,3,1,0:T(8,128)(2,1)} fusion(f32[2,2560,512,3]{2,1,3,0:T(8,128)} %get-tuple-element.449, f32[2,3,512,2560]{2,3,1,0:T(8,128)} %get-tuple-element.433, f32[2,3,512]{2,1,0:T(4,128)S(1)} %get-tuple-element.448, f32[2,3,512]{2,1,0:T(4,128)S(1)} %log_add_fusion.1), kind=kLoop, calls=%fused_computation.15 | loop fusion | flops 31457280 | bytes 78667776 | tf_op jit(solution)/shard_map/convert_element_type | solution.py:525
  1882.7 9.5 fusion.151
  1892.2 28.1 %fusion = (f32[2,3,512]{2,1,0:T(4,128)S(1)}, f32[2,3072,512,3]{2,1,3,0:T(8,128)}) fusion(f32[2,3,512,3072]{2,3,1,0:T(8,128)} %get-tuple-element.435, f32[2,3,512]{2,1,0:T(4,128)S(1)} %copy-done.70, bf16[3072,2,64,1]{0,2,3,1:T(8,128)(2,1)S(1)} %bitcast.526, bf16[512,2,3,64]{0,3,2,1:T(8,128)(2,1)S(1)} %bitcast.533), kind=kOutput, calls=%fused_computation.3 | convolution fusion | flops 1236268032 | bytes 76701696 | tf_op jit(solution)/shard_map/qgrd,kgd->grqk/dot_general | solution.py:521
  1920.4 32.7 %fusion.2 = bf16[2,3,512,3072]{2,3,1,0:T(8,128)(2,1)} fusion(f32[2,3072,512,3]{2,1,3,0:T(8,128)} %get-tuple-element.451, f32[2,3,512,3072]{2,3,1,0:T(8,128)} %get-tuple-element.435, f32[2,3,512]{2,1,0:T(4,128)S(1)} %get-tuple-element.450, f32[2,3,512]{2,1,0:T(4,128)S(1)} %copy-done.70), kind=kLoop, calls=%fused_computation.5 | loop fusion | flops 37748736 | bytes 94396416 | tf_op jit(solution)/shard_map/convert_element_type | solution.py:525
  1953.1 15.5 fusion.141
  2005.2 8.5 fusion.120
  2013.7 10.5 fusion.87
  2024.1 11.7 fusion.137
  2035.8 13.2 fusion.98
  2065.7 95.3 %reduce-scatter.22.cloned.1.call-done = bf16[10,192,512]{2,1,0:T(8,128)(2,1)} async-done(((bf16[10,1536,512]{2,1,0:T(8,128)(2,1)}), bf16[10,192,512]{2,1,0:T(8,128)(2,1)}) %reduce-scatter.22.cloned.1.call-update) | async-done | bytes 1966096 | tf_op jit(solution)/shard_map/reduce_scatter | solution.py:291
  2165.0 13.5 fusion.88
  2182.7 15.1 fusion.105
  2198.4 8.2 pad_maximum_fusion
  2225.2 76.4 %all-to-all-done.2 = bf16[4,768,640]{1,2,0:T(8,128)(2,1)} async-done(((bf16[4,768,640]{1,2,0:T(8,128)(2,1)}), bf16[4,768,640]{1,2,0:T(8,128)(2,1)}, u32[]{:S(2)}, u32[]{:S(2)}) %all-to-all-start.2) | async-done | bytes 3932192 | tf_op jit(solution)/shard_map/all_to_all | solution.py:571
  2301.6 11.4 fusion.254
  2320.8 37.0 %all-reduce.6 = f32[1536]{0:T(1024)S(1)} all-reduce(f32[1536]{0:T(1024)S(1)} %get-tuple-element.376), channel_id=10, replica_groups=mesh['dp'=8,'tensor'=4] {'dp','tensor'}, use_global_device_ids=true, to_apply=%region_45.46.clone | all-reduce | flops 1536 | bytes 12288
  (521 shorter events, 370.7 us)
Async XLA Ops:
  7.2 192.6 %all-gather.11.cloned.1.call-start = ((), (), s32[]{:S(2)}) async-start(), calls=%async_computation.12 | async-start | bytes 11796480 | tf_op jit(solution)/shard_map/all_gather | solution.py:337
  26.9 173.5 %copy-start.90 = (bf16[384,192]{0,1:T(8,128)(2,1)S(1)}, bf16[384,192]{0,1:T(8,128)(2,1)}, u32[]{:S(2)}) copy-start(bf16[384,192]{0,1:T(8,128)(2,1)} %param.52) | copy-start | bytes 442372
  29.1 188.8 %copy-start.124 = (s32[1,1024]{1,0:T(1,128)S(1)}, s32[1,1024]{1,0:T(1,128)}, u32[]{:S(2)}) copy-start(s32[1,1024]{1,0:T(1,128)} %param.45) | copy-start | bytes 12292
  29.8 189.4 %copy-start.86 = (bf16[192,128]{1,0:T(8,128)(2,1)S(1)}, bf16[192,128]{1,0:T(8,128)(2,1)}, u32[]{:S(2)}) copy-start(bf16[192,128]{1,0:T(8,128)(2,1)} %param.50) | copy-start | bytes 147460
  29.8 199.0 %copy-start.84 = (bf16[192,128]{1,0:T(8,128)(2,1)S(1)}, bf16[192,128]{1,0:T(8,128)(2,1)}, u32[]{:S(2)}) copy-start(bf16[192,128]{1,0:T(8,128)(2,1)} %param.51) | copy-start | bytes 147460
  33.5 231.7 %all-gather.13.cloned.1.call-start = ((), (), s32[]{:S(2)}) async-start(), calls=%async_computation.13 | async-start | bytes 1327104 | tf_op jit(solution)/shard_map/all_gather | solution.py:324
  34.2 404.4 %all-gather.15.cloned.1.call-start = ((), (), s32[]{:S(2)}) async-start(), calls=%async_computation.14 | async-start | bytes 17694720 | tf_op jit(solution)/shard_map/all_gather | solution.py:341
  199.8 238.9 %all-gather.17.cloned.1.call-start = ((), (), s32[]{:S(2)}) async-start(), calls=%async_computation.15 | async-start | bytes 17694720 | tf_op jit(solution)/shard_map/all_gather | solution.py:342
  200.3 302.1 %all-gather.19.cloned.1.call-start = ((), (), s32[]{:S(2)}) async-start(), calls=%async_computation.16 | async-start | bytes 5308416 | tf_op jit(solution)/shard_map/all_gather | solution.py:330
  244.2 29.6 %copy-start.26 = (f32[3072,32]{0,1:T(8,128)}, f32[3072,32]{0,1:T(8,128)S(1)}, u32[]{:S(2)}) copy-start(f32[3072,32]{0,1:T(8,128)S(1)} %get-tuple-element.419) | copy-start | bytes 1179652
  244.2 29.6 %copy-start.28 = (f32[3072,32]{0,1:T(8,128)}, f32[3072,32]{0,1:T(8,128)S(1)}, u32[]{:S(2)}) copy-start(f32[3072,32]{0,1:T(8,128)S(1)} %get-tuple-element.420) | copy-start | bytes 1179652
  258.0 48.6 %copy-start.18 = (bf16[3072,128]{0,1:T(8,128)(2,1)}, bf16[3072,128]{0,1:T(8,128)(2,1)S(1)}, u32[]{:S(2)}) copy-start(bf16[3072,128]{0,1:T(8,128)(2,1)S(1)} %convolution_convert_fusion.4) | copy-start | bytes 2359300
  275.8 46.5 %copy-start.11 = (bf16[3072,2,32]{0,2,1:T(8,128)(2,1)}, bf16[3072,2,32]{0,2,1:T(8,128)(2,1)S(1)}, u32[]{:S(2)}) copy-start(bf16[3072,2,32]{0,2,1:T(8,128)(2,1)S(1)} %get-tuple-element.408) | copy-start | bytes 1179652
  275.8 152.8 %copy-start.9 = (bf16[3072,2,32]{0,2,1:T(8,128)(2,1)}, bf16[3072,2,32]{0,2,1:T(8,128)(2,1)S(1)}, u32[]{:S(2)}) copy-start(bf16[3072,2,32]{0,2,1:T(8,128)(2,1)S(1)} %get-tuple-element.407) | copy-start | bytes 1179652
  277.2 14.6 copy-start.38
  277.2 45.1 %copy-start.47 = (bf16[512,6,64]{0,2,1:T(8,128)(2,1)}, bf16[512,6,64]{0,2,1:T(8,128)(2,1)S(1)}, u32[]{:S(2)}) copy-start(bf16[512,6,64]{0,2,1:T(8,128)(2,1)S(1)} %get-tuple-element.406) | copy-start | bytes 1179652
  291.8 14.8 copy-start.102
  306.6 14.8 copy-start.104
  349.1 16.0 copy-start.108
  434.4 68.0 %copy-start.7 = (bf16[768,1536]{1,0:T(8,128)(2,1)S(1)}, bf16[768,1536]{1,0:T(8,128)(2,1)}, u32[]{:S(2)}) copy-start(bf16[768,1536]{1,0:T(8,128)(2,1)} %param.43) | copy-start | bytes 7077892
  438.7 59.3 %all-to-all-start = ((bf16[4,768,384]{2,1,0:T(8,128)(2,1)}), bf16[4,768,384]{2,1,0:T(8,128)(2,1)}, u32[]{:S(2)}, u32[]{:S(2)}) async-start(bf16[4,768,384]{2,1,0:T(8,128)(2,1)} %bitcast.60), calls=%async_computation | async-start | bytes 4718592 | tf_op jit(solution)/shard_map/all_to_all | solution.py:377
  443.2 235.6 %all-gather.21.cloned.1.call-start = ((), (), s32[]{:S(2)}) async-start(), calls=%async_computation.17 | async-start | bytes 11796480 | tf_op jit(solution)/shard_map/all_gather | solution.py:381
  443.2 66.1 %copy-start.97 = (f32[1536]{0:T(1024)}, f32[1536]{0:T(1024)S(1)}, u32[]{:S(2)}) copy-start(f32[1536]{0:T(1024)S(1)} %convert_element_type.297) | copy-start | bytes 18436
  509.3 169.6 %copy-start.125 = (bf16[192,40]{0,1:T(8,128)(2,1)S(1)}, bf16[192,40]{0,1:T(8,128)(2,1)}, u32[]{:S(2)}) copy-start(bf16[192,40]{0,1:T(8,128)(2,1)} %param.54) | copy-start | bytes 46084
  509.3 179.0 %copy-start.68 = (s32[3072,8]{0,1:T(8,128)S(1)}, s32[3072,8]{0,1:T(8,128)}, u32[]{:S(2)}) copy-start(s32[3072,8]{0,1:T(8,128)} %param.46) | copy-start | bytes 294916
  509.4 179.4 %copy-start.100 = (f32[768]{0:T(1024)}, f32[768]{0:T(1024)S(1)}, u32[]{:S(2)}) copy-start(f32[768]{0:T(1024)S(1)} %add_rsqrt_fusion) | copy-start | bytes 9220
  511.5 178.0 %copy-start.99 = (s32[1,24576]{1,0:T(1,128)S(1)}, s32[1,24576]{1,0:T(1,128)}, u32[]{:S(2)}) copy-start(s32[1,24576]{1,0:T(1,128)} %param.47) | copy-start | bytes 294916
  513.4 250.8 %all-gather.23.cloned.1.call-start = ((), (), s32[]{:S(2)}) async-start(), calls=%async_computation.18 | async-start | bytes 17694720 | tf_op jit(solution)/shard_map/all_gather | solution.py:383
  678.8 253.7 %all-gather.25.cloned.1.call-start = ((), (), s32[]{:S(2)}) async-start(), calls=%async_computation.19 | async-start | bytes 11796480 | tf_op jit(solution)/shard_map/all_gather | solution.py:418
  688.3 109.8 %copy-start.64 = (bf16[1536,40]{0,1:T(8,128)(2,1)}, bf16[1536,40]{0,1:T(8,128)(2,1)S(1)}, u32[]{:S(2)}) copy-start(bf16[1536,40]{0,1:T(8,128)(2,1)S(1)} %reshape.1188) | copy-start | bytes 368644
  764.3 656.0 %all-gather.27.cloned.1.call-start = ((), (), s32[]{:S(2)}) async-start(), calls=%async_computation.20 | async-start | bytes 8847360 | tf_op jit(solution)/shard_map/all_gather | solution.py:422
  785.2 222.3 %copy-start.93 = (s32[7680]{0:T(1024)}, s32[7680]{0:T(1024)S(1)}, u32[]{:S(2)}) copy-start(s32[7680]{0:T(1024)S(1)} %get-tuple-element.417) | copy-start | bytes 92164
  953.3 481.3 %reduce-scatter.16.cloned.1.call-start = ((), (), s32[]{:S(2)}) async-start(), calls=%async_computation.21 | async-start | bytes 11796480 | tf_op jit(solution)/shard_map/reduce_scatter | solution.py:429
  953.4 54.1 %copy-start.82 = (f32[3072]{0:T(1024)}, f32[3072]{0:T(1024)S(1)}, u32[]{:S(2)}) copy-start(f32[3072]{0:T(1024)S(1)} %get-tuple-element.382) | copy-start | bytes 36868
  953.9 53.6 %copy-start.16 = (f32[3072,8]{1,0:T(8,128)}, f32[3072,8]{1,0:T(8,128)S(1)}, u32[]{:S(2)}) copy-start(f32[3072,8]{1,0:T(8,128)S(1)} %copy.585) | copy-start | bytes 294916
  1194.2 404.4 %reduce-scatter.18.cloned.1.call-start = ((), (), s32[]{:S(2)}) async-start(), calls=%async_computation.22 | async-start | bytes 11796480 | tf_op jit(solution)/shard_map/reduce_scatter | solution.py:477
  1238.9 34.4 %copy-start.94 = (s32[7680]{0:T(1024)S(1)}, s32[7680]{0:T(1024)}, u32[]{:S(2)}) copy-start(s32[7680]{0:T(1024)} %copy-done.93) | copy-start | bytes 92164
  1342.3 71.8 %copy-start.17 = (f32[3072,8]{1,0:T(8,128)S(1)}, f32[3072,8]{1,0:T(8,128)}, u32[]{:S(2)}) copy-start(f32[3072,8]{1,0:T(8,128)} %copy-done.16) | copy-start | bytes 294916
  1342.3 71.8 %copy-start.83 = (f32[3072]{0:T(1024)S(1)}, f32[3072]{0:T(1024)}, u32[]{:S(2)}) copy-start(f32[3072]{0:T(1024)} %copy-done.82) | copy-start | bytes 36868
  1439.1 159.5 %copy-start.98 = (f32[1536]{0:T(1024)S(1)}, f32[1536]{0:T(1024)}, u32[]{:S(2)}) copy-start(f32[1536]{0:T(1024)} %copy-done.97) | copy-start | bytes 18436
  1439.1 159.5 %copy-start.101 = (f32[768]{0:T(1024)S(1)}, f32[768]{0:T(1024)}, u32[]{:S(2)}) copy-start(f32[768]{0:T(1024)} %copy-done.100) | copy-start | bytes 9220
  1439.1 269.6 %reduce-scatter.26.cloned.1.call-start = ((), (), s32[]{:S(2)}) async-start(), calls=%async_computation.26 | async-start | bytes 5308416 | tf_op jit(solution)/shard_map/reduce_scatter | solution.py:504
  1446.7 156.5 %copy-start.30 = (bf16[768,1536]{1,0:T(8,128)(2,1)S(1)}, bf16[768,1536]{1,0:T(8,128)(2,1)}, u32[]{:S(2)}) copy-start(bf16[768,1536]{1,0:T(8,128)(2,1)} %param.44) | copy-start | bytes 7077892
  1649.1 58.4 %all-to-all-start.1 = ((bf16[768,4,384]{2,0,1:T(8,128)(2,1)}), bf16[768,4,384]{2,0,1:T(8,128)(2,1)S(1)}, u32[]{:S(2)}, u32[]{:S(2)}) async-start(bf16[768,4,384]{2,0,1:T(8,128)(2,1)} %bitcast.532), calls=%async_computation.3 | async-start | bytes 4718592 | tf_op jit(solution)/shard_map/all_to_all | solution.py:488
  1653.7 395.4 %reduce-scatter.28.cloned.1.call-start = ((), (), s32[]{:S(2)}) async-start(), calls=%async_computation.27 | async-start | bytes 811008
  1708.7 344.5 %reduce-scatter.30.cloned.1.call-start = ((), (), s32[]{:S(2)}) async-start(), calls=%async_computation.28 | async-start | bytes 983040
  1711.0 345.6 %reduce-scatter.20.cloned.1.call-start = ((), (), s32[]{:S(2)}) async-start(), calls=%async_computation.23 | async-start | bytes 17694720 | tf_op jit(solution)/shard_map/reduce_scatter | solution.py:290
  1711.7 348.9 %reduce-scatter.24.cloned.1.call-start = ((), (), s32[]{:S(2)}) async-start(), calls=%async_computation.25 | async-start | bytes 17694720 | tf_op jit(solution)/shard_map/reduce_scatter | solution.py:293
  1712.3 448.7 %reduce-scatter.22.cloned.1.call-start = ((), (), s32[]{:S(2)}) async-start(), calls=%async_computation.24 | async-start | bytes 17694720 | tf_op jit(solution)/shard_map/reduce_scatter | solution.py:291
  1718.0 20.0 copy-start.49
  1720.6 35.1 %copy-start.40 = (bf16[512,384]{0,1:T(8,128)(2,1)}, bf16[512,384]{0,1:T(8,128)(2,1)S(1)}, u32[]{:S(2)}) copy-start(bf16[512,384]{0,1:T(8,128)(2,1)S(1)} %copy.604) | copy-start | bytes 1179652
  1722.0 65.1 %copy-start.39 = (bf16[512,384]{0,1:T(8,128)(2,1)}, bf16[512,384]{0,1:T(8,128)(2,1)S(1)}, u32[]{:S(2)}) copy-start(bf16[512,384]{0,1:T(8,128)(2,1)S(1)} %copy.606) | copy-start | bytes 1179652
  1722.2 105.7 %copy-start.35 = (bf16[512,384]{0,1:T(8,128)(2,1)}, bf16[512,384]{0,1:T(8,128)(2,1)S(1)}, u32[]{:S(2)}) copy-start(bf16[512,384]{0,1:T(8,128)(2,1)S(1)} %copy.608) | copy-start | bytes 1179652
  1722.4 169.9 %copy-start.33 = (bf16[512,384]{0,1:T(8,128)(2,1)}, bf16[512,384]{0,1:T(8,128)(2,1)S(1)}, u32[]{:S(2)}) copy-start(bf16[512,384]{0,1:T(8,128)(2,1)S(1)} %copy.610) | copy-start | bytes 1179652
  1722.4 15.6 slice-start.6
  1722.4 15.5 slice-start.7
  1953.1 15.5 copy-start.27
  1953.1 15.5 copy-start.29
  1985.8 14.4 slice-start.9
  1985.8 14.4 slice-start.10
  2209.0 92.6 %all-to-all-start.2 = ((bf16[4,768,640]{1,2,0:T(8,128)(2,1)}), bf16[4,768,640]{1,2,0:T(8,128)(2,1)}, u32[]{:S(2)}, u32[]{:S(2)}) async-start(bf16[4,768,640]{1,2,0:T(8,128)(2,1)} %copy.624), calls=%async_computation.8 | async-start | bytes 7864320 | tf_op jit(solution)/shard_map/all_to_all | solution.py:571
  2213.9 151.5 %reduce-scatter.32.cloned.1.call-start = ((), (), s32[]{:S(2)}) async-start(), calls=%async_computation.29 | async-start | bytes 2211840
  2301.6 15.6 copy-start.96
  2301.6 15.6 copy-start.123
  (96 other events, 553.6 us)
Sparse Core Ops, SparseCore 0:
  33.6 166.1 all-gather.10
  201.6 22.0 all-gather.12
  225.7 86.2 all-gather.14
  313.7 85.2 all-gather.16
  400.7 38.7 all-gather.18
  513.5 165.2 all-gather.20
  680.7 83.4 all-gather.22
  765.8 166.7 all-gather.24
  953.4 51.3 all-gather.26
  1194.3 159.9 reduce-scatter.15
  1439.2 159.3 reduce-scatter.17
  1616.3 54.7 reduce-scatter.25
  1708.8 95.2 reduce-scatter.27
  1806.9 22.2 reduce-scatter.29
  1832.5 106.8 reduce-scatter.19
  1942.8 107.4 reduce-scatter.23
  2053.6 107.3 reduce-scatter.21
  2317.3 38.3 reduce-scatter.31

commit v6 on v5

--- a/solution.py
+++ b/solution.py
@@ -416,16 +416,19 @@
     (mixture_sum,) = combine_rows(slot_token, (expert_out.reshape(slot_count, D),), CAP, TOK_GRP)
     out_grad_held, down_full = lax.optimization_barrier((out_grad, down_full))
     cotangent_full = lax.all_gather(out_grad_held, "tensor", axis=0, tiled=True)
-    projection_local, cotangent_full = lax.optimization_barrier(
-        (jnp.concatenate([query_weight, key_weight, value_weight], axis=1), cotangent_full)
+    scaled_cotangent = (
+        (RESIDUAL_SCALE * cotangent_full.astype(jnp.float32)).astype(jnp.bfloat16).astype(jnp.float32)
+    )
+    scaled_cotangent, mixture_sum, projection_local = lax.optimization_barrier(
+        (
+            scaled_cotangent,
+            mixture_sum,
+            jnp.concatenate([query_weight, key_weight, value_weight], axis=1),
+        )
     )
     projection_all = lax.all_gather(
         lax.all_gather(projection_local, "tensor", axis=1, tiled=True), "dp", axis=0, tiled=True
     )
-    scaled_cotangent = (
-        (RESIDUAL_SCALE * cotangent_full.astype(jnp.float32)).astype(jnp.bfloat16).astype(jnp.float32)
-    )
-    scaled_cotangent, mixture_sum = lax.optimization_barrier((scaled_cotangent, mixture_sum))
     mixture_part = lax.psum_scatter(
         mixture_sum.astype(jnp.bfloat16), "tensor", scatter_dimension=0, tiled=True
     ).astype(jnp.float32)
@@ -536,7 +539,7 @@
         value_grad = value_grad.at[:key_end].add(
             jnp.einsum("grqk,qgrd->kgd", soft_low, out_block, preferred_element_type=jnp.float32)
         )
-        if block_index == block_count - 2:
+        if block_index == block_count - 1:
             (
                 key_grad,
                 value_grad,

time: 2390 us -> 2230 us (0.933)
  waiting for transfers between devices: 889 us -> 735 us
    all_gather x1, waiting for transfers between devices: 127 us -> 0.02 us  [local(): cotangent_full = lax.all_gather(out_grad_held, 'tensor', axis=0, tiled=True)]
    reduce_scatter x1, waiting for transfers between devices: 95.3 us -> 64.9 us  [reduce_experts(): lax.psum_scatter(grads[1], 'dp', scatter_dimension=1, tiled=True)]
    unnamed x300 -> x304, local copies, waits for them, and re-layouts: 51.8 us -> 47.3 us
  transfers between devices with their start and end apart: 21 -> 21, of which waited for: 9 -> 8; matrix products, arithmetic and copies ran while one was open for 41% -> 44% of each run, Pallas kernels for 10% -> 10%
where the time goes in v6:
time: 2230 us
  waiting for transfers between devices  735 us (33%)
  matrix products  713 us (32%)
  other arithmetic  297 us (13%)
  Pallas kernels  233 us (10%)
  blocking collectives  122 us (5%)
  local copies, waits for them, and re-layouts  92.2 us (4%)
    all_gather x1, waiting for transfers between devices, local(): lax.all_gather(normed_shard.astype(jnp.bfloat16), 'tensor', axis=0, tiled...  165 us
    all_gather x1, waiting for transfers between devices, local(): lax.all_gather(normed_two.astype(jnp.bfloat16), 'tensor', axis=0, tiled=T...  165 us
    reduce_scatter x1, waiting for transfers between devices, local(): lax.psum_scatter(mixture_grad_low, 'tensor', scatter_dimension=0, tiled=T...  153 us
    pallas_call x2, Pallas kernels, combine_rows(): pl.pallas_call(_combine_rows_kernel, grid_spec=pltpu.PrefetchScalarGridSp...  139 us
    convert_element_type x6, other arithmetic, local(): score_grad = (soft_full * (weight_grad - delta)).astype(jnp.bfloat16)  104 us
    dot_general x6, matrix products, local(): jnp.einsum('qgrd,kgd->grqk', out_block, value_low[:key_end], preferred_el...  95.8 us
    pallas_call x2, Pallas kernels, gather_rows(): pl.pallas_call(_gather_rows_kernel, grid_spec=pltpu.PrefetchScalarGridSpe...  94.4 us
    all_to_all x1, waiting for transfers between devices, local(): lax.all_to_all(projection_grad, 'tensor', 0, 1, tiled=True)  74.7 us
  transfers between devices with their start and end apart: 21, of which 8 were waited for; matrix products, arithmetic and copies ran while one was open for 44% of the time, Pallas kernels for 10%

profile of v6, /device:TPU:0, one launch (start us, length us, event | category | flops | bytes accessed | tf_op | source)
XLA Modules:
  0.0 2225.1 jit_solution(9027857403595833616)
XLA Ops:
  10.8 16.0 all-reduce.7
  34.3 165.5 %all-gather.11.cloned.1.call-done = bf16[3072,1536]{1,0:T(8,128)(2,1)} async-done(((bf16[768,1536]{1,0:T(8,128)(2,1)}), bf16[3072,1536]{1,0:T(8,128)(2,1)}) %all-gather.11.cloned.1.call-update) | async-done | bytes 9437200 | tf_op jit(solution)/shard_map/all_gather | solution.py:337
  200.4 17.5 all_gather.55
  219.2 9.5 all_gather.51
  228.7 9.5 all_gather.50
  265.3 8.6 fusion.245
  277.3 14.6 fusion.242
  291.9 14.8 fusion.3
  306.7 14.9 fusion.154
  322.6 14.1 fusion.241
  336.8 12.6 fusion.8
  349.4 15.7 fusion.153
  380.2 11.0 fusion.152
  392.1 8.3 fusion.239
  400.4 8.9 fusion.22
  409.4 8.4 fusion.151
  443.2 54.8 %all-to-all-done = bf16[4,768,384]{2,1,0:T(8,128)(2,1)} async-done(((bf16[4,768,384]{2,1,0:T(8,128)(2,1)}), bf16[4,768,384]{2,1,0:T(8,128)(2,1)}, u32[]{:S(2)}, u32[]{:S(2)}) %all-to-all-start) | async-done | bytes 2359328 | tf_op jit(solution)/shard_map/all_to_all | solution.py:377
  513.6 165.3 %all-gather.21.cloned.1.call-done = bf16[3072,1536]{1,0:T(8,128)(2,1)} async-done(((bf16[768,1536]{1,0:T(8,128)(2,1)}), bf16[3072,1536]{1,0:T(8,128)(2,1)}) %all-gather.21.cloned.1.call-update) | async-done | bytes 9437200 | tf_op jit(solution)/shard_map/all_gather | solution.py:381
  681.1 14.5 fusion.101
  720.9 43.5 %all-gather.23.cloned.1.call-done = bf16[10,512,1536]{1,2,0:T(8,128)(2,1)} async-done(((bf16[10,512,192]{1,2,0:T(8,128)(2,1)}), bf16[10,512,1536]{1,2,0:T(8,128)(2,1)}) %all-gather.23.cloned.1.call-update) | async-done | bytes 15728656 | tf_op jit(solution)/shard_map/all_gather | solution.py:383
  765.3 9.4 all-gather
  790.7 12.7 convert_element_type.299.refs_0_
  812.9 50.7 %shard_map.248 = (bf16[7680,1536]{1,0:T(8,128)(2,1)}, f32[7680,128]{1,0:T(8,128)}) custom-call(s32[7680]{0:T(1024)} %get-tuple-element.416.tok_ref, f32[3072,1536]{1,0:T(8,128)} %convert_element_type.299.refs_0_, f32[3072,128]{1,0:T(8,128)} %pad.33.refs_1_), custom_call_target="tpu_custom_call" | custom-call | tf_op jit(solution)/shard_map/pallas_call | solution.py:156
  869.8 27.8 %fusion.247 = f32[10,768,512]{1,2,0:T(8,128)} fusion(bf16[10,768,1536]{2,1,0:T(8,128)(2,1)} %bitcast.586, bf16[10,1536,512]{2,1,0:T(8,128)(2,1)} %all-gather.15.cloned.1.call-done), kind=kOutput, calls=%fused_computation.402 | convolution fusion | flops 12079595520 | bytes 55050240 | tf_op jit(solution)/shard_map/ecd,edf->ecf/dot_general | solution.py:409
  897.6 32.8 %multiply_convert_fusion.3 = (bf16[10,768,512]{1,2,0:T(8,128)(2,1)}, f32[10,768,512]{1,2,0:T(8,128)}) fusion(f32[10,768]{1,0:T(8,128)S(1)} %broadcast_select_fusion, f32[10,768,512]{1,2,0:T(8,128)} %fusion.247, bf16[10,768,1536]{2,1,0:T(8,128)(2,1)} %bitcast.587, bf16[10,1536,512]{2,1,0:T(8,128)(2,1)} %all-gather.17.cloned.1.call-done), kind=kOutput, calls=%fused_computation.56 | convolution fusion | flops 12107120640 | bytes 78673920 | tf_op jit(solution)/shard_map/ecd,edf->ecf/dot_general | solution.py:410
  930.4 27.3 %fusion.248 = f32[10,768,1536]{2,1,0:T(8,128)} fusion(bf16[10,768,512]{1,2,0:T(8,128)(2,1)} %get-tuple-element.237, bf16[10,512,1536]{1,2,0:T(8,128)(2,1)} %all-gather.23.cloned.1.call-done), kind=kOutput, calls=%fused_computation.403 | convolution fusion | flops 12079595520 | bytes 70778880 | tf_op jit(solution)/shard_map/ecf,efd->ecd/dot_general | solution.py:413
  957.7 67.9 %shard_map.249 = f32[3072,1536]{1,0:T(8,128)} custom-call(s32[7680]{0:T(1024)} %get-tuple-element.416.tok_ref, f32[7680,1536]{1,0:T(8,128)} %bitcast.517), custom_call_target="tpu_custom_call" | custom-call | tf_op jit(solution)/shard_map/pallas_call | solution.py:211
  1025.6 13.0 fusion.40.refs_0_
  1038.6 23.3 %all_gather.62 = bf16[192,2560]{1,0:T(8,128)(2,1)} all-gather(bf16[192,640]{1,0:T(8,128)(2,1)S(1)} %pad_maximum_fusion.5), channel_id=1, replica_groups=mesh['dp'=8,'tensor'=4] {'tensor'}, dimensions={1}, use_global_device_ids=true | all-gather | bytes 1228800 | tf_op jit(solution)/shard_map/all_gather | solution.py:430
  1062.0 11.6 convert_element_type.308
  1073.7 43.8 %shard_map.250 = bf16[7680,1536]{1,0:T(8,128)(2,1)} custom-call(s32[7680]{0:T(1024)} %get-tuple-element.416.tok_ref, f32[3072,1536]{1,0:T(8,128)} %fusion.40.refs_0_), custom_call_target="tpu_custom_call" | custom-call | tf_op jit(solution)/shard_map/pallas_call | solution.py:156
  1117.5 35.0 %multiply_reduce_fusion = (f32[10,768]{1,0:T(8,128)S(1)}, bf16[10,768,512]{1,2,0:T(8,128)(2,1)}, bf16[10,768,512]{1,2,0:T(8,128)(2,1)}) fusion(f32[10,768,512]{1,2,0:T(8,128)} %get-tuple-element.437, f32[10,768,512]{1,2,0:T(8,128)} %fusion.247, f32[10,768]{1,0:T(8,128)S(1)} %broadcast_select_fusion, bf16[10,768,1536]{2,1,0:T(8,128)(2,1)} %bitcast.521, ...), kind=kOutput, calls=%fused_computation.53 | convolution fusion | flops 12146434048 | bytes 86568960 | tf_op jit(solution)/shard_map/ecd,efd->ecf/dot_general | solution.py:437
  1160.4 27.3 %fusion.249 = f32[10,768,1536]{2,1,0:T(8,128)} fusion(bf16[10,768,512]{1,2,0:T(8,128)(2,1)} %get-tuple-element.234, bf16[10,1536,512]{2,1,0:T(8,128)(2,1)} %all-gather.15.cloned.1.call-done), kind=kOutput, calls=%fused_computation.404 | convolution fusion | flops 12079595520 | bytes 70778880 | tf_op jit(solution)/shard_map/ecf,edf->ecd/dot_general | solution.py:445
  1187.7 34.2 %add_convert_fusion = bf16[10,768,1536]{2,1,0:T(8,128)(2,1)} fusion(f32[10,768,1536]{2,1,0:T(8,128)} %fusion.249, bf16[10,768,512]{1,2,0:T(8,128)(2,1)} %get-tuple-element.235, bf16[10,1536,512]{2,1,0:T(8,128)(2,1)} %all-gather.17.cloned.1.call-done), kind=kOutput, calls=%fused_computation | convolution fusion | flops 12103188480 | bytes 94371840 | tf_op jit(solution)/shard_map/ecf,edf->ecd/dot_general | solution.py:447
  1221.9 71.1 %shard_map.251 = (f32[3072,1536]{1,0:T(8,128)}, f32[3072,128]{1,0:T(8,128)}) custom-call(s32[7680]{0:T(1024)} %get-tuple-element.416.tok_ref, bf16[7680,1536]{1,0:T(8,128)(2,1)} %bitcast.520, f32[7680,128]{1,0:T(8,128)} %fusion.81.refs_1_), custom_call_target="tpu_custom_call" | custom-call | tf_op jit(solution)/shard_map/pallas_call | solution.py:211
  1299.2 14.3 add_convert_fusion.1
  1325.8 152.9 %reduce-scatter.18.cloned.1.call-done = bf16[768,1536]{1,0:T(8,128)(2,1)} async-done(((bf16[3072,1536]{1,0:T(8,128)(2,1)}), bf16[768,1536]{1,0:T(8,128)(2,1)}) %reduce-scatter.18.cloned.1.call-update) | async-done | bytes 2359312 | tf_op jit(solution)/shard_map/reduce_scatter | solution.py:480
  1496.3 22.8 %convolution_convert_fusion.1 = bf16[10,1536,512]{2,1,0:T(8,128)(2,1)} fusion(bf16[10,768,1536]{2,1,0:T(8,128)(2,1)} %bitcast.588, bf16[10,768,512]{1,2,0:T(8,128)(2,1)} %get-tuple-element.235), kind=kOutput, calls=%fused_computation.62 | convolution fusion | flops 12087459840 | bytes 47185920 | tf_op jit(solution)/shard_map/ecd,ecf->edf/dot_general | solution.py:463
  1519.2 8.3 convolution_convert_fusion.5
  1533.5 21.5 convolution_convert_fusion.2
  1555.0 21.4 convolution_convert_fusion
  1576.4 10.9 all-to-all-done.1
  1635.6 11.9 fusion.17
  1647.4 13.4 fusion.19
  1667.2 15.8 fusion.9
  1682.9 17.4 fusion.11
  1705.2 26.8 %fusion.4 = (f32[2,3,512]{2,1,0:T(4,128)S(1)}, f32[2,2560,512,3]{2,1,3,0:T(8,128)}) fusion(f32[2,3,512,2560]{2,3,1,0:T(8,128)} %get-tuple-element.431, f32[2,3,512]{2,1,0:T(4,128)S(1)} %log_add_fusion.1, bf16[2560,2,64,1]{0,2,3,1:T(8,128)(2,1)S(1)} %bitcast.556, bf16[512,2,3,64]{0,3,2,1:T(8,128)(2,1)S(1)} %bitcast.533), kind=kOutput, calls=%fused_computation.13 | convolution fusion | flops 1030222848 | bytes 63987712 | tf_op jit(solution)/shard_map/qgrd,kgd->grqk/dot_general | solution.py:524
  1732.1 28.5 %fusion.6 = bf16[2,3,512,2560]{2,3,1,0:T(8,128)(2,1)} fusion(f32[2,2560,512,3]{2,1,3,0:T(8,128)} %get-tuple-element.447, f32[2,3,512,2560]{2,3,1,0:T(8,128)} %get-tuple-element.431, f32[2,3,512]{2,1,0:T(4,128)S(1)} %get-tuple-element.446, f32[2,3,512]{2,1,0:T(4,128)S(1)} %log_add_fusion.1), kind=kLoop, calls=%fused_computation.15 | loop fusion | flops 31457280 | bytes 78667776 | tf_op jit(solution)/shard_map/convert_element_type | solution.py:528
  1760.6 9.8 fusion.148
  1770.4 28.4 %fusion = (f32[2,3,512]{2,1,0:T(4,128)S(1)}, f32[2,3072,512,3]{2,1,3,0:T(8,128)}) fusion(f32[2,3,512,3072]{2,3,1,0:T(8,128)} %get-tuple-element.433, f32[2,3,512]{2,1,0:T(4,128)S(1)} %copy-done.71, bf16[3072,2,64,1]{0,2,3,1:T(8,128)(2,1)S(1)} %bitcast.524, bf16[512,2,3,64]{0,3,2,1:T(8,128)(2,1)S(1)} %bitcast.531), kind=kOutput, calls=%fused_computation.3 | convolution fusion | flops 1236268032 | bytes 76701696 | tf_op jit(solution)/shard_map/qgrd,kgd->grqk/dot_general | solution.py:524
  1798.8 31.4 %fusion.2 = bf16[2,3,512,3072]{2,3,1,0:T(8,128)(2,1)} fusion(f32[2,3072,512,3]{2,1,3,0:T(8,128)} %get-tuple-element.449, f32[2,3,512,3072]{2,3,1,0:T(8,128)} %get-tuple-element.433, f32[2,3,512]{2,1,0:T(4,128)S(1)} %get-tuple-element.448, f32[2,3,512]{2,1,0:T(4,128)S(1)} %copy-done.71), kind=kLoop, calls=%fused_computation.5 | loop fusion | flops 37748736 | bytes 94396416 | tf_op jit(solution)/shard_map/convert_element_type | solution.py:528
  1830.2 16.2 fusion.138
  1883.8 8.5 fusion.117
  1892.3 10.5 fusion.87
  1902.8 14.7 fusion.88
  1917.5 10.8 fusion.134
  1928.3 12.7 fusion.98
  1941.1 21.9 fusion.102
  1975.9 64.9 %reduce-scatter.22.cloned.1.call-done = bf16[10,192,512]{2,1,0:T(8,128)(2,1)} async-done(((bf16[10,1536,512]{2,1,0:T(8,128)(2,1)}), bf16[10,192,512]{2,1,0:T(8,128)(2,1)}) %reduce-scatter.22.cloned.1.call-update) | async-done | bytes 1966096 | tf_op jit(solution)/shard_map/reduce_scatter | solution.py:291
  2046.2 9.3 pad_maximum_fusion
  2063.2 8.4 convolution_convert_fusion.6
  2075.9 74.7 %all-to-all-done.2 = bf16[4,768,640]{1,2,0:T(8,128)(2,1)} async-done(((bf16[4,768,640]{1,2,0:T(8,128)(2,1)}), bf16[4,768,640]{1,2,0:T(8,128)(2,1)}, u32[]{:S(2)}, u32[]{:S(2)}) %all-to-all-start.2) | async-done | bytes 3932192 | tf_op jit(solution)/shard_map/all_to_all | solution.py:574
  2150.6 11.4 fusion.251
  2169.8 37.0 %all-reduce.6 = f32[1536]{0:T(1024)S(1)} all-reduce(f32[1536]{0:T(1024)S(1)} %get-tuple-element.374), channel_id=10, replica_groups=mesh['dp'=8,'tensor'=4] {'dp','tensor'}, use_global_device_ids=true, to_apply=%region_45.46.clone | all-reduce | flops 1536 | bytes 12288
  (525 shorter events, 354.9 us)
Async XLA Ops:
  7.2 192.6 %all-gather.11.cloned.1.call-start = ((), (), s32[]{:S(2)}) async-start(), calls=%async_computation.12 | async-start | bytes 11796480 | tf_op jit(solution)/shard_map/all_gather | solution.py:337
  26.9 173.5 %copy-start.90 = (bf16[384,192]{0,1:T(8,128)(2,1)S(1)}, bf16[384,192]{0,1:T(8,128)(2,1)}, u32[]{:S(2)}) copy-start(bf16[384,192]{0,1:T(8,128)(2,1)} %param.52) | copy-start | bytes 442372
  29.1 188.8 %copy-start.126 = (s32[1,1024]{1,0:T(1,128)S(1)}, s32[1,1024]{1,0:T(1,128)}, u32[]{:S(2)}) copy-start(s32[1,1024]{1,0:T(1,128)} %param.45) | copy-start | bytes 12292
  29.7 189.4 %copy-start.86 = (bf16[192,128]{1,0:T(8,128)(2,1)S(1)}, bf16[192,128]{1,0:T(8,128)(2,1)}, u32[]{:S(2)}) copy-start(bf16[192,128]{1,0:T(8,128)(2,1)} %param.50) | copy-start | bytes 147460
  29.7 199.0 %copy-start.84 = (bf16[192,128]{1,0:T(8,128)(2,1)S(1)}, bf16[192,128]{1,0:T(8,128)(2,1)}, u32[]{:S(2)}) copy-start(bf16[192,128]{1,0:T(8,128)(2,1)} %param.51) | copy-start | bytes 147460
  33.5 231.8 %all-gather.13.cloned.1.call-start = ((), (), s32[]{:S(2)}) async-start(), calls=%async_computation.13 | async-start | bytes 1327104 | tf_op jit(solution)/shard_map/all_gather | solution.py:324
  34.2 404.4 %all-gather.15.cloned.1.call-start = ((), (), s32[]{:S(2)}) async-start(), calls=%async_computation.14 | async-start | bytes 17694720 | tf_op jit(solution)/shard_map/all_gather | solution.py:341
  199.8 238.8 %all-gather.17.cloned.1.call-start = ((), (), s32[]{:S(2)}) async-start(), calls=%async_computation.15 | async-start | bytes 17694720 | tf_op jit(solution)/shard_map/all_gather | solution.py:342
  200.3 302.3 %all-gather.19.cloned.1.call-start = ((), (), s32[]{:S(2)}) async-start(), calls=%async_computation.16 | async-start | bytes 5308416 | tf_op jit(solution)/shard_map/all_gather | solution.py:330
  244.2 29.7 %copy-start.25 = (f32[3072,32]{0,1:T(8,128)}, f32[3072,32]{0,1:T(8,128)S(1)}, u32[]{:S(2)}) copy-start(f32[3072,32]{0,1:T(8,128)S(1)} %get-tuple-element.417) | copy-start | bytes 1179652
  244.2 29.7 %copy-start.27 = (f32[3072,32]{0,1:T(8,128)}, f32[3072,32]{0,1:T(8,128)S(1)}, u32[]{:S(2)}) copy-start(f32[3072,32]{0,1:T(8,128)S(1)} %get-tuple-element.418) | copy-start | bytes 1179652
  258.0 48.7 %copy-start.18 = (bf16[3072,128]{0,1:T(8,128)(2,1)}, bf16[3072,128]{0,1:T(8,128)(2,1)S(1)}, u32[]{:S(2)}) copy-start(bf16[3072,128]{0,1:T(8,128)(2,1)S(1)} %convolution_convert_fusion.4) | copy-start | bytes 2359300
  275.9 46.7 %copy-start.11 = (bf16[3072,2,32]{0,2,1:T(8,128)(2,1)}, bf16[3072,2,32]{0,2,1:T(8,128)(2,1)S(1)}, u32[]{:S(2)}) copy-start(bf16[3072,2,32]{0,2,1:T(8,128)(2,1)S(1)} %get-tuple-element.406) | copy-start | bytes 1179652
  275.9 152.7 %copy-start.9 = (bf16[3072,2,32]{0,2,1:T(8,128)(2,1)}, bf16[3072,2,32]{0,2,1:T(8,128)(2,1)S(1)}, u32[]{:S(2)}) copy-start(bf16[3072,2,32]{0,2,1:T(8,128)(2,1)S(1)} %get-tuple-element.405) | copy-start | bytes 1179652
  277.3 14.6 copy-start.39
  277.3 45.3 %copy-start.48 = (bf16[512,6,64]{0,2,1:T(8,128)(2,1)}, bf16[512,6,64]{0,2,1:T(8,128)(2,1)S(1)}, u32[]{:S(2)}) copy-start(bf16[512,6,64]{0,2,1:T(8,128)(2,1)S(1)} %get-tuple-element.404) | copy-start | bytes 1179652
  291.9 14.8 copy-start.104
  306.7 15.0 copy-start.106
  349.4 15.7 copy-start.110
  434.3 68.3 %copy-start.7 = (bf16[768,1536]{1,0:T(8,128)(2,1)S(1)}, bf16[768,1536]{1,0:T(8,128)(2,1)}, u32[]{:S(2)}) copy-start(bf16[768,1536]{1,0:T(8,128)(2,1)} %param.43) | copy-start | bytes 7077892
  438.6 59.3 %all-to-all-start = ((bf16[4,768,384]{2,1,0:T(8,128)(2,1)}), bf16[4,768,384]{2,1,0:T(8,128)(2,1)}, u32[]{:S(2)}, u32[]{:S(2)}) async-start(bf16[4,768,384]{2,1,0:T(8,128)(2,1)} %bitcast.60), calls=%async_computation | async-start | bytes 4718592 | tf_op jit(solution)/shard_map/all_to_all | solution.py:377
  443.1 235.9 %all-gather.21.cloned.1.call-start = ((), (), s32[]{:S(2)}) async-start(), calls=%async_computation.17 | async-start | bytes 11796480 | tf_op jit(solution)/shard_map/all_gather | solution.py:381
  443.2 66.4 %copy-start.97 = (f32[1536]{0:T(1024)}, f32[1536]{0:T(1024)S(1)}, u32[]{:S(2)}) copy-start(f32[1536]{0:T(1024)S(1)} %convert_element_type.297) | copy-start | bytes 18436
  509.5 169.5 %copy-start.69 = (s32[3072,8]{0,1:T(8,128)S(1)}, s32[3072,8]{0,1:T(8,128)}, u32[]{:S(2)}) copy-start(s32[3072,8]{0,1:T(8,128)} %param.46) | copy-start | bytes 294916
  509.5 170.7 %copy-start.102 = (f32[768]{0:T(1024)}, f32[768]{0:T(1024)S(1)}, u32[]{:S(2)}) copy-start(f32[768]{0:T(1024)S(1)} %add_rsqrt_fusion) | copy-start | bytes 9220
  511.7 168.5 %copy-start.100 = (s32[1,24576]{1,0:T(1,128)S(1)}, s32[1,24576]{1,0:T(1,128)}, u32[]{:S(2)}) copy-start(s32[1,24576]{1,0:T(1,128)} %param.47) | copy-start | bytes 294916
  513.6 250.8 %all-gather.23.cloned.1.call-start = ((), (), s32[]{:S(2)}) async-start(), calls=%async_computation.18 | async-start | bytes 17694720 | tf_op jit(solution)/shard_map/all_gather | solution.py:383
  679.0 346.6 %all-gather.25.cloned.1.call-start = ((), (), s32[]{:S(2)}) async-start(), calls=%async_computation.19 | async-start | bytes 11796480 | tf_op jit(solution)/shard_map/all_gather | solution.py:418
  714.0 51.3 %copy-start.127 = (bf16[192,40]{0,1:T(8,128)(2,1)S(1)}, bf16[192,40]{0,1:T(8,128)(2,1)}, u32[]{:S(2)}) copy-start(bf16[192,40]{0,1:T(8,128)(2,1)} %param.54) | copy-start | bytes 46084
  764.4 534.8 %all-gather.27.cloned.1.call-start = ((), (), s32[]{:S(2)}) async-start(), calls=%async_computation.20 | async-start | bytes 8847360 | tf_op jit(solution)/shard_map/all_gather | solution.py:429
  774.9 28.5 %copy-start.65 = (bf16[1536,40]{0,1:T(8,128)(2,1)}, bf16[1536,40]{0,1:T(8,128)(2,1)S(1)}, u32[]{:S(2)}) copy-start(bf16[1536,40]{0,1:T(8,128)(2,1)S(1)} %reshape.1188) | copy-start | bytes 368644
  790.6 73.1 %copy-start.93 = (s32[7680]{0:T(1024)}, s32[7680]{0:T(1024)S(1)}, u32[]{:S(2)}) copy-start(s32[7680]{0:T(1024)S(1)} %get-tuple-element.415) | copy-start | bytes 92164
  810.7 52.9 %copy-start.82 = (f32[3072]{0:T(1024)}, f32[3072]{0:T(1024)S(1)}, u32[]{:S(2)}) copy-start(f32[3072]{0:T(1024)S(1)} %get-tuple-element.380) | copy-start | bytes 36868
  811.2 52.4 %copy-start.16 = (f32[3072,8]{1,0:T(8,128)}, f32[3072,8]{1,0:T(8,128)S(1)}, u32[]{:S(2)}) copy-start(f32[3072,8]{1,0:T(8,128)S(1)} %copy.585) | copy-start | bytes 294916
  1061.9 251.6 %reduce-scatter.16.cloned.1.call-start = ((), (), s32[]{:S(2)}) async-start(), calls=%async_computation.21 | async-start | bytes 11796480 | tf_op jit(solution)/shard_map/reduce_scatter | solution.py:432
  1073.6 405.1 %reduce-scatter.18.cloned.1.call-start = ((), (), s32[]{:S(2)}) async-start(), calls=%async_computation.22 | async-start | bytes 11796480 | tf_op jit(solution)/shard_map/reduce_scatter | solution.py:480
  1117.5 35.1 %copy-start.94 = (s32[7680]{0:T(1024)S(1)}, s32[7680]{0:T(1024)}, u32[]{:S(2)}) copy-start(s32[7680]{0:T(1024)} %copy-done.93) | copy-start | bytes 92164
  1221.9 71.2 %copy-start.17 = (f32[3072,8]{1,0:T(8,128)S(1)}, f32[3072,8]{1,0:T(8,128)}, u32[]{:S(2)}) copy-start(f32[3072,8]{1,0:T(8,128)} %copy-done.16) | copy-start | bytes 294916
  1221.9 71.2 %copy-start.83 = (f32[3072]{0:T(1024)S(1)}, f32[3072]{0:T(1024)}, u32[]{:S(2)}) copy-start(f32[3072]{0:T(1024)} %copy-done.82) | copy-start | bytes 36868
  1318.1 160.7 %copy-start.98 = (f32[1536]{0:T(1024)S(1)}, f32[1536]{0:T(1024)}, u32[]{:S(2)}) copy-start(f32[1536]{0:T(1024)} %copy-done.97) | copy-start | bytes 18436
  1318.1 160.7 %copy-start.103 = (f32[768]{0:T(1024)S(1)}, f32[768]{0:T(1024)}, u32[]{:S(2)}) copy-start(f32[768]{0:T(1024)} %copy-done.102) | copy-start | bytes 9220
  1318.1 270.5 %reduce-scatter.26.cloned.1.call-start = ((), (), s32[]{:S(2)}) async-start(), calls=%async_computation.26 | async-start | bytes 5308416 | tf_op jit(solution)/shard_map/reduce_scatter | solution.py:507
  1325.8 157.5 %copy-start.30 = (bf16[768,1536]{1,0:T(8,128)(2,1)S(1)}, bf16[768,1536]{1,0:T(8,128)(2,1)}, u32[]{:S(2)}) copy-start(bf16[768,1536]{1,0:T(8,128)(2,1)} %param.44) | copy-start | bytes 7077892
  1529.1 58.2 %all-to-all-start.1 = ((bf16[768,4,384]{2,0,1:T(8,128)(2,1)}), bf16[768,4,384]{2,0,1:T(8,128)(2,1)S(1)}, u32[]{:S(2)}, u32[]{:S(2)}) async-start(bf16[768,4,384]{2,0,1:T(8,128)(2,1)} %bitcast.530), calls=%async_computation.3 | async-start | bytes 4718592 | tf_op jit(solution)/shard_map/all_to_all | solution.py:491
  1533.5 429.6 %reduce-scatter.28.cloned.1.call-start = ((), (), s32[]{:S(2)}) async-start(), calls=%async_computation.27 | async-start | bytes 811008
  1588.5 377.4 %reduce-scatter.30.cloned.1.call-start = ((), (), s32[]{:S(2)}) async-start(), calls=%async_computation.28 | async-start | bytes 983040
  1590.9 376.9 %reduce-scatter.20.cloned.1.call-start = ((), (), s32[]{:S(2)}) async-start(), calls=%async_computation.23 | async-start | bytes 17694720 | tf_op jit(solution)/shard_map/reduce_scatter | solution.py:290
  1591.6 380.2 %reduce-scatter.24.cloned.1.call-start = ((), (), s32[]{:S(2)}) async-start(), calls=%async_computation.25 | async-start | bytes 17694720 | tf_op jit(solution)/shard_map/reduce_scatter | solution.py:293
  1592.1 448.6 %reduce-scatter.22.cloned.1.call-start = ((), (), s32[]{:S(2)}) async-start(), calls=%async_computation.24 | async-start | bytes 17694720 | tf_op jit(solution)/shard_map/reduce_scatter | solution.py:291
  1597.8 18.7 copy-start.50
  1600.5 35.1 %copy-start.41 = (bf16[512,384]{0,1:T(8,128)(2,1)}, bf16[512,384]{0,1:T(8,128)(2,1)S(1)}, u32[]{:S(2)}) copy-start(bf16[512,384]{0,1:T(8,128)(2,1)S(1)} %copy.604) | copy-start | bytes 1179652
  1601.8 65.4 %copy-start.40 = (bf16[512,384]{0,1:T(8,128)(2,1)}, bf16[512,384]{0,1:T(8,128)(2,1)S(1)}, u32[]{:S(2)}) copy-start(bf16[512,384]{0,1:T(8,128)(2,1)S(1)} %copy.606) | copy-start | bytes 1179652
  1602.0 103.2 %copy-start.34 = (bf16[512,384]{0,1:T(8,128)(2,1)}, bf16[512,384]{0,1:T(8,128)(2,1)S(1)}, u32[]{:S(2)}) copy-start(bf16[512,384]{0,1:T(8,128)(2,1)S(1)} %copy.608) | copy-start | bytes 1179652
  1602.2 168.2 %copy-start.32 = (bf16[512,384]{0,1:T(8,128)(2,1)}, bf16[512,384]{0,1:T(8,128)(2,1)S(1)}, u32[]{:S(2)}) copy-start(bf16[512,384]{0,1:T(8,128)(2,1)S(1)} %copy.610) | copy-start | bytes 1179652
  1830.2 16.3 copy-start.26
  1830.2 16.2 copy-start.28
  1864.1 14.6 slice-start.9
  1963.0 82.6 %copy-start.22 = (bf16[3072,2,64]{0,2,1:T(8,128)(2,1)}, bf16[3072,2,64]{0,2,1:T(8,128)(2,1)S(1)}, u32[]{:S(2)}) copy-start(bf16[3072,2,64]{0,2,1:T(8,128)(2,1)S(1)} %fusion.102) | copy-start | bytes 2359300
  1971.8 73.0 %copy-start.24 = (f32[3072,2,64]{0,2,1:T(8,128)S(1)}, f32[3072,2,64]{0,2,1:T(8,128)}, u32[]{:S(2)}) copy-start(f32[3072,2,64]{0,2,1:T(8,128)} %fusion.88) | copy-start | bytes 4718596
  1971.8 73.0 %copy-start.29 = (f32[3072,32]{0,1:T(8,128)S(1)}, f32[3072,32]{0,1:T(8,128)}, u32[]{:S(2)}) copy-start(f32[3072,32]{0,1:T(8,128)} %copy-done.27) | copy-start | bytes 1179652
  2058.0 92.6 %all-to-all-start.2 = ((bf16[4,768,640]{1,2,0:T(8,128)(2,1)}), bf16[4,768,640]{1,2,0:T(8,128)(2,1)}, u32[]{:S(2)}, u32[]{:S(2)}) async-start(bf16[4,768,640]{1,2,0:T(8,128)(2,1)} %copy.624), calls=%async_computation.8 | async-start | bytes 7864320 | tf_op jit(solution)/shard_map/all_to_all | solution.py:574
  2062.9 151.6 %reduce-scatter.32.cloned.1.call-start = ((), (), s32[]{:S(2)}) async-start(), calls=%async_computation.29 | async-start | bytes 2211840
  2150.6 15.6 copy-start.96
  2150.6 15.6 copy-start.125
  (98 other events, 615.9 us)
Sparse Core Ops, SparseCore 0:
  33.6 166.1 all-gather.10
  201.6 22.0 all-gather.12
  225.7 86.2 all-gather.14
  313.7 85.2 all-gather.16
  400.7 38.7 all-gather.18
  513.7 165.2 all-gather.20
  680.9 83.4 all-gather.22
  766.0 166.7 all-gather.24
  1062.1 50.9 all-gather.26
  1115.3 161.1 reduce-scatter.15
  1318.2 160.4 reduce-scatter.17
  1496.4 54.7 reduce-scatter.25
  1588.7 95.2 reduce-scatter.27
  1686.7 22.2 reduce-scatter.29
  1712.3 106.8 reduce-scatter.19
  1822.6 107.3 reduce-scatter.23
  1933.4 107.3 reduce-scatter.21
  2166.3 38.3 reduce-scatter.31

commit v7 on v6

--- a/solution.py
+++ b/solution.py
@@ -539,25 +539,6 @@
         value_grad = value_grad.at[:key_end].add(
             jnp.einsum("grqk,qgrd->kgd", soft_low, out_block, preferred_element_type=jnp.float32)
         )
-        if block_index == block_count - 1:
-            (
-                key_grad,
-                value_grad,
-                expert_grads,
-                router_weight_grad,
-                output_weight_grad,
-                mixture_gain_grad,
-            ) = lax.optimization_barrier(
-                (
-                    key_grad,
-                    value_grad,
-                    expert_grads,
-                    router_weight_grad,
-                    output_weight_grad,
-                    mixture_gain_grad,
-                )
-            )
-    gate_weight_grad, up_weight_grad, down_weight_grad = expert_grads
     query_rot_grad = jnp.concatenate(query_blocks, axis=0).reshape(TOK_GRP, local_heads, HD)
     query_grad = (
         rotate_back(query_rot_grad, cosine_table, sine_table)
@@ -572,6 +553,22 @@
     value_grad_low = value_grad.astype(jnp.bfloat16).reshape(TOK_GRP, local_groups * HD)
     projection_grad = jnp.concatenate([query_grad, key_grad_low, value_grad_low], axis=1)
     projection_grad_own = lax.all_to_all(projection_grad, "tensor", 0, 1, tiled=True)
+    (
+        projection_grad_own,
+        expert_grads,
+        router_weight_grad,
+        output_weight_grad,
+        mixture_gain_grad,
+    ) = lax.optimization_barrier(
+        (
+            projection_grad_own,
+            expert_grads,
+            router_weight_grad,
+            output_weight_grad,
+            mixture_gain_grad,
+        )
+    )
+    gate_weight_grad, up_weight_grad, down_weight_grad = expert_grads
     normed_grad = jnp.einsum(
         "tf,df->td", projection_grad_own, projection_all, preferred_element_type=jnp.float32
     )

time: 2230 us -> 2150 us (0.964)
  waiting for transfers between devices: 735 us -> 652 us
    reduce_scatter x1, waiting for transfers between devices: 64.9 us -> 0.01 us  [reduce_experts(): lax.psum_scatter(grads[1], 'dp', scatter_dimension=1, tiled=True)]
    all_to_all x1, waiting for transfers between devices: 74.7 us -> 24.3 us  [local(): lax.all_to_all(projection_grad, 'tensor', 0, 1, tiled=True)]
    reduce_scatter x1, waiting for transfers between devices: 0.01 us -> 33.8 us  [reduce_experts(): lax.psum_scatter(grads[2], 'dp', scatter_dimension=1, tiled=True)]
    unnamed x304 -> x302, local copies, waits for them, and re-layouts: 47.3 us -> 49.2 us
  transfers between devices with their start and end apart: 21 -> 21, of which waited for: 8 -> 8; matrix products, arithmetic and copies ran while one was open for 44% -> 47% of each run, Pallas kernels for 10% -> 11%
where the time goes in v7:
time: 2150 us; the launch traced here: 2140 us
  matrix products  706 us (33%)
  waiting for transfers between devices  652 us (30%)
  other arithmetic  299 us (14%)
  Pallas kernels  233 us (11%)
  blocking collectives  122 us (6%)
  local copies, waits for them, and re-layouts  97.2 us (5%)
    all_gather x1, waiting for transfers between devices, local(): lax.all_gather(normed_shard.astype(jnp.bfloat16), 'tensor', axis=0, tiled...  165 us
    all_gather x1, waiting for transfers between devices, local(): lax.all_gather(normed_two.astype(jnp.bfloat16), 'tensor', axis=0, tiled=T...  165 us
    reduce_scatter x1, waiting for transfers between devices, local(): lax.psum_scatter(mixture_grad_low, 'tensor', scatter_dimension=0, tiled=T...  152 us
    pallas_call x2, Pallas kernels, combine_rows(): pl.pallas_call(_combine_rows_kernel, grid_spec=pltpu.PrefetchScalarGridSp...  139 us
    convert_element_type x6, other arithmetic, local(): score_grad = (soft_full * (weight_grad - delta)).astype(jnp.bfloat16)  104 us
    dot_general x6, matrix products, local(): jnp.einsum('qgrd,kgd->grqk', out_block, value_low[:key_end], preferred_el...  95.2 us
    pallas_call x2, Pallas kernels, gather_rows(): pl.pallas_call(_gather_rows_kernel, grid_spec=pltpu.PrefetchScalarGridSpe...  94.5 us
    dot_general x6, matrix products, local(): jnp.einsum('grqk,qgrd->kgd', soft_low, out_block, preferred_element_type=...  64.2 us
  transfers between devices with their start and end apart: 21, of which 8 were waited for; matrix products, arithmetic and copies ran while one was open for 47% of the time, Pallas kernels for 11%

profile of v7, /device:TPU:0, one launch (start us, length us, event | category | flops | bytes accessed | tf_op | source)
XLA Modules:
  0.0 2141.3 jit_solution(13057891375493641797)
XLA Ops:
  10.8 16.0 all-reduce.7
  34.3 165.5 %all-gather.11.cloned.1.call-done = bf16[3072,1536]{1,0:T(8,128)(2,1)} async-done(((bf16[768,1536]{1,0:T(8,128)(2,1)}), bf16[3072,1536]{1,0:T(8,128)(2,1)}) %all-gather.11.cloned.1.call-update) | async-done | bytes 9437200 | tf_op jit(solution)/shard_map/all_gather | solution.py:337
  200.4 17.5 all_gather.55
  219.2 9.5 all_gather.51
  228.7 9.5 all_gather.50
  265.3 8.6 fusion.248
  277.4 14.6 fusion.245
  292.0 14.8 fusion.3
  306.8 14.9 fusion.157
  322.6 14.1 fusion.244
  336.8 12.6 fusion.8
  349.4 15.7 fusion.156
  380.2 11.0 fusion.155
  392.1 8.3 fusion.242
  400.5 8.9 fusion.22
  409.4 8.4 fusion.154
  443.3 54.7 %all-to-all-done = bf16[4,768,384]{2,1,0:T(8,128)(2,1)} async-done(((bf16[4,768,384]{2,1,0:T(8,128)(2,1)}), bf16[4,768,384]{2,1,0:T(8,128)(2,1)}, u32[]{:S(2)}, u32[]{:S(2)}) %all-to-all-start) | async-done | bytes 2359328 | tf_op jit(solution)/shard_map/all_to_all | solution.py:377
  513.7 165.3 %all-gather.21.cloned.1.call-done = bf16[3072,1536]{1,0:T(8,128)(2,1)} async-done(((bf16[768,1536]{1,0:T(8,128)(2,1)}), bf16[3072,1536]{1,0:T(8,128)(2,1)}) %all-gather.21.cloned.1.call-update) | async-done | bytes 9437200 | tf_op jit(solution)/shard_map/all_gather | solution.py:381
  681.1 14.6 fusion.101
  720.9 43.5 %all-gather.23.cloned.1.call-done = bf16[10,512,1536]{1,2,0:T(8,128)(2,1)} async-done(((bf16[10,512,192]{1,2,0:T(8,128)(2,1)}), bf16[10,512,1536]{1,2,0:T(8,128)(2,1)}) %all-gather.23.cloned.1.call-update) | async-done | bytes 15728656 | tf_op jit(solution)/shard_map/all_gather | solution.py:383
  765.4 9.4 all-gather
  790.7 12.7 convert_element_type.299.refs_0_
  813.0 50.7 %shard_map.248 = (bf16[7680,1536]{1,0:T(8,128)(2,1)}, f32[7680,128]{1,0:T(8,128)}) custom-call(s32[7680]{0:T(1024)} %get-tuple-element.414.tok_ref, f32[3072,1536]{1,0:T(8,128)} %convert_element_type.299.refs_0_, f32[3072,128]{1,0:T(8,128)} %pad.33.refs_1_), custom_call_target="tpu_custom_call" | custom-call | tf_op jit(solution)/shard_map/pallas_call | solution.py:156
  870.0 27.9 %fusion.250 = f32[10,768,512]{1,2,0:T(8,128)} fusion(bf16[10,768,1536]{2,1,0:T(8,128)(2,1)} %bitcast.588, bf16[10,1536,512]{2,1,0:T(8,128)(2,1)} %all-gather.15.cloned.1.call-done), kind=kOutput, calls=%fused_computation.403 | convolution fusion | flops 12079595520 | bytes 55050240 | tf_op jit(solution)/shard_map/ecd,edf->ecf/dot_general | solution.py:409
  897.9 32.6 %multiply_convert_fusion.3 = (bf16[10,768,512]{1,2,0:T(8,128)(2,1)}, f32[10,768,512]{1,2,0:T(8,128)}) fusion(f32[10,768]{1,0:T(8,128)S(1)} %broadcast_select_fusion, f32[10,768,512]{1,2,0:T(8,128)} %fusion.250, bf16[10,768,1536]{2,1,0:T(8,128)(2,1)} %bitcast.589, bf16[10,1536,512]{2,1,0:T(8,128)(2,1)} %all-gather.17.cloned.1.call-done), kind=kOutput, calls=%fused_computation.56 | convolution fusion | flops 12107120640 | bytes 78673920 | tf_op jit(solution)/shard_map/ecd,edf->ecf/dot_general | solution.py:410
  930.5 27.2 %fusion.251 = f32[10,768,1536]{2,1,0:T(8,128)} fusion(bf16[10,768,512]{1,2,0:T(8,128)(2,1)} %get-tuple-element.236, bf16[10,512,1536]{1,2,0:T(8,128)(2,1)} %all-gather.23.cloned.1.call-done), kind=kOutput, calls=%fused_computation.404 | convolution fusion | flops 12079595520 | bytes 70778880 | tf_op jit(solution)/shard_map/ecf,efd->ecd/dot_general | solution.py:413
  957.7 67.9 %shard_map.249 = f32[3072,1536]{1,0:T(8,128)} custom-call(s32[7680]{0:T(1024)} %get-tuple-element.414.tok_ref, f32[7680,1536]{1,0:T(8,128)} %bitcast.519), custom_call_target="tpu_custom_call" | custom-call | tf_op jit(solution)/shard_map/pallas_call | solution.py:211
  1025.6 12.9 fusion.40.refs_0_
  1038.6 22.2 %all_gather.62 = bf16[192,2560]{1,0:T(8,128)(2,1)} all-gather(bf16[192,640]{1,0:T(8,128)(2,1)S(1)} %pad_maximum_fusion.5), channel_id=1, replica_groups=mesh['dp'=8,'tensor'=4] {'tensor'}, dimensions={1}, use_global_device_ids=true | all-gather | bytes 1228800 | tf_op jit(solution)/shard_map/all_gather | solution.py:430
  1060.8 11.7 convert_element_type.308
  1072.6 43.8 %shard_map.250 = bf16[7680,1536]{1,0:T(8,128)(2,1)} custom-call(s32[7680]{0:T(1024)} %get-tuple-element.414.tok_ref, f32[3072,1536]{1,0:T(8,128)} %fusion.40.refs_0_), custom_call_target="tpu_custom_call" | custom-call | tf_op jit(solution)/shard_map/pallas_call | solution.py:156
  1116.4 35.1 %multiply_reduce_fusion = (f32[10,768]{1,0:T(8,128)S(1)}, bf16[10,768,512]{1,2,0:T(8,128)(2,1)}, bf16[10,768,512]{1,2,0:T(8,128)(2,1)}) fusion(f32[10,768,512]{1,2,0:T(8,128)} %get-tuple-element.435, f32[10,768,512]{1,2,0:T(8,128)} %fusion.250, f32[10,768]{1,0:T(8,128)S(1)} %broadcast_select_fusion, bf16[10,768,1536]{2,1,0:T(8,128)(2,1)} %bitcast.523, ...), kind=kOutput, calls=%fused_computation.53 | convolution fusion | flops 12146434048 | bytes 86568960 | tf_op jit(solution)/shard_map/ecd,efd->ecf/dot_general | solution.py:437
  1159.3 27.3 %fusion.252 = f32[10,768,1536]{2,1,0:T(8,128)} fusion(bf16[10,768,512]{1,2,0:T(8,128)(2,1)} %get-tuple-element.233, bf16[10,1536,512]{2,1,0:T(8,128)(2,1)} %all-gather.15.cloned.1.call-done), kind=kOutput, calls=%fused_computation.405 | convolution fusion | flops 12079595520 | bytes 70778880 | tf_op jit(solution)/shard_map/ecf,edf->ecd/dot_general | solution.py:445
  1186.6 34.2 %add_convert_fusion = bf16[10,768,1536]{2,1,0:T(8,128)(2,1)} fusion(f32[10,768,1536]{2,1,0:T(8,128)} %fusion.252, bf16[10,768,512]{1,2,0:T(8,128)(2,1)} %get-tuple-element.234, bf16[10,1536,512]{2,1,0:T(8,128)(2,1)} %all-gather.17.cloned.1.call-done), kind=kOutput, calls=%fused_computation | convolution fusion | flops 12103188480 | bytes 94371840 | tf_op jit(solution)/shard_map/ecf,edf->ecd/dot_general | solution.py:447
  1220.8 71.0 %shard_map.251 = (f32[3072,1536]{1,0:T(8,128)}, f32[3072,128]{1,0:T(8,128)}) custom-call(s32[7680]{0:T(1024)} %get-tuple-element.414.tok_ref, bf16[7680,1536]{1,0:T(8,128)(2,1)} %bitcast.522, f32[7680,128]{1,0:T(8,128)} %fusion.81.refs_1_), custom_call_target="tpu_custom_call" | custom-call | tf_op jit(solution)/shard_map/pallas_call | solution.py:211
  1298.0 14.3 add_convert_fusion.1
  1324.6 151.6 %reduce-scatter.18.cloned.1.call-done = bf16[768,1536]{1,0:T(8,128)(2,1)} async-done(((bf16[3072,1536]{1,0:T(8,128)(2,1)}), bf16[768,1536]{1,0:T(8,128)(2,1)}) %reduce-scatter.18.cloned.1.call-update) | async-done | bytes 2359312 | tf_op jit(solution)/shard_map/reduce_scatter | solution.py:480
  1493.7 22.8 %convolution_convert_fusion.1 = bf16[10,1536,512]{2,1,0:T(8,128)(2,1)} fusion(bf16[10,768,1536]{2,1,0:T(8,128)(2,1)} %bitcast.590, bf16[10,768,512]{1,2,0:T(8,128)(2,1)} %get-tuple-element.234), kind=kOutput, calls=%fused_computation.62 | convolution fusion | flops 12087459840 | bytes 47185920 | tf_op jit(solution)/shard_map/ecd,ecf->edf/dot_general | solution.py:463
  1516.5 8.3 convolution_convert_fusion.5
  1531.0 21.6 %convolution_convert_fusion.2 = bf16[10,1536,512]{2,1,0:T(8,128)(2,1)} fusion(bf16[10,768,1536]{2,1,0:T(8,128)(2,1)} %bitcast.591, bf16[10,768,512]{1,2,0:T(8,128)(2,1)} %get-tuple-element.233), kind=kOutput, calls=%fused_computation.63 | convolution fusion | flops 12087459840 | bytes 47185920 | tf_op jit(solution)/shard_map/ecd,ecf->edf/dot_general | solution.py:462
  1552.6 21.4 convolution_convert_fusion
  1574.0 10.9 all-to-all-done.1
  1633.3 11.8 fusion.17
  1645.1 13.4 fusion.19
  1664.7 15.8 fusion.9
  1680.5 17.4 fusion.11
  1702.8 26.6 %fusion.4 = (f32[2,3,512]{2,1,0:T(4,128)S(1)}, f32[2,2560,512,3]{2,1,3,0:T(8,128)}) fusion(f32[2,3,512,2560]{2,3,1,0:T(8,128)} %get-tuple-element.429, f32[2,3,512]{2,1,0:T(4,128)S(1)} %log_add_fusion.1, bf16[2560,2,64,1]{0,2,3,1:T(8,128)(2,1)S(1)} %bitcast.558, bf16[512,2,3,64]{0,3,2,1:T(8,128)(2,1)S(1)} %bitcast.535), kind=kOutput, calls=%fused_computation.13 | convolution fusion | flops 1030222848 | bytes 63987712 | tf_op jit(solution)/shard_map/qgrd,kgd->grqk/dot_general | solution.py:524
  1729.4 28.5 %fusion.6 = bf16[2,3,512,2560]{2,3,1,0:T(8,128)(2,1)} fusion(f32[2,2560,512,3]{2,1,3,0:T(8,128)} %get-tuple-element.445, f32[2,3,512,2560]{2,3,1,0:T(8,128)} %get-tuple-element.429, f32[2,3,512]{2,1,0:T(4,128)S(1)} %get-tuple-element.444, f32[2,3,512]{2,1,0:T(4,128)S(1)} %log_add_fusion.1), kind=kLoop, calls=%fused_computation.15 | loop fusion | flops 31457280 | bytes 78667776 | tf_op jit(solution)/shard_map/convert_element_type | solution.py:528
  1757.9 9.7 fusion.151
  1767.6 28.2 %fusion = (f32[2,3,512]{2,1,0:T(4,128)S(1)}, f32[2,3072,512,3]{2,1,3,0:T(8,128)}) fusion(f32[2,3,512,3072]{2,3,1,0:T(8,128)} %get-tuple-element.431, f32[2,3,512]{2,1,0:T(4,128)S(1)} %copy-done.68, bf16[3072,2,64,1]{0,2,3,1:T(8,128)(2,1)S(1)} %bitcast.526, bf16[512,2,3,64]{0,3,2,1:T(8,128)(2,1)S(1)} %bitcast.533), kind=kOutput, calls=%fused_computation.3 | convolution fusion | flops 1236268032 | bytes 76701696 | tf_op jit(solution)/shard_map/qgrd,kgd->grqk/dot_general | solution.py:524
  1795.8 31.5 %fusion.2 = bf16[2,3,512,3072]{2,3,1,0:T(8,128)(2,1)} fusion(f32[2,3072,512,3]{2,1,3,0:T(8,128)} %get-tuple-element.447, f32[2,3,512,3072]{2,3,1,0:T(8,128)} %get-tuple-element.431, f32[2,3,512]{2,1,0:T(4,128)S(1)} %get-tuple-element.446, f32[2,3,512]{2,1,0:T(4,128)S(1)} %copy-done.68), kind=kLoop, calls=%fused_computation.5 | loop fusion | flops 37748736 | bytes 94396416 | tf_op jit(solution)/shard_map/convert_element_type | solution.py:528
  1827.3 16.4 fusion.141
  1872.7 10.8 fusion.87
  1883.6 10.3 fusion.88
  1900.8 8.0 fusion.168
  1908.8 8.2 fusion.120
  1917.0 10.5 fusion.137
  1927.5 13.9 fusion.98
  1941.4 19.9 fusion.105
  1961.8 8.2 pad_maximum_fusion
  2003.9 33.8 %reduce-scatter.24.cloned.1.call-done = bf16[10,192,512]{2,1,0:T(8,128)(2,1)} async-done(((bf16[10,1536,512]{2,1,0:T(8,128)(2,1)}), bf16[10,192,512]{2,1,0:T(8,128)(2,1)}) %reduce-scatter.24.cloned.1.call-update) | async-done | bytes 1966096 | tf_op jit(solution)/shard_map/reduce_scatter | solution.py:293
  2041.7 24.3 %all-to-all-done.2 = bf16[4,768,640]{1,2,0:T(8,128)(2,1)} async-done(((bf16[4,768,640]{1,2,0:T(8,128)(2,1)}), bf16[4,768,640]{1,2,0:T(8,128)(2,1)}, u32[]{:S(2)}, u32[]{:S(2)}) %all-to-all-start.2) | async-done | bytes 3932192 | tf_op jit(solution)/shard_map/all_to_all | solution.py:555
  2066.0 11.3 fusion.254
  2085.1 38.0 %all-reduce.6 = f32[1536]{0:T(1024)S(1)} all-reduce(f32[1536]{0:T(1024)S(1)} %get-tuple-element.372), channel_id=10, replica_groups=mesh['dp'=8,'tensor'=4] {'dp','tensor'}, use_global_device_ids=true, to_apply=%region_45.46.clone | all-reduce | flops 1536 | bytes 12288
  (523 shorter events, 361.8 us)
Async XLA Ops:
  7.2 192.6 %all-gather.11.cloned.1.call-start = ((), (), s32[]{:S(2)}) async-start(), calls=%async_computation.12 | async-start | bytes 11796480 | tf_op jit(solution)/shard_map/all_gather | solution.py:337
  26.9 173.5 %copy-start.89 = (bf16[384,192]{0,1:T(8,128)(2,1)S(1)}, bf16[384,192]{0,1:T(8,128)(2,1)}, u32[]{:S(2)}) copy-start(bf16[384,192]{0,1:T(8,128)(2,1)} %param.52) | copy-start | bytes 442372
  29.1 188.8 %copy-start.125 = (s32[1,1024]{1,0:T(1,128)S(1)}, s32[1,1024]{1,0:T(1,128)}, u32[]{:S(2)}) copy-start(s32[1,1024]{1,0:T(1,128)} %param.45) | copy-start | bytes 12292
  29.8 189.4 %copy-start.85 = (bf16[192,128]{1,0:T(8,128)(2,1)S(1)}, bf16[192,128]{1,0:T(8,128)(2,1)}, u32[]{:S(2)}) copy-start(bf16[192,128]{1,0:T(8,128)(2,1)} %param.50) | copy-start | bytes 147460
  29.8 199.0 %copy-start.83 = (bf16[192,128]{1,0:T(8,128)(2,1)S(1)}, bf16[192,128]{1,0:T(8,128)(2,1)}, u32[]{:S(2)}) copy-start(bf16[192,128]{1,0:T(8,128)(2,1)} %param.51) | copy-start | bytes 147460
  33.5 231.8 %all-gather.13.cloned.1.call-start = ((), (), s32[]{:S(2)}) async-start(), calls=%async_computation.13 | async-start | bytes 1327104 | tf_op jit(solution)/shard_map/all_gather | solution.py:324
  34.2 404.5 %all-gather.15.cloned.1.call-start = ((), (), s32[]{:S(2)}) async-start(), calls=%async_computation.14 | async-start | bytes 17694720 | tf_op jit(solution)/shard_map/all_gather | solution.py:341
  199.8 238.9 %all-gather.17.cloned.1.call-start = ((), (), s32[]{:S(2)}) async-start(), calls=%async_computation.15 | async-start | bytes 17694720 | tf_op jit(solution)/shard_map/all_gather | solution.py:342
  200.3 302.3 %all-gather.19.cloned.1.call-start = ((), (), s32[]{:S(2)}) async-start(), calls=%async_computation.16 | async-start | bytes 5308416 | tf_op jit(solution)/shard_map/all_gather | solution.py:330
  244.2 29.7 %copy-start.22 = (f32[3072,32]{0,1:T(8,128)}, f32[3072,32]{0,1:T(8,128)S(1)}, u32[]{:S(2)}) copy-start(f32[3072,32]{0,1:T(8,128)S(1)} %get-tuple-element.415) | copy-start | bytes 1179652
  244.2 29.7 %copy-start.24 = (f32[3072,32]{0,1:T(8,128)}, f32[3072,32]{0,1:T(8,128)S(1)}, u32[]{:S(2)}) copy-start(f32[3072,32]{0,1:T(8,128)S(1)} %get-tuple-element.416) | copy-start | bytes 1179652
  248.0 14.0 slice-start
  258.0 48.7 %copy-start.18 = (bf16[3072,128]{0,1:T(8,128)(2,1)}, bf16[3072,128]{0,1:T(8,128)(2,1)S(1)}, u32[]{:S(2)}) copy-start(bf16[3072,128]{0,1:T(8,128)(2,1)S(1)} %convolution_convert_fusion.4) | copy-start | bytes 2359300
  275.9 46.7 %copy-start.11 = (bf16[3072,2,32]{0,2,1:T(8,128)(2,1)}, bf16[3072,2,32]{0,2,1:T(8,128)(2,1)S(1)}, u32[]{:S(2)}) copy-start(bf16[3072,2,32]{0,2,1:T(8,128)(2,1)S(1)} %get-tuple-element.404) | copy-start | bytes 1179652
  275.9 152.7 %copy-start.9 = (bf16[3072,2,32]{0,2,1:T(8,128)(2,1)}, bf16[3072,2,32]{0,2,1:T(8,128)(2,1)S(1)}, u32[]{:S(2)}) copy-start(bf16[3072,2,32]{0,2,1:T(8,128)(2,1)S(1)} %get-tuple-element.403) | copy-start | bytes 1179652
  277.3 14.6 copy-start.35
  277.3 45.3 %copy-start.45 = (bf16[512,6,64]{0,2,1:T(8,128)(2,1)}, bf16[512,6,64]{0,2,1:T(8,128)(2,1)S(1)}, u32[]{:S(2)}) copy-start(bf16[512,6,64]{0,2,1:T(8,128)(2,1)S(1)} %get-tuple-element.402) | copy-start | bytes 1179652
  292.0 14.8 copy-start.103
  306.7 15.0 copy-start.105
  349.4 15.7 copy-start.109
  434.4 68.3 %copy-start.7 = (bf16[768,1536]{1,0:T(8,128)(2,1)S(1)}, bf16[768,1536]{1,0:T(8,128)(2,1)}, u32[]{:S(2)}) copy-start(bf16[768,1536]{1,0:T(8,128)(2,1)} %param.43) | copy-start | bytes 7077892
  438.7 59.3 %all-to-all-start = ((bf16[4,768,384]{2,1,0:T(8,128)(2,1)}), bf16[4,768,384]{2,1,0:T(8,128)(2,1)}, u32[]{:S(2)}, u32[]{:S(2)}) async-start(bf16[4,768,384]{2,1,0:T(8,128)(2,1)} %bitcast.60), calls=%async_computation | async-start | bytes 4718592 | tf_op jit(solution)/shard_map/all_to_all | solution.py:377
  443.2 235.8 %all-gather.21.cloned.1.call-start = ((), (), s32[]{:S(2)}) async-start(), calls=%async_computation.17 | async-start | bytes 11796480 | tf_op jit(solution)/shard_map/all_gather | solution.py:381
  443.3 66.4 %copy-start.96 = (f32[1536]{0:T(1024)}, f32[1536]{0:T(1024)S(1)}, u32[]{:S(2)}) copy-start(f32[1536]{0:T(1024)S(1)} %convert_element_type.297) | copy-start | bytes 18436
  509.6 169.5 %copy-start.66 = (s32[3072,8]{0,1:T(8,128)S(1)}, s32[3072,8]{0,1:T(8,128)}, u32[]{:S(2)}) copy-start(s32[3072,8]{0,1:T(8,128)} %param.46) | copy-start | bytes 294916
  509.6 170.7 %copy-start.101 = (f32[768]{0:T(1024)}, f32[768]{0:T(1024)S(1)}, u32[]{:S(2)}) copy-start(f32[768]{0:T(1024)S(1)} %add_rsqrt_fusion) | copy-start | bytes 9220
  511.8 168.5 %copy-start.99 = (s32[1,24576]{1,0:T(1,128)S(1)}, s32[1,24576]{1,0:T(1,128)}, u32[]{:S(2)}) copy-start(s32[1,24576]{1,0:T(1,128)} %param.47) | copy-start | bytes 294916
  513.6 250.8 %all-gather.23.cloned.1.call-start = ((), (), s32[]{:S(2)}) async-start(), calls=%async_computation.18 | async-start | bytes 17694720 | tf_op jit(solution)/shard_map/all_gather | solution.py:383
  679.1 346.6 %all-gather.25.cloned.1.call-start = ((), (), s32[]{:S(2)}) async-start(), calls=%async_computation.19 | async-start | bytes 11796480 | tf_op jit(solution)/shard_map/all_gather | solution.py:418
  714.0 51.4 %copy-start.126 = (bf16[192,40]{0,1:T(8,128)(2,1)S(1)}, bf16[192,40]{0,1:T(8,128)(2,1)}, u32[]{:S(2)}) copy-start(bf16[192,40]{0,1:T(8,128)(2,1)} %param.54) | copy-start | bytes 46084
  764.5 533.5 %all-gather.27.cloned.1.call-start = ((), (), s32[]{:S(2)}) async-start(), calls=%async_computation.20 | async-start | bytes 8847360 | tf_op jit(solution)/shard_map/all_gather | solution.py:429
  774.9 28.5 %copy-start.62 = (bf16[1536,40]{0,1:T(8,128)(2,1)}, bf16[1536,40]{0,1:T(8,128)(2,1)S(1)}, u32[]{:S(2)}) copy-start(bf16[1536,40]{0,1:T(8,128)(2,1)S(1)} %reshape.1188) | copy-start | bytes 368644
  790.6 73.1 %copy-start.92 = (s32[7680]{0:T(1024)}, s32[7680]{0:T(1024)S(1)}, u32[]{:S(2)}) copy-start(s32[7680]{0:T(1024)S(1)} %get-tuple-element.413) | copy-start | bytes 92164
  810.8 53.0 %copy-start.81 = (f32[3072]{0:T(1024)}, f32[3072]{0:T(1024)S(1)}, u32[]{:S(2)}) copy-start(f32[3072]{0:T(1024)S(1)} %get-tuple-element.378) | copy-start | bytes 36868
  811.3 52.5 %copy-start.16 = (f32[3072,8]{1,0:T(8,128)}, f32[3072,8]{1,0:T(8,128)S(1)}, u32[]{:S(2)}) copy-start(f32[3072,8]{1,0:T(8,128)S(1)} %copy.585) | copy-start | bytes 294916
  1060.8 251.6 %reduce-scatter.16.cloned.1.call-start = ((), (), s32[]{:S(2)}) async-start(), calls=%async_computation.21 | async-start | bytes 11796480 | tf_op jit(solution)/shard_map/reduce_scatter | solution.py:432
  1072.5 403.6 %reduce-scatter.18.cloned.1.call-start = ((), (), s32[]{:S(2)}) async-start(), calls=%async_computation.22 | async-start | bytes 11796480 | tf_op jit(solution)/shard_map/reduce_scatter | solution.py:480
  1116.4 35.2 %copy-start.93 = (s32[7680]{0:T(1024)S(1)}, s32[7680]{0:T(1024)}, u32[]{:S(2)}) copy-start(s32[7680]{0:T(1024)} %copy-done.92) | copy-start | bytes 92164
  1220.8 71.0 %copy-start.17 = (f32[3072,8]{1,0:T(8,128)S(1)}, f32[3072,8]{1,0:T(8,128)}, u32[]{:S(2)}) copy-start(f32[3072,8]{1,0:T(8,128)} %copy-done.16) | copy-start | bytes 294916
  1220.8 71.0 %copy-start.82 = (f32[3072]{0:T(1024)S(1)}, f32[3072]{0:T(1024)}, u32[]{:S(2)}) copy-start(f32[3072]{0:T(1024)} %copy-done.81) | copy-start | bytes 36868
  1316.9 159.3 %copy-start.97 = (f32[1536]{0:T(1024)S(1)}, f32[1536]{0:T(1024)}, u32[]{:S(2)}) copy-start(f32[1536]{0:T(1024)} %copy-done.96) | copy-start | bytes 18436
  1316.9 159.3 %copy-start.102 = (f32[768]{0:T(1024)S(1)}, f32[768]{0:T(1024)}, u32[]{:S(2)}) copy-start(f32[768]{0:T(1024)} %copy-done.101) | copy-start | bytes 9220
  1316.9 269.3 %reduce-scatter.26.cloned.1.call-start = ((), (), s32[]{:S(2)}) async-start(), calls=%async_computation.26 | async-start | bytes 5308416 | tf_op jit(solution)/shard_map/reduce_scatter | solution.py:507
  1324.6 156.1 %copy-start.26 = (bf16[768,1536]{1,0:T(8,128)(2,1)S(1)}, bf16[768,1536]{1,0:T(8,128)(2,1)}, u32[]{:S(2)}) copy-start(bf16[768,1536]{1,0:T(8,128)(2,1)} %param.44) | copy-start | bytes 7077892
  1526.5 58.4 %all-to-all-start.1 = ((bf16[768,4,384]{2,0,1:T(8,128)(2,1)}), bf16[768,4,384]{2,0,1:T(8,128)(2,1)S(1)}, u32[]{:S(2)}, u32[]{:S(2)}) async-start(bf16[768,4,384]{2,0,1:T(8,128)(2,1)} %bitcast.532), calls=%async_computation.3 | async-start | bytes 4718592 | tf_op jit(solution)/shard_map/all_to_all | solution.py:491
  1531.0 460.2 %reduce-scatter.28.cloned.1.call-start = ((), (), s32[]{:S(2)}) async-start(), calls=%async_computation.27 | async-start | bytes 811008
  1586.1 407.8 %reduce-scatter.30.cloned.1.call-start = ((), (), s32[]{:S(2)}) async-start(), calls=%async_computation.28 | async-start | bytes 983040
  1588.6 407.1 %reduce-scatter.20.cloned.1.call-start = ((), (), s32[]{:S(2)}) async-start(), calls=%async_computation.23 | async-start | bytes 17694720 | tf_op jit(solution)/shard_map/reduce_scatter | solution.py:290
  1589.2 410.7 %reduce-scatter.22.cloned.1.call-start = ((), (), s32[]{:S(2)}) async-start(), calls=%async_computation.24 | async-start | bytes 17694720 | tf_op jit(solution)/shard_map/reduce_scatter | solution.py:291
  1594.9 19.7 copy-start.47
  1597.5 35.8 %copy-start.39 = (bf16[512,384]{0,1:T(8,128)(2,1)}, bf16[512,384]{0,1:T(8,128)(2,1)S(1)}, u32[]{:S(2)}) copy-start(bf16[512,384]{0,1:T(8,128)(2,1)S(1)} %copy.604) | copy-start | bytes 1179652
  1598.8 65.8 %copy-start.37 = (bf16[512,384]{0,1:T(8,128)(2,1)}, bf16[512,384]{0,1:T(8,128)(2,1)S(1)}, u32[]{:S(2)}) copy-start(bf16[512,384]{0,1:T(8,128)(2,1)S(1)} %copy.606) | copy-start | bytes 1179652
  1599.0 103.7 %copy-start.30 = (bf16[512,384]{0,1:T(8,128)(2,1)}, bf16[512,384]{0,1:T(8,128)(2,1)S(1)}, u32[]{:S(2)}) copy-start(bf16[512,384]{0,1:T(8,128)(2,1)S(1)} %copy.608) | copy-start | bytes 1179652
  1599.3 168.3 %copy-start.28 = (bf16[512,384]{0,1:T(8,128)(2,1)}, bf16[512,384]{0,1:T(8,128)(2,1)S(1)}, u32[]{:S(2)}) copy-start(bf16[512,384]{0,1:T(8,128)(2,1)S(1)} %copy.610) | copy-start | bytes 1179652
  1599.3 438.4 %reduce-scatter.24.cloned.1.call-start = ((), (), s32[]{:S(2)}) async-start(), calls=%async_computation.25 | async-start | bytes 17694720 | tf_op jit(solution)/shard_map/reduce_scatter | solution.py:293
  1600.3 14.2 slice-start.6
  1600.3 14.2 slice-start.7
  1827.3 16.4 copy-start.23
  1827.3 16.4 copy-start.25
  1854.2 14.6 slice-start.9
  1972.5 93.5 %all-to-all-start.2 = ((bf16[4,768,640]{1,2,0:T(8,128)(2,1)}), bf16[4,768,640]{1,2,0:T(8,128)(2,1)}, u32[]{:S(2)}, u32[]{:S(2)}) async-start(bf16[4,768,640]{1,2,0:T(8,128)(2,1)} %copy.624), calls=%async_computation.4 | async-start | bytes 7864320 | tf_op jit(solution)/shard_map/all_to_all | solution.py:555
  1977.4 153.4 %reduce-scatter.32.cloned.1.call-start = ((), (), s32[]{:S(2)}) async-start(), calls=%async_computation.29 | async-start | bytes 2211840
  2066.0 15.5 copy-start.95
  2066.0 15.5 copy-start.124
  (97 other events, 567.7 us)
Sparse Core Ops, SparseCore 0:
  33.6 166.1 all-gather.10
  201.6 22.0 all-gather.12
  225.7 86.2 all-gather.14
  313.7 85.2 all-gather.16
  400.7 38.7 all-gather.18
  513.8 165.2 all-gather.20
  680.9 83.4 all-gather.22
  766.0 166.7 all-gather.24
  1060.9 50.9 all-gather.26
  1114.1 161.1 reduce-scatter.15
  1317.0 159.1 reduce-scatter.17
  1493.8 54.7 reduce-scatter.25
  1586.2 95.2 reduce-scatter.27
  1683.7 22.1 reduce-scatter.29
  1709.3 106.8 reduce-scatter.19
  1819.6 107.2 reduce-scatter.21
  1930.3 107.3 reduce-scatter.23
  2081.6 39.4 reduce-scatter.31

commit v8 on v7

--- a/solution.py
+++ b/solution.py
@@ -596,7 +596,10 @@
     value_weight_grad = projection_grads[:, query_width + key_width :]
 
     attention_gain_grad = lax.psum_scatter(
-        gain_one_grad, ("dp", "tensor"), scatter_dimension=0, tiled=True
+        lax.psum_scatter(gain_one_grad, "dp", scatter_dimension=0, tiled=True),
+        "tensor",
+        scatter_dimension=0,
+        tiled=True,
     )
     return (
         block_output,

time: 2150 us -> 2140 us (level)
    unnamed x2 -> x3, blocking collectives: 54.1 us -> 39.2 us
    unnamed x302 -> x306, local copies, waits for them, and re-layouts: 49.2 us -> 49.9 us
  transfers between devices with their start and end apart: 21 -> 21, of which waited for: 8 -> 9; matrix products, arithmetic and copies ran while one was open for 47% -> 47% of each run, Pallas kernels for 11% -> 11%
where the time goes in v8:
time: 2140 us; the launch traced here: 2130 us
  matrix products  706 us (33%)
  waiting for transfers between devices  655 us (31%)
  other arithmetic  299 us (14%)
  Pallas kernels  234 us (11%)
  blocking collectives  108 us (5%)
  local copies, waits for them, and re-layouts  97.9 us (5%)
    all_gather x1, waiting for transfers between devices, local(): lax.all_gather(normed_shard.astype(jnp.bfloat16), 'tensor', axis=0, tiled...  165 us
    all_gather x1, waiting for transfers between devices, local(): lax.all_gather(normed_two.astype(jnp.bfloat16), 'tensor', axis=0, tiled=T...  165 us
    reduce_scatter x1, waiting for transfers between devices, local(): lax.psum_scatter(mixture_grad_low, 'tensor', scatter_dimension=0, tiled=T...  152 us
    pallas_call x2, Pallas kernels, combine_rows(): pl.pallas_call(_combine_rows_kernel, grid_spec=pltpu.PrefetchScalarGridSp...  139 us
    convert_element_type x6, other arithmetic, local(): score_grad = (soft_full * (weight_grad - delta)).astype(jnp.bfloat16)  104 us
    dot_general x6, matrix products, local(): jnp.einsum('qgrd,kgd->grqk', out_block, value_low[:key_end], preferred_el...  95.3 us
    pallas_call x2, Pallas kernels, gather_rows(): pl.pallas_call(_gather_rows_kernel, grid_spec=pltpu.PrefetchScalarGridSpe...  94.5 us
    dot_general x6, matrix products, local(): jnp.einsum('grqk,qgrd->kgd', soft_low, out_block, preferred_element_type=...  64.3 us
  transfers between devices with their start and end apart: 21, of which 9 were waited for; matrix products, arithmetic and copies ran while one was open for 47% of the time, Pallas kernels for 11%

profile of v8, /device:TPU:0, one launch (start us, length us, event | category | flops | bytes accessed | tf_op | source)
XLA Modules:
  0.0 2132.7 jit_solution(8069315040371332370)
XLA Ops:
  10.9 16.0 all-reduce.8
  34.3 165.5 %all-gather.11.cloned.1.call-done = bf16[3072,1536]{1,0:T(8,128)(2,1)} async-done(((bf16[768,1536]{1,0:T(8,128)(2,1)}), bf16[3072,1536]{1,0:T(8,128)(2,1)}) %all-gather.11.cloned.1.call-update) | async-done | bytes 9437200 | tf_op jit(solution)/shard_map/all_gather | solution.py:337
  200.5 17.5 all_gather.55
  219.3 9.5 all_gather.51
  228.8 9.5 all_gather.50
  265.3 8.6 fusion.249
  277.4 14.6 fusion.246
  292.0 14.8 fusion.3
  306.8 14.9 fusion.157
  322.7 14.2 fusion.245
  336.9 12.6 fusion.8
  349.5 15.7 fusion.156
  380.3 11.0 fusion.155
  392.2 8.4 fusion.243
  400.5 8.9 fusion.22
  409.5 8.4 fusion.154
  443.3 54.8 %all-to-all-done = bf16[4,768,384]{2,1,0:T(8,128)(2,1)} async-done(((bf16[4,768,384]{2,1,0:T(8,128)(2,1)}), bf16[4,768,384]{2,1,0:T(8,128)(2,1)}, u32[]{:S(2)}, u32[]{:S(2)}) %all-to-all-start) | async-done | bytes 2359328 | tf_op jit(solution)/shard_map/all_to_all | solution.py:377
  513.8 165.3 %all-gather.21.cloned.1.call-done = bf16[3072,1536]{1,0:T(8,128)(2,1)} async-done(((bf16[768,1536]{1,0:T(8,128)(2,1)}), bf16[3072,1536]{1,0:T(8,128)(2,1)}) %all-gather.21.cloned.1.call-update) | async-done | bytes 9437200 | tf_op jit(solution)/shard_map/all_gather | solution.py:381
  681.2 14.5 fusion.101
  721.0 43.5 %all-gather.23.cloned.1.call-done = bf16[10,512,1536]{1,2,0:T(8,128)(2,1)} async-done(((bf16[10,512,192]{1,2,0:T(8,128)(2,1)}), bf16[10,512,1536]{1,2,0:T(8,128)(2,1)}) %all-gather.23.cloned.1.call-update) | async-done | bytes 15728656 | tf_op jit(solution)/shard_map/all_gather | solution.py:383
  765.5 9.4 all-gather
  790.8 12.7 convert_element_type.299.refs_0_
  813.1 50.7 %shard_map.248 = (bf16[7680,1536]{1,0:T(8,128)(2,1)}, f32[7680,128]{1,0:T(8,128)}) custom-call(s32[7680]{0:T(1024)} %get-tuple-element.414.tok_ref, f32[3072,1536]{1,0:T(8,128)} %convert_element_type.299.refs_0_, f32[3072,128]{1,0:T(8,128)} %pad.33.refs_1_), custom_call_target="tpu_custom_call" | custom-call | tf_op jit(solution)/shard_map/pallas_call | solution.py:156
  870.1 27.7 %fusion.251 = f32[10,768,512]{1,2,0:T(8,128)} fusion(bf16[10,768,1536]{2,1,0:T(8,128)(2,1)} %bitcast.590, bf16[10,1536,512]{2,1,0:T(8,128)(2,1)} %all-gather.15.cloned.1.call-done), kind=kOutput, calls=%fused_computation.404 | convolution fusion | flops 12079595520 | bytes 55050240 | tf_op jit(solution)/shard_map/ecd,edf->ecf/dot_general | solution.py:409
  897.8 32.7 %multiply_convert_fusion.3 = (bf16[10,768,512]{1,2,0:T(8,128)(2,1)}, f32[10,768,512]{1,2,0:T(8,128)}) fusion(f32[10,768]{1,0:T(8,128)S(1)} %broadcast_select_fusion, f32[10,768,512]{1,2,0:T(8,128)} %fusion.251, bf16[10,768,1536]{2,1,0:T(8,128)(2,1)} %bitcast.591, bf16[10,1536,512]{2,1,0:T(8,128)(2,1)} %all-gather.17.cloned.1.call-done), kind=kOutput, calls=%fused_computation.56 | convolution fusion | flops 12107120640 | bytes 78673920 | tf_op jit(solution)/shard_map/ecd,edf->ecf/dot_general | solution.py:410
  930.5 27.2 %fusion.252 = f32[10,768,1536]{2,1,0:T(8,128)} fusion(bf16[10,768,512]{1,2,0:T(8,128)(2,1)} %get-tuple-element.236, bf16[10,512,1536]{1,2,0:T(8,128)(2,1)} %all-gather.23.cloned.1.call-done), kind=kOutput, calls=%fused_computation.405 | convolution fusion | flops 12079595520 | bytes 70778880 | tf_op jit(solution)/shard_map/ecf,efd->ecd/dot_general | solution.py:413
  957.7 68.0 %shard_map.249 = f32[3072,1536]{1,0:T(8,128)} custom-call(s32[7680]{0:T(1024)} %get-tuple-element.414.tok_ref, f32[7680,1536]{1,0:T(8,128)} %bitcast.521), custom_call_target="tpu_custom_call" | custom-call | tf_op jit(solution)/shard_map/pallas_call | solution.py:211
  1025.8 12.9 fusion.40.refs_0_
  1038.7 22.9 %all_gather.62 = bf16[192,2560]{1,0:T(8,128)(2,1)} all-gather(bf16[192,640]{1,0:T(8,128)(2,1)S(1)} %pad_maximum_fusion.5), channel_id=1, replica_groups=mesh['dp'=8,'tensor'=4] {'tensor'}, dimensions={1}, use_global_device_ids=true | all-gather | bytes 1228800 | tf_op jit(solution)/shard_map/all_gather | solution.py:430
  1061.7 11.7 convert_element_type.308
  1073.5 43.8 %shard_map.250 = bf16[7680,1536]{1,0:T(8,128)(2,1)} custom-call(s32[7680]{0:T(1024)} %get-tuple-element.414.tok_ref, f32[3072,1536]{1,0:T(8,128)} %fusion.40.refs_0_), custom_call_target="tpu_custom_call" | custom-call | tf_op jit(solution)/shard_map/pallas_call | solution.py:156
  1117.3 35.2 %multiply_reduce_fusion = (f32[10,768]{1,0:T(8,128)S(1)}, bf16[10,768,512]{1,2,0:T(8,128)(2,1)}, bf16[10,768,512]{1,2,0:T(8,128)(2,1)}) fusion(f32[10,768,512]{1,2,0:T(8,128)} %get-tuple-element.437, f32[10,768,512]{1,2,0:T(8,128)} %fusion.251, f32[10,768]{1,0:T(8,128)S(1)} %broadcast_select_fusion, bf16[10,768,1536]{2,1,0:T(8,128)(2,1)} %bitcast.525, ...), kind=kOutput, calls=%fused_computation.53 | convolution fusion | flops 12146434048 | bytes 86568960 | tf_op jit(solution)/shard_map/ecd,efd->ecf/dot_general | solution.py:437
  1160.3 27.3 %fusion.253 = f32[10,768,1536]{2,1,0:T(8,128)} fusion(bf16[10,768,512]{1,2,0:T(8,128)(2,1)} %get-tuple-element.233, bf16[10,1536,512]{2,1,0:T(8,128)(2,1)} %all-gather.15.cloned.1.call-done), kind=kOutput, calls=%fused_computation.406 | convolution fusion | flops 12079595520 | bytes 70778880 | tf_op jit(solution)/shard_map/ecf,edf->ecd/dot_general | solution.py:445
  1187.5 34.1 %add_convert_fusion = bf16[10,768,1536]{2,1,0:T(8,128)(2,1)} fusion(f32[10,768,1536]{2,1,0:T(8,128)} %fusion.253, bf16[10,768,512]{1,2,0:T(8,128)(2,1)} %get-tuple-element.234, bf16[10,1536,512]{2,1,0:T(8,128)(2,1)} %all-gather.17.cloned.1.call-done), kind=kOutput, calls=%fused_computation | convolution fusion | flops 12103188480 | bytes 94371840 | tf_op jit(solution)/shard_map/ecf,edf->ecd/dot_general | solution.py:447
  1221.6 71.1 %shard_map.251 = (f32[3072,1536]{1,0:T(8,128)}, f32[3072,128]{1,0:T(8,128)}) custom-call(s32[7680]{0:T(1024)} %get-tuple-element.414.tok_ref, bf16[7680,1536]{1,0:T(8,128)(2,1)} %bitcast.524, f32[7680,128]{1,0:T(8,128)} %fusion.81.refs_1_), custom_call_target="tpu_custom_call" | custom-call | tf_op jit(solution)/shard_map/pallas_call | solution.py:211
  1299.0 14.3 add_convert_fusion.1
  1325.5 151.7 %reduce-scatter.18.cloned.1.call-done = bf16[768,1536]{1,0:T(8,128)(2,1)} async-done(((bf16[3072,1536]{1,0:T(8,128)(2,1)}), bf16[768,1536]{1,0:T(8,128)(2,1)}) %reduce-scatter.18.cloned.1.call-update) | async-done | bytes 2359312 | tf_op jit(solution)/shard_map/reduce_scatter | solution.py:480
  1494.8 22.8 %convolution_convert_fusion.1 = bf16[10,1536,512]{2,1,0:T(8,128)(2,1)} fusion(bf16[10,768,1536]{2,1,0:T(8,128)(2,1)} %bitcast.592, bf16[10,768,512]{1,2,0:T(8,128)(2,1)} %get-tuple-element.234), kind=kOutput, calls=%fused_computation.62 | convolution fusion | flops 12087459840 | bytes 47185920 | tf_op jit(solution)/shard_map/ecd,ecf->edf/dot_general | solution.py:463
  1517.6 8.3 convolution_convert_fusion.5
  1532.1 21.6 %convolution_convert_fusion.2 = bf16[10,1536,512]{2,1,0:T(8,128)(2,1)} fusion(bf16[10,768,1536]{2,1,0:T(8,128)(2,1)} %bitcast.593, bf16[10,768,512]{1,2,0:T(8,128)(2,1)} %get-tuple-element.233), kind=kOutput, calls=%fused_computation.63 | convolution fusion | flops 12087459840 | bytes 47185920 | tf_op jit(solution)/shard_map/ecd,ecf->edf/dot_general | solution.py:462
  1553.7 21.4 %convolution_convert_fusion = bf16[10,1536,512]{2,1,0:T(8,128)(2,1)} fusion(bf16[10,768,1536]{2,1,0:T(8,128)(2,1)} %bitcast.526, bf16[10,768,512]{1,2,0:T(8,128)(2,1)} %get-tuple-element.236), kind=kOutput, calls=%fused_computation.61 | convolution fusion | flops 12087459840 | bytes 47185920 | tf_op jit(solution)/shard_map/ecd,ecf->edf/dot_general | solution.py:464
  1575.1 10.7 all-to-all-done.1
  1634.3 11.9 fusion.17
  1646.1 13.4 fusion.19
  1665.6 15.8 fusion.9
  1681.5 17.4 fusion.11
  1703.7 26.6 %fusion.4 = (f32[2,3,512]{2,1,0:T(4,128)S(1)}, f32[2,2560,512,3]{2,1,3,0:T(8,128)}) fusion(f32[2,3,512,2560]{2,3,1,0:T(8,128)} %get-tuple-element.431, f32[2,3,512]{2,1,0:T(4,128)S(1)} %log_add_fusion.1, bf16[2560,2,64,1]{0,2,3,1:T(8,128)(2,1)S(1)} %bitcast.560, bf16[512,2,3,64]{0,3,2,1:T(8,128)(2,1)S(1)} %bitcast.537), kind=kOutput, calls=%fused_computation.13 | convolution fusion | flops 1030222848 | bytes 63987712 | tf_op jit(solution)/shard_map/qgrd,kgd->grqk/dot_general | solution.py:524
  1730.3 28.5 %fusion.6 = bf16[2,3,512,2560]{2,3,1,0:T(8,128)(2,1)} fusion(f32[2,2560,512,3]{2,1,3,0:T(8,128)} %get-tuple-element.447, f32[2,3,512,2560]{2,3,1,0:T(8,128)} %get-tuple-element.431, f32[2,3,512]{2,1,0:T(4,128)S(1)} %get-tuple-element.446, f32[2,3,512]{2,1,0:T(4,128)S(1)} %log_add_fusion.1), kind=kLoop, calls=%fused_computation.15 | loop fusion | flops 31457280 | bytes 78667776 | tf_op jit(solution)/shard_map/convert_element_type | solution.py:528
  1758.8 9.7 fusion.151
  1768.5 28.3 %fusion = (f32[2,3,512]{2,1,0:T(4,128)S(1)}, f32[2,3072,512,3]{2,1,3,0:T(8,128)}) fusion(f32[2,3,512,3072]{2,3,1,0:T(8,128)} %get-tuple-element.433, f32[2,3,512]{2,1,0:T(4,128)S(1)} %copy-done.68, bf16[3072,2,64,1]{0,2,3,1:T(8,128)(2,1)S(1)} %bitcast.528, bf16[512,2,3,64]{0,3,2,1:T(8,128)(2,1)S(1)} %bitcast.535), kind=kOutput, calls=%fused_computation.3 | convolution fusion | flops 1236268032 | bytes 76701696 | tf_op jit(solution)/shard_map/qgrd,kgd->grqk/dot_general | solution.py:524
  1796.8 31.5 %fusion.2 = bf16[2,3,512,3072]{2,3,1,0:T(8,128)(2,1)} fusion(f32[2,3072,512,3]{2,1,3,0:T(8,128)} %get-tuple-element.449, f32[2,3,512,3072]{2,3,1,0:T(8,128)} %get-tuple-element.433, f32[2,3,512]{2,1,0:T(4,128)S(1)} %get-tuple-element.448, f32[2,3,512]{2,1,0:T(4,128)S(1)} %copy-done.68), kind=kLoop, calls=%fused_computation.5 | loop fusion | flops 37748736 | bytes 94396416 | tf_op jit(solution)/shard_map/convert_element_type | solution.py:528
  1828.3 16.3 fusion.141
  1873.7 10.8 fusion.87
  1884.5 10.3 fusion.88
  1909.7 8.2 fusion.120
  1917.9 10.5 fusion.137
  1928.4 13.9 fusion.98
  1942.3 20.0 fusion.105
  1962.9 8.2 pad_maximum_fusion
  2004.9 33.8 %reduce-scatter.24.cloned.1.call-done = bf16[10,192,512]{2,1,0:T(8,128)(2,1)} async-done(((bf16[10,1536,512]{2,1,0:T(8,128)(2,1)}), bf16[10,192,512]{2,1,0:T(8,128)(2,1)}) %reduce-scatter.24.cloned.1.call-update) | async-done | bytes 1966096 | tf_op jit(solution)/shard_map/reduce_scatter | solution.py:293
  2042.8 24.3 %all-to-all-done.2 = bf16[4,768,640]{1,2,0:T(8,128)(2,1)} async-done(((bf16[4,768,640]{1,2,0:T(8,128)(2,1)}), bf16[4,768,640]{1,2,0:T(8,128)(2,1)}, u32[]{:S(2)}, u32[]{:S(2)}) %all-to-all-start.2) | async-done | bytes 3932192 | tf_op jit(solution)/shard_map/all_to_all | solution.py:555
  2067.0 11.4 fusion.255
  2088.1 13.3 all-reduce.6
  2101.5 9.8 all-reduce.7
  (528 shorter events, 373.5 us)
Async XLA Ops:
  7.2 192.6 %all-gather.11.cloned.1.call-start = ((), (), s32[]{:S(2)}) async-start(), calls=%async_computation.12 | async-start | bytes 11796480 | tf_op jit(solution)/shard_map/all_gather | solution.py:337
  27.0 173.5 %copy-start.89 = (bf16[384,192]{0,1:T(8,128)(2,1)S(1)}, bf16[384,192]{0,1:T(8,128)(2,1)}, u32[]{:S(2)}) copy-start(bf16[384,192]{0,1:T(8,128)(2,1)} %param.52) | copy-start | bytes 442372
  29.2 188.8 %copy-start.125 = (s32[1,1024]{1,0:T(1,128)S(1)}, s32[1,1024]{1,0:T(1,128)}, u32[]{:S(2)}) copy-start(s32[1,1024]{1,0:T(1,128)} %param.45) | copy-start | bytes 12292
  29.8 189.4 %copy-start.85 = (bf16[192,128]{1,0:T(8,128)(2,1)S(1)}, bf16[192,128]{1,0:T(8,128)(2,1)}, u32[]{:S(2)}) copy-start(bf16[192,128]{1,0:T(8,128)(2,1)} %param.50) | copy-start | bytes 147460
  29.8 199.0 %copy-start.83 = (bf16[192,128]{1,0:T(8,128)(2,1)S(1)}, bf16[192,128]{1,0:T(8,128)(2,1)}, u32[]{:S(2)}) copy-start(bf16[192,128]{1,0:T(8,128)(2,1)} %param.51) | copy-start | bytes 147460
  33.5 231.8 %all-gather.13.cloned.1.call-start = ((), (), s32[]{:S(2)}) async-start(), calls=%async_computation.13 | async-start | bytes 1327104 | tf_op jit(solution)/shard_map/all_gather | solution.py:324
  34.3 404.4 %all-gather.15.cloned.1.call-start = ((), (), s32[]{:S(2)}) async-start(), calls=%async_computation.14 | async-start | bytes 17694720 | tf_op jit(solution)/shard_map/all_gather | solution.py:341
  199.8 238.9 %all-gather.17.cloned.1.call-start = ((), (), s32[]{:S(2)}) async-start(), calls=%async_computation.15 | async-start | bytes 17694720 | tf_op jit(solution)/shard_map/all_gather | solution.py:342
  200.4 302.3 %all-gather.19.cloned.1.call-start = ((), (), s32[]{:S(2)}) async-start(), calls=%async_computation.16 | async-start | bytes 5308416 | tf_op jit(solution)/shard_map/all_gather | solution.py:330
  244.2 29.7 %copy-start.22 = (f32[3072,32]{0,1:T(8,128)}, f32[3072,32]{0,1:T(8,128)S(1)}, u32[]{:S(2)}) copy-start(f32[3072,32]{0,1:T(8,128)S(1)} %get-tuple-element.415) | copy-start | bytes 1179652
  244.3 29.7 %copy-start.24 = (f32[3072,32]{0,1:T(8,128)}, f32[3072,32]{0,1:T(8,128)S(1)}, u32[]{:S(2)}) copy-start(f32[3072,32]{0,1:T(8,128)S(1)} %get-tuple-element.416) | copy-start | bytes 1179652
  258.1 48.7 %copy-start.18 = (bf16[3072,128]{0,1:T(8,128)(2,1)}, bf16[3072,128]{0,1:T(8,128)(2,1)S(1)}, u32[]{:S(2)}) copy-start(bf16[3072,128]{0,1:T(8,128)(2,1)S(1)} %convolution_convert_fusion.4) | copy-start | bytes 2359300
  276.0 46.7 %copy-start.11 = (bf16[3072,2,32]{0,2,1:T(8,128)(2,1)}, bf16[3072,2,32]{0,2,1:T(8,128)(2,1)S(1)}, u32[]{:S(2)}) copy-start(bf16[3072,2,32]{0,2,1:T(8,128)(2,1)S(1)} %get-tuple-element.404) | copy-start | bytes 1179652
  276.0 152.7 %copy-start.9 = (bf16[3072,2,32]{0,2,1:T(8,128)(2,1)}, bf16[3072,2,32]{0,2,1:T(8,128)(2,1)S(1)}, u32[]{:S(2)}) copy-start(bf16[3072,2,32]{0,2,1:T(8,128)(2,1)S(1)} %get-tuple-element.403) | copy-start | bytes 1179652
  277.4 14.6 copy-start.35
  277.4 45.3 %copy-start.45 = (bf16[512,6,64]{0,2,1:T(8,128)(2,1)}, bf16[512,6,64]{0,2,1:T(8,128)(2,1)S(1)}, u32[]{:S(2)}) copy-start(bf16[512,6,64]{0,2,1:T(8,128)(2,1)S(1)} %get-tuple-element.402) | copy-start | bytes 1179652
  292.0 14.8 copy-start.103
  306.8 15.0 copy-start.105
  349.4 15.7 copy-start.109
  434.4 68.3 %copy-start.7 = (bf16[768,1536]{1,0:T(8,128)(2,1)S(1)}, bf16[768,1536]{1,0:T(8,128)(2,1)}, u32[]{:S(2)}) copy-start(bf16[768,1536]{1,0:T(8,128)(2,1)} %param.43) | copy-start | bytes 7077892
  438.7 59.4 %all-to-all-start = ((bf16[4,768,384]{2,1,0:T(8,128)(2,1)}), bf16[4,768,384]{2,1,0:T(8,128)(2,1)}, u32[]{:S(2)}, u32[]{:S(2)}) async-start(bf16[4,768,384]{2,1,0:T(8,128)(2,1)} %bitcast.60), calls=%async_computation | async-start | bytes 4718592 | tf_op jit(solution)/shard_map/all_to_all | solution.py:377
  443.3 235.9 %all-gather.21.cloned.1.call-start = ((), (), s32[]{:S(2)}) async-start(), calls=%async_computation.17 | async-start | bytes 11796480 | tf_op jit(solution)/shard_map/all_gather | solution.py:381
  443.3 66.4 %copy-start.96 = (f32[1536]{0:T(1024)}, f32[1536]{0:T(1024)S(1)}, u32[]{:S(2)}) copy-start(f32[1536]{0:T(1024)S(1)} %convert_element_type.297) | copy-start | bytes 18436
  509.7 169.5 %copy-start.66 = (s32[3072,8]{0,1:T(8,128)S(1)}, s32[3072,8]{0,1:T(8,128)}, u32[]{:S(2)}) copy-start(s32[3072,8]{0,1:T(8,128)} %param.46) | copy-start | bytes 294916
  509.7 170.7 %copy-start.101 = (f32[768]{0:T(1024)}, f32[768]{0:T(1024)S(1)}, u32[]{:S(2)}) copy-start(f32[768]{0:T(1024)S(1)} %add_rsqrt_fusion) | copy-start | bytes 9220
  511.9 168.5 %copy-start.99 = (s32[1,24576]{1,0:T(1,128)S(1)}, s32[1,24576]{1,0:T(1,128)}, u32[]{:S(2)}) copy-start(s32[1,24576]{1,0:T(1,128)} %param.47) | copy-start | bytes 294916
  513.8 250.8 %all-gather.23.cloned.1.call-start = ((), (), s32[]{:S(2)}) async-start(), calls=%async_computation.18 | async-start | bytes 17694720 | tf_op jit(solution)/shard_map/all_gather | solution.py:383
  679.2 346.6 %all-gather.25.cloned.1.call-start = ((), (), s32[]{:S(2)}) async-start(), calls=%async_computation.19 | async-start | bytes 11796480 | tf_op jit(solution)/shard_map/all_gather | solution.py:418
  714.1 51.3 %copy-start.126 = (bf16[192,40]{0,1:T(8,128)(2,1)S(1)}, bf16[192,40]{0,1:T(8,128)(2,1)}, u32[]{:S(2)}) copy-start(bf16[192,40]{0,1:T(8,128)(2,1)} %param.54) | copy-start | bytes 46084
  764.6 534.4 %all-gather.27.cloned.1.call-start = ((), (), s32[]{:S(2)}) async-start(), calls=%async_computation.20 | async-start | bytes 8847360 | tf_op jit(solution)/shard_map/all_gather | solution.py:429
  775.0 28.5 %copy-start.62 = (bf16[1536,40]{0,1:T(8,128)(2,1)}, bf16[1536,40]{0,1:T(8,128)(2,1)S(1)}, u32[]{:S(2)}) copy-start(bf16[1536,40]{0,1:T(8,128)(2,1)S(1)} %reshape.1188) | copy-start | bytes 368644
  790.7 73.2 %copy-start.92 = (s32[7680]{0:T(1024)}, s32[7680]{0:T(1024)S(1)}, u32[]{:S(2)}) copy-start(s32[7680]{0:T(1024)S(1)} %get-tuple-element.413) | copy-start | bytes 92164
  810.9 53.0 %copy-start.81 = (f32[3072]{0:T(1024)}, f32[3072]{0:T(1024)S(1)}, u32[]{:S(2)}) copy-start(f32[3072]{0:T(1024)S(1)} %get-tuple-element.378) | copy-start | bytes 36868
  811.4 52.5 %copy-start.16 = (f32[3072,8]{1,0:T(8,128)}, f32[3072,8]{1,0:T(8,128)S(1)}, u32[]{:S(2)}) copy-start(f32[3072,8]{1,0:T(8,128)S(1)} %copy.585) | copy-start | bytes 294916
  1061.6 251.6 %reduce-scatter.16.cloned.1.call-start = ((), (), s32[]{:S(2)}) async-start(), calls=%async_computation.21 | async-start | bytes 11796480 | tf_op jit(solution)/shard_map/reduce_scatter | solution.py:432
  1073.4 403.8 %reduce-scatter.18.cloned.1.call-start = ((), (), s32[]{:S(2)}) async-start(), calls=%async_computation.22 | async-start | bytes 11796480 | tf_op jit(solution)/shard_map/reduce_scatter | solution.py:480
  1117.3 35.2 %copy-start.93 = (s32[7680]{0:T(1024)S(1)}, s32[7680]{0:T(1024)}, u32[]{:S(2)}) copy-start(s32[7680]{0:T(1024)} %copy-done.92) | copy-start | bytes 92164
  1221.6 71.2 %copy-start.17 = (f32[3072,8]{1,0:T(8,128)S(1)}, f32[3072,8]{1,0:T(8,128)}, u32[]{:S(2)}) copy-start(f32[3072,8]{1,0:T(8,128)} %copy-done.16) | copy-start | bytes 294916
  1221.6 71.2 %copy-start.82 = (f32[3072]{0:T(1024)S(1)}, f32[3072]{0:T(1024)}, u32[]{:S(2)}) copy-start(f32[3072]{0:T(1024)} %copy-done.81) | copy-start | bytes 36868
  1317.8 159.5 %copy-start.97 = (f32[1536]{0:T(1024)S(1)}, f32[1536]{0:T(1024)}, u32[]{:S(2)}) copy-start(f32[1536]{0:T(1024)} %copy-done.96) | copy-start | bytes 18436
  1317.8 159.4 %copy-start.102 = (f32[768]{0:T(1024)S(1)}, f32[768]{0:T(1024)}, u32[]{:S(2)}) copy-start(f32[768]{0:T(1024)} %copy-done.101) | copy-start | bytes 9220
  1317.8 269.3 %reduce-scatter.26.cloned.1.call-start = ((), (), s32[]{:S(2)}) async-start(), calls=%async_computation.26 | async-start | bytes 5308416 | tf_op jit(solution)/shard_map/reduce_scatter | solution.py:507
  1325.5 156.3 %copy-start.26 = (bf16[768,1536]{1,0:T(8,128)(2,1)S(1)}, bf16[768,1536]{1,0:T(8,128)(2,1)}, u32[]{:S(2)}) copy-start(bf16[768,1536]{1,0:T(8,128)(2,1)} %param.44) | copy-start | bytes 7077892
  1527.6 58.3 %all-to-all-start.1 = ((bf16[768,4,384]{2,0,1:T(8,128)(2,1)}), bf16[768,4,384]{2,0,1:T(8,128)(2,1)S(1)}, u32[]{:S(2)}, u32[]{:S(2)}) async-start(bf16[768,4,384]{2,0,1:T(8,128)(2,1)} %bitcast.534), calls=%async_computation.3 | async-start | bytes 4718592 | tf_op jit(solution)/shard_map/all_to_all | solution.py:491
  1532.1 460.1 %reduce-scatter.28.cloned.1.call-start = ((), (), s32[]{:S(2)}) async-start(), calls=%async_computation.27 | async-start | bytes 811008
  1587.1 407.9 %reduce-scatter.30.cloned.1.call-start = ((), (), s32[]{:S(2)}) async-start(), calls=%async_computation.28 | async-start | bytes 983040
  1589.6 407.2 %reduce-scatter.20.cloned.1.call-start = ((), (), s32[]{:S(2)}) async-start(), calls=%async_computation.23 | async-start | bytes 17694720 | tf_op jit(solution)/shard_map/reduce_scatter | solution.py:290
  1590.2 410.8 %reduce-scatter.22.cloned.1.call-start = ((), (), s32[]{:S(2)}) async-start(), calls=%async_computation.24 | async-start | bytes 17694720 | tf_op jit(solution)/shard_map/reduce_scatter | solution.py:291
  1595.8 19.7 copy-start.47
  1598.4 35.8 %copy-start.39 = (bf16[512,384]{0,1:T(8,128)(2,1)}, bf16[512,384]{0,1:T(8,128)(2,1)S(1)}, u32[]{:S(2)}) copy-start(bf16[512,384]{0,1:T(8,128)(2,1)S(1)} %copy.604) | copy-start | bytes 1179652
  1599.8 65.9 %copy-start.37 = (bf16[512,384]{0,1:T(8,128)(2,1)}, bf16[512,384]{0,1:T(8,128)(2,1)S(1)}, u32[]{:S(2)}) copy-start(bf16[512,384]{0,1:T(8,128)(2,1)S(1)} %copy.606) | copy-start | bytes 1179652
  1600.0 103.7 %copy-start.30 = (bf16[512,384]{0,1:T(8,128)(2,1)}, bf16[512,384]{0,1:T(8,128)(2,1)S(1)}, u32[]{:S(2)}) copy-start(bf16[512,384]{0,1:T(8,128)(2,1)S(1)} %copy.608) | copy-start | bytes 1179652
  1600.2 168.3 %copy-start.28 = (bf16[512,384]{0,1:T(8,128)(2,1)}, bf16[512,384]{0,1:T(8,128)(2,1)S(1)}, u32[]{:S(2)}) copy-start(bf16[512,384]{0,1:T(8,128)(2,1)S(1)} %copy.610) | copy-start | bytes 1179652
  1600.2 438.5 %reduce-scatter.24.cloned.1.call-start = ((), (), s32[]{:S(2)}) async-start(), calls=%async_computation.25 | async-start | bytes 17694720 | tf_op jit(solution)/shard_map/reduce_scatter | solution.py:293
  1601.3 14.2 slice-start.6
  1601.3 14.2 slice-start.7
  1828.3 16.4 copy-start.23
  1828.3 16.4 copy-start.25
  1855.2 14.5 slice-start.9
  1973.5 93.5 %all-to-all-start.2 = ((bf16[4,768,640]{1,2,0:T(8,128)(2,1)}), bf16[4,768,640]{1,2,0:T(8,128)(2,1)}, u32[]{:S(2)}, u32[]{:S(2)}) async-start(bf16[4,768,640]{1,2,0:T(8,128)(2,1)} %copy.624), calls=%async_computation.4 | async-start | bytes 7864320 | tf_op jit(solution)/shard_map/all_to_all | solution.py:555
  1978.4 143.7 %reduce-scatter.32.cloned.1.call-start = ((), (), s32[]{:S(2)}) async-start(), calls=%async_computation.29 | async-start | bytes 2211840
  2067.0 15.6 copy-start.128
  2067.0 17.5 copy-start.95
  2067.0 17.5 copy-start.124
  (98 other events, 583.3 us)
Sparse Core Ops, SparseCore 0:
  33.7 166.1 all-gather.10
  201.7 22.0 all-gather.12
  225.8 86.2 all-gather.14
  313.8 85.2 all-gather.16
  400.8 38.7 all-gather.18
  513.9 165.2 all-gather.20
  681.0 83.4 all-gather.22
  766.1 166.7 all-gather.24
  1061.8 50.6 all-gather.26
  1114.7 161.1 reduce-scatter.15
  1317.9 159.2 reduce-scatter.17
  1494.9 54.7 reduce-scatter.25
  1587.2 95.3 reduce-scatter.27
  1684.7 22.1 reduce-scatter.29
  1710.3 106.8 reduce-scatter.19
  1820.6 107.3 reduce-scatter.21
  1931.4 107.3 reduce-scatter.23
  2082.7 39.3 reduce-scatter.31

commit v9 on v8

--- a/solution.py
+++ b/solution.py
@@ -494,8 +494,13 @@
     )
     expert_grads = reduce_experts(expert_parts)
     router_and_gain = lax.psum_scatter(
-        jnp.concatenate([router_part, gain_two_grad[:, None]], axis=1),
-        ("dp", "tensor"),
+        lax.psum_scatter(
+            jnp.concatenate([router_part, gain_two_grad[:, None]], axis=1),
+            "dp",
+            scatter_dimension=0,
+            tiled=True,
+        ),
+        "tensor",
         scatter_dimension=0,
         tiled=True,
     )

time: 2140 us -> 2200 us (1.028)
  waiting for transfers between devices: 655 us -> 714 us
    reduce_scatter x1, waiting for transfers between devices: 0.02 us -> 57.2 us  [local(): lax.psum_scatter(output_part, 'dp', scatter_dimension=1, tiled=True)]
    all_to_all x1, waiting for transfers between devices: 24.3 us -> 58.2 us  [local(): lax.all_to_all(projection_grad, 'tensor', 0, 1, tiled=True)]
    reduce_scatter x1, waiting for transfers between devices: 33.8 us -> 0.01 us  [reduce_experts(): lax.psum_scatter(grads[2], 'dp', scatter_dimension=1, tiled=True)]
    unnamed x21 -> x23, waiting for transfers between devices: 5.08 us -> 29.3 us
    reduce_scatter x1, waiting for transfers between devices: 152 us -> 130 us  [local(): lax.psum_scatter(mixture_grad_low, 'tensor', scatter_dimension=0, tiled=T...]
    unnamed x306 -> x308, local copies, waits for them, and re-layouts: 49.9 us -> 48 us
  transfers between devices with their start and end apart: 21 -> 22, of which waited for: 9 -> 10; matrix products, arithmetic and copies ran while one was open for 47% -> 46% of each run, Pallas kernels for 11% -> 11%
where the time goes in v9:
time: 2200 us; the launch traced here: 2190 us
  waiting for transfers between devices  714 us (32%)
  matrix products  701 us (32%)
  other arithmetic  307 us (14%)
  Pallas kernels  235 us (11%)
  blocking collectives  107 us (5%)
  local copies, waits for them, and re-layouts  95.8 us (4%)
    all_gather x1, waiting for transfers between devices, local(): lax.all_gather(normed_shard.astype(jnp.bfloat16), 'tensor', axis=0, tiled...  165 us
    all_gather x1, waiting for transfers between devices, local(): lax.all_gather(normed_two.astype(jnp.bfloat16), 'tensor', axis=0, tiled=T...  165 us
    pallas_call x2, Pallas kernels, combine_rows(): pl.pallas_call(_combine_rows_kernel, grid_spec=pltpu.PrefetchScalarGridSp...  140 us
    reduce_scatter x1, waiting for transfers between devices, local(): lax.psum_scatter(mixture_grad_low, 'tensor', scatter_dimension=0, tiled=T...  130 us
    convert_element_type x6, other arithmetic, local(): score_grad = (soft_full * (weight_grad - delta)).astype(jnp.bfloat16)  112 us
    dot_general x6, matrix products, local(): jnp.einsum('qgrd,kgd->grqk', out_block, value_low[:key_end], preferred_el...  99.4 us
    pallas_call x2, Pallas kernels, gather_rows(): pl.pallas_call(_gather_rows_kernel, grid_spec=pltpu.PrefetchScalarGridSpe...  94.5 us
    all_to_all x1, waiting for transfers between devices, local(): lax.all_to_all(projection_grad, 'tensor', 0, 1, tiled=True)  58.2 us
  transfers between devices with their start and end apart: 22, of which 10 were waited for; matrix products, arithmetic and copies ran while one was open for 46% of the time, Pallas kernels for 11%

profile of v9, /device:TPU:0, one launch (start us, length us, event | category | flops | bytes accessed | tf_op | source)
XLA Modules:
  0.0 2194.1 jit_solution(11931240061693737357)
XLA Ops:
  10.9 16.0 all-reduce.8
  34.3 165.5 %all-gather.11.cloned.1.call-done = bf16[3072,1536]{1,0:T(8,128)(2,1)} async-done(((bf16[768,1536]{1,0:T(8,128)(2,1)}), bf16[3072,1536]{1,0:T(8,128)(2,1)}) %all-gather.11.cloned.1.call-update) | async-done | bytes 9437200 | tf_op jit(solution)/shard_map/all_gather | solution.py:337
  200.5 17.5 all_gather.55
  219.3 9.5 all_gather.51
  228.8 9.5 all_gather.50
  265.4 8.6 fusion.249
  277.5 14.6 fusion.246
  292.1 14.8 fusion.3
  307.0 14.9 fusion.157
  322.8 14.2 fusion.245
  337.0 12.6 fusion.8
  349.6 15.7 fusion.156
  380.4 11.0 fusion.155
  392.3 8.3 fusion.243
  400.7 8.9 fusion.22
  409.6 8.4 fusion.154
  443.5 54.7 %all-to-all-done = bf16[4,768,384]{2,1,0:T(8,128)(2,1)} async-done(((bf16[4,768,384]{2,1,0:T(8,128)(2,1)}), bf16[4,768,384]{2,1,0:T(8,128)(2,1)}, u32[]{:S(2)}, u32[]{:S(2)}) %all-to-all-start) | async-done | bytes 2359328 | tf_op jit(solution)/shard_map/all_to_all | solution.py:377
  513.8 165.4 %all-gather.21.cloned.1.call-done = bf16[3072,1536]{1,0:T(8,128)(2,1)} async-done(((bf16[768,1536]{1,0:T(8,128)(2,1)}), bf16[3072,1536]{1,0:T(8,128)(2,1)}) %all-gather.21.cloned.1.call-update) | async-done | bytes 9437200 | tf_op jit(solution)/shard_map/all_gather | solution.py:381
  681.3 14.5 fusion.101
  721.1 43.5 %all-gather.23.cloned.1.call-done = bf16[10,512,1536]{1,2,0:T(8,128)(2,1)} async-done(((bf16[10,512,192]{1,2,0:T(8,128)(2,1)}), bf16[10,512,1536]{1,2,0:T(8,128)(2,1)}) %all-gather.23.cloned.1.call-update) | async-done | bytes 15728656 | tf_op jit(solution)/shard_map/all_gather | solution.py:383
  765.5 9.4 all-gather
  790.9 12.8 convert_element_type.299.refs_0_
  813.3 50.7 %shard_map.248 = (bf16[7680,1536]{1,0:T(8,128)(2,1)}, f32[7680,128]{1,0:T(8,128)}) custom-call(s32[7680]{0:T(1024)} %get-tuple-element.414.tok_ref, f32[3072,1536]{1,0:T(8,128)} %convert_element_type.299.refs_0_, f32[3072,128]{1,0:T(8,128)} %pad.33.refs_1_), custom_call_target="tpu_custom_call" | custom-call | tf_op jit(solution)/shard_map/pallas_call | solution.py:156
  870.2 27.7 %fusion.251 = f32[10,768,512]{1,2,0:T(8,128)} fusion(bf16[10,768,1536]{2,1,0:T(8,128)(2,1)} %bitcast.591, bf16[10,1536,512]{2,1,0:T(8,128)(2,1)} %all-gather.15.cloned.1.call-done), kind=kOutput, calls=%fused_computation.404 | convolution fusion | flops 12079595520 | bytes 55050240 | tf_op jit(solution)/shard_map/ecd,edf->ecf/dot_general | solution.py:409
  897.9 32.7 %multiply_convert_fusion.3 = (bf16[10,768,512]{1,2,0:T(8,128)(2,1)}, f32[10,768,512]{1,2,0:T(8,128)}) fusion(f32[10,768]{1,0:T(8,128)S(1)} %broadcast_select_fusion, f32[10,768,512]{1,2,0:T(8,128)} %fusion.251, bf16[10,768,1536]{2,1,0:T(8,128)(2,1)} %bitcast.592, bf16[10,1536,512]{2,1,0:T(8,128)(2,1)} %all-gather.17.cloned.1.call-done), kind=kOutput, calls=%fused_computation.56 | convolution fusion | flops 12107120640 | bytes 78673920 | tf_op jit(solution)/shard_map/ecd,edf->ecf/dot_general | solution.py:410
  930.7 27.2 %fusion.252 = f32[10,768,1536]{2,1,0:T(8,128)} fusion(bf16[10,768,512]{1,2,0:T(8,128)(2,1)} %get-tuple-element.236, bf16[10,512,1536]{1,2,0:T(8,128)(2,1)} %all-gather.23.cloned.1.call-done), kind=kOutput, calls=%fused_computation.405 | convolution fusion | flops 12079595520 | bytes 70778880 | tf_op jit(solution)/shard_map/ecf,efd->ecd/dot_general | solution.py:413
  957.9 68.5 %shard_map.249 = f32[3072,1536]{1,0:T(8,128)} custom-call(s32[7680]{0:T(1024)} %get-tuple-element.414.tok_ref, f32[7680,1536]{1,0:T(8,128)} %bitcast.522), custom_call_target="tpu_custom_call" | custom-call | tf_op jit(solution)/shard_map/pallas_call | solution.py:211
  1026.5 13.0 fusion.40.refs_0_
  1039.4 21.1 all_gather.62
  1060.6 11.7 convert_element_type.308
  1072.4 43.8 %shard_map.250 = bf16[7680,1536]{1,0:T(8,128)(2,1)} custom-call(s32[7680]{0:T(1024)} %get-tuple-element.414.tok_ref, f32[3072,1536]{1,0:T(8,128)} %fusion.40.refs_0_), custom_call_target="tpu_custom_call" | custom-call | tf_op jit(solution)/shard_map/pallas_call | solution.py:156
  1116.2 35.2 %multiply_reduce_fusion = (f32[10,768]{1,0:T(8,128)S(1)}, bf16[10,768,512]{1,2,0:T(8,128)(2,1)}, bf16[10,768,512]{1,2,0:T(8,128)(2,1)}) fusion(f32[10,768,512]{1,2,0:T(8,128)} %get-tuple-element.437, f32[10,768,512]{1,2,0:T(8,128)} %fusion.251, f32[10,768]{1,0:T(8,128)S(1)} %broadcast_select_fusion, bf16[10,768,1536]{2,1,0:T(8,128)(2,1)} %bitcast.526, ...), kind=kOutput, calls=%fused_computation.53 | convolution fusion | flops 12146434048 | bytes 86568960 | tf_op jit(solution)/shard_map/ecd,efd->ecf/dot_general | solution.py:437
  1159.2 27.3 %fusion.253 = f32[10,768,1536]{2,1,0:T(8,128)} fusion(bf16[10,768,512]{1,2,0:T(8,128)(2,1)} %get-tuple-element.233, bf16[10,1536,512]{2,1,0:T(8,128)(2,1)} %all-gather.15.cloned.1.call-done), kind=kOutput, calls=%fused_computation.406 | convolution fusion | flops 12079595520 | bytes 70778880 | tf_op jit(solution)/shard_map/ecf,edf->ecd/dot_general | solution.py:445
  1186.5 34.1 %add_convert_fusion = bf16[10,768,1536]{2,1,0:T(8,128)(2,1)} fusion(f32[10,768,1536]{2,1,0:T(8,128)} %fusion.253, bf16[10,768,512]{1,2,0:T(8,128)(2,1)} %get-tuple-element.234, bf16[10,1536,512]{2,1,0:T(8,128)(2,1)} %all-gather.17.cloned.1.call-done), kind=kOutput, calls=%fused_computation | convolution fusion | flops 12103188480 | bytes 94371840 | tf_op jit(solution)/shard_map/ecf,edf->ecd/dot_general | solution.py:447
  1220.6 71.8 %shard_map.251 = (f32[3072,1536]{1,0:T(8,128)}, f32[3072,128]{1,0:T(8,128)}) custom-call(s32[7680]{0:T(1024)} %get-tuple-element.414.tok_ref, bf16[7680,1536]{1,0:T(8,128)(2,1)} %bitcast.525, f32[7680,128]{1,0:T(8,128)} %fusion.81.refs_1_), custom_call_target="tpu_custom_call" | custom-call | tf_op jit(solution)/shard_map/pallas_call | solution.py:211
  1298.6 14.3 add_convert_fusion.1
  1324.7 21.8 convolution_convert_fusion.1
  1346.5 129.5 %reduce-scatter.21.cloned.1.call-done = bf16[768,1536]{1,0:T(8,128)(2,1)} async-done(((bf16[3072,1536]{1,0:T(8,128)(2,1)}), bf16[768,1536]{1,0:T(8,128)(2,1)}) %reduce-scatter.21.cloned.1.call-update) | async-done | bytes 2359312 | tf_op jit(solution)/shard_map/reduce_scatter | solution.py:480
  1496.8 21.7 convolution_convert_fusion.2
  1518.5 21.5 convolution_convert_fusion
  1540.0 10.6 all-to-all-done.1
  1551.9 9.1 convolution_convert_fusion.3
  1561.0 25.0 %reduce-scatter.31.cloned.1.call-done = f32[192,41]{1,0:T(8,128)} async-done(((f32[1536,41]{1,0:T(8,128)}), f32[192,41]{1,0:T(8,128)}) %reduce-scatter.31.cloned.1.call-update) | async-done | bytes 31504
  1586.0 57.2 %reduce-scatter.29.cloned.1.call-done = bf16[1536,192]{0,1:T(8,128)(2,1)} async-done(((bf16[1536,1536]{0,1:T(8,128)(2,1)}), bf16[1536,192]{0,1:T(8,128)(2,1)}) %reduce-scatter.29.cloned.1.call-update) | async-done | bytes 589840 | tf_op jit(solution)/shard_map/reduce_scatter | solution.py:512
  1690.6 17.0 fusion.17
  1707.6 15.4 fusion.19
  1729.2 17.6 fusion.9
  1746.9 17.5 fusion.11
  1769.2 23.3 %fusion.4 = (f32[2,3,512]{2,1,0:T(4,128)S(1)}, f32[2,2560,512,3]{2,1,3,0:T(8,128)}) fusion(f32[2,3,512,2560]{2,3,1,0:T(8,128)} %get-tuple-element.431, f32[2,3,512]{2,1,0:T(4,128)S(1)} %log_add_fusion.1, bf16[2560,2,64,1]{0,2,3,1:T(8,128)(2,1)S(1)} %bitcast.561, bf16[512,2,3,64]{0,3,2,1:T(8,128)(2,1)S(1)} %bitcast.538), kind=kOutput, calls=%fused_computation.13 | convolution fusion | flops 1030222848 | bytes 63987712 | tf_op jit(solution)/shard_map/qgrd,kgd->grqk/dot_general | solution.py:529
  1792.5 32.8 %fusion.6 = bf16[2,3,512,2560]{2,3,1,0:T(8,128)(2,1)} fusion(f32[2,2560,512,3]{2,1,3,0:T(8,128)} %get-tuple-element.447, f32[2,3,512,2560]{2,3,1,0:T(8,128)} %get-tuple-element.431, f32[2,3,512]{2,1,0:T(4,128)S(1)} %get-tuple-element.446, f32[2,3,512]{2,1,0:T(4,128)S(1)} %log_add_fusion.1), kind=kLoop, calls=%fused_computation.15 | loop fusion | flops 31457280 | bytes 78667776 | tf_op jit(solution)/shard_map/convert_element_type | solution.py:533
  1825.3 9.2 fusion.151
  1834.6 28.8 %fusion = (f32[2,3,512]{2,1,0:T(4,128)S(1)}, f32[2,3072,512,3]{2,1,3,0:T(8,128)}) fusion(f32[2,3,512,3072]{2,3,1,0:T(8,128)} %get-tuple-element.433, f32[2,3,512]{2,1,0:T(4,128)S(1)} %copy-done.67, bf16[3072,2,64,1]{0,2,3,1:T(8,128)(2,1)S(1)} %bitcast.529, bf16[512,2,3,64]{0,3,2,1:T(8,128)(2,1)S(1)} %bitcast.536), kind=kOutput, calls=%fused_computation.3 | convolution fusion | flops 1236268032 | bytes 76701696 | tf_op jit(solution)/shard_map/qgrd,kgd->grqk/dot_general | solution.py:529
  1863.4 32.7 %fusion.2 = bf16[2,3,512,3072]{2,3,1,0:T(8,128)(2,1)} fusion(f32[2,3072,512,3]{2,1,3,0:T(8,128)} %get-tuple-element.449, f32[2,3,512,3072]{2,3,1,0:T(8,128)} %get-tuple-element.433, f32[2,3,512]{2,1,0:T(4,128)S(1)} %get-tuple-element.448, f32[2,3,512]{2,1,0:T(4,128)S(1)} %copy-done.67), kind=kLoop, calls=%fused_computation.5 | loop fusion | flops 37748736 | bytes 94396416 | tf_op jit(solution)/shard_map/convert_element_type | solution.py:533
  1896.2 10.9 fusion.141
  1926.8 9.4 fusion.130
  1940.2 11.6 fusion.87
  1951.8 10.6 fusion.88
  1984.3 10.5 fusion.137
  1994.8 13.4 fusion.98
  2008.2 15.4 fusion.105
  2069.8 58.2 %all-to-all-done.2 = bf16[4,768,640]{1,2,0:T(8,128)(2,1)} async-done(((bf16[4,768,640]{1,2,0:T(8,128)(2,1)}), bf16[4,768,640]{1,2,0:T(8,128)(2,1)}, u32[]{:S(2)}, u32[]{:S(2)}) %all-to-all-start.2) | async-done | bytes 3932192 | tf_op jit(solution)/shard_map/all_to_all | solution.py:560
  2128.0 11.4 fusion.255
  2149.1 14.6 all-reduce.6
  2163.8 9.8 all-reduce.7
  (534 shorter events, 379.6 us)
Async XLA Ops:
  7.2 192.6 %all-gather.11.cloned.1.call-start = ((), (), s32[]{:S(2)}) async-start(), calls=%async_computation.13 | async-start | bytes 11796480 | tf_op jit(solution)/shard_map/all_gather | solution.py:337
  27.0 173.5 %copy-start.88 = (bf16[384,192]{0,1:T(8,128)(2,1)S(1)}, bf16[384,192]{0,1:T(8,128)(2,1)}, u32[]{:S(2)}) copy-start(bf16[384,192]{0,1:T(8,128)(2,1)} %param.52) | copy-start | bytes 442372
  29.2 188.8 %copy-start.124 = (s32[1,1024]{1,0:T(1,128)S(1)}, s32[1,1024]{1,0:T(1,128)}, u32[]{:S(2)}) copy-start(s32[1,1024]{1,0:T(1,128)} %param.45) | copy-start | bytes 12292
  29.8 189.4 %copy-start.84 = (bf16[192,128]{1,0:T(8,128)(2,1)S(1)}, bf16[192,128]{1,0:T(8,128)(2,1)}, u32[]{:S(2)}) copy-start(bf16[192,128]{1,0:T(8,128)(2,1)} %param.50) | copy-start | bytes 147460
  29.8 199.0 %copy-start.82 = (bf16[192,128]{1,0:T(8,128)(2,1)S(1)}, bf16[192,128]{1,0:T(8,128)(2,1)}, u32[]{:S(2)}) copy-start(bf16[192,128]{1,0:T(8,128)(2,1)} %param.51) | copy-start | bytes 147460
  33.5 231.8 %all-gather.13.cloned.1.call-start = ((), (), s32[]{:S(2)}) async-start(), calls=%async_computation.14 | async-start | bytes 1327104 | tf_op jit(solution)/shard_map/all_gather | solution.py:324
  34.3 404.6 %all-gather.15.cloned.1.call-start = ((), (), s32[]{:S(2)}) async-start(), calls=%async_computation.15 | async-start | bytes 17694720 | tf_op jit(solution)/shard_map/all_gather | solution.py:341
  199.8 239.0 %all-gather.17.cloned.1.call-start = ((), (), s32[]{:S(2)}) async-start(), calls=%async_computation.16 | async-start | bytes 17694720 | tf_op jit(solution)/shard_map/all_gather | solution.py:342
  200.4 302.4 %all-gather.19.cloned.1.call-start = ((), (), s32[]{:S(2)}) async-start(), calls=%async_computation.17 | async-start | bytes 5308416 | tf_op jit(solution)/shard_map/all_gather | solution.py:330
  244.2 29.7 %copy-start.21 = (f32[3072,32]{0,1:T(8,128)}, f32[3072,32]{0,1:T(8,128)S(1)}, u32[]{:S(2)}) copy-start(f32[3072,32]{0,1:T(8,128)S(1)} %get-tuple-element.415) | copy-start | bytes 1179652
  244.3 29.7 %copy-start.23 = (f32[3072,32]{0,1:T(8,128)}, f32[3072,32]{0,1:T(8,128)S(1)}, u32[]{:S(2)}) copy-start(f32[3072,32]{0,1:T(8,128)S(1)} %get-tuple-element.416) | copy-start | bytes 1179652
  258.1 48.8 %copy-start.18 = (bf16[3072,128]{0,1:T(8,128)(2,1)}, bf16[3072,128]{0,1:T(8,128)(2,1)S(1)}, u32[]{:S(2)}) copy-start(bf16[3072,128]{0,1:T(8,128)(2,1)S(1)} %convolution_convert_fusion.4) | copy-start | bytes 2359300
  276.0 46.8 %copy-start.11 = (bf16[3072,2,32]{0,2,1:T(8,128)(2,1)}, bf16[3072,2,32]{0,2,1:T(8,128)(2,1)S(1)}, u32[]{:S(2)}) copy-start(bf16[3072,2,32]{0,2,1:T(8,128)(2,1)S(1)} %get-tuple-element.404) | copy-start | bytes 1179652
  276.0 152.8 %copy-start.9 = (bf16[3072,2,32]{0,2,1:T(8,128)(2,1)}, bf16[3072,2,32]{0,2,1:T(8,128)(2,1)S(1)}, u32[]{:S(2)}) copy-start(bf16[3072,2,32]{0,2,1:T(8,128)(2,1)S(1)} %get-tuple-element.403) | copy-start | bytes 1179652
  277.5 14.7 copy-start.35
  277.5 45.4 %copy-start.45 = (bf16[512,6,64]{0,2,1:T(8,128)(2,1)}, bf16[512,6,64]{0,2,1:T(8,128)(2,1)S(1)}, u32[]{:S(2)}) copy-start(bf16[512,6,64]{0,2,1:T(8,128)(2,1)S(1)} %get-tuple-element.402) | copy-start | bytes 1179652
  292.1 14.8 copy-start.102
  306.9 15.0 copy-start.104
  349.6 15.7 copy-start.108
  434.6 68.2 %copy-start.7 = (bf16[768,1536]{1,0:T(8,128)(2,1)S(1)}, bf16[768,1536]{1,0:T(8,128)(2,1)}, u32[]{:S(2)}) copy-start(bf16[768,1536]{1,0:T(8,128)(2,1)} %param.43) | copy-start | bytes 7077892
  438.9 59.3 %all-to-all-start = ((bf16[4,768,384]{2,1,0:T(8,128)(2,1)}), bf16[4,768,384]{2,1,0:T(8,128)(2,1)}, u32[]{:S(2)}, u32[]{:S(2)}) async-start(bf16[4,768,384]{2,1,0:T(8,128)(2,1)} %bitcast.60), calls=%async_computation | async-start | bytes 4718592 | tf_op jit(solution)/shard_map/all_to_all | solution.py:377
  443.4 235.8 %all-gather.21.cloned.1.call-start = ((), (), s32[]{:S(2)}) async-start(), calls=%async_computation.18 | async-start | bytes 11796480 | tf_op jit(solution)/shard_map/all_gather | solution.py:381
  443.5 66.3 %copy-start.95 = (f32[1536]{0:T(1024)}, f32[1536]{0:T(1024)S(1)}, u32[]{:S(2)}) copy-start(f32[1536]{0:T(1024)S(1)} %convert_element_type.297) | copy-start | bytes 18436
  509.7 169.6 %copy-start.65 = (s32[3072,8]{0,1:T(8,128)S(1)}, s32[3072,8]{0,1:T(8,128)}, u32[]{:S(2)}) copy-start(s32[3072,8]{0,1:T(8,128)} %param.46) | copy-start | bytes 294916
  509.7 170.7 %copy-start.100 = (f32[768]{0:T(1024)}, f32[768]{0:T(1024)S(1)}, u32[]{:S(2)}) copy-start(f32[768]{0:T(1024)S(1)} %add_rsqrt_fusion) | copy-start | bytes 9220
  511.9 168.6 %copy-start.98 = (s32[1,24576]{1,0:T(1,128)S(1)}, s32[1,24576]{1,0:T(1,128)}, u32[]{:S(2)}) copy-start(s32[1,24576]{1,0:T(1,128)} %param.47) | copy-start | bytes 294916
  513.8 250.8 %all-gather.23.cloned.1.call-start = ((), (), s32[]{:S(2)}) async-start(), calls=%async_computation.19 | async-start | bytes 17694720 | tf_op jit(solution)/shard_map/all_gather | solution.py:383
  679.2 347.2 %all-gather.25.cloned.1.call-start = ((), (), s32[]{:S(2)}) async-start(), calls=%async_computation.20 | async-start | bytes 11796480 | tf_op jit(solution)/shard_map/all_gather | solution.py:418
  714.1 51.4 %copy-start.125 = (bf16[192,40]{0,1:T(8,128)(2,1)S(1)}, bf16[192,40]{0,1:T(8,128)(2,1)}, u32[]{:S(2)}) copy-start(bf16[192,40]{0,1:T(8,128)(2,1)} %param.54) | copy-start | bytes 46084
  764.6 534.0 %all-gather.27.cloned.1.call-start = ((), (), s32[]{:S(2)}) async-start(), calls=%async_computation.21 | async-start | bytes 8847360 | tf_op jit(solution)/shard_map/all_gather | solution.py:429
  775.1 28.6 %copy-start.61 = (bf16[1536,40]{0,1:T(8,128)(2,1)}, bf16[1536,40]{0,1:T(8,128)(2,1)S(1)}, u32[]{:S(2)}) copy-start(bf16[1536,40]{0,1:T(8,128)(2,1)S(1)} %reshape.1188) | copy-start | bytes 368644
  790.8 73.2 %copy-start.91 = (s32[7680]{0:T(1024)}, s32[7680]{0:T(1024)S(1)}, u32[]{:S(2)}) copy-start(s32[7680]{0:T(1024)S(1)} %get-tuple-element.413) | copy-start | bytes 92164
  811.0 53.0 %copy-start.80 = (f32[3072]{0:T(1024)}, f32[3072]{0:T(1024)S(1)}, u32[]{:S(2)}) copy-start(f32[3072]{0:T(1024)S(1)} %get-tuple-element.378) | copy-start | bytes 36868
  811.5 52.5 %copy-start.16 = (f32[3072,8]{1,0:T(8,128)}, f32[3072,8]{1,0:T(8,128)S(1)}, u32[]{:S(2)}) copy-start(f32[3072,8]{1,0:T(8,128)S(1)} %copy.585) | copy-start | bytes 294916
  1060.6 252.3 %reduce-scatter.19.cloned.1.call-start = ((), (), s32[]{:S(2)}) async-start(), calls=%async_computation.22 | async-start | bytes 11796480 | tf_op jit(solution)/shard_map/reduce_scatter | solution.py:432
  1072.3 403.7 %reduce-scatter.21.cloned.1.call-start = ((), (), s32[]{:S(2)}) async-start(), calls=%async_computation.23 | async-start | bytes 11796480 | tf_op jit(solution)/shard_map/reduce_scatter | solution.py:480
  1116.2 35.2 %copy-start.92 = (s32[7680]{0:T(1024)S(1)}, s32[7680]{0:T(1024)}, u32[]{:S(2)}) copy-start(s32[7680]{0:T(1024)} %copy-done.91) | copy-start | bytes 92164
  1220.6 71.8 %copy-start.17 = (f32[3072,8]{1,0:T(8,128)S(1)}, f32[3072,8]{1,0:T(8,128)}, u32[]{:S(2)}) copy-start(f32[3072,8]{1,0:T(8,128)} %copy-done.16) | copy-start | bytes 294916
  1220.6 71.9 %copy-start.81 = (f32[3072]{0:T(1024)S(1)}, f32[3072]{0:T(1024)}, u32[]{:S(2)}) copy-start(f32[3072]{0:T(1024)} %copy-done.80) | copy-start | bytes 36868
  1324.7 151.3 %copy-start.96 = (f32[1536]{0:T(1024)S(1)}, f32[1536]{0:T(1024)}, u32[]{:S(2)}) copy-start(f32[1536]{0:T(1024)} %copy-done.95) | copy-start | bytes 18436
  1324.7 151.3 %copy-start.101 = (f32[768]{0:T(1024)S(1)}, f32[768]{0:T(1024)}, u32[]{:S(2)}) copy-start(f32[768]{0:T(1024)} %copy-done.100) | copy-start | bytes 9220
  1346.5 134.1 %copy-start.25 = (bf16[768,1536]{1,0:T(8,128)(2,1)S(1)}, bf16[768,1536]{1,0:T(8,128)(2,1)}, u32[]{:S(2)}) copy-start(bf16[768,1536]{1,0:T(8,128)(2,1)} %param.44) | copy-start | bytes 7077892
  1492.2 58.4 %all-to-all-start.1 = ((bf16[768,4,384]{2,0,1:T(8,128)(2,1)}), bf16[768,4,384]{2,0,1:T(8,128)(2,1)S(1)}, u32[]{:S(2)}, u32[]{:S(2)}) async-start(bf16[768,4,384]{2,0,1:T(8,128)(2,1)} %bitcast.535), calls=%async_computation.3 | async-start | bytes 4718592 | tf_op jit(solution)/shard_map/all_to_all | solution.py:491
  1496.8 89.1 %reduce-scatter.31.cloned.1.call-start = ((), (), s32[]{:S(2)}) async-start(), calls=%async_computation.28 | async-start | bytes 884736
  1551.8 91.4 %reduce-scatter.29.cloned.1.call-start = ((), (), s32[]{:S(2)}) async-start(), calls=%async_computation.27 | async-start | bytes 5308416 | tf_op jit(solution)/shard_map/reduce_scatter | solution.py:512
  1561.0 492.2 %reduce-scatter.33.cloned.1.call-start = ((), (), s32[]{:S(2)}) async-start(), calls=%async_computation.29 | async-start | bytes 122880
  1586.0 470.0 %reduce-scatter.35.cloned.1.call-start = ((), (), s32[]{:S(2)}) async-start(), calls=%async_computation.30 | async-start | bytes 983040
  1645.6 412.2 %reduce-scatter.23.cloned.1.call-start = ((), (), s32[]{:S(2)}) async-start(), calls=%async_computation.24 | async-start | bytes 17694720 | tf_op jit(solution)/shard_map/reduce_scatter | solution.py:290
  1646.2 415.6 %reduce-scatter.25.cloned.1.call-start = ((), (), s32[]{:S(2)}) async-start(), calls=%async_computation.25 | async-start | bytes 17694720 | tf_op jit(solution)/shard_map/reduce_scatter | solution.py:291
  1652.2 19.5 copy-start.47
  1654.9 35.7 %copy-start.39 = (bf16[512,384]{0,1:T(8,128)(2,1)}, bf16[512,384]{0,1:T(8,128)(2,1)S(1)}, u32[]{:S(2)}) copy-start(bf16[512,384]{0,1:T(8,128)(2,1)S(1)} %copy.604) | copy-start | bytes 1179652
  1656.2 73.0 %copy-start.37 = (bf16[512,384]{0,1:T(8,128)(2,1)}, bf16[512,384]{0,1:T(8,128)(2,1)S(1)}, u32[]{:S(2)}) copy-start(bf16[512,384]{0,1:T(8,128)(2,1)S(1)} %copy.606) | copy-start | bytes 1179652
  1656.4 112.8 %copy-start.30 = (bf16[512,384]{0,1:T(8,128)(2,1)}, bf16[512,384]{0,1:T(8,128)(2,1)S(1)}, u32[]{:S(2)}) copy-start(bf16[512,384]{0,1:T(8,128)(2,1)S(1)} %copy.608) | copy-start | bytes 1179652
  1656.6 178.0 %copy-start.28 = (bf16[512,384]{0,1:T(8,128)(2,1)}, bf16[512,384]{0,1:T(8,128)(2,1)S(1)}, u32[]{:S(2)}) copy-start(bf16[512,384]{0,1:T(8,128)(2,1)S(1)} %copy.610) | copy-start | bytes 1179652
  1656.7 409.1 %reduce-scatter.27.cloned.1.call-start = ((), (), s32[]{:S(2)}) async-start(), calls=%async_computation.26 | async-start | bytes 17694720 | tf_op jit(solution)/shard_map/reduce_scatter | solution.py:293
  1657.7 14.1 slice-start.6
  1657.7 14.1 slice-start.7
  1917.5 18.7 slice-start.9
  1920.0 16.2 slice-start.10
  2034.7 93.3 %all-to-all-start.2 = ((bf16[4,768,640]{1,2,0:T(8,128)(2,1)}), bf16[4,768,640]{1,2,0:T(8,128)(2,1)}, u32[]{:S(2)}, u32[]{:S(2)}) async-start(bf16[4,768,640]{1,2,0:T(8,128)(2,1)} %copy.624), calls=%async_computation.4 | async-start | bytes 7864320 | tf_op jit(solution)/shard_map/all_to_all | solution.py:560
  2039.9 143.7 %reduce-scatter.37.cloned.1.call-start = ((), (), s32[]{:S(2)}) async-start(), calls=%async_computation.31 | async-start | bytes 2211840
  2128.0 15.6 copy-start.127
  2128.0 17.5 copy-start.94
  2128.0 17.5 copy-start.123
  (100 other events, 610.0 us)
Sparse Core Ops, SparseCore 0:
  33.7 166.1 all-gather.10
  201.7 22.0 all-gather.12
  225.8 86.2 all-gather.14
  313.8 85.2 all-gather.16
  400.8 38.7 all-gather.18
  513.9 165.2 all-gather.20
  681.1 83.4 all-gather.22
  766.2 166.7 all-gather.24
  1060.7 50.7 all-gather.26
  1113.7 161.1 reduce-scatter.18
  1317.6 158.4 reduce-scatter.20
  1551.9 33.9 reduce-scatter.30
  1589.4 53.7 reduce-scatter.28
  1645.3 19.3 reduce-scatter.32
  1666.9 21.3 reduce-scatter.34
  1691.6 106.8 reduce-scatter.22
  1801.9 107.3 reduce-scatter.24
  1912.6 107.3 reduce-scatter.26
  2143.8 39.8 reduce-scatter.36
